TPU v7x, 32 devices: a whole 2x2x4 slice. The times are simulated.
32 devices in a mesh: dp: 8 (over z, y), tensor: 4 (over x, core).
Axes of the slice: x: 2, y: 2, z: 4, core: 2. Of those that a mesh axis runs over, the one named last changes fastest.
Arguments:
- inputs: bfloat16 [8, 1024, 2048], P('dp', 'tensor'), may hold values from -6 to 6
- cotangent: bfloat16 [8, 1024, 2048], P('dp', 'tensor'), may hold values from -6 to 6
- lengths: int32 [8], P('dp'), may hold values from 256 to 1024, as said below
- norm1_gain: float32 [2048], replicated, may hold values from 0.5 to 1.5
- w_query: bfloat16 [2048, 2048], P('dp', 'tensor'), may hold values from -0.125 to 0.125
- w_key: bfloat16 [2048, 2048], P('dp', 'tensor'), may hold values from -0.125 to 0.125
- w_value: bfloat16 [2048, 4096], P('dp', 'tensor'), may hold values from -0.125 to 0.125
- w_outgate: bfloat16 [2048, 4096], P('dp', 'tensor'), may hold values from -0.125 to 0.125
- w_beta: bfloat16 [2048, 16], P('dp', 'tensor'), may hold values from -0.125 to 0.125
- w_alpha: bfloat16 [2048, 16], P('dp', 'tensor'), may hold values from -0.125 to 0.125
- conv_query: bfloat16 [128, 16, 4], P('dp', 'tensor'), may hold values from -3 to 3
- conv_key: bfloat16 [128, 16, 4], P('dp', 'tensor'), may hold values from -3 to 3
- conv_value: bfloat16 [256, 16, 4], P('dp', 'tensor'), may hold values from -3 to 3
- a_log: float32 [16], replicated, may hold values from -6.5 to -3
- dt_bias: float32 [16], replicated, may hold values from -1.5 to 0.5
- head_gain: float32 [256], replicated, may hold values from 0.5 to 1.5
- w_out: bfloat16 [2048, 4096], P('dp', 'tensor'), may hold values from -0.125 to 0.125
- norm2_gain: float32 [2048], replicated, may hold values from 0.5 to 1.5
- w_gate: bfloat16 [2048, 5632], P('dp', 'tensor'), may hold values from -0.125 to 0.125
- w_up: bfloat16 [2048, 5632], P('dp', 'tensor'), may hold values from -0.125 to 0.125
- w_down: bfloat16 [2048, 5632], P('dp', 'tensor'), may hold values from -0.109375 to 0.109375
Outputs:
- outputs: bfloat16 [8, 1024, 2048], P('dp', 'tensor')
- grad_inputs: float32 [8, 1024, 2048], P('dp', 'tensor')
- grad_norm1: float32 [2048], replicated
- grad_query: float32 [2048, 2048], P('dp', 'tensor')
- grad_key: float32 [2048, 2048], P('dp', 'tensor')
- grad_value: float32 [2048, 4096], P('dp', 'tensor')
- grad_outgate: float32 [2048, 4096], P('dp', 'tensor')
- grad_beta: float32 [2048, 16], P('dp', 'tensor')
- grad_alpha: float32 [2048, 16], P('dp', 'tensor')
- grad_convq: float32 [128, 16, 4], P('dp', 'tensor')
- grad_convk: float32 [128, 16, 4], P('dp', 'tensor')
- grad_convv: float32 [256, 16, 4], P('dp', 'tensor')
- grad_alog: float32 [16], replicated
- grad_dtbias: float32 [16], replicated
- grad_headgain: float32 [256], replicated
- grad_out: float32 [2048, 4096], P('dp', 'tensor')
- grad_norm2: float32 [2048], replicated
- grad_gate: float32 [2048, 5632], P('dp', 'tensor')
- grad_up: float32 [2048, 5632], P('dp', 'tensor')
- grad_down: float32 [2048, 5632], P('dp', 'tensor')
Inputs may be any that keep to these rules, and one draw needn't show every extreme that they name: `lengths`: each sequence's valid tokens start at its slot's first position; in every draw some sequence fills its whole slot of 1024 positions.
All inputs are finite; a program needn't handle non-finite values.
Results may differ from a plain program's by a relative error of at most 0.025.
Values may be sent and summed in bfloat16 or wider, within the bound.
A program may use at most 320 MiB of HBM per device.

v0:
```python
import jax
import jax.numpy as jnp
from jax import lax
from jax.sharding import PartitionSpec as P

BLOCK = 64


def plain_dot(left_mat, right_mat):
    return jnp.dot(left_mat, right_mat, preferred_element_type=jnp.float32)


def dot_rows(left_mat, right_mat):
    return lax.dot_general(
        left_mat, right_mat, (((1,), (1,)), ((), ())), preferred_element_type=jnp.float32
    )


def dot_tokens(left_mat, right_mat):
    return lax.dot_general(
        left_mat, right_mat, (((0,), (0,)), ((), ())), preferred_element_type=jnp.float32
    )


def rms_apply(values, gain_vec):
    return values * lax.rsqrt(jnp.mean(values * values, axis=-1, keepdims=True) + 1e-05) * gain_vec


def unit_rows(values):
    return values * lax.rsqrt(jnp.sum(values * values, axis=-1, keepdims=True) + 1e-06)


def swiglu(gate_pre, up_pre):
    return jax.nn.silu(gate_pre) * up_pre


def short_conv(values, weight):
    tap_count = weight.shape[2]
    row_count = values.shape[0]
    tap_table = jnp.transpose(weight, (1, 0, 2)).reshape(-1, tap_count)
    padded = jnp.pad(values, ((tap_count - 1, 0), (0, 0)))
    summed = padded[0:row_count] * tap_table[:, 0]
    for tap_index in range(1, tap_count):
        summed = summed + padded[tap_index : tap_index + row_count] * tap_table[:, tap_index]
    return jax.nn.silu(summed)


def block_step(carry_state, pieces):
    query_rows, key_rows, value_rows, beta_rows, decay_rows = pieces
    running = jnp.cumsum(decay_rows, axis=0)
    query_h = jnp.transpose(query_rows, (1, 0, 2))
    key_h = jnp.transpose(key_rows, (1, 0, 2))
    value_h = jnp.transpose(value_rows, (1, 0, 2))
    beta_h = jnp.transpose(beta_rows)
    cum_h = jnp.transpose(running)
    size_c = query_rows.shape[0]
    pos_row = lax.broadcasted_iota(jnp.int32, (size_c, size_c), 0)
    pos_col = lax.broadcasted_iota(jnp.int32, (size_c, size_c), 1)
    lower_inc = pos_row >= pos_col
    lower_strict = pos_row > pos_col
    differ = cum_h[:, :, None] - cum_h[:, None, :]
    within = jnp.where(lower_inc, jnp.exp(jnp.where(lower_inc, differ, 0.0)), 0.0)
    key_key = jnp.einsum("htd,hjd->htj", key_h, key_h, preferred_element_type=jnp.float32)
    coupling = jnp.where(lower_strict, beta_h[:, :, None] * within * key_key, 0.0)
    start_decay = jnp.exp(cum_h)
    key_state = jnp.einsum("htd,hde->hte", key_h, carry_state, preferred_element_type=jnp.float32)
    right_side = beta_h[:, :, None] * value_h - (beta_h * start_decay)[:, :, None] * key_state
    identity_mat = jnp.eye(size_c, dtype=jnp.float32)
    new_values = jax.scipy.linalg.solve_triangular(
        identity_mat + coupling, right_side, lower=True, unit_diagonal=True
    )
    query_key = jnp.einsum("htd,hjd->htj", query_h, key_h, preferred_element_type=jnp.float32)
    query_state = jnp.einsum(
        "htd,hde->hte", query_h, carry_state, preferred_element_type=jnp.float32
    )
    output = start_decay[:, :, None] * query_state + jnp.einsum(
        "htj,hje->hte", query_key * within, new_values, preferred_element_type=jnp.float32
    )
    end_decay = cum_h[:, -1]
    tail_decay = jnp.exp(end_decay[:, None] - cum_h)
    carry_state = jnp.exp(end_decay)[:, None, None] * carry_state + jnp.einsum(
        "hjd,hje->hde",
        key_h * tail_decay[:, :, None],
        new_values,
        preferred_element_type=jnp.float32,
    )
    return (carry_state, jnp.transpose(output, (1, 0, 2)))


def delta_rule(query_rows, key_rows, value_rows, beta_rows, decay_rows):
    row_count, heads_n, key_size = query_rows.shape
    value_size = value_rows.shape[2]
    blocks = row_count // BLOCK

    def to_blocks(array_in):
        return array_in.reshape((blocks, BLOCK) + array_in.shape[1:])

    carry_state = jnp.zeros((heads_n, key_size, value_size), jnp.float32)
    unused, outputs = lax.scan(
        jax.checkpoint(block_step),
        carry_state,
        (
            to_blocks(query_rows),
            to_blocks(key_rows),
            to_blocks(value_rows),
            to_blocks(beta_rows),
            to_blocks(decay_rows),
        ),
    )
    return outputs.reshape(row_count, heads_n, value_size)


def mixer_core(
    q_raw, k_raw, v_raw, og_raw, b_raw, a_raw, conv_q, conv_k, conv_v, a_log, dt_bias, head_gain
):
    row_count = q_raw.shape[0]
    heads_n = a_log.shape[0]
    key_size = conv_q.shape[0]
    value_size = conv_v.shape[0]
    query_rows = unit_rows(
        short_conv(q_raw, conv_q).reshape(row_count, heads_n, key_size)
    ) * key_size ** (-0.5)
    key_rows = unit_rows(short_conv(k_raw, conv_k).reshape(row_count, heads_n, key_size))
    value_rows = short_conv(v_raw, conv_v).reshape(row_count, heads_n, value_size)
    beta_rows = jax.nn.sigmoid(b_raw)
    decay_rows = -jnp.exp(a_log) * jax.nn.softplus(a_raw + dt_bias)
    delta_out = delta_rule(query_rows, key_rows, value_rows, beta_rows, decay_rows)
    normed = rms_apply(delta_out, head_gain) * jax.nn.silu(
        og_raw.reshape(row_count, heads_n, value_size)
    )
    return normed.reshape(row_count, heads_n * value_size)


def shards(
    inputs,
    cotangent,
    lengths,
    norm1_gain,
    w_query,
    w_key,
    w_value,
    w_outgate,
    w_beta,
    w_alpha,
    conv_query,
    conv_key,
    conv_value,
    a_log,
    dt_bias,
    head_gain,
    w_out,
    norm2_gain,
    w_gate,
    w_up,
    w_down,
):
    local_rows = inputs[0].astype(jnp.float32)
    row_count = local_rows.shape[0]
    tensor_pos = lax.axis_index("tensor")
    positions = tensor_pos * row_count + jnp.arange(row_count, dtype=jnp.int32)
    valid_rows = (positions < lengths[0]).astype(jnp.float32)[:, None]
    (
        full_query,
        full_key,
        full_value,
        full_outgate,
        full_beta,
        full_alpha,
        full_out,
        full_gate,
        full_up,
        full_down,
        whole_convq,
        whole_convk,
        whole_convv,
    ) = (
        lax.all_gather(w_query, "dp", axis=0, tiled=True),
        lax.all_gather(w_key, "dp", axis=0, tiled=True),
        lax.all_gather(w_value, "dp", axis=0, tiled=True),
        lax.all_gather(w_outgate, "dp", axis=0, tiled=True),
        lax.all_gather(w_beta, "dp", axis=0, tiled=True),
        lax.all_gather(w_alpha, "dp", axis=0, tiled=True),
        lax.all_gather(w_out, "dp", axis=0, tiled=True),
        lax.all_gather(w_gate, "dp", axis=0, tiled=True),
        lax.all_gather(w_up, "dp", axis=0, tiled=True),
        lax.all_gather(w_down, "dp", axis=0, tiled=True),
        lax.all_gather(conv_query, "dp", axis=0, tiled=True),
        lax.all_gather(conv_key, "dp", axis=0, tiled=True),
        lax.all_gather(conv_value, "dp", axis=0, tiled=True),
    )
    heads_local = w_beta.shape[1]
    head_start = tensor_pos * heads_local
    alog_local = lax.dynamic_slice_in_dim(a_log, head_start, heads_local)
    dtb_local = lax.dynamic_slice_in_dim(dt_bias, head_start, heads_local)
    normed_one, norm_one_back = jax.vjp(rms_apply, local_rows, norm1_gain)
    rows_one = lax.all_gather(normed_one.astype(jnp.bfloat16), "tensor", axis=0, tiled=True)
    q_raw = plain_dot(rows_one, full_query)
    k_raw = plain_dot(rows_one, full_key)
    v_raw = plain_dot(rows_one, full_value)
    og_raw = plain_dot(rows_one, full_outgate)
    b_raw = plain_dot(rows_one, full_beta)
    a_raw = plain_dot(rows_one, full_alpha)
    head_out, core_back = jax.vjp(
        mixer_core,
        q_raw,
        k_raw,
        v_raw,
        og_raw,
        b_raw,
        a_raw,
        whole_convq.astype(jnp.float32),
        whole_convk.astype(jnp.float32),
        whole_convv.astype(jnp.float32),
        alog_local,
        dtb_local,
        head_gain,
    )
    head_bf = head_out.astype(jnp.bfloat16)
    part_rows = head_bf
    mixed_rows = lax.psum_scatter(
        dot_rows(part_rows, full_out), "tensor", scatter_dimension=0, tiled=True
    )
    after_mix = local_rows + mixed_rows
    normed_two, norm_two_back = jax.vjp(rms_apply, after_mix, norm2_gain)
    rows_two = lax.all_gather(normed_two.astype(jnp.bfloat16), "tensor", axis=0, tiled=True)
    gate_pre = plain_dot(rows_two, full_gate)
    up_pre = plain_dot(rows_two, full_up)
    hidden, swiglu_back = jax.vjp(swiglu, gate_pre, up_pre)
    hidden_bf = hidden.astype(jnp.bfloat16)
    part_rows = hidden_bf
    ffn_part = lax.psum_scatter(
        dot_rows(part_rows, full_down).astype(jnp.bfloat16),
        "tensor",
        scatter_dimension=0,
        tiled=True,
    ).astype(jnp.float32)
    after_ffn = after_mix + ffn_part
    outputs = (after_ffn * valid_rows).astype(jnp.bfloat16)[None]
    (
        back_query,
        back_key,
        back_value,
        back_outgate,
        back_beta,
        back_alpha,
        back_out,
        back_gate,
        back_up,
        back_down,
    ) = (
        lax.all_gather(w_query, "dp", axis=0, tiled=True),
        lax.all_gather(w_key, "dp", axis=0, tiled=True),
        lax.all_gather(w_value, "dp", axis=0, tiled=True),
        lax.all_gather(w_outgate, "dp", axis=0, tiled=True),
        lax.all_gather(w_beta, "dp", axis=0, tiled=True),
        lax.all_gather(w_alpha, "dp", axis=0, tiled=True),
        lax.all_gather(w_out, "dp", axis=0, tiled=True),
        lax.all_gather(w_gate, "dp", axis=0, tiled=True),
        lax.all_gather(w_up, "dp", axis=0, tiled=True),
        lax.all_gather(w_down, "dp", axis=0, tiled=True),
    )
    grad_after = valid_rows * cotangent[0].astype(jnp.float32)
    grad_ffn = grad_after.astype(jnp.bfloat16)
    incoming = lax.all_gather(grad_ffn, "tensor", axis=0, tiled=True)
    grad_hidden = plain_dot(incoming, back_down)
    grad_down_w = dot_tokens(incoming, hidden_bf)
    grad_hidden, grad_down_w = (grad_hidden, grad_down_w)
    grad_gate_pre, grad_up_pre = swiglu_back(grad_hidden)
    gate_low = grad_gate_pre.astype(jnp.bfloat16)
    up_low = grad_up_pre.astype(jnp.bfloat16)
    grad_gate_w = dot_tokens(rows_two, gate_low)
    grad_up_w = dot_tokens(rows_two, up_low)
    grad_normed_two = lax.psum_scatter(
        dot_rows(gate_low, back_gate) + dot_rows(up_low, back_up),
        "tensor",
        scatter_dimension=0,
        tiled=True,
    )
    grad_mid, grad_norm2 = norm_two_back(grad_normed_two)
    grad_mid = grad_mid + grad_after
    grad_mix = grad_mid.astype(jnp.bfloat16)
    incoming = lax.all_gather(grad_mix, "tensor", axis=0, tiled=True)
    grad_head = plain_dot(incoming, back_out)
    grad_out_w = dot_tokens(incoming, head_bf)
    grad_head, grad_out_w = (grad_head, grad_out_w)
    (
        grad_q_f,
        grad_k_f,
        grad_v_f,
        grad_og_f,
        grad_b_f,
        grad_a_f,
        grad_cq,
        grad_ck,
        grad_cv,
        grad_alog_local,
        grad_dtb_local,
        grad_head_gain,
    ) = core_back(grad_head)
    grad_q_low = grad_q_f.astype(jnp.bfloat16)
    grad_k_low = grad_k_f.astype(jnp.bfloat16)
    grad_v_low = grad_v_f.astype(jnp.bfloat16)
    grad_og_low = grad_og_f.astype(jnp.bfloat16)
    grad_b_low = grad_b_f.astype(jnp.bfloat16)
    grad_a_low = grad_a_f.astype(jnp.bfloat16)
    grad_query_w = dot_tokens(rows_one, grad_q_low)
    grad_key_w = dot_tokens(rows_one, grad_k_low)
    grad_value_w = dot_tokens(rows_one, grad_v_low)
    grad_outgate_w = dot_tokens(rows_one, grad_og_low)
    grad_beta_w = dot_tokens(rows_one, grad_b_low)
    grad_alpha_w = dot_tokens(rows_one, grad_a_low)
    summed = dot_rows(grad_q_low, back_query) + dot_rows(grad_k_low, back_key)
    summed = summed + dot_rows(grad_v_low, back_value) + dot_rows(grad_og_low, back_outgate)
    grad_normed_one = lax.psum_scatter(
        (summed + dot_rows(grad_b_low, back_beta) + dot_rows(grad_a_low, back_alpha)).astype(
            jnp.bfloat16
        ),
        "tensor",
        scatter_dimension=0,
        tiled=True,
    ).astype(jnp.float32)
    grad_first, grad_norm1 = norm_one_back(grad_normed_one)
    grad_inputs = (grad_mid + grad_first)[None]
    all_shards = (
        lax.psum_scatter(
            grad_query_w.astype(jnp.bfloat16), "dp", scatter_dimension=0, tiled=True
        ).astype(jnp.float32),
        lax.psum_scatter(
            grad_key_w.astype(jnp.bfloat16), "dp", scatter_dimension=0, tiled=True
        ).astype(jnp.float32),
        lax.psum_scatter(
            grad_value_w.astype(jnp.bfloat16), "dp", scatter_dimension=0, tiled=True
        ).astype(jnp.float32),
        lax.psum_scatter(
            grad_outgate_w.astype(jnp.bfloat16), "dp", scatter_dimension=0, tiled=True
        ).astype(jnp.float32),
        lax.psum_scatter(
            grad_beta_w.astype(jnp.bfloat16), "dp", scatter_dimension=0, tiled=True
        ).astype(jnp.float32),
        lax.psum_scatter(
            grad_alpha_w.astype(jnp.bfloat16), "dp", scatter_dimension=0, tiled=True
        ).astype(jnp.float32),
        lax.psum_scatter(
            grad_out_w.astype(jnp.bfloat16), "dp", scatter_dimension=0, tiled=True
        ).astype(jnp.float32),
        lax.psum_scatter(
            grad_cq.astype(jnp.bfloat16), "dp", scatter_dimension=0, tiled=True
        ).astype(jnp.float32),
        lax.psum_scatter(
            grad_ck.astype(jnp.bfloat16), "dp", scatter_dimension=0, tiled=True
        ).astype(jnp.float32),
        lax.psum_scatter(
            grad_cv.astype(jnp.bfloat16), "dp", scatter_dimension=0, tiled=True
        ).astype(jnp.float32),
        lax.psum_scatter(
            grad_gate_w.astype(jnp.bfloat16), "dp", scatter_dimension=0, tiled=True
        ).astype(jnp.float32),
        lax.psum_scatter(
            grad_up_w.astype(jnp.bfloat16), "dp", scatter_dimension=0, tiled=True
        ).astype(jnp.float32),
        lax.psum_scatter(
            grad_down_w.astype(jnp.bfloat16), "dp", scatter_dimension=0, tiled=True
        ).astype(jnp.float32),
    )
    alog_full = lax.dynamic_update_slice_in_dim(
        jnp.zeros_like(a_log), grad_alog_local, head_start, 0
    )
    dtb_full = lax.dynamic_update_slice_in_dim(
        jnp.zeros_like(dt_bias), grad_dtb_local, head_start, 0
    )
    small_sums = lax.psum(
        (grad_norm1, grad_norm2, grad_head_gain, alog_full, dtb_full), ("dp", "tensor")
    )
    return (
        outputs,
        grad_inputs,
        small_sums[0],
        all_shards[0],
        all_shards[1],
        all_shards[2],
        all_shards[3],
        all_shards[4],
        all_shards[5],
        all_shards[7],
        all_shards[8],
        all_shards[9],
        small_sums[3],
        small_sums[4],
        small_sums[2],
        all_shards[6],
        small_sums[1],
        all_shards[10],
        all_shards[11],
        all_shards[12],
    )


def solution(mesh):
    in_specs = (
        P("dp", "tensor", None),
        P("dp", "tensor", None),
        P("dp"),
        P(),
        P("dp", "tensor"),
        P("dp", "tensor"),
        P("dp", "tensor"),
        P("dp", "tensor"),
        P("dp", "tensor"),
        P("dp", "tensor"),
        P("dp", "tensor", None),
        P("dp", "tensor", None),
        P("dp", "tensor", None),
        P(),
        P(),
        P(),
        P("dp", "tensor"),
        P(),
        P("dp", "tensor"),
        P("dp", "tensor"),
        P("dp", "tensor"),
    )
    out_specs = (
        P("dp", "tensor", None),
        P("dp", "tensor", None),
        P(),
        P("dp", "tensor"),
        P("dp", "tensor"),
        P("dp", "tensor"),
        P("dp", "tensor"),
        P("dp", "tensor"),
        P("dp", "tensor"),
        P("dp", "tensor", None),
        P("dp", "tensor", None),
        P("dp", "tensor", None),
        P(),
        P(),
        P(),
        P("dp", "tensor"),
        P(),
        P("dp", "tensor"),
        P("dp", "tensor"),
        P("dp", "tensor"),
    )
    return jax.shard_map(shards, mesh=mesh, in_specs=in_specs, out_specs=out_specs, check_vma=False)
```

profile of v0, /device:TPU:14, one launch (start us, length us, event | category | flops | bytes accessed | tf_op | source)
XLA Modules:
  0.0 2828.8 jit_solution(6911755327145607036)
XLA Ops:
  16.0 28.4 %all_gather.64 = bf16[128,4,4]{2,1,0:T(4,128)(2,1)S(1)} all-gather(bf16[16,4,4]{2,1,0:T(4,128)(2,1)S(1)} %copy.363), channel_id=1, replica_groups=mesh['dp'=8,'tensor'=4] {'dp'}, dimensions={0}, use_global_device_ids=true | all-gather | bytes 4608 | tf_op jit(solution)/shard_map/all_gather | solution.py:188
  44.8 30.8 %all_gather.69 = bf16[128,4,4]{2,1,0:T(4,128)(2,1)S(1)} all-gather(bf16[16,4,4]{2,1,0:T(4,128)(2,1)S(1)} %copy.370), channel_id=1, replica_groups=mesh['dp'=8,'tensor'=4] {'dp'}, dimensions={0}, use_global_device_ids=true | all-gather | bytes 4608 | tf_op jit(solution)/shard_map/all_gather | solution.py:187
  76.0 27.5 all_gather.62
  103.6 28.4 %all_gather.67 = bf16[256,4,4]{2,1,0:T(4,128)(2,1)S(1)} all-gather(bf16[32,4,4]{2,1,0:T(4,128)(2,1)S(1)} %copy.368), channel_id=1, replica_groups=mesh['dp'=8,'tensor'=4] {'dp'}, dimensions={0}, use_global_device_ids=true | all-gather | bytes 9216 | tf_op jit(solution)/shard_map/all_gather | solution.py:189
  132.4 27.5 all_gather.65
  203.9 18.2 all-gather.17.cloned.1.call-done
  245.0 475.4 %while.44 = (s32[]{:T(128)}, f32[4,128,256]{2,1,0:T(8,128)S(1)}, f32[16,64,4,256]{3,1,2,0:T(8,128)}, f32[16,4,128,256]{3,2,1,0:T(8,128)}, f32[16,64,4]{2,1,0:T(8...) while((s32[]{:T(128)}, f32[4,128,256]{2,1,0:T(8,128)S(1)}, ...), condition=%wide.region_5.7_spmd.clone.clone, body=%wide.region_3.6_spmd.clone.clone.sunk | while | flops 118853952 | bytes 5871870 | solution.py:99
  248.1 19.7 custom-call.27
  277.9 19.7 custom-call.27
  307.6 19.7 custom-call.27
  337.3 19.7 custom-call.27
  367.0 19.7 custom-call.27
  396.7 19.7 custom-call.27
  426.4 19.7 custom-call.27
  456.1 19.7 custom-call.27
  485.8 19.7 custom-call.27
  515.5 19.7 custom-call.27
  545.3 19.7 custom-call.27
  575.0 19.7 custom-call.27
  604.7 19.7 custom-call.27
  634.4 19.7 custom-call.27
  664.1 19.7 custom-call.27
  693.8 19.7 custom-call.27
  737.0 12.8 multiply_convert_fusion.2
  760.3 70.1 %reduce-scatter.28.cloned.1.call-done = f32[256,2048]{1,0:T(8,128)} async-done(((f32[1024,2048]{1,0:T(8,128)}), f32[256,2048]{1,0:T(8,128)}) %reduce-scatter.28.cloned.1.call-update) | async-done | bytes 2097168 | tf_op jit(solution)/shard_map/reduce_scatter | solution.py:220
  836.7 87.4 %all-gather.27.cloned.1.call-done = bf16[2048,1408]{1,0:T(8,128)(2,1)} async-done(((bf16[256,1408]{1,0:T(8,128)(2,1)}), bf16[2048,1408]{1,0:T(8,128)(2,1)}) %all-gather.27.cloned.1.call-update) | async-done | bytes 5767184 | tf_op jit(solution)/shard_map/all_gather | solution.py:184
  924.2 36.2 %all-gather.25.cloned.1.call-done = bf16[1024,2048]{1,0:T(8,128)(2,1)} async-done(((bf16[256,2048]{1,0:T(8,128)(2,1)}), bf16[1024,2048]{1,0:T(8,128)(2,1)}) %all-gather.25.cloned.1.call-update) | async-done | bytes 4194320 | tf_op jit(solution)/shard_map/all_gather | solution.py:225
  960.3 11.8 fusion.240
  972.2 81.9 %all-gather.29.cloned.1.call-done = bf16[2048,1408]{1,0:T(8,128)(2,1)} async-done(((bf16[256,1408]{1,0:T(8,128)(2,1)}), bf16[2048,1408]{1,0:T(8,128)(2,1)}) %all-gather.29.cloned.1.call-update) | async-done | bytes 5767184 | tf_op jit(solution)/shard_map/all_gather | solution.py:185
  1054.0 11.7 fusion.241
  1065.7 24.5 all-gather.33.cloned.1.call-done
  1090.2 93.7 %all-gather.31.cloned.1.call-done = bf16[2048,1408]{1,0:T(8,128)(2,1)} async-done(((bf16[256,1408]{1,0:T(8,128)(2,1)}), bf16[2048,1408]{1,0:T(8,128)(2,1)}) %all-gather.31.cloned.1.call-update) | async-done | bytes 5767184 | tf_op jit(solution)/shard_map/all_gather | solution.py:186
  1183.9 15.5 multiply_convert_fusion
  1230.7 60.0 %reduce-scatter.32.cloned.1.call-done = f32[256,2048]{1,0:T(8,128)} async-done(((f32[1024,2048]{1,0:T(8,128)}), f32[256,2048]{1,0:T(8,128)}) %reduce-scatter.32.cloned.1.call-update) | async-done | bytes 2097168 | tf_op jit(solution)/shard_map/reduce_scatter | solution.py:273
  1293.4 44.2 %reduce-scatter.30.cloned.1.call-done = bf16[256,2048]{1,0:T(8,128)(2,1)} async-done(((bf16[1024,2048]{1,0:T(8,128)(2,1)}), bf16[256,2048]{1,0:T(8,128)(2,1)}) %reduce-scatter.30.cloned.1.call-update) | async-done | bytes 1048592 | tf_op jit(solution)/shard_map/reduce_scatter | solution.py:231
  1385.1 15.8 fusion.154
  1424.7 588.7 %while.43 = (s32[]{:T(128)}, f32[4,128,256]{2,1,0:T(8,128)S(1)}, f32[16,64,4,128]{3,1,2,0:T(8,128)}, f32[16,64,4,128]{3,1,2,0:T(8,128)}, f32[16,64,4,256]{3,2,1,...) while((s32[]{:T(128)}, f32[4,128,256]{2,1,0:T(8,128)S(1)}, ...), condition=%wide.region_25.27_spmd.clone, body=%wide.region_13.26_spmd.clone.sunk | while | flops 342849856 | bytes 21298192 | solution.py:99
  1430.8 19.7 custom-call.26
  1467.6 19.7 custom-call.26
  1504.3 19.7 custom-call.26
  1541.1 19.7 custom-call.26
  1577.9 19.7 custom-call.26
  1614.7 19.7 custom-call.26
  1651.5 19.7 custom-call.26
  1688.3 19.7 custom-call.26
  1725.1 19.7 custom-call.26
  1761.9 19.7 custom-call.26
  1798.6 19.7 custom-call.26
  1835.4 19.7 custom-call.26
  1872.2 19.7 custom-call.26
  1908.9 19.7 custom-call.26
  1945.7 19.7 custom-call.26
  1982.5 19.7 custom-call.26
  2145.1 16.4 add_convert_fusion
  2180.4 42.9 %reduce-scatter.60.cloned.1.call-done = bf16[32,16]{1,0:T(8,128)(2,1)} async-done(((bf16[256,16]{1,0:T(8,128)(2,1)}), bf16[32,16]{1,0:T(8,128)(2,1)}) %reduce-scatter.60.cloned.1.call-update) | async-done | bytes 1040
  2224.7 63.8 %reduce-scatter.54.cloned.1.call-done = bf16[256,4]{1,0:T(8,128)(2,1)} async-done(((bf16[2048,4]{1,0:T(8,128)(2,1)}), bf16[256,4]{1,0:T(8,128)(2,1)}) %reduce-scatter.54.cloned.1.call-update) | async-done | bytes 2064
  2290.0 63.4 %reduce-scatter.52.cloned.1.call-done = bf16[256,4]{1,0:T(8,128)(2,1)} async-done(((bf16[2048,4]{1,0:T(8,128)(2,1)}), bf16[256,4]{1,0:T(8,128)(2,1)}) %reduce-scatter.52.cloned.1.call-update) | async-done | bytes 2064
  2354.9 68.6 %reduce-scatter.38.cloned.1.call-done = bf16[256,512]{1,0:T(8,128)(2,1)} async-done(((bf16[2048,512]{1,0:T(8,128)(2,1)}), bf16[256,512]{1,0:T(8,128)(2,1)}) %reduce-scatter.38.cloned.1.call-update) | async-done | bytes 262160 | tf_op jit(solution)/shard_map/reduce_scatter | solution.py:328
  2425.3 68.9 %reduce-scatter.36.cloned.1.call-done = bf16[256,512]{1,0:T(8,128)(2,1)} async-done(((bf16[2048,512]{1,0:T(8,128)(2,1)}), bf16[256,512]{1,0:T(8,128)(2,1)}) %reduce-scatter.36.cloned.1.call-update) | async-done | bytes 262160 | tf_op jit(solution)/shard_map/reduce_scatter | solution.py:325
  2496.0 89.8 %reduce-scatter.44.cloned.1.call-done = bf16[256,1024]{1,0:T(8,128)(2,1)} async-done(((bf16[2048,1024]{1,0:T(8,128)(2,1)}), bf16[256,1024]{1,0:T(8,128)(2,1)}) %reduce-scatter.44.cloned.1.call-update) | async-done | bytes 524304 | tf_op jit(solution)/shard_map/reduce_scatter | solution.py:343
  2587.9 89.0 %reduce-scatter.40.cloned.1.call-done = bf16[256,1024]{1,0:T(8,128)(2,1)} async-done(((bf16[2048,1024]{1,0:T(8,128)(2,1)}), bf16[256,1024]{1,0:T(8,128)(2,1)}) %reduce-scatter.40.cloned.1.call-update) | async-done | bytes 524304 | tf_op jit(solution)/shard_map/reduce_scatter | solution.py:331
  2679.1 43.7 %reduce-scatter.34.cloned.1.call-done = bf16[256,2048]{1,0:T(8,128)(2,1)} async-done(((bf16[1024,2048]{1,0:T(8,128)(2,1)}), bf16[256,2048]{1,0:T(8,128)(2,1)}) %reduce-scatter.34.cloned.1.call-update) | async-done | bytes 1048592 | tf_op jit(solution)/shard_map/reduce_scatter | solution.py:314
  2725.1 43.7 %all-reduce.28 = (f32[2048]{0:T(1024)}, f32[16]{0:T(128)}, f32[16]{0:T(128)}, f32[256]{0:T(256)}, f32[2048]{0:T(1024)}) all-reduce(f32[2048]{0:T(1024)S(1)} %get-tuple-element.756, f32[16]{0:T(128)S(1)} %multiply_dynamic-update-slice_fusion, f32[16]{0:T(128)S(1)} %dynamic_update_slice.68, ...), channel_id=1, replica_groups=mesh['dp'=8,'tensor'=4] {'dp','tensor'}, use_global_device_ids=true, to_apply=%region_31.33 | all-reduce | flops 4384 | bytes 35072 | tf_op jit(solution)/shard_map/psum | solution.py:371
  2768.8 47.9 %reduce-scatter.42.cloned.1.call-done = bf16[256,1024]{1,0:T(8,128)(2,1)} async-done(((bf16[2048,1024]{1,0:T(8,128)(2,1)}), bf16[256,1024]{1,0:T(8,128)(2,1)}) %reduce-scatter.42.cloned.1.call-update) | async-done | bytes 524304 | tf_op jit(solution)/shard_map/reduce_scatter | solution.py:334
  (1622 shorter events, 814.5 us)
Async XLA Ops:
  7.2 152.8 %all-gather.15.cloned.1.call-start = ((), (), s32[]{:S(2)}) async-start(), calls=%async_computation.18 | async-start | bytes 2359296 | tf_op jit(solution)/shard_map/all_gather | solution.py:178
  7.9 152.1 %all-gather.13.cloned.1.call-start = ((), (), s32[]{:S(2)}) async-start(), calls=%async_computation.17 | async-start | bytes 5242880 | tf_op jit(solution)/shard_map/all_gather | solution.py:196
  10.7 33.9 %copy-start.92 = (bf16[16,4,4]{0,2,1:T(4,128)(2,1)S(1)}, bf16[16,4,4]{0,2,1:T(4,128)(2,1)}, u32[]{:S(2)}) copy-start(bf16[16,4,4]{0,2,1:T(4,128)(2,1)} %param.37) | copy-start | bytes 1540
  10.7 65.2 %copy-start.96 = (f32[16]{0:T(128)S(1)}, f32[16]{0:T(128)}, u32[]{:S(2)}) copy-start(f32[16]{0:T(128)} %param.40) | copy-start | bytes 196
  10.7 65.2 %copy-start.103 = (f32[16]{0:T(128)S(1)}, f32[16]{0:T(128)}, u32[]{:S(2)}) copy-start(f32[16]{0:T(128)} %param.41) | copy-start | bytes 196
  10.7 65.3 %copy-start.94 = (bf16[256,4]{0,1:T(4,128)(2,1)S(1)}, bf16[256,4]{0,1:T(4,128)(2,1)}, u32[]{:S(2)}) copy-start(bf16[256,4]{0,1:T(4,128)(2,1)} %param.36) | copy-start | bytes 6148
  10.7 92.8 %copy-start.93 = (bf16[32,4,4]{0,2,1:T(4,128)(2,1)S(1)}, bf16[32,4,4]{0,2,1:T(4,128)(2,1)}, u32[]{:S(2)}) copy-start(bf16[32,4,4]{0,2,1:T(4,128)(2,1)} %param.39) | copy-start | bytes 3076
  13.3 119.1 %copy-start.95 = (bf16[256,4]{0,1:T(4,128)(2,1)S(1)}, bf16[256,4]{0,1:T(4,128)(2,1)}, u32[]{:S(2)}) copy-start(bf16[256,4]{0,1:T(4,128)(2,1)} %param.35) | copy-start | bytes 6148
  13.3 146.6 %copy-start.84 = (f32[256]{0:T(256)S(1)}, f32[256]{0:T(256)}, u32[]{:S(2)}) copy-start(f32[256]{0:T(256)} %param.42) | copy-start | bytes 3076
  13.3 160.0 %all-gather.19.cloned.1.call-start = ((), (), s32[]{:S(2)}) async-start(), calls=%async_computation.20 | async-start | bytes 2359296 | tf_op jit(solution)/shard_map/all_gather | solution.py:177
  14.0 208.1 %all-gather.17.cloned.1.call-start = ((), (), s32[]{:S(2)}) async-start(), calls=%async_computation.19 | async-start | bytes 4718592 | tf_op jit(solution)/shard_map/all_gather | solution.py:179
  14.6 722.3 %all-gather.21.cloned.1.call-start = ((), (), s32[]{:S(2)}) async-start(), calls=%async_computation.21 | async-start | bytes 4718592 | tf_op jit(solution)/shard_map/all_gather | solution.py:180
  15.2 734.5 %all-gather.23.cloned.1.call-start = ((), (), s32[]{:S(2)}) async-start(), calls=%async_computation.22 | async-start | bytes 4718592 | tf_op jit(solution)/shard_map/all_gather | solution.py:183
  15.8 814.6 %reduce-scatter.28.cloned.1.call-start = ((), (), s32[]{:S(2)}) async-start(), calls=%async_computation.23 | async-start | bytes 10485760 | tf_op jit(solution)/shard_map/reduce_scatter | solution.py:220
  44.6 120.6 %copy-start.74 = (f32[512,1]{0,1:T(1,128)}, f32[512,1]{0,1:T(1,128)S(1)}, u32[]{:S(2)}) copy-start(f32[512,1]{0,1:T(1,128)S(1)} %get-tuple-element.877) | copy-start | bytes 6148
  44.6 120.6 %copy-start.76 = (f32[512,1]{0,1:T(1,128)}, f32[512,1]{0,1:T(1,128)S(1)}, u32[]{:S(2)}) copy-start(f32[512,1]{0,1:T(1,128)S(1)} %get-tuple-element.878) | copy-start | bytes 6148
  44.6 120.6 %copy-start.78 = (f32[512,1]{0,1:T(1,128)}, f32[512,1]{0,1:T(1,128)S(1)}, u32[]{:S(2)}) copy-start(f32[512,1]{0,1:T(1,128)S(1)} %get-tuple-element.879) | copy-start | bytes 6148
  44.6 120.6 %copy-start.80 = (f32[512,1]{0,1:T(1,128)}, f32[512,1]{0,1:T(1,128)S(1)}, u32[]{:S(2)}) copy-start(f32[512,1]{0,1:T(1,128)S(1)} %get-tuple-element.880) | copy-start | bytes 6148
  75.8 102.8 %copy-start.66 = (f32[512,1]{0,1:T(1,128)}, f32[512,1]{0,1:T(1,128)S(1)}, u32[]{:S(2)}) copy-start(f32[512,1]{0,1:T(1,128)S(1)} %get-tuple-element.873) | copy-start | bytes 6148
  75.8 102.8 %copy-start.68 = (f32[512,1]{0,1:T(1,128)}, f32[512,1]{0,1:T(1,128)S(1)}, u32[]{:S(2)}) copy-start(f32[512,1]{0,1:T(1,128)S(1)} %get-tuple-element.874) | copy-start | bytes 6148
  75.8 102.8 %copy-start.70 = (f32[512,1]{0,1:T(1,128)}, f32[512,1]{0,1:T(1,128)S(1)}, u32[]{:S(2)}) copy-start(f32[512,1]{0,1:T(1,128)S(1)} %get-tuple-element.875) | copy-start | bytes 6148
  75.8 102.8 %copy-start.72 = (f32[512,1]{0,1:T(1,128)}, f32[512,1]{0,1:T(1,128)S(1)}, u32[]{:S(2)}) copy-start(f32[512,1]{0,1:T(1,128)S(1)} %get-tuple-element.876) | copy-start | bytes 6148
  75.9 119.3 %copy-start.88 = (f32[4]{0:T(128)}, f32[4]{0:T(128)S(1)}, u32[]{:S(2)}) copy-start(f32[4]{0:T(128)S(1)} %fusion.192) | copy-start | bytes 52
  103.5 91.8 %copy-start.44 = (bf16[2048,4]{0,1:T(4,128)(2,1)}, bf16[2048,4]{0,1:T(4,128)(2,1)S(1)}, u32[]{:S(2)}) copy-start(bf16[2048,4]{0,1:T(4,128)(2,1)S(1)} %all_gather.62) | copy-start | bytes 49156
  132.3 97.3 %copy-start.57 = (f32[1024,1]{0,1:T(1,128)}, f32[1024,1]{0,1:T(1,128)S(1)}, u32[]{:S(2)}) copy-start(f32[1024,1]{0,1:T(1,128)S(1)} %get-tuple-element.869) | copy-start | bytes 12292
  132.4 97.3 %copy-start.59 = (f32[1024,1]{0,1:T(1,128)}, f32[1024,1]{0,1:T(1,128)S(1)}, u32[]{:S(2)}) copy-start(f32[1024,1]{0,1:T(1,128)S(1)} %get-tuple-element.870) | copy-start | bytes 12292
  132.4 97.3 %copy-start.61 = (f32[1024,1]{0,1:T(1,128)}, f32[1024,1]{0,1:T(1,128)S(1)}, u32[]{:S(2)}) copy-start(f32[1024,1]{0,1:T(1,128)S(1)} %get-tuple-element.871) | copy-start | bytes 12292
  132.4 97.3 %copy-start.63 = (f32[1024,1]{0,1:T(1,128)}, f32[1024,1]{0,1:T(1,128)S(1)}, u32[]{:S(2)}) copy-start(f32[1024,1]{0,1:T(1,128)S(1)} %get-tuple-element.872) | copy-start | bytes 12292
  159.9 38.1 %copy-start.46 = (bf16[2048,4]{0,1:T(4,128)(2,1)}, bf16[2048,4]{0,1:T(4,128)(2,1)S(1)}, u32[]{:S(2)}) copy-start(bf16[2048,4]{0,1:T(4,128)(2,1)S(1)} %all_gather.65) | copy-start | bytes 49156
  201.5 28.2 copy-start.42
  759.4 70.9 %copy-start.6 = (bf16[1,256,2048]{2,1,0:T(8,128)(2,1)S(1)}, bf16[1,256,2048]{2,1,0:T(8,128)(2,1)}, u32[]{:S(2)}) copy-start(bf16[1,256,2048]{2,1,0:T(8,128)(2,1)} %param.27) | copy-start | bytes 3145732
  759.5 72.8 %copy-start.56 = (f32[2048]{0:T(1024)S(1)}, f32[2048]{0:T(1024)}, u32[]{:S(2)}) copy-start(f32[2048]{0:T(1024)} %param.44) | copy-start | bytes 24580
  759.5 164.7 %all-gather.27.cloned.1.call-start = ((), (), s32[]{:S(2)}) async-start(), calls=%async_computation.25 | async-start | bytes 6488064 | tf_op jit(solution)/shard_map/all_gather | solution.py:184
  760.2 200.1 %all-gather.25.cloned.1.call-start = ((), (), s32[]{:S(2)}) async-start(), calls=%async_computation.24 | async-start | bytes 5242880 | tf_op jit(solution)/shard_map/all_gather | solution.py:225
  833.6 220.5 %all-gather.29.cloned.1.call-start = ((), (), s32[]{:S(2)}) async-start(), calls=%async_computation.26 | async-start | bytes 6488064 | tf_op jit(solution)/shard_map/all_gather | solution.py:185
  834.2 256.1 %all-gather.33.cloned.1.call-start = ((), (), s32[]{:S(2)}) async-start(), calls=%async_computation.29 | async-start | bytes 5242880 | tf_op jit(solution)/shard_map/all_gather | solution.py:264
  836.1 347.8 %all-gather.31.cloned.1.call-start = ((), (), s32[]{:S(2)}) async-start(), calls=%async_computation.27 | async-start | bytes 6488064 | tf_op jit(solution)/shard_map/all_gather | solution.py:186
  836.7 454.0 %reduce-scatter.32.cloned.1.call-start = ((), (), s32[]{:S(2)}) async-start(), calls=%async_computation.30 | async-start | bytes 10485760 | tf_op jit(solution)/shard_map/reduce_scatter | solution.py:273
  1199.4 10.9 copy-start.109
  1199.4 10.9 copy-start.107
  1199.4 10.9 copy-start.98
  1219.3 118.2 %reduce-scatter.30.cloned.1.call-start = ((), (), s32[]{:S(2)}) async-start(), calls=%async_computation.28 | async-start | bytes 5242880 | tf_op jit(solution)/shard_map/reduce_scatter | solution.py:231
  1230.6 154.5 %all-gather.35.cloned.1.call-start = ((), (), s32[]{:S(2)}) async-start(), calls=%async_computation.31 | async-start | bytes 5242880 | tf_op jit(solution)/shard_map/all_gather | solution.py:282
  1342.4 827.9 %reduce-scatter.46.cloned.1.call-start = ((), (), s32[]{:S(2)}) async-start(), calls=%async_computation.38 | async-start | bytes 6488064 | tf_op jit(solution)/shard_map/reduce_scatter | solution.py:355
  1353.5 819.1 %reduce-scatter.48.cloned.1.call-start = ((), (), s32[]{:S(2)}) async-start(), calls=%async_computation.39 | async-start | bytes 6488064 | tf_op jit(solution)/shard_map/reduce_scatter | solution.py:358
  1366.2 808.7 %reduce-scatter.50.cloned.1.call-start = ((), (), s32[]{:S(2)}) async-start(), calls=%async_computation.40 | async-start | bytes 6488064 | tf_op jit(solution)/shard_map/reduce_scatter | solution.py:361
  1385.0 792.6 %reduce-scatter.58.cloned.1.call-start = ((), (), s32[]{:S(2)}) async-start(), calls=%async_computation.44 | async-start | bytes 36864
  2048.2 130.8 %reduce-scatter.56.cloned.1.call-start = ((), (), s32[]{:S(2)}) async-start(), calls=%async_computation.43 | async-start | bytes 36864
  2056.3 167.0 %reduce-scatter.60.cloned.1.call-start = ((), (), s32[]{:S(2)}) async-start(), calls=%async_computation.45 | async-start | bytes 73728
  2057.5 231.0 %reduce-scatter.54.cloned.1.call-start = ((), (), s32[]{:S(2)}) async-start(), calls=%async_computation.42 | async-start | bytes 589824
  2061.7 291.6 %reduce-scatter.52.cloned.1.call-start = ((), (), s32[]{:S(2)}) async-start(), calls=%async_computation.41 | async-start | bytes 589824
  2065.9 357.6 %reduce-scatter.38.cloned.1.call-start = ((), (), s32[]{:S(2)}) async-start(), calls=%async_computation.34 | async-start | bytes 2359296 | tf_op jit(solution)/shard_map/reduce_scatter | solution.py:328
  2074.0 420.2 %reduce-scatter.36.cloned.1.call-start = ((), (), s32[]{:S(2)}) async-start(), calls=%async_computation.33 | async-start | bytes 2359296 | tf_op jit(solution)/shard_map/reduce_scatter | solution.py:325
  2082.9 502.9 %reduce-scatter.44.cloned.1.call-start = ((), (), s32[]{:S(2)}) async-start(), calls=%async_computation.37 | async-start | bytes 4718592 | tf_op jit(solution)/shard_map/reduce_scatter | solution.py:343
  2091.6 585.3 %reduce-scatter.40.cloned.1.call-start = ((), (), s32[]{:S(2)}) async-start(), calls=%async_computation.35 | async-start | bytes 4718592 | tf_op jit(solution)/shard_map/reduce_scatter | solution.py:331
  2114.9 607.9 %reduce-scatter.34.cloned.1.call-start = ((), (), s32[]{:S(2)}) async-start(), calls=%async_computation.32 | async-start | bytes 5242880 | tf_op jit(solution)/shard_map/reduce_scatter | solution.py:314
  2161.6 655.2 %reduce-scatter.42.cloned.1.call-start = ((), (), s32[]{:S(2)}) async-start(), calls=%async_computation.36 | async-start | bytes 4718592 | tf_op jit(solution)/shard_map/reduce_scatter | solution.py:334
  2177.2 545.6 %copy-start.7 = (bf16[1,256,2048]{2,1,0:T(8,128)(2,1)S(1)}, bf16[1,256,2048]{2,1,0:T(8,128)(2,1)}, u32[]{:S(2)}) copy-start(bf16[1,256,2048]{2,1,0:T(8,128)(2,1)} %param.27) | copy-start | bytes 3145732
  2177.2 545.6 %copy-start.55 = (f32[2048]{0:T(1024)S(1)}, f32[2048]{0:T(1024)}, u32[]{:S(2)}) copy-start(f32[2048]{0:T(1024)} %param.30) | copy-start | bytes 24580
  2177.2 545.6 %copy-start.83 = (f32[256]{0:T(256)S(1)}, f32[256]{0:T(256)}, u32[]{:S(2)}) copy-start(f32[256]{0:T(256)} %copy-done.82) | copy-start | bytes 3076
  2425.3 299.8 %copy-start.65 = (f32[2048]{0:T(1024)S(1)}, f32[2048]{0:T(1024)}, u32[]{:S(2)}) copy-start(f32[2048]{0:T(1024)} %get-tuple-element.746) | copy-start | bytes 24580
  2425.3 299.8 %copy-start.90 = (f32[256]{0:T(256)S(1)}, f32[256]{0:T(256)}, u32[]{:S(2)}) copy-start(f32[256]{0:T(256)} %get-tuple-element.740) | copy-start | bytes 3076
  2425.3 343.5 %copy-start.87 = (f32[256]{0:T(256)S(1)}, f32[256]{0:T(256)}, u32[]{:S(2)}) copy-start(f32[256]{0:T(256)} %copy-done.86) | copy-start | bytes 3076
  2587.9 230.9 %copy-start.20 = (f32[256,2048]{1,0:T(8,128)S(1)}, f32[256,2048]{1,0:T(8,128)}, u32[]{:S(2)}) copy-start(f32[256,2048]{1,0:T(8,128)} %get-tuple-element.828) | copy-start | bytes 6291460
  (76 other events, 288.9 us)
Sparse Core Ops, SparseCore 0:
  10.1 50.7 all-gather.14
  63.1 33.2 all-gather.12
  98.5 50.3 all-gather.18
  150.9 71.2 all-gather.16
  224.1 71.8 all-gather.20
  298.0 72.3 all-gather.22
  759.6 70.7 reduce-scatter.27
  832.8 91.3 all-gather.26
  926.4 33.9 all-gather.24
  962.6 91.3 all-gather.28
  1056.2 33.9 all-gather.32
  1092.5 91.3 all-gather.30
  1219.4 71.1 reduce-scatter.31
  1293.0 44.4 reduce-scatter.29
  1342.5 34.4 all-gather.34
  1381.0 110.9 reduce-scatter.45
  1495.8 109.7 reduce-scatter.47
  1609.5 109.9 reduce-scatter.49
  2048.3 54.4 reduce-scatter.57
  2106.1 52.5 reduce-scatter.55
  2163.0 60.2 reduce-scatter.59
  2227.6 60.8 reduce-scatter.53
  2292.4 60.9 reduce-scatter.51
  2357.2 66.2 reduce-scatter.37
  2427.5 66.6 reduce-scatter.35
  2498.1 87.6 reduce-scatter.43
  2589.3 87.6 reduce-scatter.39
  2679.6 43.1 reduce-scatter.33
  2726.4 90.2 reduce-scatter.41
where the time goes:
time: 2840 us; the launch traced here: 2830 us
  waiting for transfers between devices  1100 us (39%)
  other arithmetic  805 us (28%)
  matrix products  475 us (17%)
  local copies, waits for them, and re-layouts  241 us (8%)
  blocking collectives  186 us (7%)
    another operation x128, other arithmetic, block_step(): jax.scipy.linalg.solve_triangular(identity_mat + coupling, right_side, lo...  634 us
    unnamed x34, waiting for transfers between devices  175 us
    squeeze x112, local copies, waits for them, and re-layouts, delta_rule(): lax.scan(jax.checkpoint(block_step), carry_state, (to_blocks(query_rows),...  98.1 us
    all_gather x1, waiting for transfers between devices, shards(): lax.all_gather(w_down, 'dp', axis=0, tiled=True)  93.7 us
    dot_general x10, matrix products, plain_dot(): return jnp.dot(left_mat, right_mat, preferred_element_type=jnp.float32)  90.6 us
    reduce_scatter x1, waiting for transfers between devices, shards(): lax.psum_scatter(grad_out_w.astype(jnp.bfloat16), 'dp', scatter_dimension...  89.8 us
    reduce_scatter x1, waiting for transfers between devices, shards(): lax.psum_scatter(grad_value_w.astype(jnp.bfloat16), 'dp', scatter_dimensi...  89 us
    all_gather x1, waiting for transfers between devices, shards(): lax.all_gather(w_gate, 'dp', axis=0, tiled=True)  87.4 us
  transfers between devices with their start and end apart: 29, of which 18 were waited for; matrix products, arithmetic and copies ran while one was open for 51% of the time, Pallas kernels for 0%

commit v1 on v0

v1 whole, which is shorter than its diff:
```python
import functools

import jax
import jax.numpy as jnp
from jax import lax
from jax.experimental import pallas as pl
from jax.experimental.pallas import tpu as pltpu
from jax.sharding import PartitionSpec as P

CH = 128
HALO = 8
LANES = 128
F32 = jnp.float32
BF = jnp.bfloat16


def mm(a, b, dims=((1,), (0,))):
    return lax.dot_general(a, b, (dims, ((), ())), preferred_element_type=F32)


NT = ((1,), (1,))
TN = ((0,), (0,))


def split(x):
    hi = x.astype(BF)
    return hi, (x - hi.astype(F32)).astype(BF)


def mm3(a, b):
    return mm(a[0], b[0]) + (mm(a[0], b[1]) + mm(a[1], b[0]))


def exact_mm(a, b):
    return lax.dot_general(
        a, b, (((1,), (0,)), ((), ())), precision=lax.Precision.HIGHEST, preferred_element_type=F32
    )


def unit_lower_inverse(mats):
    n = mats[0].shape[0]
    row = lax.broadcasted_iota(jnp.int32, (n, n), 0)
    col = lax.broadcasted_iota(jnp.int32, (n, n), 1)

    def off_block(size):
        same = (row // (2 * size)) == (col // (2 * size))
        return same & ((row // size) % 2 == 1) & ((col // size) % 2 == 0)

    eye = jnp.where(row == col, 1.0, 0.0)
    inv = [eye - jnp.where(off_block(1), a, 0.0) for a in mats]
    size = 2
    while size < n:
        mask = off_block(size)
        halves = [split(x) for x in inv]
        low = [split(jnp.where(mask, a, 0.0)) for a in mats]
        mid = [split(mm3(b, x)) for b, x in zip(low, halves)]
        inv = [x - mm3(xs, y) for x, xs, y in zip(inv, halves, mid)]
        size *= 2
    return inv


def softplus(x):
    return jnp.maximum(x, 0.0) + jnp.log1p(jnp.exp(-jnp.abs(x)))


def sigmoid(x):
    return 1.0 / (1.0 + jnp.exp(-x))


def conv_of(buf, taps, rows):
    out = buf[HALO - 3 : HALO - 3 + rows, :] * taps[0:1, :]
    for i in range(1, 4):
        out = out + buf[HALO - 3 + i : HALO - 3 + i + rows, :] * taps[i : i + 1, :]
    return out


def decay_tables(ab, par, rows):
    beta = sigmoid(ab)
    decay = -jnp.exp(par[0:1, :]) * softplus(ab + par[1:2, :])
    row = lax.broadcasted_iota(jnp.int32, (rows, rows), 0)
    col = lax.broadcasted_iota(jnp.int32, (rows, rows), 1)
    run = exact_mm(jnp.where(row >= col, 1.0, 0.0), decay)
    return beta, decay, run, jnp.transpose(run), row, col


def fwd_body(
    heads, dk, dv, q_ref, k_ref, v_ref, og_ref, ab_ref, tq_ref, tk_ref, tv_ref, par_ref, gain_ref,
    head_ref, o_ref, u_ref, t_ref, s_ref, qb, kb, vb, state,
):
    rows = CH

    @pl.when(pl.program_id(0) == 0)
    def _():
        for buf in (qb, kb, vb):
            buf[0:HALO, :] = jnp.zeros((HALO, buf.shape[1]), F32)
        state[...] = jnp.zeros_like(state)

    hs = range(heads)
    raw = []
    for buf, ref, taps in ((qb, q_ref, tq_ref), (kb, k_ref, tk_ref), (vb, v_ref, tv_ref)):
        buf[HALO : HALO + rows, :] = ref[...]
        raw.append(conv_of(buf, taps, rows))
        buf[0:HALO, :] = buf[rows : rows + HALO, :]
    zq, zk, zv = raw
    beta, _, run, run_t, row, col = decay_tables(ab_ref[...], par_ref, rows)
    low_inc = row >= col
    low_strict = row > col
    scale = dk ** (-0.5)

    def unit(z):
        y = z * sigmoid(z)
        return y * lax.rsqrt(jnp.sum(y * y, axis=-1, keepdims=True) + 1e-6)

    q = [unit(zq[:, h * dk : (h + 1) * dk]) * scale for h in hs]
    k = [unit(zk[:, h * dk : (h + 1) * dk]) for h in hs]
    qk_b = [(a.astype(BF), b.astype(BF)) for a, b in zip(q, k)]
    bt = [beta[:, h : h + 1] for h in hs]
    g_col = [run[:, heads + h : heads + h + 1] for h in hs]
    g_row = [run_t[heads + h : heads + h + 1, :] for h in hs]
    dec = [jnp.where(low_inc, jnp.exp(jnp.where(low_inc, g_col[h] - g_row[h], 0.0)), 0.0) for h in hs]
    kk = [mm(qk_b[h][1], qk_b[h][1], NT) for h in hs]
    inv = unit_lower_inverse([jnp.where(low_strict, bt[h] * dec[h] * kk[h], 0.0) for h in hs])
    inv_b = [x.astype(BF) for x in inv]
    p_b = [(mm(qk_b[h][0], qk_b[h][1], NT) * dec[h]).astype(BF) for h in hs]
    start = [jnp.exp(g) for g in g_col]
    end = [run[rows - 1 : rows, heads + h : heads + h + 1] for h in hs]
    s0 = [state[h] for h in hs]
    s0_b = [x.astype(BF) for x in s0]
    for h in hs:
        t_ref[:, h * rows : (h + 1) * rows] = inv_b[h]
        s_ref[:, h * dv : (h + 1) * dv] = s0_b[h]
    rhs = []
    for h in hs:
        z = zv[:, h * dv : (h + 1) * dv]
        val = z * sigmoid(z)
        rhs.append((bt[h] * val - (bt[h] * start[h]) * mm(qk_b[h][1], s0_b[h])).astype(BF))
    u_b = [mm(inv_b[h], rhs[h]).astype(BF) for h in hs]
    for h in hs:
        u_ref[:, h * dv : (h + 1) * dv] = u_b[h]
        tail = (k[h] * jnp.exp(end[h] - g_col[h])).astype(BF)
        state[h] = jnp.exp(end[h]) * s0[h] + mm(tail, u_b[h], TN)
    for h in hs:
        o = start[h] * mm(qk_b[h][0], s0_b[h]) + mm(p_b[h], u_b[h])
        o_ref[:, h * dv : (h + 1) * dv] = o
        og = og_ref[:, h * dv : (h + 1) * dv]
        r = lax.rsqrt(jnp.mean(o * o, axis=-1, keepdims=True) + 1e-5)
        head_ref[:, h * dv : (h + 1) * dv] = (o * r * gain_ref[...] * (og * sigmoid(og))).astype(BF)


def bwd_body(
    heads, dk, dv, q_ref, k_ref, v_ref, og_ref, ab_ref, qh_ref, kh_ref, vh_ref,
    tq_ref, tk_ref, tv_ref, par_ref, gain_ref, g_ref, o_ref, u_ref, t_ref, s_ref,
    dqk_ref, dv_ref, dog_ref, dab_ref, dtq_ref, dtk_ref, dtv_ref, dpar_ref, dgain_ref,
    qb, kb, vb, qn, kn, vn, dstate,
):
    rows = CH
    step = pl.program_id(0)
    first = step == 0
    is_top = step == pl.num_programs(0) - 1

    @pl.when(first)
    def _():
        for buf in (qn, kn, vn):
            buf[rows : rows + HALO, :] = jnp.zeros((HALO, buf.shape[1]), F32)
        for ref in (dtq_ref, dtk_ref, dtv_ref, dpar_ref, dgain_ref, dstate):
            ref[...] = jnp.zeros_like(ref)

    hs = range(heads)
    raw = []
    for buf, ref, halo, taps in (
        (qb, q_ref, qh_ref, tq_ref), (kb, k_ref, kh_ref, tk_ref), (vb, v_ref, vh_ref, tv_ref)
    ):
        buf[0:HALO, :] = jnp.where(is_top, 0.0, halo[...])
        buf[HALO : HALO + rows, :] = ref[...]
        raw.append(conv_of(buf, taps, rows))
    zq, zk, zv = raw
    ab = ab_ref[...]
    beta, decay, run, run_t, row, col = decay_tables(ab, par_ref, rows)
    low_inc = row >= col
    low_strict = row > col
    scale = dk ** (-0.5)

    def unit(z):
        sg = sigmoid(z)
        y = z * sg
        n = lax.rsqrt(jnp.sum(y * y, axis=-1, keepdims=True) + 1e-6)
        return y * n, n, sg * (1.0 + z * (1.0 - sg))

    qu = [unit(zq[:, h * dk : (h + 1) * dk]) for h in hs]
    ku = [unit(zk[:, h * dk : (h + 1) * dk]) for h in hs]
    q = [x[0] * scale for x in qu]
    k = [x[0] for x in ku]
    q_b = [x.astype(BF) for x in q]
    k_b = [x.astype(BF) for x in k]
    bt = [beta[:, h : h + 1] for h in hs]
    g_col = [run[:, heads + h : heads + h + 1] for h in hs]
    g_row = [run_t[heads + h : heads + h + 1, :] for h in hs]
    dec = [jnp.where(low_inc, jnp.exp(jnp.where(low_inc, g_col[h] - g_row[h], 0.0)), 0.0) for h in hs]
    start = [jnp.exp(g) for g in g_col]
    end = [run[rows - 1 : rows, heads + h : heads + h + 1] for h in hs]
    tail = [jnp.exp(end[h] - g_col[h]) for h in hs]
    dkk = [mm(k_b[h], k_b[h], NT) * dec[h] for h in hs]
    prob = [mm(q_b[h], k_b[h], NT) * dec[h] for h in hs]
    u_b = [u_ref[:, h * dv : (h + 1) * dv] for h in hs]
    s0_b = [s_ref[:, h * dv : (h + 1) * dv] for h in hs]
    ds1 = [dstate[h] for h in hs]
    ds1_b = [x.astype(BF) for x in ds1]

    gain = gain_ref[...]
    do_b = []
    dgain = jnp.zeros_like(gain)
    for h in hs:
        sl = slice(h * dv, (h + 1) * dv)
        o = o_ref[:, sl]
        og = og_ref[:, sl]
        g = g_ref[:, sl]
        r = lax.rsqrt(jnp.mean(o * o, axis=-1, keepdims=True) + 1e-5)
        sg = sigmoid(og)
        gor = g * (o * r)
        dgain = dgain + jnp.sum(gor * (og * sg), axis=0, keepdims=True)
        dog_ref[:, sl] = (gor * gain * (sg * (1.0 + og * (1.0 - sg)))).astype(BF)
        m = g * gain * (og * sg)
        d_o = r * m - o * (r * r * r * jnp.mean(m * o, axis=-1, keepdims=True))
        do_b.append(d_o.astype(BF))
    dgain_ref[...] += dgain

    d_u = [
        mm(prob[h].astype(BF), do_b[h], TN) + mm((k[h] * tail[h]).astype(BF), ds1_b[h]) for h in hs
    ]
    d_r = [mm(t_ref[:, h * rows : (h + 1) * rows], d_u[h].astype(BF), TN) for h in hs]
    dr_b = [x.astype(BF) for x in d_r]
    for h in hs:
        left = jnp.concatenate(
            [(q[h] * start[h]).astype(BF), (k[h] * (-(bt[h] * start[h]))).astype(BF)], axis=0
        )
        right = jnp.concatenate([do_b[h], dr_b[h]], axis=0)
        dstate[h] = jnp.exp(end[h]) * ds1[h] + mm(left, right, TN)

    lane = lax.broadcasted_iota(jnp.int32, (rows, LANES), 1)
    sub = lax.broadcasted_iota(jnp.int32, (LANES, rows), 0)
    dab_cols = jnp.zeros((rows, LANES), F32)
    dg_cols = jnp.zeros((rows, LANES), F32)
    dg_rows = jnp.zeros((LANES, rows), F32)
    dend = jnp.zeros((1, LANES), F32)
    lane_one = lax.broadcasted_iota(jnp.int32, (1, LANES), 1)
    for h in hs:
        sl = slice(h * dv, (h + 1) * dv)
        ks = slice(h * dk, (h + 1) * dk)
        d_p = jnp.where(low_inc, mm(do_b[h], u_b[h], NT), 0.0)
        d_a = jnp.where(low_strict, -mm(dr_b[h], u_b[h], NT), 0.0)
        pp = d_p * prob[h]
        dqk_b = (d_p * dec[h]).astype(BF)
        ad = d_a * dkk[h]
        d_kk = d_a * (bt[h] * dec[h])
        d_kk = (d_kk + jnp.transpose(d_kk)).astype(BF)
        y = mm(do_b[h], s0_b[h], NT)
        x = mm(dr_b[h], s0_b[h], NT)
        z = mm(u_b[h], ds1_b[h], NT)
        dq = mm(dqk_b, k_b[h]) + start[h] * y
        bstart = bt[h] * start[h]
        kx = jnp.sum(k[h] * x, axis=-1, keepdims=True)
        kz = tail[h] * jnp.sum(k[h] * z, axis=-1, keepdims=True)
        dkey = mm(d_kk, k_b[h]) + mm(dqk_b, q_b[h], TN) - bstart * x + tail[h] * z
        zval = zv[:, sl]
        sgv = sigmoid(zval)
        val = zval * sgv
        ad_row = jnp.sum(ad, axis=-1, keepdims=True)
        d_beta = jnp.sum(d_r[h] * val, axis=-1, keepdims=True) - start[h] * kx + ad_row
        d_g = (
            jnp.sum(pp, axis=-1, keepdims=True)
            + bt[h] * ad_row
            + start[h] * jnp.sum(q[h] * y, axis=-1, keepdims=True)
            - bstart * kx
            - kz
        )
        d_g_row = -jnp.sum(pp + bt[h] * ad, axis=0, keepdims=True)
        d_end = jnp.sum(kz, axis=0, keepdims=True) + jnp.exp(end[h]) * jnp.sum(
            jnp.sum(s0_b[h].astype(F32) * ds1[h], axis=-1, keepdims=True), axis=0, keepdims=True
        )
        dab_cols = dab_cols + jnp.where(lane == h, d_beta, 0.0)
        dg_cols = dg_cols + jnp.where(lane == heads + h, d_g, 0.0)
        dg_rows = dg_rows + jnp.where(sub == heads + h, d_g_row, 0.0)
        dend = dend + jnp.where(lane_one == heads + h, d_end, 0.0)
        vn[0:rows, sl] = (bt[h] * d_r[h]) * (sgv * (1.0 + zval * (1.0 - sgv)))
        for buf, du, (un, n, slope) in ((qn, dq * scale, qu[h]), (kn, dkey, ku[h])):
            dy = n * (du - un * jnp.sum(un * du, axis=-1, keepdims=True))
            buf[0:rows, ks] = dy * slope

    d_run = dg_cols + jnp.transpose(dg_rows)
    d_decay = exact_mm(jnp.where(col >= row, 1.0, 0.0), d_run) + dend
    pick = (lane >= heads) & (lane < 2 * heads)
    d_decay = jnp.where(pick, d_decay, 0.0)
    d_alpha = d_decay * (-jnp.exp(par_ref[0:1, :])) * sigmoid(ab + par_ref[1:2, :])
    dpar_ref[0:1, :] += jnp.sum(d_decay * decay, axis=0, keepdims=True)
    dpar_ref[1:2, :] += jnp.sum(d_alpha, axis=0, keepdims=True)
    dab_ref[...] = (dab_cols * beta * (1.0 - beta) + d_alpha).astype(BF)

    wide = heads * dk
    for buf, cur, taps, out, at, dtap in (
        (qn, qb, tq_ref, dqk_ref, 0, dtq_ref),
        (kn, kb, tk_ref, dqk_ref, wide, dtk_ref),
        (vn, vb, tv_ref, dv_ref, 0, dtv_ref),
    ):
        here = cur[HALO : HALO + rows, :]
        total = None
        for i in range(4):
            moved = buf[3 - i : 3 - i + rows, :]
            term = moved * taps[i : i + 1, :]
            total = term if total is None else total + term
            dtap[i : i + 1, :] += jnp.sum(here * moved, axis=0, keepdims=True)
        out[:, at : at + total.shape[1]] = total.astype(BF)
        buf[rows : rows + HALO, :] = buf[0:HALO, :]


def mixer_specs(heads, dk, dv, at):
    wide_k, wide_v = heads * dk, heads * dv
    full = lambda shape: pl.BlockSpec(shape, lambda c: (0,) * len(shape))
    return {
        "q": pl.BlockSpec((CH, wide_k), lambda c: (at(c), 0)),
        "k": pl.BlockSpec((CH, wide_k), lambda c: (at(c), 1)),
        "qk": pl.BlockSpec((CH, 2 * wide_k), lambda c: (at(c), 0)),
        "v": pl.BlockSpec((CH, wide_v), lambda c: (at(c), 0)),
        "ab": pl.BlockSpec((CH, LANES), lambda c: (at(c), 0)),
        "t": pl.BlockSpec((CH, heads * CH), lambda c: (at(c), 0)),
        "s": pl.BlockSpec((None, dk, wide_v), lambda c: (at(c), 0, 0)),
        "tk": full((8, wide_k)),
        "tv": full((8, wide_v)),
        "par": full((8, LANES)),
        "gain": full((1, dv)),
    }


def mixer_forward(qk_raw, v_raw, og_raw, ab, tq, tk, tv, par, gain):
    length, wide_k = qk_raw.shape[0], qk_raw.shape[1] // 2
    wide_v = v_raw.shape[1]
    dv = gain.shape[1]
    heads = wide_v // dv
    dk = wide_k // heads
    steps = length // CH
    sp = mixer_specs(heads, dk, dv, lambda c: c)
    return pl.pallas_call(
        functools.partial(fwd_body, heads, dk, dv),
        grid=(steps,),
        in_specs=[sp[n] for n in ("q", "k", "v", "v", "ab", "tk", "tk", "tv", "par", "gain")],
        out_specs=[sp[n] for n in ("v", "v", "v", "t", "s")],
        out_shape=[
            jax.ShapeDtypeStruct((length, wide_v), BF),
            jax.ShapeDtypeStruct((length, wide_v), F32),
            jax.ShapeDtypeStruct((length, wide_v), BF),
            jax.ShapeDtypeStruct((length, heads * CH), BF),
            jax.ShapeDtypeStruct((steps, dk, wide_v), BF),
        ],
        scratch_shapes=[
            pltpu.VMEM((CH + HALO, wide_k), F32),
            pltpu.VMEM((CH + HALO, wide_k), F32),
            pltpu.VMEM((CH + HALO, wide_v), F32),
            pltpu.VMEM((heads, dk, dv), F32),
        ],
        compiler_params=pltpu.CompilerParams(
            dimension_semantics=("arbitrary",), vmem_limit_bytes=40 << 20
        ),
        cost_estimate=pl.CostEstimate(flops=20_000_000_000, bytes_accessed=40_000_000, transcendentals=6_000_000),
        name="mixer_forward",
    )(qk_raw, qk_raw, v_raw, og_raw, ab, tq, tk, tv, par, gain)


def mixer_backward(qk_raw, v_raw, og_raw, ab, tq, tk, tv, par, gain, grad, o, u, t, s):
    length, wide_k = qk_raw.shape[0], qk_raw.shape[1] // 2
    wide_v = v_raw.shape[1]
    dv = gain.shape[1]
    heads = wide_v // dv
    dk = wide_k // heads
    steps = length // CH
    at = lambda c: steps - 1 - c
    sp = mixer_specs(heads, dk, dv, at)
    before = lambda c: jnp.maximum(at(c) * (CH // HALO) - 1, 0)
    hq = pl.BlockSpec((HALO, wide_k), lambda c: (before(c), 0))
    hk = pl.BlockSpec((HALO, wide_k), lambda c: (before(c), 1))
    hv = pl.BlockSpec((HALO, wide_v), lambda c: (before(c), 0))
    names = ("q", "k", "v", "v", "ab")
    rest = ("tk", "tk", "tv", "par", "gain", "v", "v", "v", "t", "s")
    return pl.pallas_call(
        functools.partial(bwd_body, heads, dk, dv),
        grid=(steps,),
        in_specs=[sp[n] for n in names] + [hq, hk, hv] + [sp[n] for n in rest],
        out_specs=[sp[n] for n in ("qk", "v", "v", "ab", "tk", "tk", "tv", "par", "gain")],
        out_shape=[
            jax.ShapeDtypeStruct((length, 2 * wide_k), BF),
            jax.ShapeDtypeStruct((length, wide_v), BF),
            jax.ShapeDtypeStruct((length, wide_v), BF),
            jax.ShapeDtypeStruct((length, LANES), BF),
            jax.ShapeDtypeStruct((8, wide_k), F32),
            jax.ShapeDtypeStruct((8, wide_k), F32),
            jax.ShapeDtypeStruct((8, wide_v), F32),
            jax.ShapeDtypeStruct((8, LANES), F32),
            jax.ShapeDtypeStruct((1, dv), F32),
        ],
        scratch_shapes=[
            pltpu.VMEM((CH + HALO, wide_k), F32),
            pltpu.VMEM((CH + HALO, wide_k), F32),
            pltpu.VMEM((CH + HALO, wide_v), F32),
            pltpu.VMEM((CH + HALO, wide_k), F32),
            pltpu.VMEM((CH + HALO, wide_k), F32),
            pltpu.VMEM((CH + HALO, wide_v), F32),
            pltpu.VMEM((heads, dk, dv), F32),
        ],
        compiler_params=pltpu.CompilerParams(
            dimension_semantics=("arbitrary",), vmem_limit_bytes=48 << 20
        ),
        cost_estimate=pl.CostEstimate(flops=40_000_000_000, bytes_accessed=60_000_000, transcendentals=9_000_000),
        name="mixer_backward",
    )(
        qk_raw, qk_raw, v_raw, og_raw, ab, qk_raw, qk_raw, v_raw, tq, tk, tv, par, gain, grad, o, u, t, s
    )


def plain_dot(left_mat, right_mat):
    return jnp.dot(left_mat, right_mat, preferred_element_type=F32)


def dot_rows(left_mat, right_mat):
    return lax.dot_general(left_mat, right_mat, (((1,), (1,)), ((), ())), preferred_element_type=F32)


def dot_tokens(left_mat, right_mat):
    return lax.dot_general(left_mat, right_mat, (((0,), (0,)), ((), ())), preferred_element_type=F32)


def rms_apply(values, gain_vec):
    return values * lax.rsqrt(jnp.mean(values * values, axis=-1, keepdims=True) + 1e-05) * gain_vec


def swiglu(gate_pre, up_pre):
    return jax.nn.silu(gate_pre) * up_pre


class RingRows:
    def __init__(self, dp_size):
        self.outer = dp_size // 2
        self.index = lax.axis_index("dp")
        self.last = None

    def _roll(self, x, axis, blocks):
        size = x.shape[axis] // self.outer * blocks
        return jnp.concatenate(
            [lax.slice_in_dim(x, size, None, axis=axis), lax.slice_in_dim(x, 0, size, axis=axis)], axis
        )

    def reorder(self, x, axis):
        outer_at, pair_at = self.index // 2, self.index % 2
        size = x.shape[axis] // (2 * self.outer)
        cut = [lax.slice_in_dim(x, b * size, (b + 1) * size, axis=axis) for b in range(2 * self.outer)]
        even, odd = jnp.concatenate(cut[0::2], axis), jnp.concatenate(cut[1::2], axis)
        sides = [jnp.where(pair_at == 0, even, odd), jnp.where(pair_at == 0, odd, even)]
        bit = 1
        while bit < self.outer:
            sides = [jnp.where((outer_at // bit) % 2 == 1, self._roll(s, axis, bit), s) for s in sides]
            bit *= 2
        return jnp.concatenate(sides, axis)

    def restore(self, x, axis):
        outer_at, pair_at = self.index // 2, self.index % 2
        half = x.shape[axis] // 2
        sides = [lax.slice_in_dim(x, 0, half, axis=axis), lax.slice_in_dim(x, half, None, axis=axis)]
        bit = 1
        while bit < self.outer:
            sides = [
                jnp.where((outer_at // bit) % 2 == 1, self._roll(s, axis, self.outer - bit), s) for s in sides
            ]
            bit *= 2
        even = jnp.where(pair_at == 0, sides[0], sides[1])
        odd = jnp.where(pair_at == 0, sides[1], sides[0])
        size = half // self.outer
        cut = []
        for b in range(self.outer):
            cut += [lax.slice_in_dim(s, b * size, (b + 1) * size, axis=axis) for s in (even, odd)]
        return jnp.concatenate(cut, axis)

    def _swap(self, x):
        return lax.ppermute(x, "dp", [(i, i ^ 1) for i in range(2 * self.outer)])

    def _from(self, x, steps):
        n = 2 * self.outer
        return lax.ppermute(x, "dp", [((i + 2 * steps) % n, i) for i in range(n)])

    def gather(self, block):
        if self.last is not None:
            block, self.last = lax.optimization_barrier((block, self.last))
        own = [block] + [self._from(block, k) for k in range(1, self.outer)]
        self.last = own[-1]
        other = [self._swap(b) for b in own]
        return jnp.concatenate(own + other, axis=0)

    def scatter(self, left, right):
        half = left.shape[1] // 2
        sent = dot_tokens(left[:, half:], right).astype(BF)
        came = self._swap(sent)
        pair = (dot_tokens(left[:, :half], right) + came.astype(F32)).astype(BF)
        size = half // self.outer
        n = 2 * self.outer
        total = pair[:size].astype(F32)
        for k in range(1, self.outer):
            piece = pair[k * size : (k + 1) * size]
            total = total + lax.ppermute(
                piece, "dp", [(i, (i + 2 * k) % n) for i in range(n)]
            ).astype(F32)
        return total


class PlainRows:
    def reorder(self, x, axis):
        return x

    def restore(self, x, axis):
        return x

    def gather(self, block):
        return lax.all_gather(block, "dp", axis=0, tiled=True)

    def scatter(self, left, right):
        full = dot_tokens(left, right).astype(BF)
        return lax.psum_scatter(full, "dp", scatter_dimension=0, tiled=True).astype(F32)


def tensor_gather(x):
    return lax.all_gather(x, "tensor", axis=0, tiled=True)


def tensor_scatter(x):
    return lax.psum_scatter(x, "tensor", scatter_dimension=0, tiled=True)


def shards(
    dp_size, inputs, cotangent, lengths, norm1_gain, w_query, w_key, w_value, w_outgate, w_beta, w_alpha,
    conv_query, conv_key, conv_value, a_log, dt_bias, head_gain, w_out, norm2_gain, w_gate, w_up, w_down,
):
    rows = RingRows(dp_size) if dp_size == 8 else PlainRows()
    heads = w_beta.shape[1]
    wide_k, wide_v = w_query.shape[1], w_value.shape[1]
    dk, dv = wide_k // heads, wide_v // heads
    taps_n = conv_query.shape[2]
    block = w_query.shape[0]
    tensor_pos = lax.axis_index("tensor")
    head_start = tensor_pos * heads

    row_count = inputs.shape[1]
    positions = tensor_pos * row_count + jnp.arange(row_count, dtype=jnp.int32)
    valid_rows = (positions < lengths[0]).astype(F32)[:, None]

    small = jnp.concatenate(
        [w_beta.reshape(-1), w_alpha.reshape(-1), conv_query.reshape(-1), conv_key.reshape(-1), conv_value.reshape(-1)]
    )[None]
    small = lax.all_gather(small, "dp", axis=0, tiled=True)
    cuts = [0]
    for part in (w_beta, w_alpha, conv_query, conv_key, conv_value):
        cuts.append(cuts[-1] + part.size)
    pieces = [small[:, a:b] for a, b in zip(cuts[:-1], cuts[1:])]
    full_ab = rows.reorder(
        jnp.concatenate([p.reshape(dp_size * block, heads) for p in pieces[:2]], axis=1), 0
    )
    full_ab = jnp.pad(full_ab, ((0, 0), (0, LANES - 2 * heads)))

    def tap_table(piece, size):
        table = piece.reshape(size, heads, taps_n).astype(F32)
        return jnp.pad(jnp.transpose(table, (2, 1, 0)).reshape(taps_n, heads * size), ((0, 8 - taps_n), (0, 0)))

    tq, tk, tv = tap_table(pieces[2], dk), tap_table(pieces[3], dk), tap_table(pieces[4], dv)
    alog_local = lax.dynamic_slice_in_dim(a_log, head_start, heads)
    dtb_local = lax.dynamic_slice_in_dim(dt_bias, head_start, heads)
    par = jnp.pad(jnp.stack([alog_local, dtb_local]), ((0, 6), (heads, LANES - 2 * heads)))
    gain = head_gain[None]

    local_rows = rows.reorder(inputs[0], 1).astype(F32)
    gain_one = rows.reorder(norm1_gain[None], 1)[0]
    gain_two = rows.reorder(norm2_gain[None], 1)[0]
    normed_one, norm_one_back = jax.vjp(rms_apply, local_rows, gain_one)
    rows_one = tensor_gather(normed_one.astype(BF))
    full_qk = rows.gather(jnp.concatenate([w_query, w_key], axis=1))
    full_value = rows.gather(w_value)
    full_outgate = rows.gather(w_outgate)
    full_out = rows.gather(w_out)
    full_gate = rows.gather(w_gate)
    full_up = rows.gather(w_up)
    full_down = rows.gather(w_down)
    grad_after = valid_rows * rows.reorder(cotangent[0], 1).astype(F32)
    incoming_ffn = tensor_gather(grad_after.astype(BF))

    ab_raw = plain_dot(rows_one, full_ab)
    qk_raw = plain_dot(rows_one, full_qk)
    v_raw = plain_dot(rows_one, full_value)
    og_raw = plain_dot(rows_one, full_outgate)
    core_in = (qk_raw, v_raw, og_raw, ab_raw, tq, tk, tv, par, gain)
    head_bf, delta_out, new_values, inverses, states = mixer_forward(*core_in)
    after_mix = local_rows + tensor_scatter(dot_rows(head_bf, full_out))
    normed_two, norm_two_back = jax.vjp(rms_apply, after_mix, gain_two)
    rows_two = tensor_gather(normed_two.astype(BF))
    gate_pre = plain_dot(rows_two, full_gate)
    up_pre = plain_dot(rows_two, full_up)
    hidden, swiglu_back = jax.vjp(swiglu, gate_pre, up_pre)
    hidden_bf = hidden.astype(BF)
    ffn_part = tensor_scatter(dot_rows(hidden_bf, full_down).astype(BF)).astype(F32)
    outputs = rows.restore(((after_mix + ffn_part) * valid_rows).astype(BF), 1)[None]

    grad_hidden = plain_dot(incoming_ffn, full_down)
    out_down = rows.scatter(incoming_ffn, hidden_bf)
    grad_gate_pre, grad_up_pre = swiglu_back(grad_hidden)
    gate_low = grad_gate_pre.astype(BF)
    up_low = grad_up_pre.astype(BF)
    grad_normed_two = tensor_scatter(dot_rows(gate_low, full_gate) + dot_rows(up_low, full_up))
    out_gate = rows.scatter(rows_two, gate_low)
    out_up = rows.scatter(rows_two, up_low)
    grad_mid, grad_norm2 = norm_two_back(grad_normed_two)
    grad_mid = grad_mid + grad_after
    incoming_mix = tensor_gather(grad_mid.astype(BF))

    grad_head = plain_dot(incoming_mix, full_out)
    out_out = rows.scatter(incoming_mix, head_bf)
    qk_low, v_low, og_low, ab_low, dtq, dtk, dtv, dpar, dgain = mixer_backward(
        *core_in, grad_head, delta_out, new_values, inverses, states
    )
    summed = dot_rows(qk_low, full_qk) + dot_rows(v_low, full_value)
    summed = summed + dot_rows(og_low, full_outgate) + dot_rows(ab_low, full_ab)
    grad_normed_one = tensor_scatter(summed.astype(BF)).astype(F32)
    out_qk = rows.scatter(rows_one, qk_low)
    out_value = rows.scatter(rows_one, v_low)
    out_outgate = rows.scatter(rows_one, og_low)
    grad_first, grad_norm1 = norm_one_back(grad_normed_one)
    grad_inputs = rows.restore(grad_mid + grad_first, 1)[None]

    grad_ab = rows.restore(dot_tokens(rows_one, ab_low)[:, : 2 * heads], 0)
    grad_beta, grad_alpha = grad_ab[:, :heads], grad_ab[:, heads:]

    def tap_grad(table, size):
        return jnp.transpose(table[:taps_n].reshape(taps_n, heads, size), (2, 1, 0))

    small_out = [grad_beta, grad_alpha, tap_grad(dtq, dk), tap_grad(dtk, dk), tap_grad(dtv, dv)]
    small_sum = lax.psum_scatter(
        jnp.concatenate([p.reshape(dp_size, -1) for p in small_out], axis=1), "dp", scatter_dimension=0, tiled=True
    )[0]
    shapes = (w_beta, w_alpha, conv_query, conv_key, conv_value)
    out_beta, out_alpha, out_cq, out_ck, out_cv = (
        small_sum[a:b].reshape(like.shape) for a, b, like in zip(cuts[:-1], cuts[1:], shapes)
    )
    alog_full = lax.dynamic_update_slice_in_dim(
        jnp.zeros_like(a_log), dpar[0, heads : 2 * heads], head_start, 0
    )
    dtb_full = lax.dynamic_update_slice_in_dim(
        jnp.zeros_like(dt_bias), dpar[1, heads : 2 * heads], head_start, 0
    )
    norm1_sum, norm2_sum, hgain_sum, alog_sum, dtb_sum = lax.psum(
        (
            rows.restore(grad_norm1[None], 1)[0], rows.restore(grad_norm2[None], 1)[0], dgain[0],
            alog_full, dtb_full,
        ),
        ("dp", "tensor"),
    )
    return (
        outputs, grad_inputs, norm1_sum, out_qk[:, :wide_k], out_qk[:, wide_k:], out_value, out_outgate,
        out_beta, out_alpha, out_cq, out_ck, out_cv, alog_sum, dtb_sum, hgain_sum, out_out, norm2_sum,
        out_gate, out_up, out_down,
    )


def solution(mesh):
    mat, cube, whole = P("dp", "tensor"), P("dp", "tensor", None), P()
    in_specs = (
        (cube, cube, P("dp"), whole) + (mat,) * 6 + (cube,) * 3 + (whole,) * 3 + (mat, whole) + (mat,) * 3
    )
    out_specs = (
        (cube, cube, whole) + (mat,) * 6 + (cube,) * 3 + (whole,) * 3 + (mat, whole) + (mat,) * 3
    )
    return jax.shard_map(
        functools.partial(shards, mesh.shape["dp"]), mesh=mesh, in_specs=in_specs, out_specs=out_specs,
        check_vma=False,
    )
```

time: 2840 us -> 1450 us (0.51)
  other arithmetic: 805 us -> 31 us
  waiting for transfers between devices: 1100 us -> 780 us
  matrix products: 475 us -> 222 us
  local copies, waits for them, and re-layouts: 241 us -> 90.1 us
  starting transfers between devices: 1.64 us -> 118 us
  Pallas kernels: 0 us -> 90.1 us
  blocking collectives: 186 us -> 97.3 us
    ppermute x0 -> x77, waiting for transfers between devices: none -> 751 us  [the longest x35 402 us: _swap(): return lax.ppermute(x, 'dp', [(i, i ^ 1) for i in range(2 * self.outer)])]
    another operation x212 -> x1, other arithmetic: 656 us -> 0.08 us  [shards(): jnp.stack([alog_local, dtb_local])]
    reduce_scatter x12 -> x4, waiting for transfers between devices: 582 us -> 0.03 us  [tensor_scatter(): return lax.psum_scatter(x, 'tensor', scatter_dimension=0, tiled=True)]
    all_gather x12 -> x4, waiting for transfers between devices: 342 us -> 12.2 us  [tensor_gather(): return lax.all_gather(x, 'tensor', axis=0, tiled=True)]
    dot_general x362 -> x8, matrix products: 290 us -> 72.6 us  [plain_dot(): return jnp.dot(left_mat, right_mat, preferred_element_type=F32)]
    unnamed x34 -> x10, waiting for transfers between devices: 175 us -> 16.9 us
    ppermute x0 -> x77, starting transfers between devices: none -> 106 us  [the longest x35 48 us: _swap(): return lax.ppermute(x, 'dp', [(i, i ^ 1) for i in range(2 * self.outer)])]
    squeeze x112 -> x0, local copies, waits for them, and re-layouts: 98.1 us -> none  [delta_rule(): lax.scan(jax.checkpoint(block_step), carry_state, (to_blocks(query_rows),...]
  transfers between devices with their start and end apart: 29 -> 86, of which waited for: 18 -> 45; matrix products, arithmetic and copies ran while one was open for 51% -> 15% of each run, Pallas kernels for 0% -> 0%
where the time goes in v1:
time: 1450 us
  waiting for transfers between devices  780 us (54%)
  matrix products  222 us (15%)
  starting transfers between devices  118 us (8%)
  blocking collectives  97.3 us (7%)
  local copies, waits for them, and re-layouts  90.1 us (6%)
  Pallas kernels  90.1 us (6%)
  other arithmetic  31 us (2%)
  between operations  17.1 us (1%)
    ppermute x35, waiting for transfers between devices, _swap(): return lax.ppermute(x, 'dp', [(i, i ^ 1) for i in range(2 * self.outer)])  402 us
    ppermute x21, waiting for transfers between devices, scatter(): lax.ppermute(piece, 'dp', [(i, (i + 2 * k) % n) for i in range(n)])  183 us
    ppermute x21, waiting for transfers between devices, _from(): return lax.ppermute(x, 'dp', [((i + 2 * steps) % n, i) for i in range(n)])  166 us
    dot_general x8, matrix products, dot_rows(): lax.dot_general(left_mat, right_mat, (((1,), (1,)), ((), ())), preferred_...  77 us
    dot_general x15, matrix products, dot_tokens(): lax.dot_general(left_mat, right_mat, (((0,), (0,)), ((), ())), preferred_...  72.9 us
    dot_general x8, matrix products, plain_dot(): return jnp.dot(left_mat, right_mat, preferred_element_type=F32)  72.6 us
    unnamed x276, local copies, waits for them, and re-layouts  61.9 us
    all_gather x1, blocking collectives, shards(): small = lax.all_gather(small, 'dp', axis=0, tiled=True)  54.5 us
  transfers between devices with their start and end apart: 86, of which 45 were waited for; matrix products, arithmetic and copies ran while one was open for 15% of the time, Pallas kernels for 0%

profile of v1, /device:TPU:14, one launch (start us, length us, event | category | flops | bytes accessed | tf_op | source)
XLA Modules:
  0.0 1446.2 jit_solution(12613460965159127992)
XLA Ops:
  23.0 54.5 %all-gather = bf16[24576]{0:T(1024)(128)(2,1)S(1)} all-gather(bf16[3072]{0:T(1024)(128)(2,1)S(1)} %dynamic-update-slice.81), channel_id=2, replica_groups=mesh['dp'=8,'tensor'=4] {'dp'}, dimensions={0}, use_global_device_ids=true | all-gather | bytes 55296 | tf_op jit(solution)/shard_map/all_gather | solution.py:553
  96.2 21.0 %collective-permute-done.9 = bf16[256,1024]{1,0:T(8,128)(2,1)S(1)} collective-permute-done((bf16[256,1024]{1,0:T(8,128)(2,1)S(1)}, bf16[256,1024]{1,0:T(8,128)(2,1)S(1)}, u32[]{:S(2)}, u32[]{:S(2)}) %collective-permute-start.9) | collective-permute-done | bytes 524320 | tf_op jit(solution)/shard_map/ppermute | solution.py:484
  134.8 5.5 collective-permute-done.16
  140.4 19.7 %collective-permute-start.12 = (bf16[256,1024]{1,0:T(8,128)(2,1)S(1)}, bf16[256,1024]{1,0:T(8,128)(2,1)S(1)}, u32[]{:S(2)}, u32[]{:S(2)}) collective-permute-start(bf16[256,1024]{1,0:T(8,128)(2,1)S(1)} %collective-permute-done.8), channel_id=1, source_target_pairs={{0,4},{4,0},{8,12},{12,8},{16,20},{20,16},{24,28},{28,24},{1,5},{5... | collective-permute-start | bytes 1572872 | tf_op jit(solution)/shard_map/ppermute | solution.py:480
  161.9 7.9 collective-permute-done.15
  170.0 5.1 collective-permute-start.21
  177.1 6.6 collective-permute-done.13
  184.7 10.3 collective-permute-done.18
  195.9 12.6 collective-permute-done.21
  220.0 8.6 collective-permute-done.24
  229.5 10.4 collective-permute-done.25
  240.7 9.6 collective-permute-done.26
  256.8 10.0 fusion.131.og_ref
  266.8 6.1 fusion.130.v_ref.vh_ref
  272.9 6.0 fusion.129.q_ref.k_ref.qh_ref.kh_ref
  280.2 35.8 %mixer_forward.1 = (bf16[1024,1024]{1,0:T(8,128)(2,1)S(1)}, f32[1024,1024]{1,0:T(8,128)S(1)}, bf16[1024,1024]{1,0:T(8,128)(2,1)S(1)}, bf16[1024,512]{1,0:T(8,128)(2,1)S(1)}, bf16[8,128,1024]{2,1,0:T(8,128)(2,1)S(1)}) custom-call(f32[1024,1024]{1,0:T(8,128)} %fusion.129.q_ref.k_ref.qh_ref.kh_ref, f32[1024,1024]{1,0:T(8,128)} %fusion.129.q_ref.k_ref.qh_ref.kh_ref, ...), custom_call_target="tpu_custom_call" | custom-call | flops 20000000000 | bytes 40000000 | tf_op jit(solution)/shard_map/mixer_forward/pallas_call | solution.py:341
  323.1 9.1 fusion.132
  337.9 11.0 all-gather.8.cloned.1.call-start
  353.8 68.5 %collective-permute-done.30 = bf16[256,1408]{1,0:T(8,128)(2,1)S(1)} collective-permute-done((bf16[256,1408]{1,0:T(8,128)(2,1)S(1)}, bf16[256,1408]{1,0:T(8,128)(2,1)S(1)}, u32[]{:S(2)}, u32[]{:S(2)}) %collective-permute-start.30) | collective-permute-done | bytes 720928 | tf_op jit(solution)/shard_map/ppermute | solution.py:484
  429.6 16.0 %collective-permute-done.29 = bf16[256,1408]{1,0:T(8,128)(2,1)} collective-permute-done((bf16[256,1408]{1,0:T(8,128)(2,1)S(1)}, bf16[256,1408]{1,0:T(8,128)(2,1)}, u32[]{:S(2)}, u32[]{:S(2)}) %collective-permute-start.29) | collective-permute-done | bytes 720928 | tf_op jit(solution)/shard_map/ppermute | solution.py:484
  451.5 16.7 %collective-permute-done.37 = bf16[256,1408]{1,0:T(8,128)(2,1)} collective-permute-done((bf16[256,1408]{1,0:T(8,128)(2,1)}, bf16[256,1408]{1,0:T(8,128)(2,1)}, u32[]{:S(2)}, u32[]{:S(2)}) %collective-permute-start.37) | collective-permute-done | bytes 720928 | tf_op jit(solution)/shard_map/ppermute | solution.py:484
  492.1 10.8 collective-permute-done.34
  504.2 14.2 collective-permute-done.39
  519.6 6.6 collective-permute-done.42
  534.4 14.9 %collective-permute-done.40 = bf16[256,1408]{1,0:T(8,128)(2,1)S(1)} collective-permute-done((bf16[256,1408]{1,0:T(8,128)(2,1)}, bf16[256,1408]{1,0:T(8,128)(2,1)S(1)}, u32[]{:S(2)}, u32[]{:S(2)}) %collective-permute-start.40) | collective-permute-done | bytes 720928 | tf_op jit(solution)/shard_map/ppermute | solution.py:480
  550.5 14.2 collective-permute-done.41
  566.6 13.6 collective-permute-done.46
  581.1 14.5 %collective-permute-done.47 = bf16[256,1408]{1,0:T(8,128)(2,1)S(1)} collective-permute-done((bf16[256,1408]{1,0:T(8,128)(2,1)S(1)}, bf16[256,1408]{1,0:T(8,128)(2,1)S(1)}, u32[]{:S(2)}, u32[]{:S(2)}) %collective-permute-start.47) | collective-permute-done | bytes 720928 | tf_op jit(solution)/shard_map/ppermute | solution.py:480
  596.6 7.3 collective-permute-done.48
  604.8 11.7 fusion.134
  616.5 11.8 fusion.133
  628.3 15.6 %fusion.2 = (bf16[1024,1408]{1,0:T(8,128)(2,1)}, bf16[1024,1408]{1,0:T(8,128)(2,1)}, bf16[1024,1408]{1,0:T(8,128)(2,1)}) fusion(f32[1024,1408]{1,0:T(8,128)} %fusion.134, f32[1024,1408]{1,0:T(8,128)} %fusion.133, bf16[1024,2048]{1,0:T(8,128)(2,1)S(1)} %copy-done.69, bf16[2048,1408]{1,0:T(8,128)(2,1)} %constant_dynamic-update-slice_fusion.36), kind=kOutput, calls=%fused_computation.4 | convolution fusion | flops 5928648704 | bytes 30146560 | tf_op jit(solution)/shard_map/dot_general | solution.py:418
  644.0 10.5 fusion.135
  654.4 11.0 convolution_add_fusion
  665.9 8.0 convolution_convert_fusion.1
  674.3 12.3 convolution_convert_fusion
  686.6 8.3 convolution_convert_fusion.2
  702.4 37.2 %collective-permute-done.73 = bf16[1024,1408]{1,0:T(8,128)(2,1)} collective-permute-done((bf16[1024,1408]{1,0:T(8,128)(2,1)}, bf16[1024,1408]{1,0:T(8,128)(2,1)}, u32[]{:S(2)}, u32[]{:S(2)}) %collective-permute-start.73) | collective-permute-done | bytes 2883616 | tf_op jit(solution)/shard_map/ppermute | solution.py:480
  739.6 6.9 add_convert_fusion.1
  748.8 52.6 %collective-permute-done.69 = bf16[1024,1408]{1,0:T(8,128)(2,1)} collective-permute-done((bf16[1024,1408]{1,0:T(8,128)(2,1)}, bf16[1024,1408]{1,0:T(8,128)(2,1)}, u32[]{:S(2)}, u32[]{:S(2)}) %collective-permute-start.69) | collective-permute-done | bytes 2883616 | tf_op jit(solution)/shard_map/ppermute | solution.py:480
  801.4 5.2 add_convert_fusion.2
  807.0 47.8 %collective-permute-done.65 = bf16[1024,1408]{1,0:T(8,128)(2,1)} collective-permute-done((bf16[1024,1408]{1,0:T(8,128)(2,1)}, bf16[1024,1408]{1,0:T(8,128)(2,1)}, u32[]{:S(2)}, u32[]{:S(2)}) %collective-permute-start.65) | collective-permute-done | bytes 2883616 | tf_op jit(solution)/shard_map/ppermute | solution.py:480
  854.8 5.2 add_convert_fusion.3
  869.7 30.2 %collective-permute-done.71 = bf16[256,1408]{1,0:T(8,128)(2,1)S(1)} collective-permute-done((bf16[256,1408]{1,0:T(8,128)(2,1)S(1)}, bf16[256,1408]{1,0:T(8,128)(2,1)S(1)}, u32[]{:S(2)}, u32[]{:S(2)}) %collective-permute-start.71) | collective-permute-done | bytes 720928 | tf_op jit(solution)/shard_map/ppermute | solution.py:504
  899.8 27.7 %collective-permute-done.72 = bf16[256,1408]{1,0:T(8,128)(2,1)S(1)} collective-permute-done((bf16[256,1408]{1,0:T(8,128)(2,1)S(1)}, bf16[256,1408]{1,0:T(8,128)(2,1)S(1)}, u32[]{:S(2)}, u32[]{:S(2)}) %collective-permute-start.72) | collective-permute-done | bytes 720928 | tf_op jit(solution)/shard_map/ppermute | solution.py:504
  939.8 11.6 collective-permute-done.67
  956.6 12.2 all-gather.12.cloned.1.call-done
  968.7 10.0 fusion.136.g_ref
  978.8 54.3 %mixer_backward.1 = (bf16[1024,1024]{1,0:T(8,128)(2,1)S(1)}, bf16[1024,1024]{1,0:T(8,128)(2,1)S(1)}, bf16[1024,1024]{1,0:T(8,128)(2,1)}, bf16[1024,128]{1,0:T(8,...) custom-call(f32[1024,1024]{1,0:T(8,128)} %fusion.129.q_ref.k_ref.qh_, ...), custom_call_target="tpu_custom_call" | custom-call | flops 40000000000 | bytes 60000000 | tf_op jit(solution)/shard_map/mixer_backward/pallas_call | solution.py:382
  1043.3 9.6 fusion.138
  1052.9 6.7 fusion.137
  1059.6 13.4 add_convert_fusion
  1074.8 5.5 fusion.22
  1096.2 16.8 %all-reduce.9.cloned.1.call-done = f32[8,3072]{1,0:T(8,128)} async-done(((f32[8,3072]{1,0:T(8,128)}), f32[8,3072]{1,0:T(8,128)}) %all-reduce.9.cloned.1.call-update) | async-done | bytes 98320
  1121.6 7.9 collective-permute-done.61
  1137.3 37.2 %collective-permute-done.49 = bf16[1024,1024]{1,0:T(8,128)(2,1)} collective-permute-done((bf16[1024,1024]{1,0:T(8,128)(2,1)}, bf16[1024,1024]{1,0:T(8,128)(2,1)}, u32[]{:S(2)}, u32[]{:S(2)}) %collective-permute-start.49) | collective-permute-done | bytes 2097184 | tf_op jit(solution)/shard_map/ppermute | solution.py:480
  1179.3 40.1 %collective-permute-done.57 = bf16[1024,1024]{1,0:T(8,128)(2,1)} collective-permute-done((bf16[1024,1024]{1,0:T(8,128)(2,1)}, bf16[1024,1024]{1,0:T(8,128)(2,1)}, u32[]{:S(2)}, u32[]{:S(2)}) %collective-permute-start.57) | collective-permute-done | bytes 2097184 | tf_op jit(solution)/shard_map/ppermute | solution.py:480
  1225.0 38.7 %collective-permute-done.53 = bf16[1024,1024]{1,0:T(8,128)(2,1)} collective-permute-done((bf16[1024,1024]{1,0:T(8,128)(2,1)}, bf16[1024,1024]{1,0:T(8,128)(2,1)}, u32[]{:S(2)}, u32[]{:S(2)}) %collective-permute-start.53) | collective-permute-done | bytes 2097184 | tf_op jit(solution)/shard_map/ppermute | solution.py:480
  1276.2 24.6 %collective-permute-done.51 = bf16[256,1024]{1,0:T(8,128)(2,1)S(1)} collective-permute-done((bf16[256,1024]{1,0:T(8,128)(2,1)S(1)}, bf16[256,1024]{1,0:T(8,128)(2,1)S(1)}, u32[]{:S(2)}, u32[]{:S(2)}) %collective-permute-start.51) | collective-permute-done | bytes 524320 | tf_op jit(solution)/shard_map/ppermute | solution.py:504
  1300.8 39.1 %collective-permute-done.52 = bf16[256,1024]{1,0:T(8,128)(2,1)S(1)} collective-permute-done((bf16[256,1024]{1,0:T(8,128)(2,1)S(1)}, bf16[256,1024]{1,0:T(8,128)(2,1)S(1)}, u32[]{:S(2)}, u32[]{:S(2)}) %collective-permute-start.52) | collective-permute-done | bytes 524320 | tf_op jit(solution)/shard_map/ppermute | solution.py:504
  1341.6 25.3 %collective-permute-done.59 = bf16[256,1024]{1,0:T(8,128)(2,1)S(1)} collective-permute-done((bf16[256,1024]{1,0:T(8,128)(2,1)S(1)}, bf16[256,1024]{1,0:T(8,128)(2,1)S(1)}, u32[]{:S(2)}, u32[]{:S(2)}) %collective-permute-start.59) | collective-permute-done | bytes 524320 | tf_op jit(solution)/shard_map/ppermute | solution.py:504
  1369.3 8.8 collective-permute-done.54
  1378.1 11.1 collective-permute-done.55
  1396.6 42.8 %all-reduce.6 = (f32[2048]{0:T(1024)}, f32[16]{0:T(128)}, f32[16]{0:T(128)}, f32[256]{0:T(256)}, f32[2048]{0:T(1024)}) all-reduce(f32[2048]{0:T(1024)S(1)} %bitcast.124, f32[16]{0:T(128)S(1)} %bitcast_dynamic-update-slice_fusion.1, f32[16]{0:T(128)S(1)} %bitcast_dynamic-update-slice_fusion, ...), channel_id=1, replica_groups=mesh['dp'=8,'tensor'=4] {'dp','tensor'}, use_global_device_ids=true, to_apply=%region_9.10 | all-reduce | flops 4384 | bytes 35072 | tf_op jit(solution)/shard_map/psum | solution.py:650
  (615 shorter events, 264.2 us)
Async XLA Ops:
  7.2 249.5 %all-gather.6.cloned.1.call-start = ((), (), s32[]{:S(2)}) async-start(), calls=%async_computation.4 | async-start | bytes 5242880 | tf_op jit(solution)/shard_map/all_gather | solution.py:526
  10.8 71.5 %collective-permute-start.2 = (bf16[256,1024]{1,0:T(8,128)(2,1)}, bf16[256,1024]{1,0:T(8,128)(2,1)S(1)}, u32[]{:S(2)}, u32[]{:S(2)}) collective-permute-start(bf16[256,1024]{1,0:T(8,128)(2,1)} %get-tuple-element.208), channel_id=1, source_target_pairs={{24,0},{28,4},{0,8},{4,12},{8,16},{12,20},{16,24},{20,28},{25,1},{... | collective-permute-start | bytes 1572872 | tf_op jit(solution)/shard_map/ppermute | solution.py:484
  12.4 72.1 %collective-permute-start = (bf16[256,1024]{1,0:T(8,128)(2,1)}, bf16[256,1024]{1,0:T(8,128)(2,1)}, u32[]{:S(2)}, u32[]{:S(2)}) collective-permute-start(bf16[256,1024]{1,0:T(8,128)(2,1)} %get-tuple-element.208), channel_id=1, source_target_pairs={{8,0},{12,4},{16,8},{20,12},{24,16},{28,20},{0,24},{4,28},{9,1},{1... | collective-permute-start | bytes 1572872 | tf_op jit(solution)/shard_map/ppermute | solution.py:484
  12.8 76.7 %collective-permute-start.1 = (bf16[256,1024]{1,0:T(8,128)(2,1)}, bf16[256,1024]{1,0:T(8,128)(2,1)}, u32[]{:S(2)}, u32[]{:S(2)}) collective-permute-start(bf16[256,1024]{1,0:T(8,128)(2,1)} %get-tuple-element.208), channel_id=1, source_target_pairs={{16,0},{20,4},{24,8},{28,12},{0,16},{4,20},{8,24},{12,28},{17,1},{... | collective-permute-start | bytes 1572872 | tf_op jit(solution)/shard_map/ppermute | solution.py:484
  15.4 78.1 %collective-permute-start.3 = (bf16[256,1024]{1,0:T(8,128)(2,1)}, bf16[256,1024]{1,0:T(8,128)(2,1)}, u32[]{:S(2)}, u32[]{:S(2)}) collective-permute-start(bf16[256,1024]{1,0:T(8,128)(2,1)} %get-tuple-element.208), channel_id=1, source_target_pairs={{0,4},{4,0},{8,12},{12,8},{16,20},{20,16},{24,28},{28,24},{1,5},{5... | collective-permute-start | bytes 1572872 | tf_op jit(solution)/shard_map/ppermute | solution.py:480
  21.0 448.5 %reduce-scatter.5.cloned.1.call-start = ((), (), s32[]{:S(2)}) async-start(), calls=%async_computation.5 | async-start | bytes 10485760 | tf_op jit(solution)/shard_map/reduce_scatter | solution.py:530
  84.5 38.3 %collective-permute-start.8 = (bf16[256,1024]{1,0:T(8,128)(2,1)S(1)}, bf16[256,1024]{1,0:T(8,128)(2,1)S(1)}, u32[]{:S(2)}, u32[]{:S(2)}) collective-permute-start(bf16[256,1024]{1,0:T(8,128)(2,1)S(1)} %copy-done.38), channel_id=1, source_target_pairs={{16,0},{20,4},{24,8},{28,12},{0,16},{4,20},{8,24},{12,28},{17,1},{... | collective-permute-start | bytes 1572872 | tf_op jit(solution)/shard_map/ppermute | solution.py:484
  127.8 42.1 %collective-permute-start.15 = (bf16[256,1024]{1,0:T(8,128)(2,1)S(1)}, bf16[256,1024]{1,0:T(8,128)(2,1)S(1)}, u32[]{:S(2)}, u32[]{:S(2)}) collective-permute-start(bf16[256,1024]{1,0:T(8,128)(2,1)S(1)} %copy-done.39), channel_id=1, source_target_pairs={{16,0},{20,4},{24,8},{28,12},{0,16},{4,20},{8,24},{12,28},{17,1},{... | collective-permute-start | bytes 1572872 | tf_op jit(solution)/shard_map/ppermute | solution.py:484
  131.1 38.9 %collective-permute-start.17 = (bf16[256,1024]{1,0:T(8,128)(2,1)S(1)}, bf16[256,1024]{1,0:T(8,128)(2,1)S(1)}, u32[]{:S(2)}, u32[]{:S(2)}) collective-permute-start(bf16[256,1024]{1,0:T(8,128)(2,1)S(1)} %copy-done.39), channel_id=1, source_target_pairs={{0,4},{4,0},{8,12},{12,8},{16,20},{20,16},{24,28},{28,24},{1,5},{5... | collective-permute-start | bytes 1572872 | tf_op jit(solution)/shard_map/ppermute | solution.py:480
  132.2 42.9 %collective-permute-start.11 = (bf16[256,1024]{1,0:T(8,128)(2,1)S(1)}, bf16[256,1024]{1,0:T(8,128)(2,1)S(1)}, u32[]{:S(2)}, u32[]{:S(2)}) collective-permute-start(bf16[256,1024]{1,0:T(8,128)(2,1)S(1)} %collective-permute-done.7), channel_id=1, source_target_pairs={{0,4},{4,0},{8,12},{12,8},{16,20},{20,16},{24,28},{28,24},{1,5},{5... | collective-permute-start | bytes 1572872 | tf_op jit(solution)/shard_map/ppermute | solution.py:480
  170.0 38.5 %collective-permute-start.21 = (bf16[256,1024]{1,0:T(8,128)(2,1)S(1)}, bf16[256,1024]{1,0:T(8,128)(2,1)S(1)}, u32[]{:S(2)}, u32[]{:S(2)}) collective-permute-start(bf16[256,1024]{1,0:T(8,128)(2,1)S(1)} %copy-done.40), channel_id=1, source_target_pairs={{8,0},{12,4},{16,8},{20,12},{24,16},{28,20},{0,24},{4,28},{9,1},{1... | collective-permute-start | bytes 1572872 | tf_op jit(solution)/shard_map/ppermute | solution.py:484
  175.3 41.8 %collective-permute-start.23 = (bf16[256,1024]{1,0:T(8,128)(2,1)S(1)}, bf16[256,1024]{1,0:T(8,128)(2,1)S(1)}, u32[]{:S(2)}, u32[]{:S(2)}) collective-permute-start(bf16[256,1024]{1,0:T(8,128)(2,1)S(1)} %copy-done.40), channel_id=1, source_target_pairs={{24,0},{28,4},{0,8},{4,12},{8,16},{12,20},{16,24},{20,28},{25,1},{... | collective-permute-start | bytes 1572872 | tf_op jit(solution)/shard_map/ppermute | solution.py:484
  219.6 36.3 %collective-permute-start.27 = (bf16[256,1024]{1,0:T(8,128)(2,1)S(1)}, bf16[256,1024]{1,0:T(8,128)(2,1)S(1)}, u32[]{:S(2)}, u32[]{:S(2)}) collective-permute-start(bf16[256,1024]{1,0:T(8,128)(2,1)S(1)} %collective-permute-done.23), channel_id=1, source_target_pairs={{0,4},{4,0},{8,12},{12,8},{16,20},{20,16},{24,28},{28,24},{1,5},{5... | collective-permute-start | bytes 1572872 | tf_op jit(solution)/shard_map/ppermute | solution.py:480
  332.2 272.6 %all-gather.10.cloned.1.call-start = ((), (), s32[]{:S(2)}) async-start(), calls=%async_computation.8 | async-start | bytes 5242880 | tf_op jit(solution)/shard_map/all_gather | solution.py:526
  337.9 278.6 %all-gather.8.cloned.1.call-start = ((), (), s32[]{:S(2)}) async-start(), calls=%async_computation.6 | async-start | bytes 5242880 | tf_op jit(solution)/shard_map/all_gather | solution.py:526
  349.0 73.3 %collective-permute-start.30 = (bf16[256,1408]{1,0:T(8,128)(2,1)S(1)}, bf16[256,1408]{1,0:T(8,128)(2,1)S(1)}, u32[]{:S(2)}, u32[]{:S(2)}) collective-permute-start(bf16[256,1408]{1,0:T(8,128)(2,1)S(1)} %copy-done.34), channel_id=1, source_target_pairs={{24,0},{28,4},{0,8},{4,12},{8,16},{12,20},{16,24},{20,28},{25,1},{... | collective-permute-start | bytes 2162696 | tf_op jit(solution)/shard_map/ppermute | solution.py:484
  351.7 76.7 %collective-permute-start.28 = (bf16[256,1408]{1,0:T(8,128)(2,1)S(1)}, bf16[256,1408]{1,0:T(8,128)(2,1)}, u32[]{:S(2)}, u32[]{:S(2)}) collective-permute-start(bf16[256,1408]{1,0:T(8,128)(2,1)S(1)} %copy-done.34), channel_id=1, source_target_pairs={{8,0},{12,4},{16,8},{20,12},{24,16},{28,20},{0,24},{4,28},{9,1},{1... | collective-permute-start | bytes 2162696 | tf_op jit(solution)/shard_map/ppermute | solution.py:484
  351.8 93.8 %collective-permute-start.29 = (bf16[256,1408]{1,0:T(8,128)(2,1)S(1)}, bf16[256,1408]{1,0:T(8,128)(2,1)}, u32[]{:S(2)}, u32[]{:S(2)}) collective-permute-start(bf16[256,1408]{1,0:T(8,128)(2,1)S(1)} %copy-done.34), channel_id=1, source_target_pairs={{16,0},{20,4},{24,8},{28,12},{0,16},{4,20},{8,24},{12,28},{17,1},{... | collective-permute-start | bytes 2162696 | tf_op jit(solution)/shard_map/ppermute | solution.py:484
  353.3 94.0 %collective-permute-start.31 = (bf16[256,1408]{1,0:T(8,128)(2,1)S(1)}, bf16[256,1408]{1,0:T(8,128)(2,1)S(1)}, u32[]{:S(2)}, u32[]{:S(2)}) collective-permute-start(bf16[256,1408]{1,0:T(8,128)(2,1)S(1)} %copy-done.34), channel_id=1, source_target_pairs={{0,4},{4,0},{8,12},{12,8},{16,20},{20,16},{24,28},{28,24},{1,5},{5... | collective-permute-start | bytes 2162696 | tf_op jit(solution)/shard_map/ppermute | solution.py:480
  422.3 50.4 %collective-permute-start.35 = (bf16[256,1408]{1,0:T(8,128)(2,1)}, bf16[256,1408]{1,0:T(8,128)(2,1)}, u32[]{:S(2)}, u32[]{:S(2)}) collective-permute-start(bf16[256,1408]{1,0:T(8,128)(2,1)} %param.40), channel_id=1, source_target_pairs={{8,0},{12,4},{16,8},{20,12},{24,16},{28,20},{0,24},{4,28},{9,1},{1... | collective-permute-start | bytes 2162696 | tf_op jit(solution)/shard_map/ppermute | solution.py:484
  422.3 54.2 %collective-permute-start.36 = (bf16[256,1408]{1,0:T(8,128)(2,1)}, bf16[256,1408]{1,0:T(8,128)(2,1)}, u32[]{:S(2)}, u32[]{:S(2)}) collective-permute-start(bf16[256,1408]{1,0:T(8,128)(2,1)} %param.40), channel_id=1, source_target_pairs={{16,0},{20,4},{24,8},{28,12},{0,16},{4,20},{8,24},{12,28},{17,1},{... | collective-permute-start | bytes 2162696 | tf_op jit(solution)/shard_map/ppermute | solution.py:484
  428.4 39.8 %collective-permute-start.37 = (bf16[256,1408]{1,0:T(8,128)(2,1)}, bf16[256,1408]{1,0:T(8,128)(2,1)}, u32[]{:S(2)}, u32[]{:S(2)}) collective-permute-start(bf16[256,1408]{1,0:T(8,128)(2,1)} %param.40), channel_id=1, source_target_pairs={{24,0},{28,4},{0,8},{4,12},{8,16},{12,20},{16,24},{20,28},{25,1},{... | collective-permute-start | bytes 2162696 | tf_op jit(solution)/shard_map/ppermute | solution.py:484
  447.3 39.4 %collective-permute-start.32 = (bf16[256,1408]{1,0:T(8,128)(2,1)}, bf16[256,1408]{1,0:T(8,128)(2,1)}, u32[]{:S(2)}, u32[]{:S(2)}) collective-permute-start(bf16[256,1408]{1,0:T(8,128)(2,1)} %collective-permute-done.28), channel_id=1, source_target_pairs={{0,4},{4,0},{8,12},{12,8},{16,20},{20,16},{24,28},{28,24},{1,5},{5... | collective-permute-start | bytes 2162696 | tf_op jit(solution)/shard_map/ppermute | solution.py:480
  472.6 456.3 %reduce-scatter.9.cloned.1.call-start = ((), (), s32[]{:S(2)}) async-start(), calls=%async_computation.9 | async-start | bytes 10485760 | tf_op jit(solution)/shard_map/reduce_scatter | solution.py:530
  476.5 49.6 %collective-permute-start.42 = (bf16[256,1408]{1,0:T(8,128)(2,1)}, bf16[256,1408]{1,0:T(8,128)(2,1)S(1)}, u32[]{:S(2)}, u32[]{:S(2)}) collective-permute-start(bf16[256,1408]{1,0:T(8,128)(2,1)} %param.41), channel_id=1, source_target_pairs={{8,0},{12,4},{16,8},{20,12},{24,16},{28,20},{0,24},{4,28},{9,1},{1... | collective-permute-start | bytes 2162696 | tf_op jit(solution)/shard_map/ppermute | solution.py:484
  480.7 46.9 %collective-permute-start.43 = (bf16[256,1408]{1,0:T(8,128)(2,1)S(1)}, bf16[256,1408]{1,0:T(8,128)(2,1)S(1)}, u32[]{:S(2)}, u32[]{:S(2)}) collective-permute-start(bf16[256,1408]{1,0:T(8,128)(2,1)S(1)} %copy-done.36), channel_id=1, source_target_pairs={{16,0},{20,4},{24,8},{28,12},{0,16},{4,20},{8,24},{12,28},{17,1},{... | collective-permute-start | bytes 2162696 | tf_op jit(solution)/shard_map/ppermute | solution.py:484
  489.1 43.7 %collective-permute-start.44 = (bf16[256,1408]{1,0:T(8,128)(2,1)S(1)}, bf16[256,1408]{1,0:T(8,128)(2,1)S(1)}, u32[]{:S(2)}, u32[]{:S(2)}) collective-permute-start(bf16[256,1408]{1,0:T(8,128)(2,1)S(1)} %copy-done.36), channel_id=1, source_target_pairs={{24,0},{28,4},{0,8},{4,12},{8,16},{12,20},{16,24},{20,28},{25,1},{... | collective-permute-start | bytes 2162696 | tf_op jit(solution)/shard_map/ppermute | solution.py:484
  502.9 62.7 %collective-permute-start.45 = (bf16[256,1408]{1,0:T(8,128)(2,1)S(1)}, bf16[256,1408]{1,0:T(8,128)(2,1)S(1)}, u32[]{:S(2)}, u32[]{:S(2)}) collective-permute-start(bf16[256,1408]{1,0:T(8,128)(2,1)S(1)} %copy-done.36), channel_id=1, source_target_pairs={{0,4},{4,0},{8,12},{12,8},{16,20},{20,16},{24,28},{28,24},{1,5},{5... | collective-permute-start | bytes 2162696 | tf_op jit(solution)/shard_map/ppermute | solution.py:480
  526.2 38.5 %collective-permute-start.41 = (bf16[256,1408]{1,0:T(8,128)(2,1)}, bf16[256,1408]{1,0:T(8,128)(2,1)S(1)}, u32[]{:S(2)}, u32[]{:S(2)}) collective-permute-start(bf16[256,1408]{1,0:T(8,128)(2,1)} %collective-permute-done.37), channel_id=1, source_target_pairs={{0,4},{4,0},{8,12},{12,8},{16,20},{20,16},{24,28},{28,24},{1,5},{5... | collective-permute-start | bytes 2162696 | tf_op jit(solution)/shard_map/ppermute | solution.py:480
  527.6 52.5 %collective-permute-start.46 = (bf16[256,1408]{1,0:T(8,128)(2,1)S(1)}, bf16[256,1408]{1,0:T(8,128)(2,1)S(1)}, u32[]{:S(2)}, u32[]{:S(2)}) collective-permute-start(bf16[256,1408]{1,0:T(8,128)(2,1)S(1)} %collective-permute-done.42), channel_id=1, source_target_pairs={{0,4},{4,0},{8,12},{12,8},{16,20},{20,16},{24,28},{28,24},{1,5},{5... | collective-permute-start | bytes 2162696 | tf_op jit(solution)/shard_map/ppermute | solution.py:480
  532.8 62.8 %collective-permute-start.47 = (bf16[256,1408]{1,0:T(8,128)(2,1)S(1)}, bf16[256,1408]{1,0:T(8,128)(2,1)S(1)}, u32[]{:S(2)}, u32[]{:S(2)}) collective-permute-start(bf16[256,1408]{1,0:T(8,128)(2,1)S(1)} %collective-permute-done.43), channel_id=1, source_target_pairs={{0,4},{4,0},{8,12},{12,8},{16,20},{20,16},{24,28},{28,24},{1,5},{5... | collective-permute-start | bytes 2162696 | tf_op jit(solution)/shard_map/ppermute | solution.py:480
  549.3 54.5 %collective-permute-start.48 = (bf16[256,1408]{1,0:T(8,128)(2,1)S(1)}, bf16[256,1408]{1,0:T(8,128)(2,1)S(1)}, u32[]{:S(2)}, u32[]{:S(2)}) collective-permute-start(bf16[256,1408]{1,0:T(8,128)(2,1)S(1)} %collective-permute-done.44), channel_id=1, source_target_pairs={{0,4},{4,0},{8,12},{12,8},{16,20},{20,16},{24,28},{28,24},{1,5},{5... | collective-permute-start | bytes 2162696 | tf_op jit(solution)/shard_map/ppermute | solution.py:480
  665.4 265.7 %reduce-scatter.7.cloned.1.call-start = ((), (), s32[]{:S(2)}) async-start(), calls=%async_computation.7 | async-start | bytes 5242880 | tf_op jit(solution)/shard_map/reduce_scatter | solution.py:530
  673.9 65.7 %collective-permute-start.73 = (bf16[1024,1408]{1,0:T(8,128)(2,1)}, bf16[1024,1408]{1,0:T(8,128)(2,1)}, u32[]{:S(2)}, u32[]{:S(2)}) collective-permute-start(bf16[1024,1408]{1,0:T(8,128)(2,1)} %convolution_convert_fusion.1), channel_id=1, source_target_pairs={{0,4},{4,0},{8,12},{12,8},{16,20},{20,16},{24,28},{28,24},{1,5},{5... | collective-permute-start | bytes 8650760 | tf_op jit(solution)/shard_map/ppermute | solution.py:480
  686.6 282.2 %all-gather.12.cloned.1.call-start = ((), (), s32[]{:S(2)}) async-start(), calls=%async_computation.10 | async-start | bytes 5242880 | tf_op jit(solution)/shard_map/all_gather | solution.py:526
  695.0 106.5 %collective-permute-start.69 = (bf16[1024,1408]{1,0:T(8,128)(2,1)}, bf16[1024,1408]{1,0:T(8,128)(2,1)}, u32[]{:S(2)}, u32[]{:S(2)}) collective-permute-start(bf16[1024,1408]{1,0:T(8,128)(2,1)} %convolution_convert_fusion.2), channel_id=1, source_target_pairs={{0,4},{4,0},{8,12},{12,8},{16,20},{20,16},{24,28},{28,24},{1,5},{5... | collective-permute-start | bytes 8650760 | tf_op jit(solution)/shard_map/ppermute | solution.py:480
  701.2 153.6 %collective-permute-start.65 = (bf16[1024,1408]{1,0:T(8,128)(2,1)}, bf16[1024,1408]{1,0:T(8,128)(2,1)}, u32[]{:S(2)}, u32[]{:S(2)}) collective-permute-start(bf16[1024,1408]{1,0:T(8,128)(2,1)} %convolution_convert_fusion.3), channel_id=1, source_target_pairs={{0,4},{4,0},{8,12},{12,8},{16,20},{20,16},{24,28},{28,24},{1,5},{5... | collective-permute-start | bytes 8650760 | tf_op jit(solution)/shard_map/ppermute | solution.py:480
  746.7 113.3 %collective-permute-start.74 = (bf16[256,1408]{1,0:T(8,128)(2,1)S(1)}, bf16[256,1408]{1,0:T(8,128)(2,1)S(1)}, u32[]{:S(2)}, u32[]{:S(2)}) collective-permute-start(bf16[256,1408]{1,0:T(8,128)(2,1)S(1)} %get-tuple-element.128), channel_id=1, source_target_pairs={{0,8},{4,12},{8,16},{12,20},{16,24},{20,28},{24,0},{28,4},{1,9},{5... | collective-permute-start | bytes 2162696 | tf_op jit(solution)/shard_map/ppermute | solution.py:504
  746.8 114.9 %collective-permute-start.75 = (bf16[256,1408]{1,0:T(8,128)(2,1)S(1)}, bf16[256,1408]{1,0:T(8,128)(2,1)S(1)}, u32[]{:S(2)}, u32[]{:S(2)}) collective-permute-start(bf16[256,1408]{1,0:T(8,128)(2,1)S(1)} %get-tuple-element.130), channel_id=1, source_target_pairs={{0,16},{4,20},{8,24},{12,28},{16,0},{20,4},{24,8},{28,12},{1,17},{... | collective-permute-start | bytes 2162696 | tf_op jit(solution)/shard_map/ppermute | solution.py:504
  746.9 116.6 %collective-permute-start.76 = (bf16[256,1408]{1,0:T(8,128)(2,1)S(1)}, bf16[256,1408]{1,0:T(8,128)(2,1)S(1)}, u32[]{:S(2)}, u32[]{:S(2)}) collective-permute-start(bf16[256,1408]{1,0:T(8,128)(2,1)S(1)} %get-tuple-element.129), channel_id=1, source_target_pairs={{0,24},{4,28},{8,0},{12,4},{16,8},{20,12},{24,16},{28,20},{1,25},{... | collective-permute-start | bytes 2162696 | tf_op jit(solution)/shard_map/ppermute | solution.py:504
  806.8 62.9 %collective-permute-start.70 = (bf16[256,1408]{1,0:T(8,128)(2,1)S(1)}, bf16[256,1408]{1,0:T(8,128)(2,1)S(1)}, u32[]{:S(2)}, u32[]{:S(2)}) collective-permute-start(bf16[256,1408]{1,0:T(8,128)(2,1)S(1)} %get-tuple-element.131), channel_id=1, source_target_pairs={{0,8},{4,12},{8,16},{12,20},{16,24},{20,28},{24,0},{28,4},{1,9},{5... | collective-permute-start | bytes 2162696 | tf_op jit(solution)/shard_map/ppermute | solution.py:504
  854.8 45.0 %collective-permute-start.71 = (bf16[256,1408]{1,0:T(8,128)(2,1)S(1)}, bf16[256,1408]{1,0:T(8,128)(2,1)S(1)}, u32[]{:S(2)}, u32[]{:S(2)}) collective-permute-start(bf16[256,1408]{1,0:T(8,128)(2,1)S(1)} %get-tuple-element.133), channel_id=1, source_target_pairs={{0,16},{4,20},{8,24},{12,28},{16,0},{20,4},{24,8},{28,12},{1,17},{... | collective-permute-start | bytes 2162696 | tf_op jit(solution)/shard_map/ppermute | solution.py:504
  860.1 67.5 %collective-permute-start.72 = (bf16[256,1408]{1,0:T(8,128)(2,1)S(1)}, bf16[256,1408]{1,0:T(8,128)(2,1)S(1)}, u32[]{:S(2)}, u32[]{:S(2)}) collective-permute-start(bf16[256,1408]{1,0:T(8,128)(2,1)S(1)} %get-tuple-element.132), channel_id=1, source_target_pairs={{0,24},{4,28},{8,0},{12,4},{16,8},{20,12},{24,16},{28,20},{1,25},{... | collective-permute-start | bytes 2162696 | tf_op jit(solution)/shard_map/ppermute | solution.py:504
  861.7 78.2 %collective-permute-start.66 = (bf16[256,1408]{1,0:T(8,128)(2,1)}, bf16[256,1408]{1,0:T(8,128)(2,1)}, u32[]{:S(2)}, u32[]{:S(2)}) collective-permute-start(bf16[256,1408]{1,0:T(8,128)(2,1)} %get-tuple-element.134), channel_id=1, source_target_pairs={{0,8},{4,12},{8,16},{12,20},{16,24},{20,28},{24,0},{28,4},{1,9},{5... | collective-permute-start | bytes 2162696 | tf_op jit(solution)/shard_map/ppermute | solution.py:504
  863.5 87.9 %collective-permute-start.67 = (bf16[256,1408]{1,0:T(8,128)(2,1)}, bf16[256,1408]{1,0:T(8,128)(2,1)}, u32[]{:S(2)}, u32[]{:S(2)}) collective-permute-start(bf16[256,1408]{1,0:T(8,128)(2,1)} %get-tuple-element.136), channel_id=1, source_target_pairs={{0,16},{4,20},{8,24},{12,28},{16,0},{20,4},{24,8},{28,12},{1,17},{... | collective-permute-start | bytes 2162696 | tf_op jit(solution)/shard_map/ppermute | solution.py:504
  869.7 81.8 %collective-permute-start.68 = (bf16[256,1408]{1,0:T(8,128)(2,1)}, bf16[256,1408]{1,0:T(8,128)(2,1)}, u32[]{:S(2)}, u32[]{:S(2)}) collective-permute-start(bf16[256,1408]{1,0:T(8,128)(2,1)} %get-tuple-element.135), channel_id=1, source_target_pairs={{0,24},{4,28},{8,0},{12,4},{16,8},{20,12},{24,16},{28,20},{1,25},{... | collective-permute-start | bytes 2162696 | tf_op jit(solution)/shard_map/ppermute | solution.py:504
  935.9 177.0 %all-reduce.9.cloned.1.call-start = ((), (), s32[]{:S(2)}) async-start(), calls=%async_computation.12 | async-start | bytes 196608
  1043.2 347.5 %reduce-scatter.11.cloned.1.call-start = ((), (), s32[]{:S(2)}) async-start(), calls=%async_computation.11 | async-start | bytes 5242880 | tf_op jit(solution)/shard_map/reduce_scatter | solution.py:530
  1080.3 49.3 %collective-permute-start.61 = (bf16[1024,1024]{1,0:T(8,128)(2,1)}, bf16[1024,1024]{1,0:T(8,128)(2,1)}, u32[]{:S(2)}, u32[]{:S(2)}) collective-permute-start(bf16[1024,1024]{1,0:T(8,128)(2,1)} %fusion.22), channel_id=1, source_target_pairs={{0,4},{4,0},{8,12},{12,8},{16,20},{20,16},{24,28},{28,24},{1,5},{5... | collective-permute-start | bytes 6291464 | tf_op jit(solution)/shard_map/ppermute | solution.py:480
  1084.6 89.9 %collective-permute-start.49 = (bf16[1024,1024]{1,0:T(8,128)(2,1)}, bf16[1024,1024]{1,0:T(8,128)(2,1)}, u32[]{:S(2)}, u32[]{:S(2)}) collective-permute-start(bf16[1024,1024]{1,0:T(8,128)(2,1)} %convolution_convert_fusion.6), channel_id=1, source_target_pairs={{0,4},{4,0},{8,12},{12,8},{16,20},{20,16},{24,28},{28,24},{1,5},{5... | collective-permute-start | bytes 6291464 | tf_op jit(solution)/shard_map/ppermute | solution.py:480
  1089.9 129.5 %collective-permute-start.57 = (bf16[1024,1024]{1,0:T(8,128)(2,1)}, bf16[1024,1024]{1,0:T(8,128)(2,1)}, u32[]{:S(2)}, u32[]{:S(2)}) collective-permute-start(bf16[1024,1024]{1,0:T(8,128)(2,1)} %convolution_convert_fusion.4), channel_id=1, source_target_pairs={{0,4},{4,0},{8,12},{12,8},{16,20},{20,16},{24,28},{28,24},{1,5},{5... | collective-permute-start | bytes 6291464 | tf_op jit(solution)/shard_map/ppermute | solution.py:480
  1094.3 169.4 %collective-permute-start.53 = (bf16[1024,1024]{1,0:T(8,128)(2,1)}, bf16[1024,1024]{1,0:T(8,128)(2,1)}, u32[]{:S(2)}, u32[]{:S(2)}) collective-permute-start(bf16[1024,1024]{1,0:T(8,128)(2,1)} %convolution_convert_fusion.5), channel_id=1, source_target_pairs={{0,4},{4,0},{8,12},{12,8},{16,20},{20,16},{24,28},{28,24},{1,5},{5... | collective-permute-start | bytes 6291464 | tf_op jit(solution)/shard_map/ppermute | solution.py:480
  1134.3 136.0 %collective-permute-start.62 = (bf16[256,1024]{1,0:T(8,128)(2,1)S(1)}, bf16[256,1024]{1,0:T(8,128)(2,1)S(1)}, u32[]{:S(2)}, u32[]{:S(2)}) collective-permute-start(bf16[256,1024]{1,0:T(8,128)(2,1)S(1)} %get-tuple-element.138), channel_id=1, source_target_pairs={{0,8},{4,12},{8,16},{12,20},{16,24},{20,28},{24,0},{28,4},{1,9},{5... | collective-permute-start | bytes 1572872 | tf_op jit(solution)/shard_map/ppermute | solution.py:504
  1135.9 135.1 %collective-permute-start.63 = (bf16[256,1024]{1,0:T(8,128)(2,1)S(1)}, bf16[256,1024]{1,0:T(8,128)(2,1)S(1)}, u32[]{:S(2)}, u32[]{:S(2)}) collective-permute-start(bf16[256,1024]{1,0:T(8,128)(2,1)S(1)} %get-tuple-element.140), channel_id=1, source_target_pairs={{0,16},{4,20},{8,24},{12,28},{16,0},{20,4},{24,8},{28,12},{1,17},{... | collective-permute-start | bytes 1572872 | tf_op jit(solution)/shard_map/ppermute | solution.py:504
  1174.5 98.1 %collective-permute-start.64 = (bf16[256,1024]{1,0:T(8,128)(2,1)S(1)}, bf16[256,1024]{1,0:T(8,128)(2,1)S(1)}, u32[]{:S(2)}, u32[]{:S(2)}) collective-permute-start(bf16[256,1024]{1,0:T(8,128)(2,1)S(1)} %get-tuple-element.139), channel_id=1, source_target_pairs={{0,24},{4,28},{8,0},{12,4},{16,8},{20,12},{24,16},{28,20},{1,25},{... | collective-permute-start | bytes 1572872 | tf_op jit(solution)/shard_map/ppermute | solution.py:504
  1219.4 56.8 %collective-permute-start.50 = (bf16[256,1024]{1,0:T(8,128)(2,1)S(1)}, bf16[256,1024]{1,0:T(8,128)(2,1)S(1)}, u32[]{:S(2)}, u32[]{:S(2)}) collective-permute-start(bf16[256,1024]{1,0:T(8,128)(2,1)S(1)} %get-tuple-element.147), channel_id=1, source_target_pairs={{0,8},{4,12},{8,16},{12,20},{16,24},{20,28},{24,0},{28,4},{1,9},{5... | collective-permute-start | bytes 1572872 | tf_op jit(solution)/shard_map/ppermute | solution.py:504
  1263.7 37.1 %collective-permute-start.51 = (bf16[256,1024]{1,0:T(8,128)(2,1)S(1)}, bf16[256,1024]{1,0:T(8,128)(2,1)S(1)}, u32[]{:S(2)}, u32[]{:S(2)}) collective-permute-start(bf16[256,1024]{1,0:T(8,128)(2,1)S(1)} %get-tuple-element.149), channel_id=1, source_target_pairs={{0,16},{4,20},{8,24},{12,28},{16,0},{20,4},{24,8},{28,12},{1,17},{... | collective-permute-start | bytes 1572872 | tf_op jit(solution)/shard_map/ppermute | solution.py:504
  1270.3 69.6 %collective-permute-start.52 = (bf16[256,1024]{1,0:T(8,128)(2,1)S(1)}, bf16[256,1024]{1,0:T(8,128)(2,1)S(1)}, u32[]{:S(2)}, u32[]{:S(2)}) collective-permute-start(bf16[256,1024]{1,0:T(8,128)(2,1)S(1)} %get-tuple-element.148), channel_id=1, source_target_pairs={{0,24},{4,28},{8,0},{12,4},{16,8},{20,12},{24,16},{28,20},{1,25},{... | collective-permute-start | bytes 1572872 | tf_op jit(solution)/shard_map/ppermute | solution.py:504
  1271.0 69.2 %collective-permute-start.58 = (bf16[256,1024]{1,0:T(8,128)(2,1)S(1)}, bf16[256,1024]{1,0:T(8,128)(2,1)S(1)}, u32[]{:S(2)}, u32[]{:S(2)}) collective-permute-start(bf16[256,1024]{1,0:T(8,128)(2,1)S(1)} %get-tuple-element.141), channel_id=1, source_target_pairs={{0,8},{4,12},{8,16},{12,20},{16,24},{20,28},{24,0},{28,4},{1,9},{5... | collective-permute-start | bytes 1572872 | tf_op jit(solution)/shard_map/ppermute | solution.py:504
  1272.6 94.3 %collective-permute-start.59 = (bf16[256,1024]{1,0:T(8,128)(2,1)S(1)}, bf16[256,1024]{1,0:T(8,128)(2,1)S(1)}, u32[]{:S(2)}, u32[]{:S(2)}) collective-permute-start(bf16[256,1024]{1,0:T(8,128)(2,1)S(1)} %get-tuple-element.143), channel_id=1, source_target_pairs={{0,16},{4,20},{8,24},{12,28},{16,0},{20,4},{24,8},{28,12},{1,17},{... | collective-permute-start | bytes 1572872 | tf_op jit(solution)/shard_map/ppermute | solution.py:504
  1276.2 91.8 %collective-permute-start.60 = (bf16[256,1024]{1,0:T(8,128)(2,1)S(1)}, bf16[256,1024]{1,0:T(8,128)(2,1)S(1)}, u32[]{:S(2)}, u32[]{:S(2)}) collective-permute-start(bf16[256,1024]{1,0:T(8,128)(2,1)S(1)} %get-tuple-element.142), channel_id=1, source_target_pairs={{0,24},{4,28},{8,0},{12,4},{16,8},{20,12},{24,16},{28,20},{1,25},{... | collective-permute-start | bytes 1572872 | tf_op jit(solution)/shard_map/ppermute | solution.py:504
  1300.8 77.3 %collective-permute-start.54 = (bf16[256,1024]{1,0:T(8,128)(2,1)S(1)}, bf16[256,1024]{1,0:T(8,128)(2,1)S(1)}, u32[]{:S(2)}, u32[]{:S(2)}) collective-permute-start(bf16[256,1024]{1,0:T(8,128)(2,1)S(1)} %get-tuple-element.144), channel_id=1, source_target_pairs={{0,8},{4,12},{8,16},{12,20},{16,24},{20,28},{24,0},{28,4},{1,9},{5... | collective-permute-start | bytes 1572872 | tf_op jit(solution)/shard_map/ppermute | solution.py:504
  1339.9 49.4 %collective-permute-start.55 = (bf16[256,1024]{1,0:T(8,128)(2,1)S(1)}, bf16[256,1024]{1,0:T(8,128)(2,1)S(1)}, u32[]{:S(2)}, u32[]{:S(2)}) collective-permute-start(bf16[256,1024]{1,0:T(8,128)(2,1)S(1)} %get-tuple-element.146), channel_id=1, source_target_pairs={{0,16},{4,20},{8,24},{12,28},{16,0},{20,4},{24,8},{28,12},{1,17},{... | collective-permute-start | bytes 1572872 | tf_op jit(solution)/shard_map/ppermute | solution.py:504
  1340.2 49.1 %collective-permute-start.56 = (bf16[256,1024]{1,0:T(8,128)(2,1)S(1)}, bf16[256,1024]{1,0:T(8,128)(2,1)S(1)}, u32[]{:S(2)}, u32[]{:S(2)}) collective-permute-start(bf16[256,1024]{1,0:T(8,128)(2,1)S(1)} %get-tuple-element.145), channel_id=1, source_target_pairs={{0,24},{4,28},{8,0},{12,4},{16,8},{20,12},{24,16},{28,20},{1,25},{... | collective-permute-start | bytes 1572872 | tf_op jit(solution)/shard_map/ppermute | solution.py:504
  (107 other events, 3961.7 us)
Sparse Core Ops, SparseCore 0:
  21.1 33.2 all-gather.5
  332.3 71.9 reduce-scatter.4
  406.5 34.4 all-gather.9
  472.8 34.8 all-gather.7
  665.6 69.8 reduce-scatter.8
  737.8 44.5 reduce-scatter.6
  936.0 32.6 all-gather.11
  1043.3 69.6 all-reduce.8
  1115.7 43.4 reduce-scatter.10

commit v2 on v1

--- a/solution.py
+++ b/solution.py
@@ -150,7 +150,7 @@
 def bwd_body(
     heads, dk, dv, q_ref, k_ref, v_ref, og_ref, ab_ref, qh_ref, kh_ref, vh_ref,
     tq_ref, tk_ref, tv_ref, par_ref, gain_ref, g_ref, o_ref, u_ref, t_ref, s_ref,
-    dqk_ref, dv_ref, dog_ref, dab_ref, dtq_ref, dtk_ref, dtv_ref, dpar_ref, dgain_ref,
+    draw_ref, dab_ref, dtq_ref, dtk_ref, dtv_ref, dpar_ref, dgain_ref,
     qb, kb, vb, qn, kn, vn, dstate,
 ):
     rows = CH
@@ -207,6 +207,7 @@
     ds1_b = [x.astype(BF) for x in ds1]
 
     gain = gain_ref[...]
+    og_at = 2 * heads * dk + heads * dv
     do_b = []
     dgain = jnp.zeros_like(gain)
     for h in hs:
@@ -218,7 +219,7 @@
         sg = sigmoid(og)
         gor = g * (o * r)
         dgain = dgain + jnp.sum(gor * (og * sg), axis=0, keepdims=True)
-        dog_ref[:, sl] = (gor * gain * (sg * (1.0 + og * (1.0 - sg)))).astype(BF)
+        draw_ref[:, og_at + h * dv : og_at + (h + 1) * dv] = (gor * gain * (sg * (1.0 + og * (1.0 - sg)))).astype(BF)
         m = g * gain * (og * sg)
         d_o = r * m - o * (r * r * r * jnp.mean(m * o, axis=-1, keepdims=True))
         do_b.append(d_o.astype(BF))
@@ -297,9 +298,9 @@
 
     wide = heads * dk
     for buf, cur, taps, out, at, dtap in (
-        (qn, qb, tq_ref, dqk_ref, 0, dtq_ref),
-        (kn, kb, tk_ref, dqk_ref, wide, dtk_ref),
-        (vn, vb, tv_ref, dv_ref, 0, dtv_ref),
+        (qn, qb, tq_ref, draw_ref, 0, dtq_ref),
+        (kn, kb, tk_ref, draw_ref, wide, dtk_ref),
+        (vn, vb, tv_ref, draw_ref, 2 * wide, dtv_ref),
     ):
         here = cur[HALO : HALO + rows, :]
         total = None
@@ -318,7 +319,9 @@
     return {
         "q": pl.BlockSpec((CH, wide_k), lambda c: (at(c), 0)),
         "k": pl.BlockSpec((CH, wide_k), lambda c: (at(c), 1)),
-        "qk": pl.BlockSpec((CH, 2 * wide_k), lambda c: (at(c), 0)),
+        "val": pl.BlockSpec((CH, wide_v), lambda c: (at(c), 2 * wide_k // wide_v)),
+        "og": pl.BlockSpec((CH, wide_v), lambda c: (at(c), 2 * wide_k // wide_v + 1)),
+        "raw": pl.BlockSpec((CH, 2 * (wide_k + wide_v)), lambda c: (at(c), 0)),
         "v": pl.BlockSpec((CH, wide_v), lambda c: (at(c), 0)),
         "ab": pl.BlockSpec((CH, LANES), lambda c: (at(c), 0)),
         "t": pl.BlockSpec((CH, heads * CH), lambda c: (at(c), 0)),
@@ -330,9 +333,8 @@
     }
 
 
-def mixer_forward(qk_raw, v_raw, og_raw, ab, tq, tk, tv, par, gain):
-    length, wide_k = qk_raw.shape[0], qk_raw.shape[1] // 2
-    wide_v = v_raw.shape[1]
+def mixer_forward(raw, ab, tq, tk, tv, par, gain):
+    length, wide_k, wide_v = raw.shape[0], tq.shape[1], tv.shape[1]
     dv = gain.shape[1]
     heads = wide_v // dv
     dk = wide_k // heads
@@ -341,7 +343,7 @@
     return pl.pallas_call(
         functools.partial(fwd_body, heads, dk, dv),
         grid=(steps,),
-        in_specs=[sp[n] for n in ("q", "k", "v", "v", "ab", "tk", "tk", "tv", "par", "gain")],
+        in_specs=[sp[n] for n in ("q", "k", "val", "og", "ab", "tk", "tk", "tv", "par", "gain")],
         out_specs=[sp[n] for n in ("v", "v", "v", "t", "s")],
         out_shape=[
             jax.ShapeDtypeStruct((length, wide_v), BF),
@@ -361,12 +363,11 @@
         ),
         cost_estimate=pl.CostEstimate(flops=20_000_000_000, bytes_accessed=40_000_000, transcendentals=6_000_000),
         name="mixer_forward",
-    )(qk_raw, qk_raw, v_raw, og_raw, ab, tq, tk, tv, par, gain)
-
-
-def mixer_backward(qk_raw, v_raw, og_raw, ab, tq, tk, tv, par, gain, grad, o, u, t, s):
-    length, wide_k = qk_raw.shape[0], qk_raw.shape[1] // 2
-    wide_v = v_raw.shape[1]
+    )(raw, raw, raw, raw, ab, tq, tk, tv, par, gain)
+
+
+def mixer_backward(raw, ab, tq, tk, tv, par, gain, grad, o, u, t, s):
+    length, wide_k, wide_v = raw.shape[0], tq.shape[1], tv.shape[1]
     dv = gain.shape[1]
     heads = wide_v // dv
     dk = wide_k // heads
@@ -376,18 +377,16 @@
     before = lambda c: jnp.maximum(at(c) * (CH // HALO) - 1, 0)
     hq = pl.BlockSpec((HALO, wide_k), lambda c: (before(c), 0))
     hk = pl.BlockSpec((HALO, wide_k), lambda c: (before(c), 1))
-    hv = pl.BlockSpec((HALO, wide_v), lambda c: (before(c), 0))
-    names = ("q", "k", "v", "v", "ab")
+    hv = pl.BlockSpec((HALO, wide_v), lambda c: (before(c), 2 * wide_k // wide_v))
+    names = ("q", "k", "val", "og", "ab")
     rest = ("tk", "tk", "tv", "par", "gain", "v", "v", "v", "t", "s")
     return pl.pallas_call(
         functools.partial(bwd_body, heads, dk, dv),
         grid=(steps,),
         in_specs=[sp[n] for n in names] + [hq, hk, hv] + [sp[n] for n in rest],
-        out_specs=[sp[n] for n in ("qk", "v", "v", "ab", "tk", "tk", "tv", "par", "gain")],
+        out_specs=[sp[n] for n in ("raw", "ab", "tk", "tk", "tv", "par", "gain")],
         out_shape=[
-            jax.ShapeDtypeStruct((length, 2 * wide_k), BF),
-            jax.ShapeDtypeStruct((length, wide_v), BF),
-            jax.ShapeDtypeStruct((length, wide_v), BF),
+            jax.ShapeDtypeStruct((length, 2 * (wide_k + wide_v)), BF),
             jax.ShapeDtypeStruct((length, LANES), BF),
             jax.ShapeDtypeStruct((8, wide_k), F32),
             jax.ShapeDtypeStruct((8, wide_k), F32),
@@ -410,8 +409,156 @@
         cost_estimate=pl.CostEstimate(flops=40_000_000_000, bytes_accessed=60_000_000, transcendentals=9_000_000),
         name="mixer_backward",
     )(
-        qk_raw, qk_raw, v_raw, og_raw, ab, qk_raw, qk_raw, v_raw, tq, tk, tv, par, gain, grad, o, u, t, s
-    )
+        raw, raw, raw, raw, ab, raw, raw, raw, tq, tk, tv, par, gain, grad, o, u, t, s
+    )
+
+
+def on_dp(index):
+    return {"dp": index}
+
+
+def greet(peers):
+    barrier = pltpu.get_barrier_semaphore()
+    for peer in peers:
+        pl.semaphore_signal(barrier, inc=1, device_id=on_dp(peer))
+    pl.semaphore_wait(barrier, len(peers))
+
+
+GATHER_CHUNKS = 8
+
+
+def gather_body(w_ref, small_ref, full_ref, all_ref, right_s, left_s, swap_s, arrive, few_s, few_r, local):
+    me = lax.axis_index("dp")
+    outer, side = me // 2, me % 2
+    block = w_ref.shape[0]
+    part = block // GATHER_CHUNKS
+    greet([(me + j) % 8 for j in range(1, 8)])
+    keep = pltpu.make_async_copy(w_ref, full_ref.at[pl.ds(0, block)], local.at[0])
+    keep.start()
+    keep_few = pltpu.make_async_copy(small_ref, all_ref.at[0], local.at[1])
+    keep_few.start()
+
+    def few(j):
+        peer = (me + j) % 8
+        slot = (outer - peer // 2 + 4) % 4 + 4 * ((side + peer % 2) % 2)
+        return pltpu.make_async_remote_copy(
+            small_ref, all_ref.at[slot], few_s.at[j - 1], few_r.at[j - 1], device_id=on_dp(peer)
+        )
+
+    for j in range(1, 8):
+        few(j).start()
+
+    def spot(slot, c):
+        return full_ref.at[pl.ds(slot * block + c * part, part)]
+
+    def source(slot, c):
+        return w_ref.at[pl.ds(c * part, part)] if slot == 0 else spot(slot, c)
+
+    def to_right(h, c):
+        return pltpu.make_async_remote_copy(
+            source((4 - h) % 4, c), spot(3 - h, c), right_s.at[h, c], arrive.at[3 - h, c], device_id=on_dp((me + 2) % 8)
+        )
+
+    def to_left(h, c):
+        return pltpu.make_async_remote_copy(
+            source(h, c), spot(h + 1, c), left_s.at[h, c], arrive.at[h + 1, c], device_id=on_dp((me + 6) % 8)
+        )
+
+    def to_side(slot, c):
+        return pltpu.make_async_remote_copy(
+            source(slot, c), spot(4 + slot, c), swap_s.at[slot, c], arrive.at[4 + slot, c],
+            device_id=on_dp(me + 1 - 2 * side),
+        )
+
+    def landed(slot, c):
+        pltpu.make_async_copy(spot(slot, c), spot(slot, c), arrive.at[slot, c]).wait()
+
+    def step(i, carry):
+        @pl.when(i < GATHER_CHUNKS)
+        def _():
+            to_side(0, i).start()
+
+            @pl.when(outer < 3)
+            def _():
+                to_right(0, i).start()
+
+            @pl.when(outer > 0)
+            def _():
+                to_left(0, i).start()
+
+        for h in range(1, 4):
+            c = i - h
+
+            @pl.when((c >= 0) & (c < GATHER_CHUNKS) & (outer >= h))
+            def _():
+                landed(4 - h, c)
+                if h < 3:
+                    @pl.when(outer < 3)
+                    def _():
+                        to_right(h, c).start()
+
+                to_side(4 - h, c).start()
+
+            @pl.when((c >= 0) & (c < GATHER_CHUNKS) & (outer + h < 4))
+            def _():
+                landed(h, c)
+                if h < 3:
+                    @pl.when(outer > 0)
+                    def _():
+                        to_left(h, c).start()
+
+                to_side(h, c).start()
+
+        return carry
+
+    lax.fori_loop(0, GATHER_CHUNKS + 3, step, 0)
+
+    def finish(c, carry):
+        for slot in range(4):
+            to_side(slot, c).wait_send()
+            landed(4 + slot, c)
+        for h in range(3):
+            @pl.when((outer >= h) & (outer < 3))
+            def _():
+                to_right(h, c).wait_send()
+
+            @pl.when((outer + h < 4) & (outer > 0))
+            def _():
+                to_left(h, c).wait_send()
+
+        return carry
+
+    lax.fori_loop(0, GATHER_CHUNKS, finish, 0)
+    for j in range(1, 8):
+        few(j).wait()
+    keep.wait()
+    keep_few.wait()
+
+
+def ring_gather(w, small):
+    n = GATHER_CHUNKS
+    any_ref = pl.BlockSpec(memory_space=pl.ANY)
+    return pl.pallas_call(
+        gather_body,
+        in_specs=[any_ref] * 2,
+        out_specs=[any_ref] * 2,
+        out_shape=[
+            jax.ShapeDtypeStruct((8 * w.shape[0], w.shape[1]), w.dtype),
+            jax.ShapeDtypeStruct((8,) + small.shape, small.dtype),
+        ],
+        scratch_shapes=[
+            pltpu.SemaphoreType.DMA((3, n)),
+            pltpu.SemaphoreType.DMA((3, n)),
+            pltpu.SemaphoreType.DMA((4, n)),
+            pltpu.SemaphoreType.DMA((8, n)),
+            pltpu.SemaphoreType.DMA((7,)),
+            pltpu.SemaphoreType.DMA((7,)),
+            pltpu.SemaphoreType.DMA((2,)),
+        ],
+        compiler_params=pltpu.CompilerParams(collective_id=0, has_side_effects=True),
+        cost_estimate=pl.CostEstimate(flops=0, bytes_accessed=400_000_000, transcendentals=0),
+        name="ring_gather",
+    )(w, small)
 
 
 def plain_dot(left_mat, right_mat):
@@ -438,7 +585,6 @@
     def __init__(self, dp_size):
         self.outer = dp_size // 2
         self.index = lax.axis_index("dp")
-        self.last = None
 
     def _roll(self, x, axis, blocks):
         size = x.shape[axis] // self.outer * blocks
@@ -483,13 +629,71 @@
         n = 2 * self.outer
         return lax.ppermute(x, "dp", [((i + 2 * steps) % n, i) for i in range(n)])
 
-    def gather(self, block):
-        if self.last is not None:
-            block, self.last = lax.optimization_barrier((block, self.last))
-        own = [block] + [self._from(block, k) for k in range(1, self.outer)]
-        self.last = own[-1]
-        other = [self._swap(b) for b in own]
-        return jnp.concatenate(own + other, axis=0)
+    def along(self, block):
+        return [block] + [self._from(block, k) for k in range(1, self.outer)]
+
+    def across(self, blocks):
+        return blocks + [self._swap(b) for b in blocks]
+
+    def gather_first(self, w, small):
+        return ring_gather(w, small)
+
+    def scatter_small(self, parts):
+        pair = parts[: self.outer] + self._swap(parts[self.outer :])
+        n = 2 * self.outer
+        total = pair[:1]
+        for k in range(1, self.outer):
+            total = total + lax.ppermute(pair[k : k + 1], "dp", [(i, (i + 2 * k) % n) for i in range(n)])
+        return total[0]
+
+    def sum_all(self, vec, tensor_size):
+        for axis, size in (("tensor", tensor_size), ("dp", 2 * self.outer)):
+            step = 1
+            while step < size:
+                vec = vec + lax.ppermute(vec, axis, [(i, i ^ step) for i in range(size)])
+                step *= 2
+        return vec
+
+    def begin(self, left, right):
+        return self._swap(dot_tokens(left[:, left.shape[1] // 2 :], right).astype(BF))
+
+    def middle(self, left, right, came):
+        mine = dot_tokens(left[:, : left.shape[1] // 2], right)
+        return (mine + came.astype(F32)).astype(BF)
+
+    def end(self, pair):
+        size = pair.shape[0] // self.outer
+        n = 2 * self.outer
+        total = pair[:size].astype(F32)
+        for k in range(1, self.outer):
+            piece = pair[k * size : (k + 1) * size]
+            total = total + lax.ppermute(piece, "dp", [(i, (i + 2 * k) % n) for i in range(n)]).astype(F32)
+        return total
+
+    def along(self, block):
+        return [block] + [self._from(block, k) for k in range(1, self.outer)]
+
+    def across(self, blocks):
+        return blocks + [self._swap(b) for b in blocks]
+
+    def gather_first(self, w, small):
+        return ring_gather(w, small)
+
+    def scatter_small(self, parts):
+        pair = parts[: self.outer] + self._swap(parts[self.outer :])
+        n = 2 * self.outer
+        total = pair[:1]
+        for k in range(1, self.outer):
+            total = total + lax.ppermute(pair[k : k + 1], "dp", [(i, (i + 2 * k) % n) for i in range(n)])
+        return total[0]
+
+    def sum_all(self, vec, tensor_size):
+        for axis, size in (("tensor", tensor_size), ("dp", 2 * self.outer)):
+            step = 1
+            while step < size:
+                vec = vec + lax.ppermute(vec, axis, [(i, i ^ step) for i in range(size)])
+                step *= 2
+        return vec
 
     def scatter(self, left, right):
         half = left.shape[1] // 2
@@ -514,14 +718,39 @@
     def restore(self, x, axis):
         return x
 
-    def gather(self, block):
-        return lax.all_gather(block, "dp", axis=0, tiled=True)
+    def along(self, block):
+        return [block]
+
+    def across(self, blocks):
+        return [lax.all_gather(blocks[0], "dp", axis=0, tiled=True)]
+
+    def begin(self, left, right):
+        return dot_tokens(left, right).astype(BF)
+
+    def middle(self, left, right, came):
+        return came
+
+    def end(self, pair):
+        return lax.psum_scatter(pair, "dp", scatter_dimension=0, tiled=True).astype(F32)
+
+    def gather_first(self, w, small):
+        return lax.all_gather(w, "dp", axis=0, tiled=True), lax.all_gather(small, "dp", axis=0)
+
+    def scatter_small(self, parts):
+        return lax.psum_scatter(parts, "dp", scatter_dimension=0, tiled=True)[0]
+
+    def sum_all(self, vec, tensor_size):
+        return lax.psum(vec, ("dp", "tensor"))
 
     def scatter(self, left, right):
         full = dot_tokens(left, right).astype(BF)
         return lax.psum_scatter(full, "dp", scatter_dimension=0, tiled=True).astype(F32)
 
 
+def tie(value, *others):
+    return lax.optimization_barrier((value, others))[0]
+
+
 def tensor_gather(x):
     return lax.all_gather(x, "tensor", axis=0, tiled=True)
 
@@ -531,7 +760,7 @@
 
 
 def shards(
-    dp_size, inputs, cotangent, lengths, norm1_gain, w_query, w_key, w_value, w_outgate, w_beta, w_alpha,
+    dp_size, tensor_size, inputs, cotangent, lengths, norm1_gain, w_query, w_key, w_value, w_outgate, w_beta, w_alpha,
     conv_query, conv_key, conv_value, a_log, dt_bias, head_gain, w_out, norm2_gain, w_gate, w_up, w_down,
 ):
     rows = RingRows(dp_size) if dp_size == 8 else PlainRows()
@@ -549,19 +778,21 @@
 
     small = jnp.concatenate(
         [w_beta.reshape(-1), w_alpha.reshape(-1), conv_query.reshape(-1), conv_key.reshape(-1), conv_value.reshape(-1)]
-    )[None]
-    small = lax.all_gather(small, "dp", axis=0, tiled=True)
+    )
     cuts = [0]
     for part in (w_beta, w_alpha, conv_query, conv_key, conv_value):
         cuts.append(cuts[-1] + part.size)
+    small = jnp.pad(small, (0, -small.size % (32 * LANES))).reshape(-1, LANES)
+    full_raw, small = rows.gather_first(
+        jnp.concatenate([w_query, w_key, w_value, w_outgate], axis=1), small
+    )
+    small = small.reshape(dp_size, -1)
     pieces = [small[:, a:b] for a, b in zip(cuts[:-1], cuts[1:])]
-    full_ab = rows.reorder(
-        jnp.concatenate([p.reshape(dp_size * block, heads) for p in pieces[:2]], axis=1), 0
-    )
+    full_ab = jnp.concatenate([p.reshape(dp_size * block, heads) for p in pieces[:2]], axis=1)
     full_ab = jnp.pad(full_ab, ((0, 0), (0, LANES - 2 * heads)))
 
     def tap_table(piece, size):
-        table = piece.reshape(size, heads, taps_n).astype(F32)
+        table = rows.restore(piece, 0).reshape(size, heads, taps_n).astype(F32)
         return jnp.pad(jnp.transpose(table, (2, 1, 0)).reshape(taps_n, heads * size), ((0, 8 - taps_n), (0, 0)))
 
     tq, tk, tv = tap_table(pieces[2], dk), tap_table(pieces[3], dk), tap_table(pieces[4], dv)
@@ -575,85 +806,103 @@
     gain_two = rows.reorder(norm2_gain[None], 1)[0]
     normed_one, norm_one_back = jax.vjp(rms_apply, local_rows, gain_one)
     rows_one = tensor_gather(normed_one.astype(BF))
-    full_qk = rows.gather(jnp.concatenate([w_query, w_key], axis=1))
-    full_value = rows.gather(w_value)
-    full_outgate = rows.gather(w_outgate)
-    full_out = rows.gather(w_out)
-    full_gate = rows.gather(w_gate)
-    full_up = rows.gather(w_up)
-    full_down = rows.gather(w_down)
+    line_out = rows.along(tie(w_out, full_raw))
+    line_gate = rows.along(tie(w_gate, full_raw))
     grad_after = valid_rows * rows.reorder(cotangent[0], 1).astype(F32)
     incoming_ffn = tensor_gather(grad_after.astype(BF))
 
     ab_raw = plain_dot(rows_one, full_ab)
-    qk_raw = plain_dot(rows_one, full_qk)
-    v_raw = plain_dot(rows_one, full_value)
-    og_raw = plain_dot(rows_one, full_outgate)
-    core_in = (qk_raw, v_raw, og_raw, ab_raw, tq, tk, tv, par, gain)
+    core_in = (plain_dot(rows_one, full_raw), ab_raw, tq, tk, tv, par, gain)
     head_bf, delta_out, new_values, inverses, states = mixer_forward(*core_in)
-    after_mix = local_rows + tensor_scatter(dot_rows(head_bf, full_out))
+    line_out = tie(line_out, head_bf)
+    line_up = rows.along(tie(w_up, line_out))
+    full_out = jnp.concatenate(rows.across(line_out), axis=0)
+    mixed = dot_rows(head_bf, full_out).astype(BF)
+    line_gate = tie(line_gate, mixed)
+    line_down = rows.along(tie(w_down, line_gate))
+    all_gate = rows.across(line_gate)
+    after_mix = local_rows + tensor_scatter(mixed).astype(F32)
     normed_two, norm_two_back = jax.vjp(rms_apply, after_mix, gain_two)
-    rows_two = tensor_gather(normed_two.astype(BF))
+    normed_two = normed_two.astype(BF)
+    all_up = rows.across(tie(line_up, normed_two))
+    rows_two = tensor_gather(normed_two)
+    full_gate = jnp.concatenate(tie(all_gate, normed_two), axis=0)
     gate_pre = plain_dot(rows_two, full_gate)
+    all_down = rows.across(tie(line_down, gate_pre))
+    full_up = jnp.concatenate(tie(all_up, gate_pre), axis=0)
     up_pre = plain_dot(rows_two, full_up)
     hidden, swiglu_back = jax.vjp(swiglu, gate_pre, up_pre)
     hidden_bf = hidden.astype(BF)
-    ffn_part = tensor_scatter(dot_rows(hidden_bf, full_down).astype(BF)).astype(F32)
-    outputs = rows.restore(((after_mix + ffn_part) * valid_rows).astype(BF), 1)[None]
-
+
+    swap_down = rows.begin(incoming_ffn, hidden_bf)
+    full_down = jnp.concatenate(tie(all_down, hidden_bf), axis=0)
     grad_hidden = plain_dot(incoming_ffn, full_down)
-    out_down = rows.scatter(incoming_ffn, hidden_bf)
     grad_gate_pre, grad_up_pre = swiglu_back(grad_hidden)
     gate_low = grad_gate_pre.astype(BF)
     up_low = grad_up_pre.astype(BF)
-    grad_normed_two = tensor_scatter(dot_rows(gate_low, full_gate) + dot_rows(up_low, full_up))
-    out_gate = rows.scatter(rows_two, gate_low)
-    out_up = rows.scatter(rows_two, up_low)
+    back_two = (dot_rows(gate_low, full_gate) + dot_rows(up_low, full_up)).astype(BF)
+    grad_normed_two = tensor_scatter(back_two)
+    late_two = tie(rows_two, back_two)
+    swap_gate = rows.begin(late_two, gate_low)
+    swap_up = rows.begin(late_two, up_low)
+    pair_down = rows.middle(tie(incoming_ffn, back_two), hidden_bf, swap_down)
+    grad_normed_two = tie(grad_normed_two, pair_down).astype(F32)
+    out_down = rows.end(pair_down)
     grad_mid, grad_norm2 = norm_two_back(grad_normed_two)
     grad_mid = grad_mid + grad_after
-    incoming_mix = tensor_gather(grad_mid.astype(BF))
+    grad_mix = grad_mid.astype(BF)
+    incoming_mix = tensor_gather(grad_mix)
 
     grad_head = plain_dot(incoming_mix, full_out)
-    out_out = rows.scatter(incoming_mix, head_bf)
-    qk_low, v_low, og_low, ab_low, dtq, dtk, dtv, dpar, dgain = mixer_backward(
+    pair_gate = rows.middle(late_two, gate_low, tie(swap_gate, grad_head))
+    out_gate = rows.end(pair_gate)
+    swap_out = rows.begin(incoming_mix, head_bf)
+    grad_head = tie(grad_head, pair_gate)
+    raw_low, ab_low, dtq, dtk, dtv, dpar, dgain = mixer_backward(
         *core_in, grad_head, delta_out, new_values, inverses, states
     )
-    summed = dot_rows(qk_low, full_qk) + dot_rows(v_low, full_value)
-    summed = summed + dot_rows(og_low, full_outgate) + dot_rows(ab_low, full_ab)
-    grad_normed_one = tensor_scatter(summed.astype(BF)).astype(F32)
-    out_qk = rows.scatter(rows_one, qk_low)
-    out_value = rows.scatter(rows_one, v_low)
-    out_outgate = rows.scatter(rows_one, og_low)
-    grad_first, grad_norm1 = norm_one_back(grad_normed_one)
+    ffn_part = tensor_scatter(dot_rows(tie(hidden_bf, grad_mix), full_down).astype(BF)).astype(F32)
+    outputs = rows.restore(((after_mix + ffn_part) * valid_rows).astype(BF), 1)[None]
+    pair_up = rows.middle(late_two, up_low, tie(swap_up, raw_low))
+    out_up = rows.end(pair_up)
+    raw_low = tie(raw_low, pair_up)
+    summed = (dot_rows(raw_low, full_raw) + dot_rows(ab_low, full_ab)).astype(BF)
+    grad_normed_one = tensor_scatter(summed)
+    pair_out = rows.middle(incoming_mix, head_bf, tie(swap_out, summed))
+    out_out = rows.end(pair_out)
+    wide = 2 * wide_k
+    late_raw = tie(raw_low, summed)
+    parts = [late_raw[:, :wide], late_raw[:, wide : wide + wide_v], late_raw[:, wide + wide_v :]]
+    swaps = [rows.begin(rows_one, p) for p in parts]
+    out_qk, out_value, out_outgate = (
+        rows.end(rows.middle(rows_one, p, came)) for p, came in zip(parts, swaps)
+    )
+    grad_first, grad_norm1 = norm_one_back(tie(grad_normed_one, swaps).astype(F32))
     grad_inputs = rows.restore(grad_mid + grad_first, 1)[None]
 
-    grad_ab = rows.restore(dot_tokens(rows_one, ab_low)[:, : 2 * heads], 0)
-    grad_beta, grad_alpha = grad_ab[:, :heads], grad_ab[:, heads:]
+    grad_ab = dot_tokens(rows_one, ab_low)[:, : 2 * heads]
 
     def tap_grad(table, size):
-        return jnp.transpose(table[:taps_n].reshape(taps_n, heads, size), (2, 1, 0))
-
-    small_out = [grad_beta, grad_alpha, tap_grad(dtq, dk), tap_grad(dtk, dk), tap_grad(dtv, dv)]
-    small_sum = lax.psum_scatter(
-        jnp.concatenate([p.reshape(dp_size, -1) for p in small_out], axis=1), "dp", scatter_dimension=0, tiled=True
-    )[0]
+        grad = jnp.transpose(table[:taps_n].reshape(taps_n, heads, size), (2, 1, 0))
+        return rows.reorder(grad.reshape(dp_size, -1), 0)
+
+    small_out = [grad_ab[:, :heads].reshape(dp_size, -1), grad_ab[:, heads:].reshape(dp_size, -1)]
+    small_out += [tap_grad(dtq, dk), tap_grad(dtk, dk), tap_grad(dtv, dv)]
+    small_sum = rows.scatter_small(jnp.concatenate(small_out, axis=1))
     shapes = (w_beta, w_alpha, conv_query, conv_key, conv_value)
     out_beta, out_alpha, out_cq, out_ck, out_cv = (
         small_sum[a:b].reshape(like.shape) for a, b, like in zip(cuts[:-1], cuts[1:], shapes)
     )
-    alog_full = lax.dynamic_update_slice_in_dim(
-        jnp.zeros_like(a_log), dpar[0, heads : 2 * heads], head_start, 0
-    )
-    dtb_full = lax.dynamic_update_slice_in_dim(
-        jnp.zeros_like(dt_bias), dpar[1, heads : 2 * heads], head_start, 0
-    )
-    norm1_sum, norm2_sum, hgain_sum, alog_sum, dtb_sum = lax.psum(
-        (
-            rows.restore(grad_norm1[None], 1)[0], rows.restore(grad_norm2[None], 1)[0], dgain[0],
-            alog_full, dtb_full,
-        ),
-        ("dp", "tensor"),
-    )
+    alog_full, dtb_full = (
+        lax.dynamic_update_slice_in_dim(jnp.zeros_like(a_log), dpar[i, heads : 2 * heads], head_start, 0)
+        for i in range(2)
+    )
+    vec = [rows.restore(grad_norm1[None], 1)[0], rows.restore(grad_norm2[None], 1)[0], dgain[0], alog_full, dtb_full]
+    total = rows.sum_all(jnp.concatenate(vec), tensor_size)
+    ends = [0]
+    for part in vec:
+        ends.append(ends[-1] + part.size)
+    norm1_sum, norm2_sum, hgain_sum, alog_sum, dtb_sum = (total[a:b] for a, b in zip(ends[:-1], ends[1:]))
     return (
         outputs, grad_inputs, norm1_sum, out_qk[:, :wide_k], out_qk[:, wide_k:], out_value, out_outgate,
         out_beta, out_alpha, out_cq, out_ck, out_cv, alog_sum, dtb_sum, hgain_sum, out_out, norm2_sum,
@@ -670,6 +919,6 @@
         (cube, cube, whole) + (mat,) * 6 + (cube,) * 3 + (whole,) * 3 + (mat, whole) + (mat,) * 3
     )
     return jax.shard_map(
-        functools.partial(shards, mesh.shape["dp"]), mesh=mesh, in_specs=in_specs, out_specs=out_specs,
+        functools.partial(shards, mesh.shape["dp"], mesh.shape["tensor"]), mesh=mesh, in_specs=in_specs, out_specs=out_specs,
         check_vma=False,
     )

time: 1450 us -> 1370 us (0.945)
  Pallas kernels: 90.1 us -> 232 us
  blocking collectives: 97.3 us -> 0 us
  waiting for transfers between devices: 780 us -> 694 us
  starting transfers between devices: 118 us -> 73.4 us
  matrix products: 222 us -> 198 us
  other arithmetic: 31 us -> 47.5 us
    pallas_call x0 -> x1, Pallas kernels: none -> 142 us  [ring_gather(): pl.pallas_call(gather_body, in_specs=[any_ref] * 2, out_specs=[any_ref] *...]
    ppermute x35 -> x24, waiting for transfers between devices: 402 us -> 312 us  [_swap(): return lax.ppermute(x, 'dp', [(i, i ^ 1) for i in range(2 * self.outer)])]
    ppermute x21 -> x12, waiting for transfers between devices: 166 us -> 85.8 us  [_from(): return lax.ppermute(x, 'dp', [((i + 2 * steps) % n, i) for i in range(n)])]
    ppermute x21 -> x29, waiting for transfers between devices: 183 us -> 242 us  [the longest x21 189 us: end(): lax.ppermute(piece, 'dp', [(i, (i + 2 * k) % n) for i in range(n)])]
    all_gather x1 -> x0, blocking collectives: 54.5 us -> none  [shards(): small = lax.all_gather(small, 'dp', axis=0, tiled=True)]
    reduce_scatter x4, waiting for transfers between devices: 0.03 us -> 44.7 us  [tensor_scatter(): return lax.psum_scatter(x, 'tensor', scatter_dimension=0, tiled=True)]
    psum x1 -> x0, blocking collectives: 42.8 us -> none  [shards(): lax.psum((rows.restore(grad_norm1[None], 1)[0], rows.restore(grad_norm2[N...]
    ppermute x35 -> x24, starting transfers between devices: 48 us -> 21.4 us  [_swap(): return lax.ppermute(x, 'dp', [(i, i ^ 1) for i in range(2 * self.outer)])]
  transfers between devices with their start and end apart: 86 -> 73, of which waited for: 45 -> 43; matrix products, arithmetic and copies ran while one was open for 15% -> 18% of each run, Pallas kernels for 0% -> 17%
where the time goes in v2:
time: 1370 us
  waiting for transfers between devices  694 us (51%)
  Pallas kernels  232 us (17%)
  matrix products  198 us (14%)
  local copies, waits for them, and re-layouts  103 us (8%)
  starting transfers between devices  73.4 us (5%)
  other arithmetic  47.5 us (3%)
  between operations  17.7 us (1%)
    ppermute x24, waiting for transfers between devices, _swap(): return lax.ppermute(x, 'dp', [(i, i ^ 1) for i in range(2 * self.outer)])  312 us
    ppermute x21, waiting for transfers between devices, end(): lax.ppermute(piece, 'dp', [(i, (i + 2 * k) % n) for i in range(n)])  189 us
    pallas_call x1, Pallas kernels, ring_gather(): pl.pallas_call(gather_body, in_specs=[any_ref] * 2, out_specs=[any_ref] *...  142 us
    ppermute x12, waiting for transfers between devices, _from(): return lax.ppermute(x, 'dp', [((i + 2 * steps) % n, i) for i in range(n)])  85.8 us
    dot_general x15, matrix products, dot_tokens(): lax.dot_general(left_mat, right_mat, (((0,), (0,)), ((), ())), preferred_...  69 us
    dot_general x6, matrix products, plain_dot(): return jnp.dot(left_mat, right_mat, preferred_element_type=F32)  65.4 us
    dot_general x6, matrix products, dot_rows(): lax.dot_general(left_mat, right_mat, (((1,), (1,)), ((), ())), preferred_...  64 us
    unnamed x276, local copies, waits for them, and re-layouts  60 us
  transfers between devices with their start and end apart: 73, of which 43 were waited for; matrix products, arithmetic and copies ran while one was open for 18% of the time, Pallas kernels for 17%

profile of v2, /device:TPU:14, one launch (start us, length us, event | category | flops | bytes accessed | tf_op | source)
XLA Modules:
  0.0 1365.5 jit_solution(4708586104457785241)
XLA Ops:
  17.0 141.8 %ring_gather.1 = (bf16[2048,3072]{1,0:T(8,128)(2,1)}, bf16[8,32,128]{2,1,0:T(8,128)(2,1)}) custom-call(bf16[256,3072]{1,0:T(8,128)(2,1)} %pad_maximum_fusion.w_ref, bf16[32,128]{1,0:T(8,128)(2,1)} %pad_bitcast_fusion.small_ref), custom_call_target="tpu_custom_call" | custom-call | bytes 400000000 | tf_op jit(solution)/shard_map/ring_gather/pallas_call | solution.py:541
  168.2 20.3 %fusion.144.q_ref.k_ref.v_ref.og_ref.qh_ref.kh_ref.vh_ref = f32[1024,3072]{1,0:T(8,128)} fusion(bf16[1024,2048]{1,0:T(8,128)(2,1)} %all-gather.5.cloned.1.call-done, bf16[2048,3072]{1,0:T(8,128)(2,1)} %get-tuple-element.89), kind=kOutput, calls=%fused_computation.377 | convolution fusion | flops 12884901888 | bytes 29360128 | tf_op jit(solution)/shard_map/dot_general | solution.py:565
  189.8 35.6 %mixer_forward.1 = (bf16[1024,1024]{1,0:T(8,128)(2,1)S(1)}, f32[1024,1024]{1,0:T(8,128)S(1)}, bf16[1024,1024]{1,0:T(8,128)(2,1)S(1)}, bf16[1024,512]{1,0:T(8,128)(2,1)S(1)}, bf16[8,128,1024]{2,1,0:T(8,128)(2,1)S(1)}) custom-call(f32[1024,3072]{1,0:T(8,128)} %fusion.144.q_ref.k_ref.v_ref.og_ref.qh_ref.kh_ref.vh_ref, ...), custom_call_target="tpu_custom_call" | custom-call | flops 20000000000 | bytes 40000000 | tf_op jit(solution)/shard_map/mixer_forward/pallas_call | solution.py:343
  236.3 6.6 collective-permute-done.3
  243.0 11.2 collective-permute-done.4
  254.2 11.2 collective-permute-done.5
  265.4 8.3 collective-permute-done.6
  275.8 6.1 convolution_convert_fusion.4
  282.2 44.7 %reduce-scatter.5.cloned.1.call-done = bf16[256,2048]{1,0:T(8,128)(2,1)} async-done(((bf16[1024,2048]{1,0:T(8,128)(2,1)}), bf16[256,2048]{1,0:T(8,128)(2,1)}) %reduce-scatter.5.cloned.1.call-update) | async-done | bytes 1048592 | tf_op jit(solution)/shard_map/reduce_scatter | solution.py:759
  342.9 38.8 %collective-permute-done.7 = bf16[256,1408]{1,0:T(8,128)(2,1)} collective-permute-done((bf16[256,1408]{1,0:T(8,128)(2,1)}, bf16[256,1408]{1,0:T(8,128)(2,1)}, u32[]{:S(2)}, u32[]{:S(2)}) %collective-permute-start.7) | collective-permute-done | bytes 720928 | tf_op jit(solution)/shard_map/ppermute | solution.py:630
  381.7 14.5 %collective-permute-done.9 = bf16[256,1408]{1,0:T(8,128)(2,1)} collective-permute-done((bf16[256,1408]{1,0:T(8,128)(2,1)}, bf16[256,1408]{1,0:T(8,128)(2,1)}, u32[]{:S(2)}, u32[]{:S(2)}) %collective-permute-start.9) | collective-permute-done | bytes 720928 | tf_op jit(solution)/shard_map/ppermute | solution.py:630
  402.0 13.3 collective-permute-done.10
  416.2 14.7 %collective-permute-done.11 = bf16[256,1408]{1,0:T(8,128)(2,1)} collective-permute-done((bf16[256,1408]{1,0:T(8,128)(2,1)}, bf16[256,1408]{1,0:T(8,128)(2,1)}, u32[]{:S(2)}, u32[]{:S(2)}) %collective-permute-start.11) | collective-permute-done | bytes 720928 | tf_op jit(solution)/shard_map/ppermute | solution.py:626
  434.7 11.7 collective-permute-done.12
  447.6 12.5 collective-permute-done.13
  464.6 29.6 %collective-permute-done.16 = bf16[256,1408]{1,0:T(8,128)(2,1)} collective-permute-done((bf16[256,1408]{1,0:T(8,128)(2,1)}, bf16[256,1408]{1,0:T(8,128)(2,1)}, u32[]{:S(2)}, u32[]{:S(2)}) %collective-permute-start.16) | collective-permute-done | bytes 720928 | tf_op jit(solution)/shard_map/ppermute | solution.py:630
  514.3 10.5 fusion.145
  529.6 14.9 %collective-permute-done.19 = bf16[256,1408]{1,0:T(8,128)(2,1)} collective-permute-done((bf16[256,1408]{1,0:T(8,128)(2,1)}, bf16[256,1408]{1,0:T(8,128)(2,1)}, u32[]{:S(2)}, u32[]{:S(2)}) %collective-permute-start.19) | collective-permute-done | bytes 720928 | tf_op jit(solution)/shard_map/ppermute | solution.py:626
  545.1 14.9 %collective-permute-done.20 = bf16[256,1408]{1,0:T(8,128)(2,1)} collective-permute-done((bf16[256,1408]{1,0:T(8,128)(2,1)}, bf16[256,1408]{1,0:T(8,128)(2,1)}, u32[]{:S(2)}, u32[]{:S(2)}) %collective-permute-start.20) | collective-permute-done | bytes 720928 | tf_op jit(solution)/shard_map/ppermute | solution.py:626
  569.8 9.2 multiply_convert_fusion.1
  579.1 11.7 collective-permute-done.25
  590.8 15.4 %collective-permute-done.26 = bf16[256,1408]{1,0:T(8,128)(2,1)S(1)} collective-permute-done((bf16[256,1408]{1,0:T(8,128)(2,1)}, bf16[256,1408]{1,0:T(8,128)(2,1)S(1)}, u32[]{:S(2)}, u32[]{:S(2)}) %collective-permute-start.26) | collective-permute-done | bytes 720928 | tf_op jit(solution)/shard_map/ppermute | solution.py:626
  606.2 11.6 collective-permute-done.27
  628.6 14.1 %fusion.2 = (bf16[1024,1408]{1,0:T(8,128)(2,1)S(1)}, bf16[1024,1408]{1,0:T(8,128)(2,1)S(1)}) fusion(f32[1024,1408]{1,0:T(8,128)} %copy-done.93, f32[1024,1408]{1,0:T(8,128)} %get-tuple-element.453, bf16[1024,2048]{1,0:T(8,128)(2,1)} %all-gather.9.cloned.1.call-done, bf16[2048,1408]{1,0:T(8,128)(2,1)} %constant_dynamic-update-slice_fusion.25), kind=kOutput, calls=%fused_computation.5 | convolution fusion | flops 5925765120 | bytes 27262976 | tf_op jit(solution)/shard_map/dot_general | solution.py:565
  642.7 10.8 fusion.146
  653.6 11.1 add_convert_fusion.1
  664.7 6.1 convolution_convert_fusion.3
  671.4 60.2 %collective-permute-done.28 = bf16[1024,1408]{1,0:T(8,128)(2,1)S(1)} collective-permute-done((bf16[1024,1408]{1,0:T(8,128)(2,1)S(1)}, bf16[1024,1408]{1,0:T(8,128)(2,1)S(1)}, u32[]{:S(2)}, u32[]{:S(2)}) %collective-permute-start.28) | collective-permute-done | bytes 2883616 | tf_op jit(solution)/shard_map/ppermute | solution.py:626
  731.5 5.0 add_convert_fusion.4
  742.7 7.6 convolution_convert_fusion.2
  750.8 4.8 convolution_convert_fusion.1
  757.2 5.4 fusion.42
  762.6 5.3 fusion.40
  767.9 9.3 all-gather.11.cloned.1.call-done
  777.2 10.1 fusion.147.g_ref
  787.3 28.8 %collective-permute-done.29 = bf16[1024,1408]{1,0:T(8,128)(2,1)} collective-permute-done((bf16[1024,1408]{1,0:T(8,128)(2,1)}, bf16[1024,1408]{1,0:T(8,128)(2,1)}, u32[]{:S(2)}, u32[]{:S(2)}) %collective-permute-start.29) | collective-permute-done | bytes 2883616 | tf_op jit(solution)/shard_map/ppermute | solution.py:626
  816.1 3.9 add_convert_fusion.3
  820.0 54.7 %mixer_backward.1 = (bf16[1024,3072]{1,0:T(8,128)(2,1)}, bf16[1024,128]{1,0:T(8,128)(2,1)S(1)}, f32[8,512]{1,0:T(8,128)S(1)}, f32[8,512]{1,0:T(8,128)S(1)}, f32[...) custom-call(f32[1024,3072]{1,0:T(8,128)} %fusion.144.q_ref.k_ref.v_ref.og_ref.qh_ref.kh_ref.vh_ref, ...), custom_call_target="tpu_custom_call" | custom-call | flops 40000000000 | bytes 60000000 | tf_op jit(solution)/shard_map/mixer_backward/pallas_call | solution.py:383
  877.2 4.4 fusion.61
  881.6 20.7 %add_convert_fusion = bf16[1024,2048]{1,0:T(8,128)(2,1)} fusion(f32[1024,2048]{1,0:T(8,128)} %fusion.61, bf16[1024,3072]{1,0:T(8,128)(2,1)} %get-tuple-element.150, bf16[2048,3072]{1,0:T(8,128)(2,1)} %get-tuple-element.89), kind=kOutput, calls=%fused_computation.1 | convolution fusion | flops 12889096192 | bytes 31457280 | tf_op jit(solution)/shard_map/dot_general | solution.py:569
  908.2 44.1 %collective-permute-done.62 = bf16[256,1408]{1,0:T(8,128)(2,1)S(1)} collective-permute-done((bf16[256,1408]{1,0:T(8,128)(2,1)S(1)}, bf16[256,1408]{1,0:T(8,128)(2,1)S(1)}, u32[]{:S(2)}, u32[]{:S(2)}) %collective-permute-start.62) | collective-permute-done | bytes 720928 | tf_op jit(solution)/shard_map/ppermute | solution.py:670
  952.3 8.2 collective-permute-done.63
  967.5 10.8 convolution_convert_fusion
  996.0 5.6 fusion.26
  1001.7 4.4 fusion.18
  1006.1 3.8 convolution_convert_fusion.5
  1009.9 3.8 convolution_convert_fusion.6
  1013.7 4.2 convolution_convert_fusion.7
  1022.5 40.9 %collective-permute-done.49 = f32[1,3072]{1,0:T(1,128)S(1)} collective-permute-done((f32[1,3072]{1,0:T(1,128)S(1)}, f32[1,3072]{1,0:T(1,128)S(1)}, u32[]{:S(2)}, u32[]{:S(2)}) %collective-permute-start.49) | collective-permute-done | bytes 12320 | tf_op jit(solution)/shard_map/ppermute | solution.py:687
  1070.4 28.0 %collective-permute-done.61 = bf16[256,1408]{1,0:T(8,128)(2,1)S(1)} collective-permute-done((bf16[256,1408]{1,0:T(8,128)(2,1)S(1)}, bf16[256,1408]{1,0:T(8,128)(2,1)S(1)}, u32[]{:S(2)}, u32[]{:S(2)}) %collective-permute-start.61) | collective-permute-done | bytes 720928 | tf_op jit(solution)/shard_map/ppermute | solution.py:670
  1121.0 22.6 %collective-permute-done.58 = bf16[256,1408]{1,0:T(8,128)(2,1)} collective-permute-done((bf16[256,1408]{1,0:T(8,128)(2,1)S(1)}, bf16[256,1408]{1,0:T(8,128)(2,1)}, u32[]{:S(2)}, u32[]{:S(2)}) %collective-permute-start.58) | collective-permute-done | bytes 720928 | tf_op jit(solution)/shard_map/ppermute | solution.py:670
  1148.1 11.8 collective-permute-done.31
  1159.8 4.8 add_convert_fusion.8
  1164.8 33.3 %collective-permute-done.33 = bf16[1024,1024]{1,0:T(8,128)(2,1)S(1)} collective-permute-done((bf16[1024,1024]{1,0:T(8,128)(2,1)S(1)}, bf16[1024,1024]{1,0:T(8,128)(2,1)S(1)}, u32[]{:S(2)}, u32[]{:S(2)}) %collective-permute-start.33) | collective-permute-done | bytes 2097184 | tf_op jit(solution)/shard_map/ppermute | solution.py:626
  1202.7 17.8 %collective-permute-done.32 = bf16[1024,1024]{1,0:T(8,128)(2,1)S(1)} collective-permute-done((bf16[1024,1024]{1,0:T(8,128)(2,1)S(1)}, bf16[1024,1024]{1,0:T(8,128)(2,1)S(1)}, u32[]{:S(2)}, u32[]{:S(2)}) %collective-permute-start.32) | collective-permute-done | bytes 2097184 | tf_op jit(solution)/shard_map/ppermute | solution.py:626
  1231.4 27.0 %collective-permute-done.40 = bf16[256,1024]{1,0:T(8,128)(2,1)S(1)} collective-permute-done((bf16[256,1024]{1,0:T(8,128)(2,1)S(1)}, bf16[256,1024]{1,0:T(8,128)(2,1)S(1)}, u32[]{:S(2)}, u32[]{:S(2)}) %collective-permute-start.40) | collective-permute-done | bytes 524320 | tf_op jit(solution)/shard_map/ppermute | solution.py:670
  1259.5 15.3 %collective-permute-done.41 = bf16[256,1024]{1,0:T(8,128)(2,1)S(1)} collective-permute-done((bf16[256,1024]{1,0:T(8,128)(2,1)S(1)}, bf16[256,1024]{1,0:T(8,128)(2,1)S(1)}, u32[]{:S(2)}, u32[]{:S(2)}) %collective-permute-start.41) | collective-permute-done | bytes 524320 | tf_op jit(solution)/shard_map/ppermute | solution.py:670
  1277.5 18.7 %collective-permute-done.45 = bf16[256,1024]{1,0:T(8,128)(2,1)S(1)} collective-permute-done((bf16[256,1024]{1,0:T(8,128)(2,1)S(1)}, bf16[256,1024]{1,0:T(8,128)(2,1)S(1)}, u32[]{:S(2)}, u32[]{:S(2)}) %collective-permute-start.45) | collective-permute-done | bytes 524320 | tf_op jit(solution)/shard_map/ppermute | solution.py:670
  1297.5 10.0 collective-permute-done.46
  1309.8 7.7 collective-permute-done.42
  1317.5 5.6 collective-permute-done.43
  1328.6 3.6 fusion.13
  1340.6 3.8 collective-permute-done.35
  1348.2 3.7 collective-permute-done.37
  (657 shorter events, 236.9 us)
Async XLA Ops:
  7.2 161.0 %all-gather.5.cloned.1.call-start = ((), (), s32[]{:S(2)}) async-start(), calls=%async_computation.4 | async-start | bytes 5242880 | tf_op jit(solution)/shard_map/all_gather | solution.py:755
  13.0 313.8 %reduce-scatter.5.cloned.1.call-start = ((), (), s32[]{:S(2)}) async-start(), calls=%async_computation.5 | async-start | bytes 5242880 | tf_op jit(solution)/shard_map/reduce_scatter | solution.py:759
  158.8 69.0 %collective-permute-start = (bf16[256,1024]{1,0:T(8,128)(2,1)}, bf16[256,1024]{1,0:T(8,128)(2,1)}, u32[]{:S(2)}, u32[]{:S(2)}) collective-permute-start(bf16[256,1024]{1,0:T(8,128)(2,1)} %param.37), channel_id=1, source_target_pairs={{8,0},{12,4},{16,8},{20,12},{24,16},{28,20},{0,24},{4,28},{9,1},{1... | collective-permute-start | bytes 1572872 | tf_op jit(solution)/shard_map/ppermute | solution.py:630
  160.3 67.5 %collective-permute-start.1 = (bf16[256,1024]{1,0:T(8,128)(2,1)}, bf16[256,1024]{1,0:T(8,128)(2,1)}, u32[]{:S(2)}, u32[]{:S(2)}) collective-permute-start(bf16[256,1024]{1,0:T(8,128)(2,1)} %param.37), channel_id=1, source_target_pairs={{16,0},{20,4},{24,8},{28,12},{0,16},{4,20},{8,24},{12,28},{17,1},{... | collective-permute-start | bytes 1572872 | tf_op jit(solution)/shard_map/ppermute | solution.py:630
  160.8 66.9 %collective-permute-start.2 = (bf16[256,1024]{1,0:T(8,128)(2,1)}, bf16[256,1024]{1,0:T(8,128)(2,1)}, u32[]{:S(2)}, u32[]{:S(2)}) collective-permute-start(bf16[256,1024]{1,0:T(8,128)(2,1)} %param.37), channel_id=1, source_target_pairs={{24,0},{28,4},{0,8},{4,12},{8,16},{12,20},{16,24},{20,28},{25,1},{... | collective-permute-start | bytes 1572872 | tf_op jit(solution)/shard_map/ppermute | solution.py:630
  231.0 34.4 %collective-permute-start.5 = (bf16[256,1024]{1,0:T(8,128)(2,1)}, bf16[256,1024]{1,0:T(8,128)(2,1)S(1)}, u32[]{:S(2)}, u32[]{:S(2)}) collective-permute-start(bf16[256,1024]{1,0:T(8,128)(2,1)} %collective-permute-done.1), channel_id=1, source_target_pairs={{0,4},{4,0},{8,12},{12,8},{16,20},{20,16},{24,28},{28,24},{1,5},{5... | collective-permute-start | bytes 1572872 | tf_op jit(solution)/shard_map/ppermute | solution.py:626
  232.8 41.0 %collective-permute-start.6 = (bf16[256,1024]{1,0:T(8,128)(2,1)}, bf16[256,1024]{1,0:T(8,128)(2,1)S(1)}, u32[]{:S(2)}, u32[]{:S(2)}) collective-permute-start(bf16[256,1024]{1,0:T(8,128)(2,1)} %collective-permute-done.2), channel_id=1, source_target_pairs={{0,4},{4,0},{8,12},{12,8},{16,20},{20,16},{24,28},{28,24},{1,5},{5... | collective-permute-start | bytes 1572872 | tf_op jit(solution)/shard_map/ppermute | solution.py:626
  282.0 232.3 %all-gather.7.cloned.1.call-start = ((), (), s32[]{:S(2)}) async-start(), calls=%async_computation.6 | async-start | bytes 5242880 | tf_op jit(solution)/shard_map/all_gather | solution.py:755
  331.4 297.3 %all-gather.9.cloned.1.call-start = ((), (), s32[]{:S(2)}) async-start(), calls=%async_computation.7 | async-start | bytes 5242880 | tf_op jit(solution)/shard_map/all_gather | solution.py:755
  331.4 50.3 %collective-permute-start.7 = (bf16[256,1408]{1,0:T(8,128)(2,1)}, bf16[256,1408]{1,0:T(8,128)(2,1)}, u32[]{:S(2)}, u32[]{:S(2)}) collective-permute-start(bf16[256,1408]{1,0:T(8,128)(2,1)} %param.39), channel_id=1, source_target_pairs={{8,0},{12,4},{16,8},{20,12},{24,16},{28,20},{0,24},{4,28},{9,1},{1... | collective-permute-start | bytes 2162696 | tf_op jit(solution)/shard_map/ppermute | solution.py:630
  332.0 49.7 %collective-permute-start.8 = (bf16[256,1408]{1,0:T(8,128)(2,1)}, bf16[256,1408]{1,0:T(8,128)(2,1)}, u32[]{:S(2)}, u32[]{:S(2)}) collective-permute-start(bf16[256,1408]{1,0:T(8,128)(2,1)} %param.39), channel_id=1, source_target_pairs={{16,0},{20,4},{24,8},{28,12},{0,16},{4,20},{8,24},{12,28},{17,1},{... | collective-permute-start | bytes 2162696 | tf_op jit(solution)/shard_map/ppermute | solution.py:630
  334.4 61.8 %collective-permute-start.9 = (bf16[256,1408]{1,0:T(8,128)(2,1)}, bf16[256,1408]{1,0:T(8,128)(2,1)}, u32[]{:S(2)}, u32[]{:S(2)}) collective-permute-start(bf16[256,1408]{1,0:T(8,128)(2,1)} %param.39), channel_id=1, source_target_pairs={{24,0},{28,4},{0,8},{4,12},{8,16},{12,20},{16,24},{20,28},{25,1},{... | collective-permute-start | bytes 2162696 | tf_op jit(solution)/shard_map/ppermute | solution.py:630
  396.8 34.1 %collective-permute-start.11 = (bf16[256,1408]{1,0:T(8,128)(2,1)}, bf16[256,1408]{1,0:T(8,128)(2,1)}, u32[]{:S(2)}, u32[]{:S(2)}) collective-permute-start(bf16[256,1408]{1,0:T(8,128)(2,1)} %collective-permute-done.7), channel_id=1, source_target_pairs={{0,4},{4,0},{8,12},{12,8},{16,20},{20,16},{24,28},{28,24},{1,5},{5... | collective-permute-start | bytes 2162696 | tf_op jit(solution)/shard_map/ppermute | solution.py:626
  398.5 47.8 %collective-permute-start.12 = (bf16[256,1408]{1,0:T(8,128)(2,1)}, bf16[256,1408]{1,0:T(8,128)(2,1)}, u32[]{:S(2)}, u32[]{:S(2)}) collective-permute-start(bf16[256,1408]{1,0:T(8,128)(2,1)} %collective-permute-done.8), channel_id=1, source_target_pairs={{0,4},{4,0},{8,12},{12,8},{16,20},{20,16},{24,28},{28,24},{1,5},{5... | collective-permute-start | bytes 2162696 | tf_op jit(solution)/shard_map/ppermute | solution.py:626
  399.1 60.9 %collective-permute-start.13 = (bf16[256,1408]{1,0:T(8,128)(2,1)}, bf16[256,1408]{1,0:T(8,128)(2,1)}, u32[]{:S(2)}, u32[]{:S(2)}) collective-permute-start(bf16[256,1408]{1,0:T(8,128)(2,1)} %collective-permute-done.9), channel_id=1, source_target_pairs={{0,4},{4,0},{8,12},{12,8},{16,20},{20,16},{24,28},{28,24},{1,5},{5... | collective-permute-start | bytes 2162696 | tf_op jit(solution)/shard_map/ppermute | solution.py:626
  400.8 61.4 %collective-permute-start.14 = (bf16[256,1408]{1,0:T(8,128)(2,1)}, bf16[256,1408]{1,0:T(8,128)(2,1)}, u32[]{:S(2)}, u32[]{:S(2)}) collective-permute-start(bf16[256,1408]{1,0:T(8,128)(2,1)} %param.40), channel_id=1, source_target_pairs={{8,0},{12,4},{16,8},{20,12},{24,16},{28,20},{0,24},{4,28},{9,1},{1... | collective-permute-start | bytes 2162696 | tf_op jit(solution)/shard_map/ppermute | solution.py:630
  416.2 48.4 %collective-permute-start.15 = (bf16[256,1408]{1,0:T(8,128)(2,1)}, bf16[256,1408]{1,0:T(8,128)(2,1)}, u32[]{:S(2)}, u32[]{:S(2)}) collective-permute-start(bf16[256,1408]{1,0:T(8,128)(2,1)} %param.40), channel_id=1, source_target_pairs={{16,0},{20,4},{24,8},{28,12},{0,16},{4,20},{8,24},{12,28},{17,1},{... | collective-permute-start | bytes 2162696 | tf_op jit(solution)/shard_map/ppermute | solution.py:630
  430.9 63.4 %collective-permute-start.16 = (bf16[256,1408]{1,0:T(8,128)(2,1)}, bf16[256,1408]{1,0:T(8,128)(2,1)}, u32[]{:S(2)}, u32[]{:S(2)}) collective-permute-start(bf16[256,1408]{1,0:T(8,128)(2,1)} %param.40), channel_id=1, source_target_pairs={{24,0},{28,4},{0,8},{4,12},{8,16},{12,20},{16,24},{20,28},{25,1},{... | collective-permute-start | bytes 2162696 | tf_op jit(solution)/shard_map/ppermute | solution.py:630
  434.6 301.9 %reduce-scatter.7.cloned.1.call-start = ((), (), s32[]{:S(2)}) async-start(), calls=%async_computation.8 | async-start | bytes 5242880 | tf_op jit(solution)/shard_map/reduce_scatter | solution.py:759
  446.3 65.9 %collective-permute-start.21 = (bf16[256,1408]{1,0:T(8,128)(2,1)}, bf16[256,1408]{1,0:T(8,128)(2,1)}, u32[]{:S(2)}, u32[]{:S(2)}) collective-permute-start(bf16[256,1408]{1,0:T(8,128)(2,1)} %param.41), channel_id=1, source_target_pairs={{8,0},{12,4},{16,8},{20,12},{24,16},{28,20},{0,24},{4,28},{9,1},{1... | collective-permute-start | bytes 2162696 | tf_op jit(solution)/shard_map/ppermute | solution.py:630
  460.1 52.8 %collective-permute-start.22 = (bf16[256,1408]{1,0:T(8,128)(2,1)}, bf16[256,1408]{1,0:T(8,128)(2,1)}, u32[]{:S(2)}, u32[]{:S(2)}) collective-permute-start(bf16[256,1408]{1,0:T(8,128)(2,1)} %param.41), channel_id=1, source_target_pairs={{16,0},{20,4},{24,8},{28,12},{0,16},{4,20},{8,24},{12,28},{17,1},{... | collective-permute-start | bytes 2162696 | tf_op jit(solution)/shard_map/ppermute | solution.py:630
  462.1 62.7 %collective-permute-start.23 = (bf16[256,1408]{1,0:T(8,128)(2,1)}, bf16[256,1408]{1,0:T(8,128)(2,1)}, u32[]{:S(2)}, u32[]{:S(2)}) collective-permute-start(bf16[256,1408]{1,0:T(8,128)(2,1)} %param.41), channel_id=1, source_target_pairs={{24,0},{28,4},{0,8},{4,12},{8,16},{12,20},{16,24},{20,28},{25,1},{... | collective-permute-start | bytes 2162696 | tf_op jit(solution)/shard_map/ppermute | solution.py:630
  494.2 31.2 %collective-permute-start.17 = (bf16[256,1408]{1,0:T(8,128)(2,1)}, bf16[256,1408]{1,0:T(8,128)(2,1)}, u32[]{:S(2)}, u32[]{:S(2)}) collective-permute-start(bf16[256,1408]{1,0:T(8,128)(2,1)} %param.40), channel_id=1, source_target_pairs={{0,4},{4,0},{8,12},{12,8},{16,20},{20,16},{24,28},{28,24},{1,5},{5... | collective-permute-start | bytes 2162696 | tf_op jit(solution)/shard_map/ppermute | solution.py:626
  494.8 34.3 %collective-permute-start.18 = (bf16[256,1408]{1,0:T(8,128)(2,1)}, bf16[256,1408]{1,0:T(8,128)(2,1)}, u32[]{:S(2)}, u32[]{:S(2)}) collective-permute-start(bf16[256,1408]{1,0:T(8,128)(2,1)} %collective-permute-done.14), channel_id=1, source_target_pairs={{0,4},{4,0},{8,12},{12,8},{16,20},{20,16},{24,28},{28,24},{1,5},{5... | collective-permute-start | bytes 2162696 | tf_op jit(solution)/shard_map/ppermute | solution.py:626
  512.3 32.3 %collective-permute-start.19 = (bf16[256,1408]{1,0:T(8,128)(2,1)}, bf16[256,1408]{1,0:T(8,128)(2,1)}, u32[]{:S(2)}, u32[]{:S(2)}) collective-permute-start(bf16[256,1408]{1,0:T(8,128)(2,1)} %collective-permute-done.15), channel_id=1, source_target_pairs={{0,4},{4,0},{8,12},{12,8},{16,20},{20,16},{24,28},{28,24},{1,5},{5... | collective-permute-start | bytes 2162696 | tf_op jit(solution)/shard_map/ppermute | solution.py:626
  512.8 47.1 %collective-permute-start.20 = (bf16[256,1408]{1,0:T(8,128)(2,1)}, bf16[256,1408]{1,0:T(8,128)(2,1)}, u32[]{:S(2)}, u32[]{:S(2)}) collective-permute-start(bf16[256,1408]{1,0:T(8,128)(2,1)} %collective-permute-done.16), channel_id=1, source_target_pairs={{0,4},{4,0},{8,12},{12,8},{16,20},{20,16},{24,28},{28,24},{1,5},{5... | collective-permute-start | bytes 2162696 | tf_op jit(solution)/shard_map/ppermute | solution.py:626
  524.8 54.2 %collective-permute-start.24 = (bf16[256,1408]{1,0:T(8,128)(2,1)S(1)}, bf16[256,1408]{1,0:T(8,128)(2,1)S(1)}, u32[]{:S(2)}, u32[]{:S(2)}) collective-permute-start(bf16[256,1408]{1,0:T(8,128)(2,1)S(1)} %copy-done.30), channel_id=1, source_target_pairs={{0,4},{4,0},{8,12},{12,8},{16,20},{20,16},{24,28},{28,24},{1,5},{5... | collective-permute-start | bytes 2162696 | tf_op jit(solution)/shard_map/ppermute | solution.py:626
  525.5 65.3 %collective-permute-start.25 = (bf16[256,1408]{1,0:T(8,128)(2,1)}, bf16[256,1408]{1,0:T(8,128)(2,1)S(1)}, u32[]{:S(2)}, u32[]{:S(2)}) collective-permute-start(bf16[256,1408]{1,0:T(8,128)(2,1)} %collective-permute-done.21), channel_id=1, source_target_pairs={{0,4},{4,0},{8,12},{12,8},{16,20},{20,16},{24,28},{28,24},{1,5},{5... | collective-permute-start | bytes 2162696 | tf_op jit(solution)/shard_map/ppermute | solution.py:626
  529.1 77.1 %collective-permute-start.26 = (bf16[256,1408]{1,0:T(8,128)(2,1)}, bf16[256,1408]{1,0:T(8,128)(2,1)S(1)}, u32[]{:S(2)}, u32[]{:S(2)}) collective-permute-start(bf16[256,1408]{1,0:T(8,128)(2,1)} %collective-permute-done.22), channel_id=1, source_target_pairs={{0,4},{4,0},{8,12},{12,8},{16,20},{20,16},{24,28},{28,24},{1,5},{5... | collective-permute-start | bytes 2162696 | tf_op jit(solution)/shard_map/ppermute | solution.py:626
  544.5 73.3 %collective-permute-start.27 = (bf16[256,1408]{1,0:T(8,128)(2,1)}, bf16[256,1408]{1,0:T(8,128)(2,1)S(1)}, u32[]{:S(2)}, u32[]{:S(2)}) collective-permute-start(bf16[256,1408]{1,0:T(8,128)(2,1)} %collective-permute-done.23), channel_id=1, source_target_pairs={{0,4},{4,0},{8,12},{12,8},{16,20},{20,16},{24,28},{28,24},{1,5},{5... | collective-permute-start | bytes 2162696 | tf_op jit(solution)/shard_map/ppermute | solution.py:626
  664.7 112.6 %all-gather.11.cloned.1.call-start = ((), (), s32[]{:S(2)}) async-start(), calls=%async_computation.10 | async-start | bytes 5242880 | tf_op jit(solution)/shard_map/all_gather | solution.py:755
  670.8 60.7 %collective-permute-start.28 = (bf16[1024,1408]{1,0:T(8,128)(2,1)S(1)}, bf16[1024,1408]{1,0:T(8,128)(2,1)S(1)}, u32[]{:S(2)}, u32[]{:S(2)}) collective-permute-start(bf16[1024,1408]{1,0:T(8,128)(2,1)S(1)} %convolution_convert_fusion.3), channel_id=1, source_target_pairs={{0,4},{4,0},{8,12},{12,8},{16,20},{20,16},{24,28},{28,24},{1,5},{5... | collective-permute-start | bytes 8650760 | tf_op jit(solution)/shard_map/ppermute | solution.py:626
  742.4 582.7 %reduce-scatter.11.cloned.1.call-start = ((), (), s32[]{:S(2)}) async-start(), calls=%async_computation.11 | async-start | bytes 5242880 | tf_op jit(solution)/shard_map/reduce_scatter | solution.py:759
  750.3 65.7 %collective-permute-start.29 = (bf16[1024,1408]{1,0:T(8,128)(2,1)}, bf16[1024,1408]{1,0:T(8,128)(2,1)}, u32[]{:S(2)}, u32[]{:S(2)}) collective-permute-start(bf16[1024,1408]{1,0:T(8,128)(2,1)} %convolution_convert_fusion.2), channel_id=1, source_target_pairs={{0,4},{4,0},{8,12},{12,8},{16,20},{20,16},{24,28},{28,24},{1,5},{5... | collective-permute-start | bytes 8650760 | tf_op jit(solution)/shard_map/ppermute | solution.py:626
  755.6 119.1 %collective-permute-start.30 = (bf16[1024,1408]{1,0:T(8,128)(2,1)}, bf16[1024,1408]{1,0:T(8,128)(2,1)}, u32[]{:S(2)}, u32[]{:S(2)}) collective-permute-start(bf16[1024,1408]{1,0:T(8,128)(2,1)} %convolution_convert_fusion.1), channel_id=1, source_target_pairs={{0,4},{4,0},{8,12},{12,8},{16,20},{20,16},{24,28},{28,24},{1,5},{5... | collective-permute-start | bytes 8650760 | tf_op jit(solution)/shard_map/ppermute | solution.py:626
  902.3 426.2 %reduce-scatter.9.cloned.1.call-start = ((), (), s32[]{:S(2)}) async-start(), calls=%async_computation.9 | async-start | bytes 5242880 | tf_op jit(solution)/shard_map/reduce_scatter | solution.py:759
  904.1 48.2 %collective-permute-start.62 = (bf16[256,1408]{1,0:T(8,128)(2,1)S(1)}, bf16[256,1408]{1,0:T(8,128)(2,1)S(1)}, u32[]{:S(2)}, u32[]{:S(2)}) collective-permute-start(bf16[256,1408]{1,0:T(8,128)(2,1)S(1)} %get-tuple-element.216), channel_id=1, source_target_pairs={{0,8},{4,12},{8,16},{12,20},{16,24},{20,28},{24,0},{28,4},{1,9},{5... | collective-permute-start | bytes 2162696 | tf_op jit(solution)/shard_map/ppermute | solution.py:670
  906.6 53.8 %collective-permute-start.63 = (bf16[256,1408]{1,0:T(8,128)(2,1)S(1)}, bf16[256,1408]{1,0:T(8,128)(2,1)S(1)}, u32[]{:S(2)}, u32[]{:S(2)}) collective-permute-start(bf16[256,1408]{1,0:T(8,128)(2,1)S(1)} %get-tuple-element.218), channel_id=1, source_target_pairs={{0,16},{4,20},{8,24},{12,28},{16,0},{20,4},{24,8},{28,12},{1,17},{... | collective-permute-start | bytes 2162696 | tf_op jit(solution)/shard_map/ppermute | solution.py:670
  906.6 53.8 %collective-permute-start.64 = (bf16[256,1408]{1,0:T(8,128)(2,1)S(1)}, bf16[256,1408]{1,0:T(8,128)(2,1)S(1)}, u32[]{:S(2)}, u32[]{:S(2)}) collective-permute-start(bf16[256,1408]{1,0:T(8,128)(2,1)S(1)} %get-tuple-element.217), channel_id=1, source_target_pairs={{0,24},{4,28},{8,0},{12,4},{16,8},{20,12},{24,16},{28,20},{1,25},{... | collective-permute-start | bytes 2162696 | tf_op jit(solution)/shard_map/ppermute | solution.py:670
  986.2 80.7 %collective-permute-start.59 = (bf16[256,1408]{1,0:T(8,128)(2,1)}, bf16[256,1408]{1,0:T(8,128)(2,1)}, u32[]{:S(2)}, u32[]{:S(2)}) collective-permute-start(bf16[256,1408]{1,0:T(8,128)(2,1)} %get-tuple-element.219), channel_id=1, source_target_pairs={{0,8},{4,12},{8,16},{12,20},{16,24},{20,28},{24,0},{28,4},{1,9},{5... | collective-permute-start | bytes 2162696 | tf_op jit(solution)/shard_map/ppermute | solution.py:670
  986.5 81.9 %collective-permute-start.60 = (bf16[256,1408]{1,0:T(8,128)(2,1)}, bf16[256,1408]{1,0:T(8,128)(2,1)}, u32[]{:S(2)}, u32[]{:S(2)}) collective-permute-start(bf16[256,1408]{1,0:T(8,128)(2,1)} %get-tuple-element.221), channel_id=1, source_target_pairs={{0,16},{4,20},{8,24},{12,28},{16,0},{20,4},{24,8},{28,12},{1,17},{... | collective-permute-start | bytes 2162696 | tf_op jit(solution)/shard_map/ppermute | solution.py:670
  1018.1 45.3 %collective-permute-start.49 = (f32[1,3072]{1,0:T(1,128)S(1)}, f32[1,3072]{1,0:T(1,128)S(1)}, u32[]{:S(2)}, u32[]{:S(2)}) collective-permute-start(f32[1,3072]{1,0:T(1,128)S(1)} %get-tuple-element.337), channel_id=1, source_target_pairs={{0,8},{4,12},{8,16},{12,20},{16,24},{20,28},{24,0},{28,4},{1,9},{5... | collective-permute-start | bytes 36872 | tf_op jit(solution)/shard_map/ppermute | solution.py:687
  1019.0 44.7 %collective-permute-start.50 = (f32[1,3072]{1,0:T(1,128)S(1)}, f32[1,3072]{1,0:T(1,128)S(1)}, u32[]{:S(2)}, u32[]{:S(2)}) collective-permute-start(f32[1,3072]{1,0:T(1,128)S(1)} %get-tuple-element.339), channel_id=1, source_target_pairs={{0,16},{4,20},{8,24},{12,28},{16,0},{20,4},{24,8},{28,12},{1,17},{... | collective-permute-start | bytes 36872 | tf_op jit(solution)/shard_map/ppermute | solution.py:687
  1022.4 43.6 %collective-permute-start.51 = (f32[1,3072]{1,0:T(1,128)S(1)}, f32[1,3072]{1,0:T(1,128)S(1)}, u32[]{:S(2)}, u32[]{:S(2)}) collective-permute-start(f32[1,3072]{1,0:T(1,128)S(1)} %get-tuple-element.338), channel_id=1, source_target_pairs={{0,24},{4,28},{8,0},{12,4},{16,8},{20,12},{24,16},{28,20},{1,25},{... | collective-permute-start | bytes 36872 | tf_op jit(solution)/shard_map/ppermute | solution.py:687
  1063.4 35.0 %collective-permute-start.61 = (bf16[256,1408]{1,0:T(8,128)(2,1)S(1)}, bf16[256,1408]{1,0:T(8,128)(2,1)S(1)}, u32[]{:S(2)}, u32[]{:S(2)}) collective-permute-start(bf16[256,1408]{1,0:T(8,128)(2,1)S(1)} %copy-done.35), channel_id=1, source_target_pairs={{0,24},{4,28},{8,0},{12,4},{16,8},{20,12},{24,16},{28,20},{1,25},{... | collective-permute-start | bytes 2162696 | tf_op jit(solution)/shard_map/ppermute | solution.py:670
  1063.7 55.2 %collective-permute-start.56 = (bf16[256,1408]{1,0:T(8,128)(2,1)}, bf16[256,1408]{1,0:T(8,128)(2,1)}, u32[]{:S(2)}, u32[]{:S(2)}) collective-permute-start(bf16[256,1408]{1,0:T(8,128)(2,1)} %get-tuple-element.222), channel_id=1, source_target_pairs={{0,8},{4,12},{8,16},{12,20},{16,24},{20,28},{24,0},{28,4},{1,9},{5... | collective-permute-start | bytes 2162696 | tf_op jit(solution)/shard_map/ppermute | solution.py:670
  1066.0 80.9 %collective-permute-start.52 = (bf16[1024,1024]{1,0:T(8,128)(2,1)}, bf16[1024,1024]{1,0:T(8,128)(2,1)S(1)}, u32[]{:S(2)}, u32[]{:S(2)}) collective-permute-start(bf16[1024,1024]{1,0:T(8,128)(2,1)} %fusion.26), channel_id=1, source_target_pairs={{0,4},{4,0},{8,12},{12,8},{16,20},{20,16},{24,28},{28,24},{1,5},{5... | collective-permute-start | bytes 6291464 | tf_op jit(solution)/shard_map/ppermute | solution.py:626
  1067.0 53.7 %collective-permute-start.57 = (bf16[256,1408]{1,0:T(8,128)(2,1)S(1)}, bf16[256,1408]{1,0:T(8,128)(2,1)}, u32[]{:S(2)}, u32[]{:S(2)}) collective-permute-start(bf16[256,1408]{1,0:T(8,128)(2,1)S(1)} %copy-done.34), channel_id=1, source_target_pairs={{0,16},{4,20},{8,24},{12,28},{16,0},{20,4},{24,8},{28,12},{1,17},{... | collective-permute-start | bytes 2162696 | tf_op jit(solution)/shard_map/ppermute | solution.py:670
  1068.4 75.2 %collective-permute-start.58 = (bf16[256,1408]{1,0:T(8,128)(2,1)S(1)}, bf16[256,1408]{1,0:T(8,128)(2,1)}, u32[]{:S(2)}, u32[]{:S(2)}) collective-permute-start(bf16[256,1408]{1,0:T(8,128)(2,1)S(1)} %copy-done.33), channel_id=1, source_target_pairs={{0,24},{4,28},{8,0},{12,4},{16,8},{20,12},{24,16},{28,20},{1,25},{... | collective-permute-start | bytes 2162696 | tf_op jit(solution)/shard_map/ppermute | solution.py:670
  1099.3 60.5 %collective-permute-start.31 = (bf16[1024,1024]{1,0:T(8,128)(2,1)}, bf16[1024,1024]{1,0:T(8,128)(2,1)}, u32[]{:S(2)}, u32[]{:S(2)}) collective-permute-start(bf16[1024,1024]{1,0:T(8,128)(2,1)} %convolution_convert_fusion.7), channel_id=1, source_target_pairs={{0,4},{4,0},{8,12},{12,8},{16,20},{20,16},{24,28},{28,24},{1,5},{5... | collective-permute-start | bytes 6291464 | tf_op jit(solution)/shard_map/ppermute | solution.py:626
  1118.9 79.1 %collective-permute-start.33 = (bf16[1024,1024]{1,0:T(8,128)(2,1)S(1)}, bf16[1024,1024]{1,0:T(8,128)(2,1)S(1)}, u32[]{:S(2)}, u32[]{:S(2)}) collective-permute-start(bf16[1024,1024]{1,0:T(8,128)(2,1)S(1)} %copy-done.86), channel_id=1, source_target_pairs={{0,4},{4,0},{8,12},{12,8},{16,20},{20,16},{24,28},{28,24},{1,5},{5... | collective-permute-start | bytes 6291464 | tf_op jit(solution)/shard_map/ppermute | solution.py:626
  1120.7 99.8 %collective-permute-start.32 = (bf16[1024,1024]{1,0:T(8,128)(2,1)S(1)}, bf16[1024,1024]{1,0:T(8,128)(2,1)S(1)}, u32[]{:S(2)}, u32[]{:S(2)}) collective-permute-start(bf16[1024,1024]{1,0:T(8,128)(2,1)S(1)} %copy-done.85), channel_id=1, source_target_pairs={{0,4},{4,0},{8,12},{12,8},{16,20},{20,16},{24,28},{28,24},{1,5},{5... | collective-permute-start | bytes 6291464 | tf_op jit(solution)/shard_map/ppermute | solution.py:626
  1147.9 77.1 %collective-permute-start.53 = (bf16[256,1024]{1,0:T(8,128)(2,1)S(1)}, bf16[256,1024]{1,0:T(8,128)(2,1)S(1)}, u32[]{:S(2)}, u32[]{:S(2)}) collective-permute-start(bf16[256,1024]{1,0:T(8,128)(2,1)S(1)} %get-tuple-element.227), channel_id=1, source_target_pairs={{0,8},{4,12},{8,16},{12,20},{16,24},{20,28},{24,0},{28,4},{1,9},{5... | collective-permute-start | bytes 1572872 | tf_op jit(solution)/shard_map/ppermute | solution.py:670
  1148.0 78.9 %collective-permute-start.54 = (bf16[256,1024]{1,0:T(8,128)(2,1)S(1)}, bf16[256,1024]{1,0:T(8,128)(2,1)S(1)}, u32[]{:S(2)}, u32[]{:S(2)}) collective-permute-start(bf16[256,1024]{1,0:T(8,128)(2,1)S(1)} %get-tuple-element.229), channel_id=1, source_target_pairs={{0,16},{4,20},{8,24},{12,28},{16,0},{20,4},{24,8},{28,12},{1,17},{... | collective-permute-start | bytes 1572872 | tf_op jit(solution)/shard_map/ppermute | solution.py:670
  1159.8 67.4 %collective-permute-start.55 = (bf16[256,1024]{1,0:T(8,128)(2,1)S(1)}, bf16[256,1024]{1,0:T(8,128)(2,1)S(1)}, u32[]{:S(2)}, u32[]{:S(2)}) collective-permute-start(bf16[256,1024]{1,0:T(8,128)(2,1)S(1)} %get-tuple-element.228), channel_id=1, source_target_pairs={{0,24},{4,28},{8,0},{12,4},{16,8},{20,12},{24,16},{28,20},{1,25},{... | collective-permute-start | bytes 1572872 | tf_op jit(solution)/shard_map/ppermute | solution.py:670
  1198.0 33.4 %collective-permute-start.39 = (bf16[256,1024]{1,0:T(8,128)(2,1)S(1)}, bf16[256,1024]{1,0:T(8,128)(2,1)S(1)}, u32[]{:S(2)}, u32[]{:S(2)}) collective-permute-start(bf16[256,1024]{1,0:T(8,128)(2,1)S(1)} %get-tuple-element.236), channel_id=1, source_target_pairs={{0,8},{4,12},{8,16},{12,20},{16,24},{20,28},{24,0},{28,4},{1,9},{5... | collective-permute-start | bytes 1572872 | tf_op jit(solution)/shard_map/ppermute | solution.py:670
  1220.5 37.9 %collective-permute-start.40 = (bf16[256,1024]{1,0:T(8,128)(2,1)S(1)}, bf16[256,1024]{1,0:T(8,128)(2,1)S(1)}, u32[]{:S(2)}, u32[]{:S(2)}) collective-permute-start(bf16[256,1024]{1,0:T(8,128)(2,1)S(1)} %get-tuple-element.238), channel_id=1, source_target_pairs={{0,16},{4,20},{8,24},{12,28},{16,0},{20,4},{24,8},{28,12},{1,17},{... | collective-permute-start | bytes 1572872 | tf_op jit(solution)/shard_map/ppermute | solution.py:670
  1225.0 49.7 %collective-permute-start.41 = (bf16[256,1024]{1,0:T(8,128)(2,1)S(1)}, bf16[256,1024]{1,0:T(8,128)(2,1)S(1)}, u32[]{:S(2)}, u32[]{:S(2)}) collective-permute-start(bf16[256,1024]{1,0:T(8,128)(2,1)S(1)} %get-tuple-element.237), channel_id=1, source_target_pairs={{0,24},{4,28},{8,0},{12,4},{16,8},{20,12},{24,16},{28,20},{1,25},{... | collective-permute-start | bytes 1572872 | tf_op jit(solution)/shard_map/ppermute | solution.py:670
  1226.8 69.4 %collective-permute-start.45 = (bf16[256,1024]{1,0:T(8,128)(2,1)S(1)}, bf16[256,1024]{1,0:T(8,128)(2,1)S(1)}, u32[]{:S(2)}, u32[]{:S(2)}) collective-permute-start(bf16[256,1024]{1,0:T(8,128)(2,1)S(1)} %get-tuple-element.230), channel_id=1, source_target_pairs={{0,8},{4,12},{8,16},{12,20},{16,24},{20,28},{24,0},{28,4},{1,9},{5... | collective-permute-start | bytes 1572872 | tf_op jit(solution)/shard_map/ppermute | solution.py:670
  1227.2 80.2 %collective-permute-start.46 = (bf16[256,1024]{1,0:T(8,128)(2,1)S(1)}, bf16[256,1024]{1,0:T(8,128)(2,1)S(1)}, u32[]{:S(2)}, u32[]{:S(2)}) collective-permute-start(bf16[256,1024]{1,0:T(8,128)(2,1)S(1)} %get-tuple-element.232), channel_id=1, source_target_pairs={{0,16},{4,20},{8,24},{12,28},{16,0},{20,4},{24,8},{28,12},{1,17},{... | collective-permute-start | bytes 1572872 | tf_op jit(solution)/shard_map/ppermute | solution.py:670
  1231.4 77.0 %collective-permute-start.47 = (bf16[256,1024]{1,0:T(8,128)(2,1)S(1)}, bf16[256,1024]{1,0:T(8,128)(2,1)S(1)}, u32[]{:S(2)}, u32[]{:S(2)}) collective-permute-start(bf16[256,1024]{1,0:T(8,128)(2,1)S(1)} %get-tuple-element.231), channel_id=1, source_target_pairs={{0,24},{4,28},{8,0},{12,4},{16,8},{20,12},{24,16},{28,20},{1,25},{... | collective-permute-start | bytes 1572872 | tf_op jit(solution)/shard_map/ppermute | solution.py:670
  1258.4 59.1 %collective-permute-start.42 = (bf16[256,1024]{1,0:T(8,128)(2,1)S(1)}, bf16[256,1024]{1,0:T(8,128)(2,1)S(1)}, u32[]{:S(2)}, u32[]{:S(2)}) collective-permute-start(bf16[256,1024]{1,0:T(8,128)(2,1)S(1)} %get-tuple-element.233), channel_id=1, source_target_pairs={{0,8},{4,12},{8,16},{12,20},{16,24},{20,28},{24,0},{28,4},{1,9},{5... | collective-permute-start | bytes 1572872 | tf_op jit(solution)/shard_map/ppermute | solution.py:670
  1274.7 48.4 %collective-permute-start.43 = (bf16[256,1024]{1,0:T(8,128)(2,1)S(1)}, bf16[256,1024]{1,0:T(8,128)(2,1)S(1)}, u32[]{:S(2)}, u32[]{:S(2)}) collective-permute-start(bf16[256,1024]{1,0:T(8,128)(2,1)S(1)} %get-tuple-element.235), channel_id=1, source_target_pairs={{0,16},{4,20},{8,24},{12,28},{16,0},{20,4},{24,8},{28,12},{1,17},{... | collective-permute-start | bytes 1572872 | tf_op jit(solution)/shard_map/ppermute | solution.py:670
  1296.2 27.6 %collective-permute-start.44 = (bf16[256,1024]{1,0:T(8,128)(2,1)S(1)}, bf16[256,1024]{1,0:T(8,128)(2,1)S(1)}, u32[]{:S(2)}, u32[]{:S(2)}) collective-permute-start(bf16[256,1024]{1,0:T(8,128)(2,1)S(1)} %get-tuple-element.234), channel_id=1, source_target_pairs={{0,24},{4,28},{8,0},{12,4},{16,8},{20,12},{24,16},{28,20},{1,25},{... | collective-permute-start | bytes 1572872 | tf_op jit(solution)/shard_map/ppermute | solution.py:670
  (109 other events, 4100.6 us)
Sparse Core Ops, SparseCore 0:
  13.1 34.6 all-gather.4
  282.1 44.6 reduce-scatter.4
  331.5 34.4 all-gather.6
  434.7 33.1 all-gather.8
  664.8 44.6 reduce-scatter.6
  742.5 34.6 all-gather.10
  902.5 44.6 reduce-scatter.10
  978.5 45.6 reduce-scatter.8

commit v3 on v1

--- a/solution.py
+++ b/solution.py
@@ -150,7 +150,7 @@
 def bwd_body(
     heads, dk, dv, q_ref, k_ref, v_ref, og_ref, ab_ref, qh_ref, kh_ref, vh_ref,
     tq_ref, tk_ref, tv_ref, par_ref, gain_ref, g_ref, o_ref, u_ref, t_ref, s_ref,
-    dqk_ref, dv_ref, dog_ref, dab_ref, dtq_ref, dtk_ref, dtv_ref, dpar_ref, dgain_ref,
+    draw_ref, dab_ref, dtq_ref, dtk_ref, dtv_ref, dpar_ref, dgain_ref,
     qb, kb, vb, qn, kn, vn, dstate,
 ):
     rows = CH
@@ -207,6 +207,7 @@
     ds1_b = [x.astype(BF) for x in ds1]
 
     gain = gain_ref[...]
+    og_at = 2 * heads * dk + heads * dv
     do_b = []
     dgain = jnp.zeros_like(gain)
     for h in hs:
@@ -218,7 +219,7 @@
         sg = sigmoid(og)
         gor = g * (o * r)
         dgain = dgain + jnp.sum(gor * (og * sg), axis=0, keepdims=True)
-        dog_ref[:, sl] = (gor * gain * (sg * (1.0 + og * (1.0 - sg)))).astype(BF)
+        draw_ref[:, og_at + h * dv : og_at + (h + 1) * dv] = (gor * gain * (sg * (1.0 + og * (1.0 - sg)))).astype(BF)
         m = g * gain * (og * sg)
         d_o = r * m - o * (r * r * r * jnp.mean(m * o, axis=-1, keepdims=True))
         do_b.append(d_o.astype(BF))
@@ -297,9 +298,9 @@
 
     wide = heads * dk
     for buf, cur, taps, out, at, dtap in (
-        (qn, qb, tq_ref, dqk_ref, 0, dtq_ref),
-        (kn, kb, tk_ref, dqk_ref, wide, dtk_ref),
-        (vn, vb, tv_ref, dv_ref, 0, dtv_ref),
+        (qn, qb, tq_ref, draw_ref, 0, dtq_ref),
+        (kn, kb, tk_ref, draw_ref, wide, dtk_ref),
+        (vn, vb, tv_ref, draw_ref, 2 * wide, dtv_ref),
     ):
         here = cur[HALO : HALO + rows, :]
         total = None
@@ -318,7 +319,9 @@
     return {
         "q": pl.BlockSpec((CH, wide_k), lambda c: (at(c), 0)),
         "k": pl.BlockSpec((CH, wide_k), lambda c: (at(c), 1)),
-        "qk": pl.BlockSpec((CH, 2 * wide_k), lambda c: (at(c), 0)),
+        "val": pl.BlockSpec((CH, wide_v), lambda c: (at(c), 2 * wide_k // wide_v)),
+        "og": pl.BlockSpec((CH, wide_v), lambda c: (at(c), 2 * wide_k // wide_v + 1)),
+        "raw": pl.BlockSpec((CH, 2 * (wide_k + wide_v)), lambda c: (at(c), 0)),
         "v": pl.BlockSpec((CH, wide_v), lambda c: (at(c), 0)),
         "ab": pl.BlockSpec((CH, LANES), lambda c: (at(c), 0)),
         "t": pl.BlockSpec((CH, heads * CH), lambda c: (at(c), 0)),
@@ -330,43 +333,84 @@
     }
 
 
-def mixer_forward(qk_raw, v_raw, og_raw, ab, tq, tk, tv, par, gain):
-    length, wide_k = qk_raw.shape[0], qk_raw.shape[1] // 2
-    wide_v = v_raw.shape[1]
+def fwd_gather_body(heads, dk, dv, *refs):
+    ins, w_ref, outs, full_ref, rest = refs[:10], refs[10], refs[11:16], refs[16], refs[17:]
+    step, steps = pl.program_id(0), pl.num_programs(0)
+    gather = Gather(w_ref, full_ref, *rest[4:])
+
+    @pl.when(step == 0)
+    def _():
+        greet_near(gather.me, gather.outer, gather.side)
+        gather.begin()
+
+    gather.step(step)
+    fwd_body(heads, dk, dv, *ins, *outs, *rest[:4])
+
+    @pl.when(step == steps - 1)
+    def _():
+        gather.steps(steps, CHUNKS + 3)
+        gather.finish()
+
+
+def bwd_scatter_body(heads, dk, dv, *refs):
+    ins, pair, outs, own, rest = refs[:18], refs[18:20], refs[20:27], refs[27], refs[28:]
+    step, steps = pl.program_id(0), pl.num_programs(0)
+    scatter = Scatter(*pair, own, *rest[7:])
+
+    @pl.when(step == 0)
+    def _():
+        greet_near(scatter.me, scatter.outer, scatter.side)
+        scatter.begin()
+
+    scatter.step(step)
+    bwd_body(heads, dk, dv, *ins, *outs, *rest[:7])
+
+    @pl.when(step == steps - 1)
+    def _():
+        scatter.steps(steps, CHUNKS + 3)
+        scatter.finish()
+
+
+def mixer_forward(raw, ab, tq, tk, tv, par, gain, w=None, ident=None):
+    length, wide_k, wide_v = raw.shape[0], tq.shape[1], tv.shape[1]
     dv = gain.shape[1]
     heads = wide_v // dv
     dk = wide_k // heads
     steps = length // CH
     sp = mixer_specs(heads, dk, dv, lambda c: c)
+    any_ref = [pl.BlockSpec(memory_space=pl.ANY)]
+    fused = w is not None
     return pl.pallas_call(
-        functools.partial(fwd_body, heads, dk, dv),
+        functools.partial(fwd_gather_body if fused else fwd_body, heads, dk, dv),
         grid=(steps,),
-        in_specs=[sp[n] for n in ("q", "k", "v", "v", "ab", "tk", "tk", "tv", "par", "gain")],
-        out_specs=[sp[n] for n in ("v", "v", "v", "t", "s")],
+        in_specs=[sp[n] for n in ("q", "k", "val", "og", "ab", "tk", "tk", "tv", "par", "gain")] + any_ref * fused,
+        out_specs=[sp[n] for n in ("v", "v", "v", "t", "s")] + any_ref * fused,
         out_shape=[
             jax.ShapeDtypeStruct((length, wide_v), BF),
             jax.ShapeDtypeStruct((length, wide_v), F32),
             jax.ShapeDtypeStruct((length, wide_v), BF),
             jax.ShapeDtypeStruct((length, heads * CH), BF),
             jax.ShapeDtypeStruct((steps, dk, wide_v), BF),
-        ],
+        ]
+        + [jax.ShapeDtypeStruct((8 * w.shape[0], w.shape[1]), w.dtype) for _ in any_ref * fused],
         scratch_shapes=[
             pltpu.VMEM((CH + HALO, wide_k), F32),
             pltpu.VMEM((CH + HALO, wide_k), F32),
             pltpu.VMEM((CH + HALO, wide_v), F32),
             pltpu.VMEM((heads, dk, dv), F32),
-        ],
+        ]
+        + gather_sems() * fused,
         compiler_params=pltpu.CompilerParams(
-            dimension_semantics=("arbitrary",), vmem_limit_bytes=40 << 20
+            dimension_semantics=("arbitrary",), vmem_limit_bytes=40 << 20, collective_id=ident,
+            has_side_effects=fused,
         ),
         cost_estimate=pl.CostEstimate(flops=20_000_000_000, bytes_accessed=40_000_000, transcendentals=6_000_000),
         name="mixer_forward",
-    )(qk_raw, qk_raw, v_raw, og_raw, ab, tq, tk, tv, par, gain)
-
-
-def mixer_backward(qk_raw, v_raw, og_raw, ab, tq, tk, tv, par, gain, grad, o, u, t, s):
-    length, wide_k = qk_raw.shape[0], qk_raw.shape[1] // 2
-    wide_v = v_raw.shape[1]
+    )(raw, raw, raw, raw, ab, tq, tk, tv, par, gain, *([w] * fused))
+
+
+def mixer_backward(raw, ab, tq, tk, tv, par, gain, grad, o, u, t, s, left=None, right=None, ident=None):
+    length, wide_k, wide_v = raw.shape[0], tq.shape[1], tv.shape[1]
     dv = gain.shape[1]
     heads = wide_v // dv
     dk = wide_k // heads
@@ -376,25 +420,32 @@
     before = lambda c: jnp.maximum(at(c) * (CH // HALO) - 1, 0)
     hq = pl.BlockSpec((HALO, wide_k), lambda c: (before(c), 0))
     hk = pl.BlockSpec((HALO, wide_k), lambda c: (before(c), 1))
-    hv = pl.BlockSpec((HALO, wide_v), lambda c: (before(c), 0))
-    names = ("q", "k", "v", "v", "ab")
+    hv = pl.BlockSpec((HALO, wide_v), lambda c: (before(c), 2 * wide_k // wide_v))
+    names = ("q", "k", "val", "og", "ab")
     rest = ("tk", "tk", "tv", "par", "gain", "v", "v", "v", "t", "s")
+    fused = left is not None
+    pair, own, extra = [], [], []
+    if fused:
+        whole = lambda x: pl.BlockSpec(x.shape, lambda c: (0, 0), pipeline_mode=pl.Buffered(1))
+        mine = (left.shape[1] // 8, right.shape[1])
+        pair = [whole(left), whole(right)]
+        own = [pl.BlockSpec(mine, lambda c: (0, 0))]
+        extra = scatter_scratch(*mine)
     return pl.pallas_call(
-        functools.partial(bwd_body, heads, dk, dv),
+        functools.partial(bwd_scatter_body if fused else bwd_body, heads, dk, dv),
         grid=(steps,),
-        in_specs=[sp[n] for n in names] + [hq, hk, hv] + [sp[n] for n in rest],
-        out_specs=[sp[n] for n in ("qk", "v", "v", "ab", "tk", "tk", "tv", "par", "gain")],
+        in_specs=[sp[n] for n in names] + [hq, hk, hv] + [sp[n] for n in rest] + pair,
+        out_specs=[sp[n] for n in ("raw", "ab", "tk", "tk", "tv", "par", "gain")] + own,
         out_shape=[
-            jax.ShapeDtypeStruct((length, 2 * wide_k), BF),
-            jax.ShapeDtypeStruct((length, wide_v), BF),
-            jax.ShapeDtypeStruct((length, wide_v), BF),
+            jax.ShapeDtypeStruct((length, 2 * (wide_k + wide_v)), BF),
             jax.ShapeDtypeStruct((length, LANES), BF),
             jax.ShapeDtypeStruct((8, wide_k), F32),
             jax.ShapeDtypeStruct((8, wide_k), F32),
             jax.ShapeDtypeStruct((8, wide_v), F32),
             jax.ShapeDtypeStruct((8, LANES), F32),
             jax.ShapeDtypeStruct((1, dv), F32),
-        ],
+        ]
+        + [jax.ShapeDtypeStruct(spec.block_shape, F32) for spec in own],
         scratch_shapes=[
             pltpu.VMEM((CH + HALO, wide_k), F32),
             pltpu.VMEM((CH + HALO, wide_k), F32),
@@ -403,15 +454,483 @@
             pltpu.VMEM((CH + HALO, wide_k), F32),
             pltpu.VMEM((CH + HALO, wide_v), F32),
             pltpu.VMEM((heads, dk, dv), F32),
-        ],
+        ]
+        + extra,
         compiler_params=pltpu.CompilerParams(
-            dimension_semantics=("arbitrary",), vmem_limit_bytes=48 << 20
+            dimension_semantics=("arbitrary",), vmem_limit_bytes=60 << 20, collective_id=ident,
+            has_side_effects=fused,
         ),
         cost_estimate=pl.CostEstimate(flops=40_000_000_000, bytes_accessed=60_000_000, transcendentals=9_000_000),
         name="mixer_backward",
     )(
-        qk_raw, qk_raw, v_raw, og_raw, ab, qk_raw, qk_raw, v_raw, tq, tk, tv, par, gain, grad, o, u, t, s
+        raw, raw, raw, raw, ab, raw, raw, raw, tq, tk, tv, par, gain, grad, o, u, t, s,
+        *([left, right] if fused else []),
     )
+
+
+def on_dp(index):
+    return {"dp": index}
+
+
+def greet_all(me):
+    barrier = pltpu.get_barrier_semaphore()
+    for j in range(1, 8):
+        pl.semaphore_signal(barrier, inc=1, device_id=on_dp((me + j) % 8))
+    pl.semaphore_wait(barrier, 7)
+
+
+def greet_near(me, outer, side):
+    barrier = pltpu.get_barrier_semaphore()
+    pl.semaphore_signal(barrier, inc=1, device_id=on_dp(me + 1 - 2 * side))
+
+    @pl.when(outer < 3)
+    def _():
+        pl.semaphore_signal(barrier, inc=1, device_id=on_dp((me + 2) % 8))
+
+    @pl.when(outer > 0)
+    def _():
+        pl.semaphore_signal(barrier, inc=1, device_id=on_dp((me + 6) % 8))
+
+    pl.semaphore_wait(barrier, 1 + (outer + 2) // 3 + (5 - outer) // 3)
+
+
+CHUNKS = 8
+
+
+def gather_sems():
+    return [
+        pltpu.SemaphoreType.DMA((3, CHUNKS)),
+        pltpu.SemaphoreType.DMA((3, CHUNKS)),
+        pltpu.SemaphoreType.DMA((4, CHUNKS)),
+        pltpu.SemaphoreType.DMA((8, CHUNKS)),
+        pltpu.SemaphoreType.DMA,
+    ]
+
+
+class Gather:
+    def __init__(self, w_ref, full_ref, right_s, left_s, swap_s, arrive, local):
+        self.w, self.full, self.sems, self.arrive = w_ref, full_ref, (right_s, left_s, swap_s), arrive
+        self.me = lax.axis_index("dp")
+        self.outer, self.side = self.me // 2, self.me % 2
+        self.block = w_ref.shape[0]
+        self.part = self.block // CHUNKS
+        self.keep = pltpu.make_async_copy(w_ref, full_ref.at[pl.ds(0, self.block)], local)
+
+    def spot(self, slot, c):
+        return self.full.at[pl.ds(slot * self.block + c * self.part, self.part)]
+
+    def source(self, slot, c):
+        return self.w.at[pl.ds(c * self.part, self.part)] if slot == 0 else self.spot(slot, c)
+
+    def copy(self, slot, to, c, sem, index, peer):
+        return pltpu.make_async_remote_copy(
+            self.source(slot, c), self.spot(to, c), sem.at[index, c], self.arrive.at[to, c], device_id=on_dp(peer)
+        )
+
+    def to_right(self, h, c):
+        return self.copy((4 - h) % 4, 3 - h, c, self.sems[0], h, (self.me + 2) % 8)
+
+    def to_left(self, h, c):
+        return self.copy(h, h + 1, c, self.sems[1], h, (self.me + 6) % 8)
+
+    def to_side(self, slot, c):
+        return self.copy(slot, 4 + slot, c, self.sems[2], slot, self.me + 1 - 2 * self.side)
+
+    def landed(self, slot, c):
+        pltpu.make_async_copy(self.spot(slot, c), self.spot(slot, c), self.arrive.at[slot, c]).wait()
+
+    def begin(self):
+        self.keep.start()
+
+    def step(self, i):
+        outer = self.outer
+
+        @pl.when(i < CHUNKS)
+        def _():
+            self.to_side(0, i).start()
+
+            @pl.when(outer < 3)
+            def _():
+                self.to_right(0, i).start()
+
+            @pl.when(outer > 0)
+            def _():
+                self.to_left(0, i).start()
+
+        for h in range(1, 4):
+            c = i - h
+
+            @pl.when((c >= 0) & (c < CHUNKS) & (outer >= h))
+            def _():
+                self.landed(4 - h, c)
+                if h < 3:
+                    @pl.when(outer < 3)
+                    def _():
+                        self.to_right(h, c).start()
+
+                self.to_side(4 - h, c).start()
+
+            @pl.when((c >= 0) & (c < CHUNKS) & (outer + h < 4))
+            def _():
+                self.landed(h, c)
+                if h < 3:
+                    @pl.when(outer > 0)
+                    def _():
+                        self.to_left(h, c).start()
+
+                self.to_side(h, c).start()
+
+    def finish(self):
+        outer = self.outer
+
+        def one(c, carry):
+            for slot in range(4):
+                self.to_side(slot, c).wait_send()
+                self.landed(4 + slot, c)
+            for h in range(3):
+                @pl.when((outer >= h) & (outer < 3))
+                def _():
+                    self.to_right(h, c).wait_send()
+
+                @pl.when((outer + h < 4) & (outer > 0))
+                def _():
+                    self.to_left(h, c).wait_send()
+
+            return carry
+
+        lax.fori_loop(0, CHUNKS, one, 0)
+        self.keep.wait()
+
+    def steps(self, first, last):
+        def one(i, carry):
+            self.step(i)
+            return carry
+
+        lax.fori_loop(first, last, one, 0)
+
+
+def gather_small_body(w_ref, small_ref, full_ref, all_ref, *sems):
+    gather = Gather(w_ref, full_ref, *sems[:5])
+    few_s, few_r, local = sems[5:]
+    me, outer, side = gather.me, gather.outer, gather.side
+    greet_all(me)
+    gather.begin()
+    keep = pltpu.make_async_copy(small_ref, all_ref.at[0], local)
+    keep.start()
+
+    def few(j):
+        peer = (me + j) % 8
+        slot = (outer - peer // 2 + 4) % 4 + 4 * ((side + peer % 2) % 2)
+        return pltpu.make_async_remote_copy(
+            small_ref, all_ref.at[slot], few_s.at[j - 1], few_r.at[j - 1], device_id=on_dp(peer)
+        )
+
+    for j in range(1, 8):
+        few(j).start()
+    gather.steps(0, CHUNKS + 3)
+    gather.finish()
+    for j in range(1, 8):
+        few(j).wait()
+    keep.wait()
+
+
+def gather_body(w_ref, full_ref, *sems):
+    gather = Gather(w_ref, full_ref, *sems)
+    greet_near(gather.me, gather.outer, gather.side)
+    gather.begin()
+    gather.steps(0, CHUNKS + 3)
+    gather.finish()
+
+
+def ring_gather(w, ident, small=None):
+    any_ref = pl.BlockSpec(memory_space=pl.ANY)
+    full = jax.ShapeDtypeStruct((8 * w.shape[0], w.shape[1]), w.dtype)
+    params = pltpu.CompilerParams(collective_id=ident, has_side_effects=True)
+    cost = pl.CostEstimate(flops=0, bytes_accessed=150 * w.size, transcendentals=0)
+    if small is None:
+        return pl.pallas_call(
+            gather_body, in_specs=[any_ref], out_specs=any_ref, out_shape=full, scratch_shapes=gather_sems(),
+            compiler_params=params, cost_estimate=cost, name=f"ring_gather_{ident}",
+        )(w)
+    return pl.pallas_call(
+        gather_small_body,
+        in_specs=[any_ref] * 2,
+        out_specs=[any_ref] * 2,
+        out_shape=[full, jax.ShapeDtypeStruct((8,) + small.shape, small.dtype)],
+        scratch_shapes=gather_sems()
+        + [pltpu.SemaphoreType.DMA((7,)), pltpu.SemaphoreType.DMA((7,)), pltpu.SemaphoreType.DMA],
+        compiler_params=params, cost_estimate=cost, name=f"ring_gather_{ident}",
+    )(w, small)
+
+
+def scatter_sems():
+    return [pltpu.SemaphoreType.DMA((4, CHUNKS)) for _ in range(6)]
+
+
+class Scatter:
+    def __init__(self, left, right, out, mine, came, from_left, from_right, *sems):
+        self.left, self.right, self.out, self.mine, self.came = left, right, out, mine, came
+        self.acc = (from_left, from_right)
+        self.swap_s, self.swap_r, self.send_l, self.recv_l, self.send_r, self.recv_r = sems
+        self.me = lax.axis_index("dp")
+        self.outer, self.side = self.me // 2, self.me % 2
+        self.block, self.cols = out.shape
+        self.part = self.block // CHUNKS
+
+    def dots(self, half):
+        tile = self.cols if self.cols <= 1536 else 1024
+
+        def one(k, carry):
+            at = pl.multiple_of((4 * half + k) * self.block, self.block)
+            rows = self.left[:, pl.ds(at, self.block)]
+            for j in range(0, self.cols, tile):
+                self.mine[pl.ds(at, self.block), j : j + tile] = mm(rows, self.right[:, j : j + tile], TN).astype(BF)
+            return carry
+
+        lax.fori_loop(0, 4, one, 0)
+
+    def rows(self, slot, c):
+        return pl.ds(pl.multiple_of(slot * self.block + c * self.part, self.part), self.part)
+
+    def swap(self, slot, c):
+        return pltpu.make_async_remote_copy(
+            self.mine.at[self.rows(4 + slot, c)], self.came.at[self.rows(slot, c)],
+            self.swap_s.at[slot, c], self.swap_r.at[slot, c], device_id=on_dp(self.me + 1 - 2 * self.side),
+        )
+
+    def onward(self, way, dest, c):
+        ref, rows = self.acc[way], self.rows(dest, c)
+        send, recv = ((self.send_l, self.recv_l), (self.send_r, self.recv_r))[way]
+        peer = (self.me + (2, 6)[way]) % 8
+        return pltpu.make_async_remote_copy(
+            ref.at[rows], ref.at[rows], send.at[dest, c], recv.at[dest, c], device_id=on_dp(peer)
+        )
+
+    def arrived(self, way, dest, c):
+        ref, rows = self.acc[way], self.rows(dest, c)
+        recv = (self.recv_l, self.recv_r)[way]
+        pltpu.make_async_copy(ref.at[rows], ref.at[rows], recv.at[dest, c]).wait()
+
+    def pair(self, slot, c):
+        return self.mine[self.rows(slot, c), :].astype(F32) + self.came[self.rows(slot, c), :].astype(F32)
+
+    def begin(self):
+        self.dots(1)
+
+        def one(c, carry):
+            for slot in range(4):
+                self.swap(slot, c).start()
+            return carry
+
+        lax.fori_loop(0, CHUNKS, one, 0)
+        self.dots(0)
+
+    def step(self, i):
+        outer = self.outer
+
+        @pl.when(i < CHUNKS)
+        def _():
+            for slot in range(4):
+                self.swap(slot, i).wait_recv()
+
+        for way in range(2):
+            behind = outer if way == 0 else 3 - outer
+            c = i - behind
+            for dest in range(4):
+                ahead = (outer < dest) if way == 0 else (outer > dest)
+
+                @pl.when((c >= 0) & (c < CHUNKS) & ahead)
+                def _():
+                    total = self.pair((dest - outer + 4) % 4, c)
+                    ref, rows = self.acc[way], self.rows(dest, c)
+
+                    @pl.when(behind == 0)
+                    def _():
+                        ref[rows, :] = total.astype(BF)
+
+                    @pl.when(behind > 0)
+                    def _():
+                        self.arrived(way, dest, c)
+                        ref[rows, :] = (total + ref[rows, :].astype(F32)).astype(BF)
+
+                    self.onward(way, dest, c).start()
+
+        c = i - 3
+
+        @pl.when((c >= 0) & (c < CHUNKS))
+        def _():
+            at = pl.ds(pl.multiple_of(c * self.part, self.part), self.part)
+            self.out[at, :] = self.pair(0, c)
+            for way in range(2):
+                @pl.when((outer if way == 0 else 3 - outer) > 0)
+                def _():
+                    self.arrived(way, outer, c)
+                    self.out[at, :] += self.acc[way][self.rows(outer, c), :].astype(F32)
+
+    def steps(self, first, last):
+        def one(i, carry):
+            self.step(i)
+            return carry
+
+        lax.fori_loop(first, last, one, 0)
+
+    def finish(self):
+        outer = self.outer
+
+        def one(c, carry):
+            for slot in range(4):
+                self.swap(slot, c).wait_send()
+            for way in range(2):
+                for dest in range(4):
+                    ahead = (outer < dest) if way == 0 else (outer > dest)
+
+                    @pl.when(ahead)
+                    def _():
+                        self.onward(way, dest, c).wait_send()
+
+            return carry
+
+        lax.fori_loop(0, CHUNKS, one, 0)
+
+
+def scatter_scratch(block, cols):
+    return [
+        pltpu.VMEM((8 * block, cols), BF),
+        pltpu.VMEM((4 * block, cols), BF),
+        pltpu.VMEM((4 * block, cols), BF),
+        pltpu.VMEM((4 * block, cols), BF),
+    ] + scatter_sems()
+
+
+def scatter_body(left_ref, right_ref, out_ref, *scratch):
+    scatter = Scatter(left_ref, right_ref, out_ref, *scratch)
+    greet_near(scatter.me, scatter.outer, scatter.side)
+    scatter.begin()
+    scatter.steps(0, CHUNKS + 3)
+    scatter.finish()
+
+
+def scatter_last_body(t_size, left_ref, right_ref, few_ref, tap_ref, vec_ref, out_ref, few_out, tap_out, vec_out, *scratch):
+    few_in, tap_in, vec_t, vec_d, few_sem, tap_sem, t_sem, d_sem = scratch[-8:]
+    scatter = Scatter(left_ref, right_ref, out_ref, *scratch[:-8])
+    me, outer, side = scatter.me, scatter.outer, scatter.side
+    mine = lax.axis_index("tensor")
+    barrier = pltpu.get_barrier_semaphore()
+    for j in range(1, t_size):
+        pl.semaphore_signal(barrier, inc=1, device_id={"tensor": (mine + j) % t_size})
+    for j in range(1, 8):
+        pl.semaphore_signal(barrier, inc=1, device_id=on_dp((me + j) % 8))
+    pl.semaphore_wait(barrier, 6 + t_size)
+
+    def few(j):
+        peer = (me + j) % 8
+        slot = (peer // 2 - outer + 4) % 4 + 4 * ((side + peer % 2) % 2)
+        return pltpu.make_async_remote_copy(
+            few_ref.at[slot], few_in.at[j], few_sem.at[0, j], few_sem.at[1, j], device_id=on_dp(peer)
+        )
+
+    def tap(j):
+        peer = (me + j) % 8
+        return pltpu.make_async_remote_copy(
+            tap_ref.at[peer], tap_in.at[j], tap_sem.at[0, j], tap_sem.at[1, j], device_id=on_dp(peer)
+        )
+
+    def across(j):
+        return pltpu.make_async_remote_copy(
+            vec_ref, vec_t.at[mine], t_sem.at[0, j], t_sem.at[1, j], device_id={"tensor": (mine + j) % t_size}
+        )
+
+    def along(j):
+        return pltpu.make_async_remote_copy(
+            vec_d.at[me], vec_d.at[me], d_sem.at[0, j], d_sem.at[1, j], device_id=on_dp((me + j) % 8)
+        )
+
+    for j in range(1, t_size):
+        across(j).start()
+    for j in range(1, 8):
+        few(j).start()
+        tap(j).start()
+    scatter.begin()
+    vec_t[mine] = vec_ref[...]
+    for j in range(1, t_size):
+        pltpu.make_async_copy(vec_ref, vec_t.at[(mine + t_size - j) % t_size], t_sem.at[1, j]).wait()
+    total = vec_t[0]
+    for j in range(1, t_size):
+        total = total + vec_t[j]
+    vec_d[me] = total
+    for j in range(1, 8):
+        along(j).start()
+    scatter.steps(0, CHUNKS + 3)
+    few_total, tap_total = few_ref[0], tap_ref[me]
+    for j in range(1, 8):
+        few(j).wait_recv()
+        few_total = few_total + few_in[j]
+        tap(j).wait_recv()
+        tap_total = tap_total + tap_in[j]
+    few_out[...] = few_total
+    tap_out[...] = tap_total
+    for j in range(1, 8):
+        pltpu.make_async_copy(vec_d.at[me], vec_d.at[(me + 8 - j) % 8], d_sem.at[1, j]).wait()
+    total = vec_d[0]
+    for j in range(1, 8):
+        total = total + vec_d[j]
+    vec_out[...] = total
+    for j in range(1, t_size):
+        across(j).wait_send()
+    for j in range(1, 8):
+        few(j).wait_send()
+        tap(j).wait_send()
+        along(j).wait_send()
+    scatter.finish()
+
+
+def ring_scatter_last(left, right, few, taps, vec, t_size, ident):
+    block, cols = left.shape[1] // 8, right.shape[1]
+    vmem = pl.BlockSpec(memory_space=pltpu.VMEM)
+    return pl.pallas_call(
+        functools.partial(scatter_last_body, t_size),
+        in_specs=[vmem] * 5,
+        out_specs=[vmem] * 4,
+        out_shape=[
+            jax.ShapeDtypeStruct((block, cols), F32),
+            jax.ShapeDtypeStruct(few.shape[1:], F32),
+            jax.ShapeDtypeStruct(taps.shape[1:], F32),
+            jax.ShapeDtypeStruct(vec.shape, F32),
+        ],
+        scratch_shapes=scatter_scratch(block, cols)
+        + [
+            pltpu.VMEM(few.shape, F32),
+            pltpu.VMEM(taps.shape, F32),
+            pltpu.VMEM((t_size,) + vec.shape, F32),
+            pltpu.VMEM((8,) + vec.shape, F32),
+            pltpu.SemaphoreType.DMA((2, 8)),
+            pltpu.SemaphoreType.DMA((2, 8)),
+            pltpu.SemaphoreType.DMA((2, t_size)),
+            pltpu.SemaphoreType.DMA((2, 8)),
+        ],
+        compiler_params=pltpu.CompilerParams(
+            collective_id=ident, has_side_effects=True, vmem_limit_bytes=60 << 20
+        ),
+        cost_estimate=pl.CostEstimate(flops=0, bytes_accessed=1200 * block * cols, transcendentals=0),
+        name=f"ring_scatter_{ident}",
+    )(left, right, few, taps, vec)
+
+
+def ring_scatter(left, right, ident):
+    block, cols = left.shape[1] // 8, right.shape[1]
+    vmem = pl.BlockSpec(memory_space=pltpu.VMEM)
+    return pl.pallas_call(
+        scatter_body,
+        in_specs=[vmem] * 2,
+        out_specs=vmem,
+        out_shape=jax.ShapeDtypeStruct((block, cols), F32),
+        scratch_shapes=scatter_scratch(block, cols),
+        compiler_params=pltpu.CompilerParams(
+            collective_id=ident, has_side_effects=True, vmem_limit_bytes=60 << 20
+        ),
+        cost_estimate=pl.CostEstimate(flops=0, bytes_accessed=1200 * block * cols, transcendentals=0),
+        name=f"ring_scatter_{ident}",
+    )(left, right)
 
 
 def plain_dot(left_mat, right_mat):
@@ -438,7 +957,6 @@
     def __init__(self, dp_size):
         self.outer = dp_size // 2
         self.index = lax.axis_index("dp")
-        self.last = None
 
     def _roll(self, x, axis, blocks):
         size = x.shape[axis] // self.outer * blocks
@@ -479,32 +997,23 @@
     def _swap(self, x):
         return lax.ppermute(x, "dp", [(i, i ^ 1) for i in range(2 * self.outer)])
 
-    def _from(self, x, steps):
-        n = 2 * self.outer
-        return lax.ppermute(x, "dp", [((i + 2 * steps) % n, i) for i in range(n)])
-
-    def gather(self, block):
-        if self.last is not None:
-            block, self.last = lax.optimization_barrier((block, self.last))
-        own = [block] + [self._from(block, k) for k in range(1, self.outer)]
-        self.last = own[-1]
-        other = [self._swap(b) for b in own]
-        return jnp.concatenate(own + other, axis=0)
-
-    def scatter(self, left, right):
-        half = left.shape[1] // 2
-        sent = dot_tokens(left[:, half:], right).astype(BF)
-        came = self._swap(sent)
-        pair = (dot_tokens(left[:, :half], right) + came.astype(F32)).astype(BF)
-        size = half // self.outer
-        n = 2 * self.outer
-        total = pair[:size].astype(F32)
-        for k in range(1, self.outer):
-            piece = pair[k * size : (k + 1) * size]
-            total = total + lax.ppermute(
-                piece, "dp", [(i, (i + 2 * k) % n) for i in range(n)]
-            ).astype(F32)
-        return total
+    def gather_first(self, w, small):
+        return ring_gather(w, 0, small)
+
+    def gather(self, w, ident):
+        return ring_gather(w, ident)
+
+    def scatter(self, left, right, ident):
+        return ring_scatter(left, right, ident)
+
+    def forward(self, core_in, w, ident):
+        return mixer_forward(*core_in, w, ident)
+
+    def backward(self, core_in, saved, left, right, ident):
+        return mixer_backward(*core_in, *saved, left, right, ident)
+
+    def scatter_last(self, left, right, few, taps, vec, tensor_size, ident):
+        return ring_scatter_last(left, right, few, taps, vec, tensor_size, ident)
 
 
 class PlainRows:
@@ -514,13 +1023,30 @@
     def restore(self, x, axis):
         return x
 
-    def gather(self, block):
-        return lax.all_gather(block, "dp", axis=0, tiled=True)
-
-    def scatter(self, left, right):
+    def gather(self, w, ident):
+        return lax.all_gather(w, "dp", axis=0, tiled=True)
+
+    def scatter(self, left, right, ident):
         full = dot_tokens(left, right).astype(BF)
         return lax.psum_scatter(full, "dp", scatter_dimension=0, tiled=True).astype(F32)
 
+    def gather_first(self, w, small):
+        return lax.all_gather(w, "dp", axis=0, tiled=True), lax.all_gather(small, "dp", axis=0)
+
+    def forward(self, core_in, w, ident):
+        return [*mixer_forward(*core_in), self.gather(w, ident)]
+
+    def backward(self, core_in, saved, left, right, ident):
+        return [*mixer_backward(*core_in, *saved), self.scatter(left, right, ident)]
+
+    def scatter_last(self, left, right, few, taps, vec, tensor_size, ident):
+        few, taps = (lax.psum_scatter(x, "dp", scatter_dimension=0, tiled=True)[0] for x in (few, taps))
+        return self.scatter(left, right, ident), few, taps, lax.psum(vec, ("dp", "tensor"))
+
+
+def tie(value, *others):
+    return lax.optimization_barrier((value, others))[0]
+
 
 def tensor_gather(x):
     return lax.all_gather(x, "tensor", axis=0, tiled=True)
@@ -531,7 +1057,7 @@
 
 
 def shards(
-    dp_size, inputs, cotangent, lengths, norm1_gain, w_query, w_key, w_value, w_outgate, w_beta, w_alpha,
+    dp_size, tensor_size, inputs, cotangent, lengths, norm1_gain, w_query, w_key, w_value, w_outgate, w_beta, w_alpha,
     conv_query, conv_key, conv_value, a_log, dt_bias, head_gain, w_out, norm2_gain, w_gate, w_up, w_down,
 ):
     rows = RingRows(dp_size) if dp_size == 8 else PlainRows()
@@ -549,19 +1075,21 @@
 
     small = jnp.concatenate(
         [w_beta.reshape(-1), w_alpha.reshape(-1), conv_query.reshape(-1), conv_key.reshape(-1), conv_value.reshape(-1)]
-    )[None]
-    small = lax.all_gather(small, "dp", axis=0, tiled=True)
+    )
     cuts = [0]
     for part in (w_beta, w_alpha, conv_query, conv_key, conv_value):
         cuts.append(cuts[-1] + part.size)
+    small = jnp.pad(small, (0, -small.size % (32 * LANES))).reshape(-1, LANES)
+    full_raw, small = rows.gather_first(
+        jnp.concatenate([w_query, w_key, w_value, w_outgate], axis=1), small
+    )
+    small = small.reshape(dp_size, -1)
     pieces = [small[:, a:b] for a, b in zip(cuts[:-1], cuts[1:])]
-    full_ab = rows.reorder(
-        jnp.concatenate([p.reshape(dp_size * block, heads) for p in pieces[:2]], axis=1), 0
-    )
+    full_ab = jnp.concatenate([p.reshape(dp_size * block, heads) for p in pieces[:2]], axis=1)
     full_ab = jnp.pad(full_ab, ((0, 0), (0, LANES - 2 * heads)))
 
     def tap_table(piece, size):
-        table = piece.reshape(size, heads, taps_n).astype(F32)
+        table = rows.restore(piece, 0).reshape(size, heads, taps_n).astype(F32)
         return jnp.pad(jnp.transpose(table, (2, 1, 0)).reshape(taps_n, heads * size), ((0, 8 - taps_n), (0, 0)))
 
     tq, tk, tv = tap_table(pieces[2], dk), tap_table(pieces[3], dk), tap_table(pieces[4], dv)
@@ -575,85 +1103,84 @@
     gain_two = rows.reorder(norm2_gain[None], 1)[0]
     normed_one, norm_one_back = jax.vjp(rms_apply, local_rows, gain_one)
     rows_one = tensor_gather(normed_one.astype(BF))
-    full_qk = rows.gather(jnp.concatenate([w_query, w_key], axis=1))
-    full_value = rows.gather(w_value)
-    full_outgate = rows.gather(w_outgate)
-    full_out = rows.gather(w_out)
-    full_gate = rows.gather(w_gate)
-    full_up = rows.gather(w_up)
-    full_down = rows.gather(w_down)
     grad_after = valid_rows * rows.reorder(cotangent[0], 1).astype(F32)
     incoming_ffn = tensor_gather(grad_after.astype(BF))
 
     ab_raw = plain_dot(rows_one, full_ab)
-    qk_raw = plain_dot(rows_one, full_qk)
-    v_raw = plain_dot(rows_one, full_value)
-    og_raw = plain_dot(rows_one, full_outgate)
-    core_in = (qk_raw, v_raw, og_raw, ab_raw, tq, tk, tv, par, gain)
-    head_bf, delta_out, new_values, inverses, states = mixer_forward(*core_in)
-    after_mix = local_rows + tensor_scatter(dot_rows(head_bf, full_out))
+    core_in = (plain_dot(rows_one, full_raw), ab_raw, tq, tk, tv, par, gain)
+    head_bf, delta_out, new_values, inverses, states, full_out = rows.forward(core_in, w_out, 1)
+    mixed = dot_rows(head_bf, full_out).astype(BF)
+    full_gate = rows.gather(tie(w_gate, mixed), 2)
+    after_mix = local_rows + tie(tensor_scatter(mixed), full_gate).astype(F32)
     normed_two, norm_two_back = jax.vjp(rms_apply, after_mix, gain_two)
-    rows_two = tensor_gather(normed_two.astype(BF))
+    normed_two = normed_two.astype(BF)
+    full_up = rows.gather(tie(w_up, normed_two), 3)
+    rows_two = tie(tensor_gather(normed_two), full_up)
     gate_pre = plain_dot(rows_two, full_gate)
     up_pre = plain_dot(rows_two, full_up)
     hidden, swiglu_back = jax.vjp(swiglu, gate_pre, up_pre)
     hidden_bf = hidden.astype(BF)
-    ffn_part = tensor_scatter(dot_rows(hidden_bf, full_down).astype(BF)).astype(F32)
-    outputs = rows.restore(((after_mix + ffn_part) * valid_rows).astype(BF), 1)[None]
+    full_down = rows.gather(tie(w_down, full_up), 4)
 
     grad_hidden = plain_dot(incoming_ffn, full_down)
-    out_down = rows.scatter(incoming_ffn, hidden_bf)
     grad_gate_pre, grad_up_pre = swiglu_back(grad_hidden)
     gate_low = grad_gate_pre.astype(BF)
     up_low = grad_up_pre.astype(BF)
-    grad_normed_two = tensor_scatter(dot_rows(gate_low, full_gate) + dot_rows(up_low, full_up))
-    out_gate = rows.scatter(rows_two, gate_low)
-    out_up = rows.scatter(rows_two, up_low)
+    back_two = (dot_rows(gate_low, full_gate) + dot_rows(up_low, full_up)).astype(BF)
+    out_down = rows.scatter(tie(incoming_ffn, back_two), hidden_bf, 5)
+    grad_normed_two = tie(tensor_scatter(back_two), out_down).astype(F32)
     grad_mid, grad_norm2 = norm_two_back(grad_normed_two)
     grad_mid = grad_mid + grad_after
-    incoming_mix = tensor_gather(grad_mid.astype(BF))
-
-    grad_head = plain_dot(incoming_mix, full_out)
-    out_out = rows.scatter(incoming_mix, head_bf)
-    qk_low, v_low, og_low, ab_low, dtq, dtk, dtv, dpar, dgain = mixer_backward(
-        *core_in, grad_head, delta_out, new_values, inverses, states
+    grad_mix = grad_mid.astype(BF)
+    out_gate = rows.scatter(tie(rows_two, grad_mix), gate_low, 6)
+    incoming_mix = tie(tensor_gather(grad_mix), out_gate)
+
+    ffn_out = dot_rows(tie(hidden_bf, incoming_mix), full_down).astype(BF)
+    ffn_part = tensor_scatter(ffn_out).astype(F32)
+    grad_head = tie(plain_dot(incoming_mix, full_out), ffn_out)
+    raw_low, ab_low, dtq, dtk, dtv, dpar, dgain, out_up = rows.backward(
+        core_in, (grad_head, delta_out, new_values, inverses, states), rows_two, up_low, 7
     )
-    summed = dot_rows(qk_low, full_qk) + dot_rows(v_low, full_value)
-    summed = summed + dot_rows(og_low, full_outgate) + dot_rows(ab_low, full_ab)
-    grad_normed_one = tensor_scatter(summed.astype(BF)).astype(F32)
-    out_qk = rows.scatter(rows_one, qk_low)
-    out_value = rows.scatter(rows_one, v_low)
-    out_outgate = rows.scatter(rows_one, og_low)
-    grad_first, grad_norm1 = norm_one_back(grad_normed_one)
+    outputs = rows.restore(((after_mix + ffn_part) * valid_rows).astype(BF), 1)[None]
+    summed = (dot_rows(raw_low, full_raw) + dot_rows(ab_low, full_ab)).astype(BF)
+    grad_normed_one = tensor_scatter(summed)
+    out_out = rows.scatter(tie(incoming_mix, summed), head_bf, 8)
+    grad_first, grad_norm1 = norm_one_back(tie(grad_normed_one, out_out).astype(F32))
     grad_inputs = rows.restore(grad_mid + grad_first, 1)[None]
 
-    grad_ab = rows.restore(dot_tokens(rows_one, ab_low)[:, : 2 * heads], 0)
-    grad_beta, grad_alpha = grad_ab[:, :heads], grad_ab[:, heads:]
+    def in_lanes(x, lead):
+        return jnp.pad(x, ((0, 0), (0, -x.shape[1] % (8 * LANES)))).reshape(lead + (-1, LANES))
+
+    grad_ab = dot_tokens(rows_one, ab_low)[:, : 2 * heads]
+    few = [grad_ab[:, :heads].reshape(dp_size, -1), grad_ab[:, heads:].reshape(dp_size, -1)]
 
     def tap_grad(table, size):
-        return jnp.transpose(table[:taps_n].reshape(taps_n, heads, size), (2, 1, 0))
-
-    small_out = [grad_beta, grad_alpha, tap_grad(dtq, dk), tap_grad(dtk, dk), tap_grad(dtv, dv)]
-    small_sum = lax.psum_scatter(
-        jnp.concatenate([p.reshape(dp_size, -1) for p in small_out], axis=1), "dp", scatter_dimension=0, tiled=True
-    )[0]
-    shapes = (w_beta, w_alpha, conv_query, conv_key, conv_value)
-    out_beta, out_alpha, out_cq, out_ck, out_cv = (
-        small_sum[a:b].reshape(like.shape) for a, b, like in zip(cuts[:-1], cuts[1:], shapes)
+        return jnp.transpose(table[:taps_n].reshape(taps_n, heads, size), (2, 1, 0)).reshape(dp_size, -1)
+
+    taps = [tap_grad(dtq, dk), tap_grad(dtk, dk), tap_grad(dtv, dv)]
+    alog_full, dtb_full = (
+        lax.dynamic_update_slice_in_dim(jnp.zeros_like(a_log), dpar[i, heads : 2 * heads], head_start, 0)
+        for i in range(2)
     )
-    alog_full = lax.dynamic_update_slice_in_dim(
-        jnp.zeros_like(a_log), dpar[0, heads : 2 * heads], head_start, 0
+    vec = [rows.restore(grad_norm1[None], 1)[0], rows.restore(grad_norm2[None], 1)[0], dgain[0], alog_full, dtb_full]
+    few, taps, vec_in = (jnp.concatenate(x, axis=-1) for x in (few, taps, vec))
+    out_raw, few_sum, tap_sum, vec_sum = rows.scatter_last(
+        tie(rows_one, out_out), raw_low, in_lanes(few, (dp_size,)), in_lanes(taps, (dp_size,)),
+        in_lanes(vec_in[None], ()), tensor_size, 9,
     )
-    dtb_full = lax.dynamic_update_slice_in_dim(
-        jnp.zeros_like(dt_bias), dpar[1, heads : 2 * heads], head_start, 0
-    )
-    norm1_sum, norm2_sum, hgain_sum, alog_sum, dtb_sum = lax.psum(
-        (
-            rows.restore(grad_norm1[None], 1)[0], rows.restore(grad_norm2[None], 1)[0], dgain[0],
-            alog_full, dtb_full,
-        ),
-        ("dp", "tensor"),
-    )
+    wide = 2 * wide_k
+    out_qk, out_value, out_outgate = out_raw[:, :wide], out_raw[:, wide : wide + wide_v], out_raw[:, wide + wide_v :]
+
+    def pieces_of(total, like):
+        flat, found, at = total.reshape(-1), [], 0
+        for part in like:
+            found.append(flat[at : at + part.size].reshape(part.shape))
+            at += part.size
+        return found
+
+    out_beta, out_alpha = pieces_of(few_sum, (w_beta, w_alpha))
+    out_cq, out_ck, out_cv = pieces_of(tap_sum, (conv_query, conv_key, conv_value))
+    norm1_sum, norm2_sum, hgain_sum, alog_sum, dtb_sum = pieces_of(vec_sum, vec)
     return (
         outputs, grad_inputs, norm1_sum, out_qk[:, :wide_k], out_qk[:, wide_k:], out_value, out_outgate,
         out_beta, out_alpha, out_cq, out_ck, out_cv, alog_sum, dtb_sum, hgain_sum, out_out, norm2_sum,
@@ -670,6 +1197,6 @@
         (cube, cube, whole) + (mat,) * 6 + (cube,) * 3 + (whole,) * 3 + (mat, whole) + (mat,) * 3
     )
     return jax.shard_map(
-        functools.partial(shards, mesh.shape["dp"]), mesh=mesh, in_specs=in_specs, out_specs=out_specs,
+        functools.partial(shards, mesh.shape["dp"], mesh.shape["tensor"]), mesh=mesh, in_specs=in_specs, out_specs=out_specs,
         check_vma=False,
     )

time: 1450 us -> 1150 us (0.79); the launches traced: 1450 us -> 1130 us
  Pallas kernels: 90.1 us -> 884 us
  waiting for transfers between devices: 780 us -> 0.88 us
  starting transfers between devices: 118 us -> 0.33 us
  blocking collectives: 97.3 us -> 0 us
  matrix products: 222 us -> 138 us
  local copies, waits for them, and re-layouts: 90.1 us -> 66.7 us
    pallas_call x2 -> x10, Pallas kernels: 90.1 us -> 884 us  [the longest x3 229 us: ring_scatter(): pl.pallas_call(scatter_body, in_specs=[vmem] * 2, out_specs=vmem, out_sha...]
    ppermute x77 -> x0, waiting for transfers between devices: 751 us -> none  [the longest x35 402 us: _swap(): return lax.ppermute(x, 'dp', [(i, i ^ 1) for i in range(2 * self.outer)])]
    ppermute x77 -> x0, starting transfers between devices: 106 us -> none  [the longest x35 48 us: _swap(): return lax.ppermute(x, 'dp', [(i, i ^ 1) for i in range(2 * self.outer)])]
    dot_general x15 -> x1, matrix products: 72.9 us -> 3.04 us  [dot_tokens(): lax.dot_general(left_mat, right_mat, (((0,), (0,)), ((), ())), preferred_...]
    all_gather x1 -> x0, blocking collectives: 54.5 us -> none  [shards(): small = lax.all_gather(small, 'dp', axis=0, tiled=True)]
    psum x1 -> x0, blocking collectives: 42.8 us -> none  [shards(): lax.psum((rows.restore(grad_norm1[None], 1)[0], rows.restore(grad_norm2[N...]
    unnamed x276 -> x193, local copies, waits for them, and re-layouts: 61.9 us -> 24.7 us
    unnamed x10 -> x8, waiting for transfers between devices: 16.9 us -> 0.75 us
  transfers between devices with their start and end apart: 86 -> 8, of which waited for: 45 -> 0; matrix products, arithmetic and copies ran while one was open for 15% -> 6% of each run, Pallas kernels for 0% -> 66%
where the time goes in v3:
time: 1150 us; the launch traced here: 1130 us
  Pallas kernels  884 us (77%)
  matrix products  138 us (12%)
  local copies, waits for them, and re-layouts  66.7 us (6%)
  other arithmetic  24 us (2%)
  between operations  16.9 us (1%)
    pallas_call x3, Pallas kernels, ring_scatter(): pl.pallas_call(scatter_body, in_specs=[vmem] * 2, out_specs=vmem, out_sha...  229 us
    pallas_call x3, Pallas kernels, ring_gather(): pl.pallas_call(gather_body, in_specs=[any_ref], out_specs=any_ref, out_sh...  197 us
    pallas_call x1, Pallas kernels, ring_scatter_last(): pl.pallas_call(functools.partial(scatter_last_body, t_size), in_specs=[vm...  175 us
    pallas_call x1, Pallas kernels, ring_gather(): pl.pallas_call(gather_small_body, in_specs=[any_ref] * 2, out_specs=[any_...  142 us
    pallas_call x1, Pallas kernels, mixer_backward(): pl.pallas_call(functools.partial(bwd_scatter_body if fused else bwd_body,...  88.3 us
    dot_general x6, matrix products, plain_dot(): return jnp.dot(left_mat, right_mat, preferred_element_type=F32)  68 us
    dot_general x6, matrix products, dot_rows(): lax.dot_general(left_mat, right_mat, (((1,), (1,)), ((), ())), preferred_...  67.4 us
    pallas_call x1, Pallas kernels, mixer_forward(): pl.pallas_call(functools.partial(fwd_gather_body if fused else fwd_body,...  52.9 us
  transfers between devices with their start and end apart: 8, of which 0 were waited for; matrix products, arithmetic and copies ran while one was open for 6% of the time, Pallas kernels for 66%

profile of v3, /device:TPU:14, one launch (start us, length us, event | category | flops | bytes accessed | tf_op | source)
XLA Modules:
  0.0 1131.1 jit_solution(14195114134790036978)
XLA Ops:
  7.3 1.4 fusion.47
  11.9 1.3 fusion.8
  15.9 1.3 pad_maximum_fusion.w_ref
  17.2 141.8 %ring_gather_0.1 = (bf16[2048,3072]{1,0:T(8,128)(2,1)}, bf16[8,32,128]{2,1,0:T(8,128)(2,1)}) custom-call(bf16[256,3072]{1,0:T(8,128)(2,1)} %pad_maximum_fusion.w_ref, bf16[32,128]{1,0:T(8,128)(2,1)} %pad_bitcast_fusion.small_ref), custom_call_target="tpu_custom_call" | custom-call | bytes 117964800 | tf_op jit(solution)/shard_map/ring_gather_0/pallas_call | solution.py:655
  161.9 1.1 reshape.1407
  163.3 1.1 reshape.1408
  165.0 19.2 %fusion.88.refs_0_.refs_1_.refs_2_.refs_3_.refs_5_.refs_6_.refs_7_ = f32[1024,3072]{1,0:T(8,128)} fusion(bf16[1024,2048]{1,0:T(8,128)(2,1)} %all-gather.5.cloned.1.call-done.left_ref, bf16[2048,3072]{1,0:T(8,128)(2,1)} %get-tuple-element.54), kind=kOutput, calls=%fused_computation.249 | convolution fusion | flops 12884901888 | bytes 29360128 | tf_op jit(solution)/shard_map/dot_general | solution.py:937
  184.2 1.2 fusion.20.refs_4_
  185.5 52.9 %mixer_forward.1 = (bf16[1024,1024]{1,0:T(8,128)(2,1)S(1)}, f32[1024,1024]{1,0:T(8,128)S(1)}, bf16[1024,1024]{1,0:T(8,128)(2,1)S(1)}, bf16[1024,512]{1,0:T(8,128...) custom-call(f32[1024,3072]{1,0:T(8,128)} %fusion.88.refs_0_.refs_1_.refs_2_.refs_3_.refs_5_.refs_6_.refs_7_, ...), custom_call_target="tpu_custom_call" | custom-call | flops 20000000000 | bytes 40000000 | tf_op jit(solution)/shard_map/mixer_forward/pallas_call | solution.py:383
  238.5 2.1 copy-done.8
  240.6 1.3 copy-done.9
  241.9 1.3 copy-done.10
  243.2 1.0 copy-done.11
  244.2 1.4 copy-done
  245.5 8.3 convolution_convert_fusion.1
  254.0 66.6 %ring_gather_2.1 = bf16[2048,1408]{1,0:T(8,128)(2,1)} custom-call(bf16[256,1408]{1,0:T(8,128)(2,1)} %w_ref), custom_call_target="tpu_custom_call" | custom-call | bytes 54067200 | tf_op jit(solution)/shard_map/ring_gather_2/pallas_call | solution.py:651
  320.7 1.7 multiply_reduce_fusion
  323.0 1.5 multiply_convert_fusion.3
  327.7 1.5 maximum_select_fusion.6
  331.0 1.2 fusion.16
  332.3 65.2 %ring_gather_3.1 = bf16[2048,1408]{1,0:T(8,128)(2,1)} custom-call(bf16[256,1408]{1,0:T(8,128)(2,1)} %w_ref.1), custom_call_target="tpu_custom_call" | custom-call | bytes 54067200 | tf_op jit(solution)/shard_map/ring_gather_3/pallas_call | solution.py:651
  397.5 65.5 %ring_gather_4.1 = bf16[2048,1408]{1,0:T(8,128)(2,1)} custom-call(bf16[256,1408]{1,0:T(8,128)(2,1)} %w_ref.2), custom_call_target="tpu_custom_call" | custom-call | bytes 54067200 | tf_op jit(solution)/shard_map/ring_gather_4/pallas_call | solution.py:651
  463.0 11.8 %fusion.90 = f32[1024,1408]{1,0:T(8,128)} fusion(bf16[1024,2048]{1,0:T(8,128)(2,1)} %all-gather.7.cloned.1.call-done.left_ref.refs_18_, bf16[2048,1408]{1,0:T(8,128)(2,1)} %ring_gather_3.1), kind=kOutput, calls=%fused_computation.251 | convolution fusion | flops 5905580032 | bytes 15728640 | tf_op jit(solution)/shard_map/dot_general | solution.py:937
  474.8 10.2 fusion.89
  485.0 15.5 %multiply_convert_fusion = (bf16[1024,1408]{1,0:T(8,128)(2,1)S(1)}, bf16[1024,1408]{1,0:T(8,128)(2,1)S(1)}, bf16[1024,1408]{1,0:T(8,128)(2,1)}) fusion(f32[1024,1408]{1,0:T(8,128)} %fusion.89, f32[1024,1408]{1,0:T(8,128)} %fusion.90, bf16[1024,2048]{1,0:T(8,128)(2,1)} %all-gather.9.cloned.1.call-done.left_ref, bf16[2048,1408]{1,0:T(8,128)(2,1)} %ring_gather_4.1), kind=kOutput, calls=%fused_computation.6 | convolution fusion | flops 5928648704 | bytes 30146560 | tf_op jit(solution)/shard_map/dot_general | solution.py:937
  500.6 10.8 fusion.91
  511.4 11.1 add_convert_fusion.1
  522.6 85.7 %ring_scatter_5.1 = f32[256,1408]{1,0:T(8,128)} custom-call(bf16[1024,2048]{1,0:T(8,128)(2,1)} %all-gather.9.cloned.1.call-done.left_ref, bf16[1024,1408]{1,0:T(8,128)(2,1)} %get-tuple-element.67.right_ref), custom_call_target="tpu_custom_call" | custom-call | bytes 432537600 | tf_op jit(solution)/shard_map/ring_scatter_5/pallas_call | solution.py:922
  608.4 2.3 fusion.10
  610.8 1.9 fusion.36
  612.7 83.3 %ring_scatter_6.1 = f32[256,1408]{1,0:T(8,128)} custom-call(bf16[1024,2048]{1,0:T(8,128)(2,1)} %all-gather.7.cloned.1.call-done.left_ref.refs_18_, bf16[1024,1408]{1,0:T(8,128)(2,1)} %copy-done.28), custom_call_target="tpu_custom_call" | custom-call | bytes 432537600 | tf_op jit(solution)/shard_map/ring_scatter_6/pallas_call | solution.py:922
  696.1 10.0 fusion.92.refs_13_
  706.1 10.9 convolution_convert_fusion
  717.0 88.3 %mixer_backward.1 = (bf16[1024,3072]{1,0:T(8,128)(2,1)}, bf16[1024,128]{1,0:T(8,128)(2,1)}, f32[8,512]{1,0:T(8,128)}, f32[8,512]{1,0:T(8,128)}, f32[8,1024]{1,0:...) custom-call(f32[1024,3072]{1,0:T(8,128)} %fusion.88.refs_0_.refs_1_.refs_2_.refs_3_.refs_5_.refs_6_.refs_7_, ...), custom_call_target="tpu_custom_call" | custom-call | flops 40000000000 | bytes 60000000 | tf_op jit(solution)/shard_map/mixer_backward/pallas_call | solution.py:434
  805.4 5.5 fusion.22
  810.9 20.7 %add_convert_fusion = bf16[1024,2048]{1,0:T(8,128)(2,1)} fusion(f32[1024,2048]{1,0:T(8,128)} %fusion.22, bf16[1024,3072]{1,0:T(8,128)(2,1)} %get-tuple-element.73.right_ref, bf16[2048,3072]{1,0:T(8,128)(2,1)} %get-tuple-element.54), kind=kOutput, calls=%fused_computation.1 | convolution fusion | flops 12889096192 | bytes 31457280 | tf_op jit(solution)/shard_map/dot_general | solution.py:941
  832.6 59.7 %ring_scatter_8.1 = f32[256,1024]{1,0:T(8,128)} custom-call(bf16[1024,2048]{1,0:T(8,128)(2,1)} %all-gather.11.cloned.1.call-done.left_ref, bf16[1024,1024]{1,0:T(8,128)(2,1)} %copy-done), custom_call_target="tpu_custom_call" | custom-call | bytes 314572800 | tf_op jit(solution)/shard_map/ring_scatter_8/pallas_call | solution.py:922
  892.3 1.0 copy.83
  893.3 1.6 reshape.1417
  895.8 1.2 reshape.1413
  897.9 1.2 reshape.1415
  899.8 3.0 fusion.93
  902.8 1.3 copy.79
  904.2 1.8 concatenate.476
  906.0 1.3 copy.80
  907.4 1.8 concatenate.477
  910.7 1.0 bitcast_dynamic-update-slice_fusion.1
  911.8 2.3 fusion.11
  914.9 174.8 %ring_scatter_9.1 = (f32[256,3072]{1,0:T(8,128)}, f32[16,128]{1,0:T(8,128)}, f32[8,128]{1,0:T(8,128)}, f32[40,128]{1,0:T(8,128)}) custom-call(bf16[1024,2048]{1,0:T(8,128)(2,1)} %all-gather.5.cloned.1.call-done.left_ref, bf16[1024,3072]{1,0:T(8,128)(2,1)} %get-tuple-element.73.right_ref, f32[8,16,128]{2,1,0:T(8,128)} %pad_maximum_fusion.7.few_ref, ...), custom_call_target="tpu_custom_call" | custom-call | bytes 943718400 | tf_op jit(solution)/shard_map/ring_scatter_9/pallas_call | solution.py:890
  1089.8 1.2 slice.905
  1091.0 1.2 slice_bitcast_fusion.2
  1092.3 1.3 fusion.67
  1093.6 1.3 slice_bitcast_fusion
  1094.9 2.2 fusion.38
  1097.1 3.1 fusion.37
  1100.2 3.4 fusion.13
  1103.6 1.4 fusion.40
  1111.6 1.3 fusion.59
  1112.9 1.9 slice_select_fusion.1
  1115.7 1.0 copy-done.17
  1119.0 1.0 copy.143
  1120.0 1.1 copy.144
  1121.1 1.1 copy.145
  1123.0 1.1 copy.146
  (349 shorter events, 30.1 us)
Async XLA Ops:
  7.2 157.8 %all-gather.5.cloned.1.call-start = ((), (), s32[]{:S(2)}) async-start(), calls=%async_computation.4 | async-start | bytes 5242880 | tf_op jit(solution)/shard_map/all_gather | solution.py:1052
  10.3 3.0 copy-start.65
  10.3 3.3 copy-start.66
  10.3 3.6 copy-start.58
  10.3 3.8 copy-start.59
  10.3 4.0 copy-start.60
  11.2 4.7 copy-start.33
  11.2 4.7 copy-start.34
  11.2 4.7 copy-start.37
  11.2 4.7 copy-start.38
  11.2 2.0 copy-start.46
  13.2 307.5 %reduce-scatter.5.cloned.1.call-start = ((), (), s32[]{:S(2)}) async-start(), calls=%async_computation.5 | async-start | bytes 5242880 | tf_op jit(solution)/shard_map/reduce_scatter | solution.py:1056
  159.0 5.7 copy-start.68
  159.0 5.7 copy-start.69
  163.3 20.9 %copy-start.41 = (bf16[2048,4]{0,1:T(4,128)(2,1)}, bf16[2048,4]{0,1:T(4,128)(2,1)S(1)}, u32[]{:S(2)}) copy-start(bf16[2048,4]{0,1:T(4,128)(2,1)S(1)} %copy.74) | copy-start | bytes 49156
  164.7 19.5 %copy-start.43 = (bf16[2048,4]{0,1:T(4,128)(2,1)}, bf16[2048,4]{0,1:T(4,128)(2,1)S(1)}, u32[]{:S(2)}) copy-start(bf16[2048,4]{0,1:T(4,128)(2,1)S(1)} %copy.75) | copy-start | bytes 49156
  164.9 20.6 %copy-start.4 = (f32[8,128]{1,0:T(8,128)}, f32[8,128]{1,0:T(8,128)S(1)}, u32[]{:S(2)}) copy-start(f32[8,128]{1,0:T(8,128)S(1)} %select_maximum_fusion.refs_8_.refs_11_) | copy-start | bytes 12292
  164.9 20.6 %copy-start.2 = (f32[8,512]{1,0:T(8,128)}, f32[8,512]{1,0:T(8,128)S(1)}, u32[]{:S(2)}) copy-start(f32[8,512]{1,0:T(8,128)S(1)} %pad_convert_fusion.1.refs_6_.refs_9_) | copy-start | bytes 49156
  164.9 20.6 %copy-start.3 = (f32[8,512]{1,0:T(8,128)}, f32[8,512]{1,0:T(8,128)S(1)}, u32[]{:S(2)}) copy-start(f32[8,512]{1,0:T(8,128)S(1)} %pad_convert_fusion.2.refs_5_.refs_8_) | copy-start | bytes 49156
  164.9 20.6 %copy-start.1 = (f32[8,1024]{1,0:T(8,128)}, f32[8,1024]{1,0:T(8,128)S(1)}, u32[]{:S(2)}) copy-start(f32[8,1024]{1,0:T(8,128)S(1)} %pad_convert_fusion.refs_7_.refs_10_) | copy-start | bytes 98308
  165.0 19.3 %copy-start.13 = (bf16[1024,2048]{1,0:T(8,128)(2,1)S(1)}, bf16[1024,2048]{1,0:T(8,128)(2,1)}, u32[]{:S(2)}) copy-start(bf16[1024,2048]{1,0:T(8,128)(2,1)} %all-gather.5.cloned.1.call-done.left_ref) | copy-start | bytes 12582916
  185.5 53.0 %copy-start.7 = (f32[1024,128]{1,0:T(8,128)}, f32[1024,128]{1,0:T(8,128)S(1)}, u32[]{:S(2)}) copy-start(f32[1024,128]{1,0:T(8,128)S(1)} %fusion.20.refs_4_) | copy-start | bytes 1572868
  238.5 2.1 copy-start.8
  253.9 209.1 %all-gather.7.cloned.1.call-start = ((), (), s32[]{:S(2)}) async-start(), calls=%async_computation.6 | async-start | bytes 5242880 | tf_op jit(solution)/shard_map/all_gather | solution.py:1052
  320.7 2.3 copy-start.12
  323.0 1.5 copy-start.32
  324.5 160.5 %all-gather.9.cloned.1.call-start = ((), (), s32[]{:S(2)}) async-start(), calls=%async_computation.7 | async-start | bytes 5242880 | tf_op jit(solution)/shard_map/all_gather | solution.py:1052
  332.2 276.1 %reduce-scatter.7.cloned.1.call-start = ((), (), s32[]{:S(2)}) async-start(), calls=%async_computation.8 | async-start | bytes 5242880 | tf_op jit(solution)/shard_map/reduce_scatter | solution.py:1056
  463.0 11.8 %copy-start.26 = (bf16[1024,2048]{1,0:T(8,128)(2,1)S(1)}, bf16[1024,2048]{1,0:T(8,128)(2,1)}, u32[]{:S(2)}) copy-start(bf16[1024,2048]{1,0:T(8,128)(2,1)} %all-gather.7.cloned.1.call-done.left_ref.refs_18_) | copy-start | bytes 12582916
  500.6 10.8 copy-start.28
  500.6 10.8 copy-start.70
  522.5 173.5 %all-gather.11.cloned.1.call-start = ((), (), s32[]{:S(2)}) async-start(), calls=%async_computation.9 | async-start | bytes 5242880 | tf_op jit(solution)/shard_map/all_gather | solution.py:1052
  608.3 2.4 copy-start.52
  608.4 2.4 copy-start.18
  608.4 2.4 copy-start.20
  608.4 2.4 copy-start.22
  612.7 299.0 %reduce-scatter.11.cloned.1.call-start = ((), (), s32[]{:S(2)}) async-start(), calls=%async_computation.11 | async-start | bytes 5242880 | tf_op jit(solution)/shard_map/reduce_scatter | solution.py:1056
  696.1 10.0 copy-start.27
  717.0 88.4 %copy-start.42 = (bf16[2048,4]{0,1:T(4,128)(2,1)S(1)}, bf16[2048,4]{0,1:T(4,128)(2,1)}, u32[]{:S(2)}) copy-start(bf16[2048,4]{0,1:T(4,128)(2,1)} %copy-done.41) | copy-start | bytes 49156
  717.0 88.4 %copy-start.44 = (bf16[2048,4]{0,1:T(4,128)(2,1)S(1)}, bf16[2048,4]{0,1:T(4,128)(2,1)}, u32[]{:S(2)}) copy-start(bf16[2048,4]{0,1:T(4,128)(2,1)} %copy-done.43) | copy-start | bytes 49156
  831.7 268.6 %reduce-scatter.9.cloned.1.call-start = ((), (), s32[]{:S(2)}) async-start(), calls=%async_computation.10 | async-start | bytes 5242880 | tf_op jit(solution)/shard_map/reduce_scatter | solution.py:1056
  832.5 59.7 %copy-start.54 = (f32[8,1024]{1,0:T(8,128)S(1)}, f32[8,1024]{1,0:T(8,128)}, u32[]{:S(2)}) copy-start(f32[8,1024]{1,0:T(8,128)} %get-tuple-element.80) | copy-start | bytes 98308
  832.5 62.4 %copy-start.62 = (f32[8,512]{1,0:T(8,128)S(1)}, f32[8,512]{1,0:T(8,128)}, u32[]{:S(2)}) copy-start(f32[8,512]{1,0:T(8,128)} %get-tuple-element.78) | copy-start | bytes 49156
  832.6 64.5 %copy-start.61 = (f32[8,512]{1,0:T(8,128)S(1)}, f32[8,512]{1,0:T(8,128)}, u32[]{:S(2)}) copy-start(f32[8,512]{1,0:T(8,128)} %get-tuple-element.79) | copy-start | bytes 49156
  892.3 7.5 copy-start.31
  902.8 8.9 copy-start.40
  902.8 8.9 copy-start.47
  906.0 8.2 copy-start.67
  914.9 176.1 %copy-start.50 = (f32[256]{0:T(256)S(1)}, f32[256]{0:T(256)}, u32[]{:S(2)}) copy-start(f32[256]{0:T(256)} %copy-done.49) | copy-start | bytes 3076
  1103.6 2.3 copy-start.14
  1103.6 3.1 copy-start.16
  1105.1 2.4 copy-start.57
  1105.1 4.0 copy-start.53
  1105.1 4.9 copy-start.64
  1105.1 5.7 copy-start.63
  1105.9 7.0 copy-start.15
  1115.4 1.7 copy-start.29
  1115.4 1.8 copy-start.35
  1115.5 1.9 copy-start.36
  1115.7 2.0 copy-start.45
  1118.2 1.8 copy-start.24
  1118.4 2.7 copy-start.48
  1119.0 2.1 copy-start.30
  1121.1 1.9 copy-start.23
  (15 other events, 14.9 us)
Sparse Core Ops, SparseCore 0:
  13.3 34.6 all-gather.4
  254.0 44.3 reduce-scatter.4
  324.6 32.7 all-gather.6
  359.5 34.4 all-gather.8
  522.7 43.4 reduce-scatter.6
  612.8 33.8 all-gather.10
  831.8 47.4 reduce-scatter.10
  881.9 45.3 reduce-scatter.8

commit v4 on v3

--- a/solution.py
+++ b/solution.py
@@ -151,7 +151,7 @@
     heads, dk, dv, q_ref, k_ref, v_ref, og_ref, ab_ref, qh_ref, kh_ref, vh_ref,
     tq_ref, tk_ref, tv_ref, par_ref, gain_ref, g_ref, o_ref, u_ref, t_ref, s_ref,
     draw_ref, dab_ref, dtq_ref, dtk_ref, dtv_ref, dpar_ref, dgain_ref,
-    qb, kb, vb, qn, kn, vn, dstate,
+    qb, kb, vb, qn, kn, vn, dstate, between=lambda part: None,
 ):
     rows = CH
     step = pl.program_id(0)
@@ -237,6 +237,7 @@
         right = jnp.concatenate([do_b[h], dr_b[h]], axis=0)
         dstate[h] = jnp.exp(end[h]) * ds1[h] + mm(left, right, TN)
 
+    between(1)
     lane = lax.broadcasted_iota(jnp.int32, (rows, LANES), 1)
     sub = lax.broadcasted_iota(jnp.int32, (LANES, rows), 0)
     dab_cols = jnp.zeros((rows, LANES), F32)
@@ -348,26 +349,30 @@
 
     @pl.when(step == steps - 1)
     def _():
-        gather.steps(steps, CHUNKS + 3)
+        gather.steps(steps, gather.STEPS)
         gather.finish()
 
 
-def bwd_scatter_body(heads, dk, dv, *refs):
+def bwd_scatter_body(length, heads, dk, dv, *refs):
     ins, pair, outs, own, rest = refs[:18], refs[18:20], refs[20:27], refs[27], refs[28:]
     step, steps = pl.program_id(0), pl.num_programs(0)
-    scatter = Scatter(*pair, own, *rest[7:])
+    each = 2 * CHUNKS // (length // CH)
+    scatter = Scatter(each, *pair, own, *rest[7:])
 
     @pl.when(step == 0)
     def _():
         greet_near(scatter.me, scatter.outer, scatter.side)
         scatter.begin()
 
-    scatter.step(step)
-    bwd_body(heads, dk, dv, *ins, *outs, *rest[:7])
+    def between(part):
+        scatter.steps((2 * step + part) * each, (2 * step + part + 1) * each)
+
+    between(0)
+    bwd_body(heads, dk, dv, *ins, *outs, *rest[:7], between)
 
     @pl.when(step == steps - 1)
     def _():
-        scatter.steps(steps, CHUNKS + 3)
+        scatter.steps(4 * CHUNKS, 4 * CHUNKS + 3 * each)
         scatter.finish()
 
 
@@ -401,7 +406,7 @@
         ]
         + gather_sems() * fused,
         compiler_params=pltpu.CompilerParams(
-            dimension_semantics=("arbitrary",), vmem_limit_bytes=40 << 20, collective_id=ident,
+            dimension_semantics=("arbitrary",), vmem_limit_bytes=60 << 20, collective_id=ident,
             has_side_effects=fused,
         ),
         cost_estimate=pl.CostEstimate(flops=20_000_000_000, bytes_accessed=40_000_000, transcendentals=6_000_000),
@@ -432,7 +437,7 @@
         own = [pl.BlockSpec(mine, lambda c: (0, 0))]
         extra = scatter_scratch(*mine)
     return pl.pallas_call(
-        functools.partial(bwd_scatter_body if fused else bwd_body, heads, dk, dv),
+        functools.partial(*([bwd_scatter_body, length] if fused else [bwd_body]), heads, dk, dv),
         grid=(steps,),
         in_specs=[sp[n] for n in names] + [hq, hk, hv] + [sp[n] for n in rest] + pair,
         out_specs=[sp[n] for n in ("raw", "ab", "tk", "tk", "tv", "par", "gain")] + own,
@@ -495,12 +500,16 @@
 
 
 CHUNKS = 8
+LAG = 2
+
+
+CROSS_FIRST = 1
 
 
 def gather_sems():
     return [
-        pltpu.SemaphoreType.DMA((3, CHUNKS)),
-        pltpu.SemaphoreType.DMA((3, CHUNKS)),
+        pltpu.SemaphoreType.DMA((6, CHUNKS)),
+        pltpu.SemaphoreType.DMA((6, CHUNKS)),
         pltpu.SemaphoreType.DMA((4, CHUNKS)),
         pltpu.SemaphoreType.DMA((8, CHUNKS)),
         pltpu.SemaphoreType.DMA,
@@ -508,6 +517,8 @@
 
 
 class Gather:
+    STEPS = CHUNKS + 4
+
     def __init__(self, w_ref, full_ref, right_s, left_s, swap_s, arrive, local):
         self.w, self.full, self.sems, self.arrive = w_ref, full_ref, (right_s, left_s, swap_s), arrive
         self.me = lax.axis_index("dp")
@@ -527,11 +538,10 @@
             self.source(slot, c), self.spot(to, c), sem.at[index, c], self.arrive.at[to, c], device_id=on_dp(peer)
         )
 
-    def to_right(self, h, c):
-        return self.copy((4 - h) % 4, 3 - h, c, self.sems[0], h, (self.me + 2) % 8)
-
-    def to_left(self, h, c):
-        return self.copy(h, h + 1, c, self.sems[1], h, (self.me + 6) % 8)
+    def along(self, way, far, h, c):
+        slot, to = ((4 - h) % 4, 3 - h) if way == 0 else (h, h + 1)
+        peer = (self.me + (2, 6)[way]) % 8
+        return self.copy(slot + 4 * far, to + 4 * far, c, self.sems[way], h + 3 * far, peer)
 
     def to_side(self, slot, c):
         return self.copy(slot, 4 + slot, c, self.sems[2], slot, self.me + 1 - 2 * self.side)
@@ -542,59 +552,64 @@
     def begin(self):
         self.keep.start()
 
+    def go_on(self, way, far, h, c):
+        if h < 3:
+            @pl.when((self.outer < 3) if way == 0 else (self.outer > 0))
+            def _():
+                self.along(way, far, h, c).start()
+
     def step(self, i):
-        outer = self.outer
-
         @pl.when(i < CHUNKS)
         def _():
             self.to_side(0, i).start()
-
-            @pl.when(outer < 3)
+            for way in range(2):
+                self.go_on(way, 0, 0, i)
+
+        far_at = i - 1
+
+        @pl.when((far_at >= 0) & (far_at < CROSS_FIRST))
+        def _():
+            self.landed(4, far_at)
+            for way in range(2):
+                self.go_on(way, 1, 0, far_at)
+
+        for far in range(2):
+            last = CROSS_FIRST if far else CHUNKS
+            for h in range(1, 4):
+                c = i - h - far
+                for way in range(2):
+                    behind = self.outer if way == 0 else 3 - self.outer
+                    slot = 4 - h if way == 0 else h
+
+                    @pl.when((c >= 0) & (c < last) & (behind >= h))
+                    def _():
+                        self.landed(slot + 4 * far, c)
+                        self.go_on(way, far, h, c)
+                        if not far:
+                            @pl.when(c >= CROSS_FIRST)
+                            def _():
+                                self.to_side(slot, c).start()
+
+    def finish(self):
+        def one(c, carry):
+            self.to_side(0, c).wait_send()
+
+            @pl.when(c >= CROSS_FIRST)
             def _():
-                self.to_right(0, i).start()
-
-            @pl.when(outer > 0)
-            def _():
-                self.to_left(0, i).start()
-
-        for h in range(1, 4):
-            c = i - h
-
-            @pl.when((c >= 0) & (c < CHUNKS) & (outer >= h))
-            def _():
-                self.landed(4 - h, c)
-                if h < 3:
-                    @pl.when(outer < 3)
-                    def _():
-                        self.to_right(h, c).start()
-
-                self.to_side(4 - h, c).start()
-
-            @pl.when((c >= 0) & (c < CHUNKS) & (outer + h < 4))
-            def _():
-                self.landed(h, c)
-                if h < 3:
-                    @pl.when(outer > 0)
-                    def _():
-                        self.to_left(h, c).start()
-
-                self.to_side(h, c).start()
-
-    def finish(self):
-        outer = self.outer
-
-        def one(c, carry):
-            for slot in range(4):
-                self.to_side(slot, c).wait_send()
-                self.landed(4 + slot, c)
-            for h in range(3):
-                @pl.when((outer >= h) & (outer < 3))
-                def _():
-                    self.to_right(h, c).wait_send()
-
-                @pl.when((outer + h < 4) & (outer > 0))
-                def _():
-                    self.to_left(h, c).wait_send()
+                self.landed(4, c)
+                for slot in range(1, 4):
+                    self.to_side(slot, c).wait_send()
+                    self.landed(4 + slot, c)
+
+            for way in range(2):
+                behind = self.outer if way == 0 else 3 - self.outer
+                for h in range(3):
+                    for far in range(2):
+                        @pl.when((behind >= h) & (c < (CROSS_FIRST if far else CHUNKS)))
+                        def _():
+                            @pl.when((self.outer < 3) if way == 0 else (self.outer > 0))
+                            def _():
+                                self.along(way, far, h, c).wait_send()
 
             return carry
 
@@ -627,7 +642,7 @@
 
     for j in range(1, 8):
         few(j).start()
-    gather.steps(0, CHUNKS + 3)
+    gather.steps(0, gather.STEPS)
     gather.finish()
     for j in range(1, 8):
         few(j).wait()
@@ -638,7 +653,7 @@
     gather = Gather(w_ref, full_ref, *sems)
     greet_near(gather.me, gather.outer, gather.side)
     gather.begin()
-    gather.steps(0, CHUNKS + 3)
+    gather.steps(0, gather.STEPS)
     gather.finish()
 
 
@@ -668,26 +683,27 @@
 
 
 class Scatter:
-    def __init__(self, left, right, out, mine, came, from_left, from_right, *sems):
-        self.left, self.right, self.out, self.mine, self.came = left, right, out, mine, came
+    def __init__(self, lag, left, right, out, mine, came, from_left, from_right, *sems):
+        self.lag = lag
+        self.left, self.right, self.mine, self.came = left, right, mine, came
+        self.outs = out if isinstance(out, tuple) else (out,)
         self.acc = (from_left, from_right)
         self.swap_s, self.swap_r, self.send_l, self.recv_l, self.send_r, self.recv_r = sems
         self.me = lax.axis_index("dp")
         self.outer, self.side = self.me // 2, self.me % 2
-        self.block, self.cols = out.shape
+        self.block, self.cols = self.outs[0].shape[0], right.shape[1]
         self.part = self.block // CHUNKS
 
-    def dots(self, half):
+    def dot(self, slot):
         tile = self.cols if self.cols <= 1536 else 1024
-
-        def one(k, carry):
-            at = pl.multiple_of((4 * half + k) * self.block, self.block)
-            rows = self.left[:, pl.ds(at, self.block)]
-            for j in range(0, self.cols, tile):
-                self.mine[pl.ds(at, self.block), j : j + tile] = mm(rows, self.right[:, j : j + tile], TN).astype(BF)
-            return carry
-
-        lax.fori_loop(0, 4, one, 0)
+        at = pl.multiple_of(slot * self.block, self.block)
+        rows = self.left[:, pl.ds(at, self.block)]
+        for j in range(0, self.cols, tile):
+            self.mine[pl.ds(at, self.block), j : j + tile] = mm(rows, self.right[:, j : j + tile], TN).astype(BF)
+
+    def item(self, t):
+        dest = (3 * (t // CHUNKS)) % 4
+        return dest, (dest - self.outer + 4) % 4, t % CHUNKS
 
     def rows(self, slot, c):
         return pl.ds(pl.multiple_of(slot * self.block + c * self.part, self.part), self.part)
@@ -699,7 +715,7 @@
         )
 
     def onward(self, way, dest, c):
-        ref, rows = self.acc[way], self.rows(dest, c)
+        ref, rows = self.acc[way], self.rows(dest - 1 + way, c)
         send, recv = ((self.send_l, self.recv_l), (self.send_r, self.recv_r))[way]
         peer = (self.me + (2, 6)[way]) % 8
         return pltpu.make_async_remote_copy(
@@ -707,7 +723,7 @@
         )
 
     def arrived(self, way, dest, c):
-        ref, rows = self.acc[way], self.rows(dest, c)
+        ref, rows = self.acc[way], self.rows(dest - 1 + way, c)
         recv = (self.recv_l, self.recv_r)[way]
         pltpu.make_async_copy(ref.at[rows], ref.at[rows], recv.at[dest, c]).wait()
 
@@ -715,57 +731,73 @@
         return self.mine[self.rows(slot, c), :].astype(F32) + self.came[self.rows(slot, c), :].astype(F32)
 
     def begin(self):
-        self.dots(1)
-
-        def one(c, carry):
-            for slot in range(4):
+        def send(j, carry):
+            _, slot, _ = self.item(j * CHUNKS)
+            self.dot(4 + slot)
+
+            def one(c, carry):
                 self.swap(slot, c).start()
-            return carry
-
-        lax.fori_loop(0, CHUNKS, one, 0)
-        self.dots(0)
-
-    def step(self, i):
+                return carry
+
+            return lax.fori_loop(0, CHUNKS, one, carry)
+
+        lax.fori_loop(0, 4, send, 0)
+
+    def step(self, t):
         outer = self.outer
-
-        @pl.when(i < CHUNKS)
+        items = 4 * CHUNKS
+
+        @pl.when(t < items)
         def _():
-            for slot in range(4):
-                self.swap(slot, i).wait_recv()
+            _, slot, c = self.item(t)
+
+            @pl.when(c == 0)
+            def _():
+                self.dot(slot)
+
+            self.swap(slot, c).wait_recv()
 
         for way in range(2):
             behind = outer if way == 0 else 3 - outer
-            c = i - behind
-            for dest in range(4):
-                ahead = (outer < dest) if way == 0 else (outer > dest)
-
-                @pl.when((c >= 0) & (c < CHUNKS) & ahead)
+            at = t - behind * self.lag
+            dest, slot, c = self.item((at + 2 * items) % items)
+            ahead = (outer < dest) if way == 0 else (outer > dest)
+
+            @pl.when((at >= 0) & (at < items) & ahead)
+            def _():
+                total = self.pair(slot, c)
+                ref, rows = self.acc[way], self.rows(dest - 1 + way, c)
+
+                @pl.when(behind == 0)
                 def _():
-                    total = self.pair((dest - outer + 4) % 4, c)
-                    ref, rows = self.acc[way], self.rows(dest, c)
-
-                    @pl.when(behind == 0)
-                    def _():
-                        ref[rows, :] = total.astype(BF)
-
-                    @pl.when(behind > 0)
-                    def _():
-                        self.arrived(way, dest, c)
-                        ref[rows, :] = (total + ref[rows, :].astype(F32)).astype(BF)
-
-                    self.onward(way, dest, c).start()
-
-        c = i - 3
-
-        @pl.when((c >= 0) & (c < CHUNKS))
+                    ref[rows, :] = total.astype(BF)
+
+                @pl.when(behind > 0)
+                def _():
+                    self.arrived(way, dest, c)
+                    ref[rows, :] = (total + ref[rows, :].astype(F32)).astype(BF)
+
+                self.onward(way, dest, c).start()
+
+        at = t - 3 * self.lag
+        dest, _, c = self.item((at + 2 * items) % items)
+
+        @pl.when((at >= 0) & (dest == outer))
         def _():
-            at = pl.ds(pl.multiple_of(c * self.part, self.part), self.part)
-            self.out[at, :] = self.pair(0, c)
+            rows = pl.ds(pl.multiple_of(c * self.part, self.part), self.part)
+            total = self.pair(0, c)
+            spans, start = [], 0
+            for out in self.outs:
+                spans.append((out, slice(start, start + out.shape[1])))
+                start += out.shape[1]
+            for out, cols in spans:
+                out[rows, :] = total[:, cols]
             for way in range(2):
                 @pl.when((outer if way == 0 else 3 - outer) > 0)
                 def _():
                     self.arrived(way, outer, c)
-                    self.out[at, :] += self.acc[way][self.rows(outer, c), :].astype(F32)
+                    for out, cols in spans:
+                        out[rows, :] += self.acc[way][self.rows(outer - 1 + way, c), cols].astype(F32)
 
     def steps(self, first, last):
         def one(i, carry):
@@ -797,24 +829,29 @@
     return [
         pltpu.VMEM((8 * block, cols), BF),
         pltpu.VMEM((4 * block, cols), BF),
-        pltpu.VMEM((4 * block, cols), BF),
-        pltpu.VMEM((4 * block, cols), BF),
+        pltpu.VMEM((3 * block, cols), BF),
+        pltpu.VMEM((3 * block, cols), BF),
     ] + scatter_sems()
 
 
 def scatter_body(left_ref, right_ref, out_ref, *scratch):
-    scatter = Scatter(left_ref, right_ref, out_ref, *scratch)
+    scatter = Scatter(LAG, left_ref, right_ref, out_ref, *scratch)
     greet_near(scatter.me, scatter.outer, scatter.side)
     scatter.begin()
-    scatter.steps(0, CHUNKS + 3)
+    scatter.steps(0, 4 * CHUNKS + 3 * LAG)
     scatter.finish()
 
 
-def scatter_last_body(t_size, left_ref, right_ref, few_ref, tap_ref, vec_ref, out_ref, few_out, tap_out, vec_out, *scratch):
-    few_in, tap_in, vec_t, vec_d, few_sem, tap_sem, t_sem, d_sem = scratch[-8:]
-    scatter = Scatter(left_ref, right_ref, out_ref, *scratch[:-8])
-    me, outer, side = scatter.me, scatter.outer, scatter.side
+def scatter_last_body(
+    t_size, left_ref, right_ref, ab_ref, few_ref, tap_ref, rest_ref, z_ref, mid_ref, gain_ref, fab_ref, full_ref,
+    out_q, out_k, out_v, out_g, few_out, tap_out, vec_out, grad_ref, *scratch,
+):
+    w_buf, sum_out, sum_in, few_in, tap_in, vec, vec_t, vec_d = scratch[:8]
+    w_sem, s_sem, few_sem, tap_sem, t_sem, d_sem = scratch[8:14]
+    scatter = Scatter(LAG, left_ref, right_ref, (out_q, out_k, out_v, out_g), *scratch[14:])
+    me, outer, side, block = scatter.me, scatter.outer, scatter.side, scatter.block
     mine = lax.axis_index("tensor")
+    tokens = z_ref.shape[0]
     barrier = pltpu.get_barrier_semaphore()
     for j in range(1, t_size):
         pl.semaphore_signal(barrier, inc=1, device_id={"tensor": (mine + j) % t_size})
@@ -837,7 +874,7 @@
 
     def across(j):
         return pltpu.make_async_remote_copy(
-            vec_ref, vec_t.at[mine], t_sem.at[0, j], t_sem.at[1, j], device_id={"tensor": (mine + j) % t_size}
+            vec, vec_t.at[mine], t_sem.at[0, j], t_sem.at[1, j], device_id={"tensor": (mine + j) % t_size}
         )
 
     def along(j):
@@ -845,22 +882,96 @@
             vec_d.at[me], vec_d.at[me], d_sem.at[0, j], d_sem.at[1, j], device_id=on_dp((me + j) % 8)
         )
 
-    for j in range(1, t_size):
-        across(j).start()
+    def load(n):
+        return pltpu.make_async_copy(full_ref.at[pl.ds(n * block, block)], w_buf.at[n % 2], w_sem.at[n % 2])
+
+    def share(j, n):
+        return pltpu.make_async_remote_copy(
+            sum_out.at[j, n], sum_in.at[j - 1, n], s_sem.at[0, j, n], s_sem.at[1, j, n],
+            device_id={"tensor": (mine + j) % t_size},
+        )
+
+    load(0).start()
+    scatter.begin()
     for j in range(1, 8):
         few(j).start()
         tap(j).start()
-    scatter.begin()
-    vec_t[mine] = vec_ref[...]
+
+    def tile(n, carry):
+        scatter.step(n)
+
+        @pl.when(n < 7)
+        def _():
+            load(n + 1).start()
+
+        load(n).wait()
+        w = w_buf[n % 2]
+        w_few = fab_ref[pl.ds(pl.multiple_of(n * block, block), block), :]
+        for j in range(t_size):
+            rows = pl.ds(pl.multiple_of(((mine + j) % t_size) * tokens, tokens), tokens)
+            sum_out[j, n] = (mm(right_ref[rows, :], w, NT) + mm(ab_ref[rows, :], w_few, NT)).astype(BF)
+            if j:
+                share(j, n).start()
+        return carry
+
+    lax.fori_loop(0, 8, tile, 0)
+    scatter.steps(8, 3 * CHUNKS)
+
+    def land(n, carry):
+        for j in range(1, t_size):
+            share(j, n).wait_recv()
+        return carry
+
+    lax.fori_loop(0, 8, land, 0)
+    size = 32
+
+    def norm(i, carry):
+        at = pl.ds(pl.multiple_of(i * size, size), size)
+        squares, inner = 0.0, 0.0
+        for n in range(8):
+            cols = slice(n * block, (n + 1) * block)
+            z = z_ref[at, cols]
+            m = sum_out[0, n, at, :].astype(F32)
+            for j in range(1, t_size):
+                m = m + sum_in[j - 1, n, at, :].astype(F32)
+            squares = squares + jnp.sum(z * z, axis=-1, keepdims=True)
+            inner = inner + jnp.sum(m * gain_ref[:, cols] * z, axis=-1, keepdims=True)
+        width = 8 * block
+        r = lax.rsqrt(squares / width + 1e-05)
+        pull = r * r * r * (inner / width)
+        found = []
+        for n in range(8):
+            cols = slice(n * block, (n + 1) * block)
+            z = z_ref[at, cols]
+            m = sum_out[0, n, at, :].astype(F32)
+            for j in range(1, t_size):
+                m = m + sum_in[j - 1, n, at, :].astype(F32)
+            home = 2 * ((outer + n) % 4) + (side + n // 4) % 2
+            to = pl.ds(pl.multiple_of(home * block, block), block)
+            grad_ref[at, to] = mid_ref[at, cols] + r * (m * gain_ref[:, cols]) - z * pull
+            found.append(carry[n] + jnp.sum(m * (z * r), axis=0, keepdims=True))
+        return tuple(found)
+
+    parts = lax.fori_loop(0, tokens // size, norm, tuple(jnp.zeros((1, block), F32) for _ in range(8)))
+    per = block // LANES
+    for n in range(8):
+        home = 2 * ((outer + n) % 4) + (side + n // 4) % 2
+        for k in range(per):
+            vec[pl.ds(home * per + k, 1), :] = parts[n][:, k * LANES : (k + 1) * LANES]
+    vec[8 * per :, :] = rest_ref[...]
     for j in range(1, t_size):
-        pltpu.make_async_copy(vec_ref, vec_t.at[(mine + t_size - j) % t_size], t_sem.at[1, j]).wait()
+        across(j).start()
+    vec_t[mine] = vec[...]
+    scatter.steps(3 * CHUNKS, 3 * CHUNKS + 4)
+    for j in range(1, t_size):
+        pltpu.make_async_copy(vec, vec_t.at[(mine + t_size - j) % t_size], t_sem.at[1, j]).wait()
     total = vec_t[0]
     for j in range(1, t_size):
         total = total + vec_t[j]
     vec_d[me] = total
     for j in range(1, 8):
         along(j).start()
-    scatter.steps(0, CHUNKS + 3)
+    scatter.steps(3 * CHUNKS + 4, 4 * CHUNKS + 3 * LAG)
     few_total, tap_total = few_ref[0], tap_ref[me]
     for j in range(1, 8):
         few(j).wait_recv()
@@ -881,39 +992,56 @@
         few(j).wait_send()
         tap(j).wait_send()
         along(j).wait_send()
+
+    def sent(n, carry):
+        for j in range(1, t_size):
+            share(j, n).wait_send()
+        return carry
+
+    lax.fori_loop(0, 8, sent, 0)
     scatter.finish()
 
 
-def ring_scatter_last(left, right, few, taps, vec, t_size, ident):
-    block, cols = left.shape[1] // 8, right.shape[1]
+def ring_scatter_last(left, right, ab, few, taps, rest, z, mid, gain, full_ab, full, widths, t_size, ident):
+    width, cols, tokens = left.shape[1], right.shape[1], z.shape[0]
+    block = width // 8
+    vec = (width // LANES + rest.shape[0], LANES)
     vmem = pl.BlockSpec(memory_space=pltpu.VMEM)
+    pair = pltpu.SemaphoreType.DMA((2, 8))
     return pl.pallas_call(
         functools.partial(scatter_last_body, t_size),
-        in_specs=[vmem] * 5,
-        out_specs=[vmem] * 4,
-        out_shape=[
-            jax.ShapeDtypeStruct((block, cols), F32),
+        in_specs=[vmem] * 10 + [pl.BlockSpec(memory_space=pl.ANY)],
+        out_specs=[vmem] * 8,
+        out_shape=[jax.ShapeDtypeStruct((block, w), F32) for w in widths]
+        + [
             jax.ShapeDtypeStruct(few.shape[1:], F32),
             jax.ShapeDtypeStruct(taps.shape[1:], F32),
-            jax.ShapeDtypeStruct(vec.shape, F32),
+            jax.ShapeDtypeStruct(vec, F32),
+            jax.ShapeDtypeStruct(z.shape, F32),
         ],
-        scratch_shapes=scatter_scratch(block, cols)
-        + [
+        scratch_shapes=[
+            pltpu.VMEM((2, block, cols), BF),
+            pltpu.VMEM((t_size, 8, tokens, block), BF),
+            pltpu.VMEM((t_size - 1, 8, tokens, block), BF),
             pltpu.VMEM(few.shape, F32),
             pltpu.VMEM(taps.shape, F32),
-            pltpu.VMEM((t_size,) + vec.shape, F32),
-            pltpu.VMEM((8,) + vec.shape, F32),
-            pltpu.SemaphoreType.DMA((2, 8)),
-            pltpu.SemaphoreType.DMA((2, 8)),
+            pltpu.VMEM(vec, F32),
+            pltpu.VMEM((t_size,) + vec, F32),
+            pltpu.VMEM((8,) + vec, F32),
+            pltpu.SemaphoreType.DMA((2,)),
+            pltpu.SemaphoreType.DMA((2, t_size, 8)),
+            pair,
+            pair,
             pltpu.SemaphoreType.DMA((2, t_size)),
-            pltpu.SemaphoreType.DMA((2, 8)),
-        ],
+            pair,
+        ]
+        + scatter_scratch(block, cols),
         compiler_params=pltpu.CompilerParams(
-            collective_id=ident, has_side_effects=True, vmem_limit_bytes=60 << 20
+            collective_id=ident, has_side_effects=True, vmem_limit_bytes=63 << 20
         ),
         cost_estimate=pl.CostEstimate(flops=0, bytes_accessed=1200 * block * cols, transcendentals=0),
         name=f"ring_scatter_{ident}",
-    )(left, right, few, taps, vec)
+    )(left, right, ab, few, taps, rest, z, mid, gain, full_ab, full)
 
 
 def ring_scatter(left, right, ident):
@@ -933,6 +1061,115 @@
     )(left, right)
 
 
+FFN_ROWS = 256
+
+
+def col_tiles(n, want):
+    return [(at, min(want, n - at)) for at in range(0, n, want)]
+
+
+def ffn_forward_body(x_ref, gate_ref, up_ref, w_ref, act_ref, slope_ref, hid_ref, full_ref, *sems):
+    step, steps = pl.program_id(0), pl.num_programs(0)
+    gather = Gather(w_ref, full_ref, *sems)
+
+    @pl.when(step == 0)
+    def _():
+        greet_near(gather.me, gather.outer, gather.side)
+        gather.begin()
+
+    x = x_ref[...]
+    for part, (at, wide) in enumerate(col_tiles(gate_ref.shape[1], 512)):
+        gather.step(3 * step + part)
+        gate = mm(x, gate_ref[:, at : at + wide])
+        up = mm(x, up_ref[:, at : at + wide])
+        sg = sigmoid(gate)
+        act = gate * sg
+        act_ref[:, at : at + wide] = act.astype(BF)
+        slope_ref[:, at : at + wide] = (up * (sg * (1.0 + gate * (1.0 - sg)))).astype(BF)
+        hid_ref[:, at : at + wide] = (act * up).astype(BF)
+
+    @pl.when(step == steps - 1)
+    def _():
+        gather.finish()
+
+
+def ffn_forward(x, full_gate, full_up, w, ident):
+    length, ff = x.shape[0], full_gate.shape[1]
+    any_ref = pl.BlockSpec(memory_space=pl.ANY)
+    once = pl.BlockSpec(full_gate.shape, lambda c: (0, 0), pipeline_mode=pl.Buffered(1))
+    tile = pl.BlockSpec((FFN_ROWS, ff), lambda c: (c, 0))
+    return pl.pallas_call(
+        ffn_forward_body,
+        grid=(length // FFN_ROWS,),
+        in_specs=[pl.BlockSpec((FFN_ROWS, x.shape[1]), lambda c: (c, 0)), once, once, any_ref],
+        out_specs=[tile] * 3 + [any_ref],
+        out_shape=[jax.ShapeDtypeStruct((length, ff), BF)] * 3
+        + [jax.ShapeDtypeStruct((8 * w.shape[0], w.shape[1]), w.dtype)],
+        scratch_shapes=gather_sems(),
+        compiler_params=pltpu.CompilerParams(
+            dimension_semantics=("arbitrary",), vmem_limit_bytes=60 << 20, collective_id=ident, has_side_effects=True
+        ),
+        cost_estimate=pl.CostEstimate(flops=70_000_000_000, bytes_accessed=30_000_000, transcendentals=1_500_000),
+        name="ffn_forward",
+    )(x, full_gate, full_up, w)
+
+
+def ffn_backward_body(
+    left_ref, hid_ref, act_ref, slope_ref, down_ref, gate_ref, up_ref,
+    glow_ref, ulow_ref, back_ref, ffn_ref, out_ref, *scratch,
+):
+    step, steps = pl.program_id(0), pl.num_programs(0)
+    scatter = Scatter(4, left_ref, hid_ref, out_ref, *scratch)
+
+    @pl.when(step == 0)
+    def _():
+        greet_near(scatter.me, scatter.outer, scatter.side)
+        scatter.begin()
+
+    rows = pl.ds(pl.multiple_of(step * FFN_ROWS, FFN_ROWS), FFN_ROWS)
+    x = left_ref[rows, :]
+    for at, wide in col_tiles(down_ref.shape[1], 512):
+        cols = slice(at, at + wide)
+        grad = mm(x, down_ref[:, cols])
+        glow_ref[:, cols] = (grad * slope_ref[:, cols].astype(F32)).astype(BF)
+        ulow_ref[:, cols] = (grad * act_ref[:, cols].astype(F32)).astype(BF)
+    hid = hid_ref[rows, :]
+    glow, ulow = glow_ref[...], ulow_ref[...]
+    for part, (at, wide) in enumerate(col_tiles(down_ref.shape[0], 512)):
+        scatter.steps(8 * step + 2 * part, 8 * step + 2 * part + 2)
+        cols = slice(at, at + wide)
+        back_ref[:, cols] = (mm(glow, gate_ref[cols, :], NT) + mm(ulow, up_ref[cols, :], NT)).astype(BF)
+        ffn_ref[:, cols] = mm(hid, down_ref[cols, :], NT).astype(BF)
+
+    @pl.when(step == steps - 1)
+    def _():
+        scatter.steps(4 * CHUNKS, 4 * CHUNKS + 12)
+        scatter.finish()
+
+
+def ffn_backward(left, hidden, act, slope, full_down, full_gate, full_up, ident):
+    (length, width), ff = left.shape, hidden.shape[1]
+    once = lambda x: pl.BlockSpec(x.shape, lambda c: (0, 0), pipeline_mode=pl.Buffered(1))
+    tile = pl.BlockSpec((FFN_ROWS, ff), lambda c: (c, 0))
+    wide = pl.BlockSpec((FFN_ROWS, width), lambda c: (c, 0))
+    mine = (width // 8, ff)
+    return pl.pallas_call(
+        ffn_backward_body,
+        grid=(length // FFN_ROWS,),
+        in_specs=[once(left), once(hidden), tile, tile, once(full_down), once(full_gate), once(full_up)],
+        out_specs=[tile, tile, wide, wide, pl.BlockSpec(mine, lambda c: (0, 0))],
+        out_shape=[jax.ShapeDtypeStruct((length, ff), BF)] * 2
+        + [jax.ShapeDtypeStruct((length, width), BF)] * 2
+        + [jax.ShapeDtypeStruct(mine, F32)],
+        scratch_shapes=scatter_scratch(*mine),
+        compiler_params=pltpu.CompilerParams(
+            dimension_semantics=("arbitrary",), vmem_limit_bytes=62 << 20, collective_id=ident, has_side_effects=True
+        ),
+        cost_estimate=pl.CostEstimate(flops=90_000_000_000, bytes_accessed=50_000_000, transcendentals=0),
+        name="ffn_backward",
+    )(left, hidden, act, slope, full_down, full_gate, full_up)
+
+
 def plain_dot(left_mat, right_mat):
     return jnp.dot(left_mat, right_mat, preferred_element_type=F32)
 
@@ -947,10 +1184,6 @@
 
 def rms_apply(values, gain_vec):
     return values * lax.rsqrt(jnp.mean(values * values, axis=-1, keepdims=True) + 1e-05) * gain_vec
-
-
-def swiglu(gate_pre, up_pre):
-    return jax.nn.silu(gate_pre) * up_pre
 
 
 class RingRows:
@@ -1006,14 +1239,20 @@
     def scatter(self, left, right, ident):
         return ring_scatter(left, right, ident)
 
+    def ffn_forward(self, x, gate, up, w, ident):
+        return ffn_forward(x, gate, up, w, ident)
+
+    def ffn_backward(self, left, hidden, act, slope, down, gate, up, ident):
+        return ffn_backward(left, hidden, act, slope, down, gate, up, ident)
+
     def forward(self, core_in, w, ident):
         return mixer_forward(*core_in, w, ident)
 
     def backward(self, core_in, saved, left, right, ident):
         return mixer_backward(*core_in, *saved, left, right, ident)
 
-    def scatter_last(self, left, right, few, taps, vec, tensor_size, ident):
-        return ring_scatter_last(left, right, few, taps, vec, tensor_size, ident)
+    def scatter_last(self, *args):
+        return ring_scatter_last(*args)
 
 
 class PlainRows:
@@ -1033,15 +1272,35 @@
     def gather_first(self, w, small):
         return lax.all_gather(w, "dp", axis=0, tiled=True), lax.all_gather(small, "dp", axis=0)
 
+    def ffn_forward(self, x, gate, up, w, ident):
+        gate_pre, up_pre = plain_dot(x, gate), plain_dot(x, up)
+        sg = jax.nn.sigmoid(gate_pre)
+        act = gate_pre * sg
+        slope = up_pre * (sg * (1.0 + gate_pre * (1.0 - sg)))
+        return act.astype(BF), slope.astype(BF), (act * up_pre).astype(BF), self.gather(w, ident)
+
+    def ffn_backward(self, left, hidden, act, slope, down, gate, up, ident):
+        grad = plain_dot(left, down)
+        gate_low, up_low = (grad * slope.astype(F32)).astype(BF), (grad * act.astype(F32)).astype(BF)
+        back = (dot_rows(gate_low, gate) + dot_rows(up_low, up)).astype(BF)
+        return gate_low, up_low, back, dot_rows(hidden, down).astype(BF), self.scatter(left, hidden, ident)
+
     def forward(self, core_in, w, ident):
         return [*mixer_forward(*core_in), self.gather(w, ident)]
 
     def backward(self, core_in, saved, left, right, ident):
         return [*mixer_backward(*core_in, *saved), self.scatter(left, right, ident)]
 
-    def scatter_last(self, left, right, few, taps, vec, tensor_size, ident):
+    def scatter_last(self, left, right, ab, few, taps, rest, z, mid, gain, full_ab, full, widths, t_size, ident):
+        summed = (dot_rows(right, full) + dot_rows(ab, full_ab)).astype(BF)
+        grad, grad_gain = jax.vjp(rms_apply, z, gain[0])[1](tensor_scatter(summed).astype(F32))
         few, taps = (lax.psum_scatter(x, "dp", scatter_dimension=0, tiled=True)[0] for x in (few, taps))
-        return self.scatter(left, right, ident), few, taps, lax.psum(vec, ("dp", "tensor"))
+        vec = lax.psum(jnp.concatenate([grad_gain.reshape(-1, LANES), rest]), ("dp", "tensor"))
+        out, found, at = self.scatter(left, right, ident), [], 0
+        for width in widths:
+            found.append(out[:, at : at + width])
+            at += width
+        return *found, few, taps, vec, mid + grad
 
 
 def tie(value, *others):
@@ -1101,7 +1360,7 @@
     local_rows = rows.reorder(inputs[0], 1).astype(F32)
     gain_one = rows.reorder(norm1_gain[None], 1)[0]
     gain_two = rows.reorder(norm2_gain[None], 1)[0]
-    normed_one, norm_one_back = jax.vjp(rms_apply, local_rows, gain_one)
+    normed_one = rms_apply(local_rows, gain_one)
     rows_one = tensor_gather(normed_one.astype(BF))
     grad_after = valid_rows * rows.reorder(cotangent[0], 1).astype(F32)
     incoming_ffn = tensor_gather(grad_after.astype(BF))
@@ -1116,38 +1375,24 @@
     normed_two = normed_two.astype(BF)
     full_up = rows.gather(tie(w_up, normed_two), 3)
     rows_two = tie(tensor_gather(normed_two), full_up)
-    gate_pre = plain_dot(rows_two, full_gate)
-    up_pre = plain_dot(rows_two, full_up)
-    hidden, swiglu_back = jax.vjp(swiglu, gate_pre, up_pre)
-    hidden_bf = hidden.astype(BF)
-    full_down = rows.gather(tie(w_down, full_up), 4)
-
-    grad_hidden = plain_dot(incoming_ffn, full_down)
-    grad_gate_pre, grad_up_pre = swiglu_back(grad_hidden)
-    gate_low = grad_gate_pre.astype(BF)
-    up_low = grad_up_pre.astype(BF)
-    back_two = (dot_rows(gate_low, full_gate) + dot_rows(up_low, full_up)).astype(BF)
-    out_down = rows.scatter(tie(incoming_ffn, back_two), hidden_bf, 5)
-    grad_normed_two = tie(tensor_scatter(back_two), out_down).astype(F32)
+    act, slope, hidden, full_down = rows.ffn_forward(rows_two, full_gate, full_up, w_down, 4)
+
+    gate_low, up_low, back_two, ffn_out, out_down = rows.ffn_backward(
+        incoming_ffn, hidden, act, slope, full_down, full_gate, full_up, 5
+    )
+    out_gate = rows.scatter(tie(rows_two, back_two), gate_low, 6)
+    grad_normed_two = tie(tensor_scatter(back_two), out_gate).astype(F32)
     grad_mid, grad_norm2 = norm_two_back(grad_normed_two)
     grad_mid = grad_mid + grad_after
     grad_mix = grad_mid.astype(BF)
-    out_gate = rows.scatter(tie(rows_two, grad_mix), gate_low, 6)
-    incoming_mix = tie(tensor_gather(grad_mix), out_gate)
-
-    ffn_out = dot_rows(tie(hidden_bf, incoming_mix), full_down).astype(BF)
-    ffn_part = tensor_scatter(ffn_out).astype(F32)
-    grad_head = tie(plain_dot(incoming_mix, full_out), ffn_out)
-    raw_low, ab_low, dtq, dtk, dtv, dpar, dgain, out_up = rows.backward(
-        core_in, (grad_head, delta_out, new_values, inverses, states), rows_two, up_low, 7
+    out_up = rows.scatter(tie(rows_two, grad_mix), up_low, 7)
+    incoming_mix = tie(tensor_gather(grad_mix), out_up)
+
+    ffn_part = tensor_scatter(tie(ffn_out, incoming_mix)).astype(F32)
+    outputs = rows.restore(((after_mix + ffn_part) * valid_rows).astype(BF), 1)[None]
+    raw_low, ab_low, dtq, dtk, dtv, dpar, dgain, out_out = rows.backward(
+        core_in, (plain_dot(incoming_mix, full_out), delta_out, new_values, inverses, states), incoming_mix, head_bf, 8
     )
-    outputs = rows.restore(((after_mix + ffn_part) * valid_rows).astype(BF), 1)[None]
-    summed = (dot_rows(raw_low, full_raw) + dot_rows(ab_low, full_ab)).astype(BF)
-    grad_normed_one = tensor_scatter(summed)
-    out_out = rows.scatter(tie(incoming_mix, summed), head_bf, 8)
-    grad_first, grad_norm1 = norm_one_back(tie(grad_normed_one, out_out).astype(F32))
-    grad_inputs = rows.restore(grad_mid + grad_first, 1)[None]
-
     def in_lanes(x, lead):
         return jnp.pad(x, ((0, 0), (0, -x.shape[1] % (8 * LANES)))).reshape(lead + (-1, LANES))
 
@@ -1162,14 +1407,13 @@
         lax.dynamic_update_slice_in_dim(jnp.zeros_like(a_log), dpar[i, heads : 2 * heads], head_start, 0)
         for i in range(2)
     )
-    vec = [rows.restore(grad_norm1[None], 1)[0], rows.restore(grad_norm2[None], 1)[0], dgain[0], alog_full, dtb_full]
-    few, taps, vec_in = (jnp.concatenate(x, axis=-1) for x in (few, taps, vec))
-    out_raw, few_sum, tap_sum, vec_sum = rows.scatter_last(
-        tie(rows_one, out_out), raw_low, in_lanes(few, (dp_size,)), in_lanes(taps, (dp_size,)),
-        in_lanes(vec_in[None], ()), tensor_size, 9,
+    rest = [rows.restore(grad_norm2[None], 1)[0], dgain[0], alog_full, dtb_full]
+    few, taps, rest_in = (jnp.concatenate(x, axis=-1) for x in (few, taps, rest))
+    out_query, out_key, out_value, out_outgate, few_sum, tap_sum, vec_sum, grad_inputs = rows.scatter_last(
+        tie(rows_one, out_out), raw_low, ab_low, in_lanes(few, (dp_size,)), in_lanes(taps, (dp_size,)),
+        in_lanes(rest_in[None], ()), local_rows, grad_mid, gain_one[None], full_ab, full_raw,
+        (wide_k, wide_k, wide_v, wide_v), tensor_size, 9,
     )
-    wide = 2 * wide_k
-    out_qk, out_value, out_outgate = out_raw[:, :wide], out_raw[:, wide : wide + wide_v], out_raw[:, wide + wide_v :]
 
     def pieces_of(total, like):
         flat, found, at = total.reshape(-1), [], 0
@@ -1180,9 +1424,9 @@
 
     out_beta, out_alpha = pieces_of(few_sum, (w_beta, w_alpha))
     out_cq, out_ck, out_cv = pieces_of(tap_sum, (conv_query, conv_key, conv_value))
-    norm1_sum, norm2_sum, hgain_sum, alog_sum, dtb_sum = pieces_of(vec_sum, vec)
+    norm1_sum, norm2_sum, hgain_sum, alog_sum, dtb_sum = pieces_of(vec_sum, [norm1_gain] + rest)
     return (
-        outputs, grad_inputs, norm1_sum, out_qk[:, :wide_k], out_qk[:, wide_k:], out_value, out_outgate,
+        outputs, grad_inputs[None], norm1_sum, out_query, out_key, out_value, out_outgate,
         out_beta, out_alpha, out_cq, out_ck, out_cv, alog_sum, dtb_sum, hgain_sum, out_out, norm2_sum,
         out_gate, out_up, out_down,
     )

time: 1150 us -> 1000 us (0.87)
  matrix products: 138 us -> 44.9 us
  Pallas kernels: 884 us -> 857 us
  local copies, waits for them, and re-layouts: 66.7 us -> 44.1 us
    pallas_call x1 -> x3, Pallas kernels: 88.3 us -> 242 us  [the longest x1 88.7 us: mixer_backward(): pl.pallas_call(functools.partial(*([bwd_scatter_body, length] if fused el...]
    pallas_call x3 -> x2, Pallas kernels: 229 us -> 135 us  [ring_scatter(): pl.pallas_call(scatter_body, in_specs=[vmem] * 2, out_specs=vmem, out_sha...]
    pallas_call x3 -> x2, Pallas kernels: 197 us -> 124 us  [ring_gather(): pl.pallas_call(gather_body, in_specs=[any_ref], out_specs=any_ref, out_sh...]
    dot_general x6 -> x1, matrix products: 67.4 us -> 9.3 us  [dot_rows(): lax.dot_general(left_mat, right_mat, (((1,), (1,)), ((), ())), preferred_...]
    dot_general x6 -> x3, matrix products: 68 us -> 32.7 us  [plain_dot(): return jnp.dot(left_mat, right_mat, preferred_element_type=F32)]
    pallas_call x1, Pallas kernels: 142 us -> 130 us  [ring_gather(): pl.pallas_call(gather_small_body, in_specs=[any_ref] * 2, out_specs=[any_...]
    unnamed x193 -> x136, local copies, waits for them, and re-layouts: 24.7 us -> 21 us
  transfers between devices with their start and end apart: 8 -> 7, of which waited for: 0 -> 0; matrix products, arithmetic and copies ran while one was open for 6% -> 5% of each run, Pallas kernels for 66% -> 72%
where the time goes in v4:
time: 1000 us; the launch traced here: 986 us
  Pallas kernels  857 us (86%)
  matrix products  44.9 us (4%)
  local copies, waits for them, and re-layouts  44.1 us (4%)
  other arithmetic  22.1 us (2%)
  between operations  16.6 us (2%)
    pallas_call x1, Pallas kernels, ring_scatter_last(): pl.pallas_call(functools.partial(scatter_last_body, t_size), in_specs=[vm...  167 us
    pallas_call x2, Pallas kernels, ring_scatter(): pl.pallas_call(scatter_body, in_specs=[vmem] * 2, out_specs=vmem, out_sha...  135 us
    pallas_call x1, Pallas kernels, ring_gather(): pl.pallas_call(gather_small_body, in_specs=[any_ref] * 2, out_specs=[any_...  130 us
    pallas_call x2, Pallas kernels, ring_gather(): pl.pallas_call(gather_body, in_specs=[any_ref], out_specs=any_ref, out_sh...  124 us
    pallas_call x1, Pallas kernels, mixer_backward(): pl.pallas_call(functools.partial(*([bwd_scatter_body, length] if fused el...  88.7 us
    pallas_call x1, Pallas kernels, ffn_backward(): pl.pallas_call(ffn_backward_body, grid=(length // FFN_ROWS,), in_specs=[o...  85.4 us
    pallas_call x1, Pallas kernels, ffn_forward(): pl.pallas_call(ffn_forward_body, grid=(length // FFN_ROWS,), in_specs=[pl...  67.6 us
    pallas_call x1, Pallas kernels, mixer_forward(): pl.pallas_call(functools.partial(fwd_gather_body if fused else fwd_body,...  59.7 us
  transfers between devices with their start and end apart: 7, of which 0 were waited for; matrix products, arithmetic and copies ran while one was open for 5% of the time, Pallas kernels for 72%

profile of v4, /device:TPU:14, one launch (start us, length us, event | category | flops | bytes accessed | tf_op | source)
XLA Modules:
  0.0 985.7 jit_solution(14000910983005920551)
XLA Ops:
  7.3 1.4 fusion.18
  11.4 1.3 multiply_convert_fusion.2
  15.4 1.3 pad_maximum_fusion.w_ref
  16.6 129.6 %ring_gather_0.1 = (bf16[2048,3072]{1,0:T(8,128)(2,1)}, bf16[8,32,128]{2,1,0:T(8,128)(2,1)}) custom-call(bf16[256,3072]{1,0:T(8,128)(2,1)} %pad_maximum_fusion.w_ref, bf16[32,128]{1,0:T(8,128)(2,1)} %pad_bitcast_fusion.small_ref), custom_call_target="tpu_custom_call" | custom-call | bytes 117964800 | tf_op jit(solution)/shard_map/ring_gather_0/pallas_call | solution.py:670
  146.2 0.9 copy.121
  149.2 1.1 reshape.1394
  150.3 1.1 reshape.1395
  151.6 0.7 select_maximum_fusion.refs_8_.refs_11_
  152.9 0.6 pad_convert_fusion.2.refs_5_.refs_8_
  153.5 0.6 pad_convert_fusion.refs_7_.refs_10_
  154.5 4.4 fusion.57.refs_4_
  159.0 18.0 %fusion.56.refs_0_.refs_1_.refs_2_.refs_3_.refs_5_.refs_6_.refs_7_ = f32[1024,3072]{1,0:T(8,128)} fusion(bf16[1024,2048]{1,0:T(8,128)(2,1)S(1)} %copy-done, bf16[2048,3072]{1,0:T(8,128)(2,1)} %get-tuple-element.63.full_ref), kind=kOutput, calls=%fused_computation.177 | convolution fusion | flops 12884901888 | bytes 29360128 | tf_op jit(solution)/shard_map/dot_general | solution.py:1174
  176.9 59.7 %mixer_forward.1 = (bf16[1024,1024]{1,0:T(8,128)(2,1)}, f32[1024,1024]{1,0:T(8,128)}, bf16[1024,1024]{1,0:T(8,128)(2,1)}, bf16[1024,512]{1,0:T(8,128)(2,1)}, bf1...) custom-call(f32[1024,3072]{1,0:T(8,128)} %fusion.56.refs_0_.refs_1_.refs_2_.refs_3_.refs_5_.refs_6_.refs_7_, ...), custom_call_target="tpu_custom_call" | custom-call | flops 20000000000 | bytes 40000000 | tf_op jit(solution)/shard_map/mixer_forward/pallas_call | solution.py:388
  236.6 9.3 convolution_convert_fusion
  246.1 63.1 %ring_gather_2.1.gate_ref = bf16[2048,1408]{1,0:T(8,128)(2,1)} custom-call(bf16[256,1408]{1,0:T(8,128)(2,1)} %w_ref.1), custom_call_target="tpu_custom_call" | custom-call | bytes 54067200 | tf_op jit(solution)/shard_map/ring_gather_2/pallas_call | solution.py:666
  309.3 1.7 multiply_reduce_fusion
  312.1 1.5 multiply_convert_fusion.1
  316.2 0.8 copy-done.11
  316.9 1.2 fusion.5
  318.2 61.1 %ring_gather_3.1.up_ref = bf16[2048,1408]{1,0:T(8,128)(2,1)} custom-call(bf16[256,1408]{1,0:T(8,128)(2,1)} %w_ref.2), custom_call_target="tpu_custom_call" | custom-call | bytes 54067200 | tf_op jit(solution)/shard_map/ring_gather_3/pallas_call | solution.py:666
  379.3 67.6 %ffn_forward.1 = (bf16[1024,1408]{1,0:T(8,128)(2,1)}, bf16[1024,1408]{1,0:T(8,128)(2,1)}, bf16[1024,1408]{1,0:T(8,128)(2,1)}, bf16[2048,1408]{1,0:T(8,128)(2,1)}) custom-call(bf16[1024,2048]{1,0:T(8,128)(2,1)} %all-gather.9.cloned.1.call-done.x_ref.left_ref, bf16[2048,1408]{1,0:T(8,128)(2,1)} %ring_gather_2.1.gate_ref, ...), custom_call_target="tpu_custom_call" | custom-call | flops 70000001024 | bytes 30000000 | tf_op jit(solution)/shard_map/ffn_forward/pallas_call | solution.py:1101
  447.0 85.4 %ffn_backward.1 = (bf16[1024,1408]{1,0:T(8,128)(2,1)}, bf16[1024,1408]{1,0:T(8,128)(2,1)}, bf16[1024,2048]{1,0:T(8,128)(2,1)}, bf16[1024,2048]{1,0:T(8,128)(2,1)}, f32[256,1408]{1,0:T(8,128)}) custom-call(bf16[1024,2048]{1,0:T(8,128)(2,1)} %all-gather.7.cloned.1.call-done.left_ref, bf16[1024,1408]{1,0:T(8,128)(2,1)} %get-tuple-element.71.hid_ref, ...), custom_call_target="tpu_custom_call" | custom-call | flops 89999998976 | bytes 50000000 | tf_op jit(solution)/shard_map/ffn_backward/pallas_call | solution.py:1156
  532.5 68.8 %ring_scatter_6.1 = f32[256,1408]{1,0:T(8,128)} custom-call(bf16[1024,2048]{1,0:T(8,128)(2,1)} %all-gather.9.cloned.1.call-done.x_ref.left_ref, bf16[1024,1408]{1,0:T(8,128)(2,1)} %get-tuple-element.78.right_ref), custom_call_target="tpu_custom_call" | custom-call | bytes 432537600 | tf_op jit(solution)/shard_map/ring_scatter_6/pallas_call | solution.py:1050
  601.4 2.3 fusion.3
  603.8 2.6 fusion.13
  606.4 1.6 fusion.12.z_ref
  608.0 66.7 %ring_scatter_7.1 = f32[256,1408]{1,0:T(8,128)} custom-call(bf16[1024,2048]{1,0:T(8,128)(2,1)} %all-gather.9.cloned.1.call-done.x_ref.left_ref, bf16[1024,1408]{1,0:T(8,128)(2,1)} %get-tuple-element.81.right_ref), custom_call_target="tpu_custom_call" | custom-call | bytes 432537600 | tf_op jit(solution)/shard_map/ring_scatter_7/pallas_call | solution.py:1050
  675.0 10.3 %fusion.58.refs_13_ = f32[1024,1024]{1,0:T(8,128)} fusion(bf16[1024,2048]{1,0:T(8,128)(2,1)} %all-gather.11.cloned.1.call-done.refs_18_, bf16[2048,1024]{1,0:T(8,128)(2,1)} %get-tuple-element.66), kind=kOutput, calls=%fused_computation.179 | convolution fusion | flops 4294967296 | bytes 12582912 | tf_op jit(solution)/shard_map/dot_general | solution.py:1174
  685.3 88.7 %mixer_backward.1 = (bf16[1024,3072]{1,0:T(8,128)(2,1)}, bf16[1024,128]{1,0:T(8,128)(2,1)}, f32[8,512]{1,0:T(8,128)}, f32[8,512]{1,0:T(8,128)}, f32[8,1024]{1,0:...) custom-call(f32[1024,3072]{1,0:T(8,128)} %fusion.56.refs_0_.refs_1_.refs_2_.refs_3_.refs_5_.refs_6_.refs_7_, ...), custom_call_target="tpu_custom_call" | custom-call | flops 40000000000 | bytes 60000000 | tf_op jit(solution)/shard_map/mixer_backward/pallas_call | solution.py:439
  774.0 0.9 bitcast_dynamic-update-slice_fusion
  774.9 0.8 bitcast_dynamic-update-slice_fusion.1
  775.7 0.8 concatenate.450
  776.5 0.8 slice.707
  778.0 0.7 slice.705
  779.2 0.7 slice.706
  780.4 0.6 copy.122
  781.0 2.9 fusion.59
  784.3 0.6 concatenate.441
  785.4 0.6 concatenate.442
  786.6 0.6 pad_maximum_fusion.7.few_ref
  787.3 166.8 %ring_scatter_9.1 = (f32[256,512]{1,0:T(8,128)}, f32[256,512]{1,0:T(8,128)}, f32[256,1024]{1,0:T(8,128)}, f32[256,1024]{1,0:T(8,128)}, f32[16,128]{1,0:T(8,128)}...) custom-call(bf16[1024,2048]{1,0:T(8,128)(2,1)} %all-gather.5.cloned.1.call-done.left_ref, ...), custom_call_target="tpu_custom_call" | custom-call | bytes 943718400 | tf_op jit(solution)/shard_map/ring_scatter_9/pallas_call | solution.py:1011
  954.1 0.7 fusion.32
  954.9 0.7 copy.106
  955.7 0.7 copy.107
  956.4 0.7 slice.734
  957.2 0.7 copy.110
  957.9 0.8 fusion.37
  958.8 0.7 copy.108
  959.6 0.7 copy.109
  960.3 1.2 slice_bitcast_fusion.2
  961.6 1.3 fusion.31
  962.9 1.3 slice_bitcast_fusion
  964.2 2.3 multiply_convert_fusion
  967.6 1.0 copy-done.15
  968.6 1.3 copy.156
  970.0 0.8 copy.157
  970.8 0.8 copy.158
  971.6 1.0 copy.159
  972.6 1.0 copy.160
  973.6 1.0 copy.161
  974.5 1.1 copy.162
  975.6 1.1 copy.163
  976.7 0.8 copy-done.16
  977.5 1.1 copy.164
  (263 shorter events, 16.2 us)
Async XLA Ops:
  7.2 147.3 %all-gather.5.cloned.1.call-start = ((), (), s32[]{:S(2)}) async-start(), calls=%async_computation.3 | async-start | bytes 5242880 | tf_op jit(solution)/shard_map/all_gather | solution.py:1311
  8.7 0.7 copy-start.38
  8.7 0.7 copy-start.39
  10.1 301.5 %copy-start.1 = (bf16[256,1024]{1,0:T(8,128)(2,1)}, bf16[256,1024]{1,0:T(8,128)(2,1)S(1)}, u32[]{:S(2)}) copy-start(bf16[256,1024]{1,0:T(8,128)(2,1)S(1)} %maximum_select_fusion.1) | copy-start | bytes 1572868
  10.3 301.3 %copy-start.3 = (bf16[256,1024]{1,0:T(8,128)(2,1)}, bf16[256,1024]{1,0:T(8,128)(2,1)S(1)}, u32[]{:S(2)}) copy-start(bf16[256,1024]{1,0:T(8,128)(2,1)S(1)} %maximum_select_fusion.3) | copy-start | bytes 1572868
  10.3 2.5 copy-start.43
  10.3 2.7 copy-start.44
  10.3 3.0 copy-start.40
  10.3 3.3 copy-start.41
  10.3 3.5 copy-start.42
  10.6 4.7 copy-start.24
  10.6 4.7 copy-start.25
  10.7 4.7 copy-start.26
  10.7 4.7 copy-start.27
  10.8 0.6 copy-start.30
  12.7 296.5 %reduce-scatter.4.cloned.1.call-start = ((), (), s32[]{:S(2)}) async-start(), calls=%async_computation.4 | async-start | bytes 5242880 | tf_op jit(solution)/shard_map/reduce_scatter | solution.py:1315
  16.6 134.8 %copy-start.45 = (f32[16]{0:T(128)S(1)}, f32[16]{0:T(128)}, u32[]{:S(2)}) copy-start(f32[16]{0:T(128)} %param.35) | copy-start | bytes 196
  16.6 134.9 %copy-start.46 = (f32[16]{0:T(128)S(1)}, f32[16]{0:T(128)}, u32[]{:S(2)}) copy-start(f32[16]{0:T(128)} %param.34) | copy-start | bytes 196
  154.5 4.5 copy-start.13
  154.5 4.5 copy-start
  246.0 133.3 %all-gather.9.cloned.1.call-start = ((), (), s32[]{:S(2)}) async-start(), calls=%async_computation.6 | async-start | bytes 5242880 | tf_op jit(solution)/shard_map/all_gather | solution.py:1311
  246.1 65.4 %copy-start.28 = (f32[1,2048]{1,0:T(1,128)}, f32[1,2048]{1,0:T(1,128)S(1)}, u32[]{:S(2)}) copy-start(f32[1,2048]{1,0:T(1,128)S(1)} %pad_maximum_fusion.9) | copy-start | bytes 24580
  309.2 2.9 copy-start.5
  311.0 0.6 copy-start.36
  311.6 0.6 copy-start.33
  312.1 1.5 copy-start.17
  313.6 133.3 %all-gather.7.cloned.1.call-start = ((), (), s32[]{:S(2)}) async-start(), calls=%async_computation.5 | async-start | bytes 5242880 | tf_op jit(solution)/shard_map/all_gather | solution.py:1311
  314.8 0.7 copy-start.31
  315.4 0.8 copy-start.9
  316.1 0.8 copy-start.11
  318.2 283.1 %reduce-scatter.6.cloned.1.call-start = ((), (), s32[]{:S(2)}) async-start(), calls=%async_computation.7 | async-start | bytes 5242880 | tf_op jit(solution)/shard_map/reduce_scatter | solution.py:1315
  532.4 142.5 %all-gather.11.cloned.1.call-start = ((), (), s32[]{:S(2)}) async-start(), calls=%async_computation.8 | async-start | bytes 5242880 | tf_op jit(solution)/shard_map/all_gather | solution.py:1311
  532.4 68.9 %copy-start.2 = (bf16[256,1024]{1,0:T(8,128)(2,1)S(1)}, bf16[256,1024]{1,0:T(8,128)(2,1)}, u32[]{:S(2)}) copy-start(bf16[256,1024]{1,0:T(8,128)(2,1)} %copy-done.1) | copy-start | bytes 1572868
  532.4 68.9 %copy-start.4 = (bf16[256,1024]{1,0:T(8,128)(2,1)S(1)}, bf16[256,1024]{1,0:T(8,128)(2,1)}, u32[]{:S(2)}) copy-start(bf16[256,1024]{1,0:T(8,128)(2,1)} %copy-done.3) | copy-start | bytes 1572868
  532.5 68.9 %copy-start.6 = (bf16[256,2048]{1,0:T(8,128)(2,1)S(1)}, bf16[256,2048]{1,0:T(8,128)(2,1)}, u32[]{:S(2)}) copy-start(bf16[256,2048]{1,0:T(8,128)(2,1)} %reduce-scatter.4.cloned.1.call-done) | copy-start | bytes 3145732
  532.5 68.9 %copy-start.29 = (f32[1,2048]{1,0:T(1,128)S(1)}, f32[1,2048]{1,0:T(1,128)}, u32[]{:S(2)}) copy-start(f32[1,2048]{1,0:T(1,128)} %copy-done.28) | copy-start | bytes 24580
  532.5 68.9 %copy-start.34 = (f32[256]{0:T(256)S(1)}, f32[256]{0:T(256)}, u32[]{:S(2)}) copy-start(f32[256]{0:T(256)} %copy-done.33) | copy-start | bytes 3076
  601.3 2.5 copy-start.37
  601.3 2.5 copy-start.10
  601.3 2.5 copy-start.32
  601.4 2.4 copy-start.12
  601.4 2.4 copy-start.14
  606.4 357.9 %reduce-scatter.8.cloned.1.call-start = ((), (), s32[]{:S(2)}) async-start(), calls=%async_computation.9 | async-start | bytes 5242880 | tf_op jit(solution)/shard_map/reduce_scatter | solution.py:1315
  774.0 7.0 copy-start.21
  967.0 1.6 copy-start.15
  967.6 2.3 copy-start.35
  968.6 1.4 copy-start.23
  968.6 2.2 copy-start.22
  968.6 3.0 copy-start.20
  970.0 2.6 copy-start.19
  971.6 1.9 copy-start.18
  972.6 1.9 copy-start.7
  973.6 2.1 copy-start.8
  975.6 1.9 copy-start.16
Sparse Core Ops, SparseCore 0:
  12.8 34.6 all-gather.4
  246.1 47.4 reduce-scatter.3
  313.7 37.0 all-gather.8
  352.9 34.4 all-gather.6
  532.5 42.6 reduce-scatter.5
  606.5 32.8 all-gather.10
  675.0 44.0 reduce-scatter.7

commit v5 on v4

--- a/solution.py
+++ b/solution.py
@@ -9,6 +9,7 @@
 
 CH = 128
 HALO = 8
+MIXER_CHUNKS = 4
 LANES = 128
 F32 = jnp.float32
 BF = jnp.bfloat16
@@ -64,7 +65,7 @@
 
 
 def sigmoid(x):
-    return 1.0 / (1.0 + jnp.exp(-x))
+    return 0.5 * jnp.tanh(0.5 * x) + 0.5
 
 
 def conv_of(buf, taps, rows):
@@ -85,7 +86,7 @@
 
 def fwd_body(
     heads, dk, dv, q_ref, k_ref, v_ref, og_ref, ab_ref, tq_ref, tk_ref, tv_ref, par_ref, gain_ref,
-    head_ref, o_ref, u_ref, t_ref, s_ref, qb, kb, vb, state,
+    head_ref, o_ref, u_ref, t_ref, s_ref, qb, kb, vb, state, between=lambda part: None,
 ):
     rows = CH
 
@@ -121,6 +122,7 @@
     kk = [mm(qk_b[h][1], qk_b[h][1], NT) for h in hs]
     inv = unit_lower_inverse([jnp.where(low_strict, bt[h] * dec[h] * kk[h], 0.0) for h in hs])
     inv_b = [x.astype(BF) for x in inv]
+    between(1)
     p_b = [(mm(qk_b[h][0], qk_b[h][1], NT) * dec[h]).astype(BF) for h in hs]
     start = [jnp.exp(g) for g in g_col]
     end = [run[rows - 1 : rows, heads + h : heads + h + 1] for h in hs]
@@ -334,7 +336,7 @@
     }
 
 
-def fwd_gather_body(heads, dk, dv, *refs):
+def fwd_gather_body(length, heads, dk, dv, *refs):
     ins, w_ref, outs, full_ref, rest = refs[:10], refs[10], refs[11:16], refs[16], refs[17:]
     step, steps = pl.program_id(0), pl.num_programs(0)
     gather = Gather(w_ref, full_ref, *rest[4:])
@@ -344,20 +346,21 @@
         greet_near(gather.me, gather.outer, gather.side)
         gather.begin()
 
-    gather.step(step)
-    fwd_body(heads, dk, dv, *ins, *outs, *rest[:4])
+    def between(part):
+        gather.steps(*spread(gather.STEPS, 2 * step + part, 2 * (length // CH)))
+
+    between(0)
+    fwd_body(heads, dk, dv, *ins, *outs, *rest[:4], between)
 
     @pl.when(step == steps - 1)
     def _():
-        gather.steps(steps, gather.STEPS)
         gather.finish()
 
 
 def bwd_scatter_body(length, heads, dk, dv, *refs):
     ins, pair, outs, own, rest = refs[:18], refs[18:20], refs[20:27], refs[27], refs[28:]
     step, steps = pl.program_id(0), pl.num_programs(0)
-    each = 2 * CHUNKS // (length // CH)
-    scatter = Scatter(each, *pair, own, *rest[7:])
+    scatter = Scatter(2, MIXER_CHUNKS, *pair, own, *rest[7:])
 
     @pl.when(step == 0)
     def _():
@@ -365,14 +368,13 @@
         scatter.begin()
 
     def between(part):
-        scatter.steps((2 * step + part) * each, (2 * step + part + 1) * each)
+        scatter.steps(*spread(scatter.last, 2 * step + part, 2 * (length // CH)))
 
     between(0)
     bwd_body(heads, dk, dv, *ins, *outs, *rest[:7], between)
 
     @pl.when(step == steps - 1)
     def _():
-        scatter.steps(4 * CHUNKS, 4 * CHUNKS + 3 * each)
         scatter.finish()
 
 
@@ -386,7 +388,7 @@
     any_ref = [pl.BlockSpec(memory_space=pl.ANY)]
     fused = w is not None
     return pl.pallas_call(
-        functools.partial(fwd_gather_body if fused else fwd_body, heads, dk, dv),
+        functools.partial(*([fwd_gather_body, length] if fused else [fwd_body]), heads, dk, dv),
         grid=(steps,),
         in_specs=[sp[n] for n in ("q", "k", "val", "og", "ab", "tk", "tk", "tv", "par", "gain")] + any_ref * fused,
         out_specs=[sp[n] for n in ("v", "v", "v", "t", "s")] + any_ref * fused,
@@ -435,7 +437,7 @@
         mine = (left.shape[1] // 8, right.shape[1])
         pair = [whole(left), whole(right)]
         own = [pl.BlockSpec(mine, lambda c: (0, 0))]
-        extra = scatter_scratch(*mine)
+        extra = scatter_scratch(*mine, MIXER_CHUNKS)
     return pl.pallas_call(
         functools.partial(*([bwd_scatter_body, length] if fused else [bwd_body]), heads, dk, dv),
         grid=(steps,),
@@ -501,30 +503,37 @@
 
 CHUNKS = 8
 LAG = 2
-
-
+LAST_CHUNKS = 8
+
+
+def spread(total, slot, slots):
+    return total * slot // slots, total * (slot + 1) // slots
+
+
+GATHER_CHUNKS = 8
 CROSS_FIRST = 1
+GATHER_LAG = 2
 
 
 def gather_sems():
     return [
-        pltpu.SemaphoreType.DMA((6, CHUNKS)),
-        pltpu.SemaphoreType.DMA((6, CHUNKS)),
-        pltpu.SemaphoreType.DMA((4, CHUNKS)),
-        pltpu.SemaphoreType.DMA((8, CHUNKS)),
+        pltpu.SemaphoreType.DMA((6, GATHER_CHUNKS)),
+        pltpu.SemaphoreType.DMA((6, GATHER_CHUNKS)),
+        pltpu.SemaphoreType.DMA((4, GATHER_CHUNKS)),
+        pltpu.SemaphoreType.DMA((8, GATHER_CHUNKS)),
         pltpu.SemaphoreType.DMA,
     ]
 
 
 class Gather:
-    STEPS = CHUNKS + 4
+    STEPS = GATHER_CHUNKS + 4 * GATHER_LAG
 
     def __init__(self, w_ref, full_ref, right_s, left_s, swap_s, arrive, local):
         self.w, self.full, self.sems, self.arrive = w_ref, full_ref, (right_s, left_s, swap_s), arrive
         self.me = lax.axis_index("dp")
         self.outer, self.side = self.me // 2, self.me % 2
         self.block = w_ref.shape[0]
-        self.part = self.block // CHUNKS
+        self.part = self.block // GATHER_CHUNKS
         self.keep = pltpu.make_async_copy(w_ref, full_ref.at[pl.ds(0, self.block)], local)
 
     def spot(self, slot, c):
@@ -559,13 +568,13 @@
                 self.along(way, far, h, c).start()
 
     def step(self, i):
-        @pl.when(i < CHUNKS)
+        @pl.when(i < GATHER_CHUNKS)
         def _():
             self.to_side(0, i).start()
             for way in range(2):
                 self.go_on(way, 0, 0, i)
 
-        far_at = i - 1
+        far_at = i - GATHER_LAG
 
         @pl.when((far_at >= 0) & (far_at < CROSS_FIRST))
         def _():
@@ -574,9 +583,9 @@
                 self.go_on(way, 1, 0, far_at)
 
         for far in range(2):
-            last = CROSS_FIRST if far else CHUNKS
+            last = CROSS_FIRST if far else GATHER_CHUNKS
             for h in range(1, 4):
-                c = i - h - far
+                c = i - GATHER_LAG * (h + far)
                 for way in range(2):
                     behind = self.outer if way == 0 else 3 - self.outer
                     slot = 4 - h if way == 0 else h
@@ -605,7 +614,7 @@
                 behind = self.outer if way == 0 else 3 - self.outer
                 for h in range(3):
                     for far in range(2):
-                        @pl.when((behind >= h) & (c < (CROSS_FIRST if far else CHUNKS)))
+                        @pl.when((behind >= h) & (c < (CROSS_FIRST if far else GATHER_CHUNKS)))
                         def _():
                             @pl.when((self.outer < 3) if way == 0 else (self.outer > 0))
                             def _():
@@ -613,7 +622,7 @@
 
             return carry
 
-        lax.fori_loop(0, CHUNKS, one, 0)
+        lax.fori_loop(0, GATHER_CHUNKS, one, 0)
         self.keep.wait()
 
     def steps(self, first, last):
@@ -678,13 +687,14 @@
     )(w, small)
 
 
-def scatter_sems():
-    return [pltpu.SemaphoreType.DMA((4, CHUNKS)) for _ in range(6)]
+def scatter_sems(chunks):
+    return [pltpu.SemaphoreType.DMA((4, chunks)) for _ in range(6)]
 
 
 class Scatter:
-    def __init__(self, lag, left, right, out, mine, came, from_left, from_right, *sems):
-        self.lag = lag
+    def __init__(self, lag, chunks, left, right, out, mine, came, from_left, from_right, *sems):
+        self.lag, self.chunks = lag, chunks
+        self.last = 4 * chunks + 3 * lag
         self.left, self.right, self.mine, self.came = left, right, mine, came
         self.outs = out if isinstance(out, tuple) else (out,)
         self.acc = (from_left, from_right)
@@ -692,7 +702,7 @@
         self.me = lax.axis_index("dp")
         self.outer, self.side = self.me // 2, self.me % 2
         self.block, self.cols = self.outs[0].shape[0], right.shape[1]
-        self.part = self.block // CHUNKS
+        self.part = self.block // chunks
 
     def dot(self, slot):
         tile = self.cols if self.cols <= 1536 else 1024
@@ -702,8 +712,8 @@
             self.mine[pl.ds(at, self.block), j : j + tile] = mm(rows, self.right[:, j : j + tile], TN).astype(BF)
 
     def item(self, t):
-        dest = (3 * (t // CHUNKS)) % 4
-        return dest, (dest - self.outer + 4) % 4, t % CHUNKS
+        dest = (3 * (t // self.chunks) + 1) % 4
+        return dest, (dest - self.outer + 4) % 4, t % self.chunks
 
     def rows(self, slot, c):
         return pl.ds(pl.multiple_of(slot * self.block + c * self.part, self.part), self.part)
@@ -732,20 +742,20 @@
 
     def begin(self):
         def send(j, carry):
-            _, slot, _ = self.item(j * CHUNKS)
+            _, slot, _ = self.item(j * self.chunks)
             self.dot(4 + slot)
 
             def one(c, carry):
                 self.swap(slot, c).start()
                 return carry
 
-            return lax.fori_loop(0, CHUNKS, one, carry)
+            return lax.fori_loop(0, self.chunks, one, carry)
 
         lax.fori_loop(0, 4, send, 0)
 
     def step(self, t):
         outer = self.outer
-        items = 4 * CHUNKS
+        items = 4 * self.chunks
 
         @pl.when(t < items)
         def _():
@@ -822,23 +832,23 @@
 
             return carry
 
-        lax.fori_loop(0, CHUNKS, one, 0)
-
-
-def scatter_scratch(block, cols):
+        lax.fori_loop(0, self.chunks, one, 0)
+
+
+def scatter_scratch(block, cols, chunks):
     return [
         pltpu.VMEM((8 * block, cols), BF),
         pltpu.VMEM((4 * block, cols), BF),
         pltpu.VMEM((3 * block, cols), BF),
         pltpu.VMEM((3 * block, cols), BF),
-    ] + scatter_sems()
+    ] + scatter_sems(chunks)
 
 
 def scatter_body(left_ref, right_ref, out_ref, *scratch):
-    scatter = Scatter(LAG, left_ref, right_ref, out_ref, *scratch)
+    scatter = Scatter(LAG, CHUNKS, left_ref, right_ref, out_ref, *scratch)
     greet_near(scatter.me, scatter.outer, scatter.side)
     scatter.begin()
-    scatter.steps(0, 4 * CHUNKS + 3 * LAG)
+    scatter.steps(0, scatter.last)
     scatter.finish()
 
 
@@ -846,9 +856,9 @@
     t_size, left_ref, right_ref, ab_ref, few_ref, tap_ref, rest_ref, z_ref, mid_ref, gain_ref, fab_ref, full_ref,
     out_q, out_k, out_v, out_g, few_out, tap_out, vec_out, grad_ref, *scratch,
 ):
-    w_buf, sum_out, sum_in, few_in, tap_in, vec, vec_t, vec_d = scratch[:8]
-    w_sem, s_sem, few_sem, tap_sem, t_sem, d_sem = scratch[8:14]
-    scatter = Scatter(LAG, left_ref, right_ref, (out_q, out_k, out_v, out_g), *scratch[14:])
+    w_buf, sum_out, sum_in, few_in, tap_in, vec, vec_t, vec_d, parts = scratch[:9]
+    w_sem, s_sem, few_sem, tap_sem, t_sem, d_sem = scratch[9:15]
+    scatter = Scatter(LAG, LAST_CHUNKS, left_ref, right_ref, (out_q, out_k, out_v, out_g), *scratch[15:])
     me, outer, side, block = scatter.me, scatter.outer, scatter.side, scatter.block
     mine = lax.axis_index("tensor")
     tokens = z_ref.shape[0]
@@ -915,7 +925,8 @@
         return carry
 
     lax.fori_loop(0, 8, tile, 0)
-    scatter.steps(8, 3 * CHUNKS)
+    late = 3 * LAST_CHUNKS
+    scatter.steps(8, late)
 
     def land(n, carry):
         for j in range(1, t_size):
@@ -925,7 +936,7 @@
     lax.fori_loop(0, 8, land, 0)
     size = 32
 
-    def norm(i, carry):
+    def norm(i):
         at = pl.ds(pl.multiple_of(i * size, size), size)
         squares, inner = 0.0, 0.0
         for n in range(8):
@@ -939,7 +950,6 @@
         width = 8 * block
         r = lax.rsqrt(squares / width + 1e-05)
         pull = r * r * r * (inner / width)
-        found = []
         for n in range(8):
             cols = slice(n * block, (n + 1) * block)
             z = z_ref[at, cols]
@@ -949,20 +959,28 @@
             home = 2 * ((outer + n) % 4) + (side + n // 4) % 2
             to = pl.ds(pl.multiple_of(home * block, block), block)
             grad_ref[at, to] = mid_ref[at, cols] + r * (m * gain_ref[:, cols]) - z * pull
-            found.append(carry[n] + jnp.sum(m * (z * r), axis=0, keepdims=True))
-        return tuple(found)
-
-    parts = lax.fori_loop(0, tokens // size, norm, tuple(jnp.zeros((1, block), F32) for _ in range(8)))
+            parts[n : n + 1, :] += jnp.sum(m * (z * r), axis=0, keepdims=True)
+
+    parts[...] = jnp.zeros_like(parts)
+    rounds = tokens // size // 4
+
+    def norms(i, carry):
+        scatter.step(late + i)
+        for k in range(rounds):
+            norm(i * rounds + k)
+        return carry
+
+    lax.fori_loop(0, 4, norms, 0)
     per = block // LANES
     for n in range(8):
         home = 2 * ((outer + n) % 4) + (side + n // 4) % 2
         for k in range(per):
-            vec[pl.ds(home * per + k, 1), :] = parts[n][:, k * LANES : (k + 1) * LANES]
+            vec[pl.ds(home * per + k, 1), :] = parts[n : n + 1, k * LANES : (k + 1) * LANES]
     vec[8 * per :, :] = rest_ref[...]
     for j in range(1, t_size):
         across(j).start()
     vec_t[mine] = vec[...]
-    scatter.steps(3 * CHUNKS, 3 * CHUNKS + 4)
+    scatter.steps(late + 4, late + 6)
     for j in range(1, t_size):
         pltpu.make_async_copy(vec, vec_t.at[(mine + t_size - j) % t_size], t_sem.at[1, j]).wait()
     total = vec_t[0]
@@ -971,7 +989,7 @@
     vec_d[me] = total
     for j in range(1, 8):
         along(j).start()
-    scatter.steps(3 * CHUNKS + 4, 4 * CHUNKS + 3 * LAG)
+    scatter.steps(late + 6, scatter.last)
     few_total, tap_total = few_ref[0], tap_ref[me]
     for j in range(1, 8):
         few(j).wait_recv()
@@ -1028,6 +1046,7 @@
             pltpu.VMEM(vec, F32),
             pltpu.VMEM((t_size,) + vec, F32),
             pltpu.VMEM((8,) + vec, F32),
+            pltpu.VMEM((8, block), F32),
             pltpu.SemaphoreType.DMA((2,)),
             pltpu.SemaphoreType.DMA((2, t_size, 8)),
             pair,
@@ -1035,7 +1054,7 @@
             pltpu.SemaphoreType.DMA((2, t_size)),
             pair,
         ]
-        + scatter_scratch(block, cols),
+        + scatter_scratch(block, cols, LAST_CHUNKS),
         compiler_params=pltpu.CompilerParams(
             collective_id=ident, has_side_effects=True, vmem_limit_bytes=63 << 20
         ),
@@ -1052,7 +1071,7 @@
         in_specs=[vmem] * 2,
         out_specs=vmem,
         out_shape=jax.ShapeDtypeStruct((block, cols), F32),
-        scratch_shapes=scatter_scratch(block, cols),
+        scratch_shapes=scatter_scratch(block, cols, CHUNKS),
         compiler_params=pltpu.CompilerParams(
             collective_id=ident, has_side_effects=True, vmem_limit_bytes=60 << 20
         ),
@@ -1068,7 +1087,7 @@
     return [(at, min(want, n - at)) for at in range(0, n, want)]
 
 
-def ffn_forward_body(x_ref, gate_ref, up_ref, w_ref, act_ref, slope_ref, hid_ref, full_ref, *sems):
+def ffn_forward_body(slots, x_ref, gate_ref, up_ref, w_ref, act_ref, slope_ref, hid_ref, full_ref, *sems):
     step, steps = pl.program_id(0), pl.num_programs(0)
     gather = Gather(w_ref, full_ref, *sems)
 
@@ -1079,7 +1098,7 @@
 
     x = x_ref[...]
     for part, (at, wide) in enumerate(col_tiles(gate_ref.shape[1], 512)):
-        gather.step(3 * step + part)
+        gather.steps(*spread(gather.STEPS, 3 * step + part, 3 * slots))
         gate = mm(x, gate_ref[:, at : at + wide])
         up = mm(x, up_ref[:, at : at + wide])
         sg = sigmoid(gate)
@@ -1099,7 +1118,7 @@
     once = pl.BlockSpec(full_gate.shape, lambda c: (0, 0), pipeline_mode=pl.Buffered(1))
     tile = pl.BlockSpec((FFN_ROWS, ff), lambda c: (c, 0))
     return pl.pallas_call(
-        ffn_forward_body,
+        functools.partial(ffn_forward_body, length // FFN_ROWS),
         grid=(length // FFN_ROWS,),
         in_specs=[pl.BlockSpec((FFN_ROWS, x.shape[1]), lambda c: (c, 0)), once, once, any_ref],
         out_specs=[tile] * 3 + [any_ref],
@@ -1115,16 +1134,23 @@
 
 
 def ffn_backward_body(
-    left_ref, hid_ref, act_ref, slope_ref, down_ref, gate_ref, up_ref,
-    glow_ref, ulow_ref, back_ref, ffn_ref, out_ref, *scratch,
+    left_ref, hid_ref, act_ref, slope_ref, down_hbm, gate_hbm, up_hbm,
+    glow_ref, ulow_ref, back_ref, ffn_ref, out_ref, down_ref, gate_ref, up_ref, load_sem, *scratch,
 ):
     step, steps = pl.program_id(0), pl.num_programs(0)
-    scatter = Scatter(4, left_ref, hid_ref, out_ref, *scratch)
+    scatter = Scatter(2, CHUNKS, left_ref, hid_ref, out_ref, *scratch)
+    loads = [
+        pltpu.make_async_copy(src, dst, load_sem.at[i])
+        for i, (src, dst) in enumerate(((down_hbm, down_ref), (gate_hbm, gate_ref), (up_hbm, up_ref)))
+    ]
 
     @pl.when(step == 0)
     def _():
         greet_near(scatter.me, scatter.outer, scatter.side)
+        for copy in loads:
+            copy.start()
         scatter.begin()
+        loads[0].wait()
 
     rows = pl.ds(pl.multiple_of(step * FFN_ROWS, FFN_ROWS), FFN_ROWS)
     x = left_ref[rows, :]
@@ -1133,17 +1159,22 @@
         grad = mm(x, down_ref[:, cols])
         glow_ref[:, cols] = (grad * slope_ref[:, cols].astype(F32)).astype(BF)
         ulow_ref[:, cols] = (grad * act_ref[:, cols].astype(F32)).astype(BF)
+
+    @pl.when(step == 0)
+    def _():
+        loads[1].wait()
+        loads[2].wait()
+
     hid = hid_ref[rows, :]
     glow, ulow = glow_ref[...], ulow_ref[...]
     for part, (at, wide) in enumerate(col_tiles(down_ref.shape[0], 512)):
-        scatter.steps(8 * step + 2 * part, 8 * step + 2 * part + 2)
+        scatter.steps(*spread(scatter.last, 4 * step + part, 4 * (left_ref.shape[0] // FFN_ROWS)))
         cols = slice(at, at + wide)
         back_ref[:, cols] = (mm(glow, gate_ref[cols, :], NT) + mm(ulow, up_ref[cols, :], NT)).astype(BF)
         ffn_ref[:, cols] = mm(hid, down_ref[cols, :], NT).astype(BF)
 
     @pl.when(step == steps - 1)
     def _():
-        scatter.steps(4 * CHUNKS, 4 * CHUNKS + 12)
         scatter.finish()
 
 
@@ -1156,12 +1187,14 @@
     return pl.pallas_call(
         ffn_backward_body,
         grid=(length // FFN_ROWS,),
-        in_specs=[once(left), once(hidden), tile, tile, once(full_down), once(full_gate), once(full_up)],
+        in_specs=[once(left), once(hidden), tile, tile] + [pl.BlockSpec(memory_space=pl.ANY)] * 3,
         out_specs=[tile, tile, wide, wide, pl.BlockSpec(mine, lambda c: (0, 0))],
         out_shape=[jax.ShapeDtypeStruct((length, ff), BF)] * 2
         + [jax.ShapeDtypeStruct((length, width), BF)] * 2
         + [jax.ShapeDtypeStruct(mine, F32)],
-        scratch_shapes=scatter_scratch(*mine),
+        scratch_shapes=[pltpu.VMEM(full_down.shape, BF)] * 3
+        + [pltpu.SemaphoreType.DMA((3,))]
+        + scatter_scratch(*mine, CHUNKS),
         compiler_params=pltpu.CompilerParams(
             dimension_semantics=("arbitrary",), vmem_limit_bytes=62 << 20, collective_id=ident, has_side_effects=True
         ),
@@ -1332,8 +1365,11 @@
     positions = tensor_pos * row_count + jnp.arange(row_count, dtype=jnp.int32)
     valid_rows = (positions < lengths[0]).astype(F32)[:, None]
 
+    def by_head(conv):
+        return jnp.transpose(conv, (1, 2, 0)).reshape(-1)
+
     small = jnp.concatenate(
-        [w_beta.reshape(-1), w_alpha.reshape(-1), conv_query.reshape(-1), conv_key.reshape(-1), conv_value.reshape(-1)]
+        [w_beta.T.reshape(-1), w_alpha.T.reshape(-1), by_head(conv_query), by_head(conv_key), by_head(conv_value)]
     )
     cuts = [0]
     for part in (w_beta, w_alpha, conv_query, conv_key, conv_value):
@@ -1343,15 +1379,17 @@
         jnp.concatenate([w_query, w_key, w_value, w_outgate], axis=1), small
     )
     small = small.reshape(dp_size, -1)
-    pieces = [small[:, a:b] for a, b in zip(cuts[:-1], cuts[1:])]
-    full_ab = jnp.concatenate([p.reshape(dp_size * block, heads) for p in pieces[:2]], axis=1)
+    few = small[:, : cuts[2]].reshape(dp_size, 2 * heads, block)
+    full_ab = jnp.transpose(few, (1, 0, 2)).reshape(2 * heads, dp_size * block).T
     full_ab = jnp.pad(full_ab, ((0, 0), (0, LANES - 2 * heads)))
-
-    def tap_table(piece, size):
-        table = rows.restore(piece, 0).reshape(size, heads, taps_n).astype(F32)
-        return jnp.pad(jnp.transpose(table, (2, 1, 0)).reshape(taps_n, heads * size), ((0, 8 - taps_n), (0, 0)))
-
-    tq, tk, tv = tap_table(pieces[2], dk), tap_table(pieces[3], dk), tap_table(pieces[4], dv)
+    taps_all = rows.restore(small[:, cuts[2] : cuts[5]], 0).astype(F32)
+
+    def tap_table(at, size):
+        table = taps_all[:, at - cuts[2] : at - cuts[2] + taps_n * heads * size // dp_size]
+        table = jnp.transpose(table.reshape(dp_size, heads, taps_n, size // dp_size), (2, 1, 0, 3))
+        return jnp.pad(table.reshape(taps_n, heads * size), ((0, 8 - taps_n), (0, 0)))
+
+    tq, tk, tv = tap_table(cuts[2], dk), tap_table(cuts[3], dk), tap_table(cuts[4], dv)
     alog_local = lax.dynamic_slice_in_dim(a_log, head_start, heads)
     dtb_local = lax.dynamic_slice_in_dim(dt_bias, head_start, heads)
     par = jnp.pad(jnp.stack([alog_local, dtb_local]), ((0, 6), (heads, LANES - 2 * heads)))
@@ -1396,11 +1434,12 @@
     def in_lanes(x, lead):
         return jnp.pad(x, ((0, 0), (0, -x.shape[1] % (8 * LANES)))).reshape(lead + (-1, LANES))
 
-    grad_ab = dot_tokens(rows_one, ab_low)[:, : 2 * heads]
-    few = [grad_ab[:, :heads].reshape(dp_size, -1), grad_ab[:, heads:].reshape(dp_size, -1)]
+    grad_ab = dot_tokens(ab_low, rows_one)[: 2 * heads].reshape(2 * heads, dp_size, block)
+    few = [jnp.transpose(grad_ab, (1, 0, 2)).reshape(dp_size, -1)]
 
     def tap_grad(table, size):
-        return jnp.transpose(table[:taps_n].reshape(taps_n, heads, size), (2, 1, 0)).reshape(dp_size, -1)
+        grad = table[:taps_n].reshape(taps_n, heads, dp_size, size // dp_size)
+        return jnp.transpose(grad, (2, 1, 0, 3)).reshape(dp_size, -1)
 
     taps = [tap_grad(dtq, dk), tap_grad(dtk, dk), tap_grad(dtv, dv)]
     alog_full, dtb_full = (
@@ -1418,12 +1457,16 @@
     def pieces_of(total, like):
         flat, found, at = total.reshape(-1), [], 0
         for part in like:
-            found.append(flat[at : at + part.size].reshape(part.shape))
+            found.append(flat[at : at + part.size])
             at += part.size
         return found
 
-    out_beta, out_alpha = pieces_of(few_sum, (w_beta, w_alpha))
-    out_cq, out_ck, out_cv = pieces_of(tap_sum, (conv_query, conv_key, conv_value))
+    grad_ab = few_sum.reshape(-1)[: cuts[2]].reshape(2 * heads, block)
+    out_beta, out_alpha = grad_ab[:heads].T, grad_ab[heads:].T
+    out_cq, out_ck, out_cv = (
+        jnp.transpose(x.reshape(heads, taps_n, -1), (2, 0, 1))
+        for x in pieces_of(tap_sum, (conv_query, conv_key, conv_value))
+    )
     norm1_sum, norm2_sum, hgain_sum, alog_sum, dtb_sum = pieces_of(vec_sum, [norm1_gain] + rest)
     return (
         outputs, grad_inputs[None], norm1_sum, out_query, out_key, out_value, out_outgate,

time: 1000 us -> 978 us (0.978)
  Pallas kernels: 857 us -> 845 us
    pallas_call x2, Pallas kernels: 127 us -> 116 us  [the longest x1 64.6 us: ffn_forward(): pl.pallas_call(functools.partial(ffn_forward_body, length // FFN_ROWS), g...]
    unnamed x136 -> x124, local copies, waits for them, and re-layouts: 21 us -> 16.7 us
  transfers between devices with their start and end apart: 7 -> 7, of which waited for: 0 -> 0; matrix products, arithmetic and copies ran while one was open for 5% -> 4% of each run, Pallas kernels for 72% -> 74%
where the time goes in v5:
time: 978 us; the launch traced here: 966 us
  Pallas kernels  845 us (86%)
  matrix products  44.6 us (5%)
  local copies, waits for them, and re-layouts  40.6 us (4%)
  other arithmetic  19.2 us (2%)
  between operations  16.4 us (2%)
    pallas_call x1, Pallas kernels, ring_scatter_last(): pl.pallas_call(functools.partial(scatter_last_body, t_size), in_specs=[vm...  167 us
    pallas_call x2, Pallas kernels, ring_scatter(): pl.pallas_call(scatter_body, in_specs=[vmem] * 2, out_specs=vmem, out_sha...  145 us
    pallas_call x1, Pallas kernels, ring_gather(): pl.pallas_call(gather_small_body, in_specs=[any_ref] * 2, out_specs=[any_...  130 us
    pallas_call x2, Pallas kernels, ring_gather(): pl.pallas_call(gather_body, in_specs=[any_ref], out_specs=any_ref, out_sh...  123 us
    pallas_call x1, Pallas kernels, ffn_backward(): pl.pallas_call(ffn_backward_body, grid=(length // FFN_ROWS,), in_specs=[o...  82.7 us
    pallas_call x1, Pallas kernels, mixer_backward(): pl.pallas_call(functools.partial(*([bwd_scatter_body, length] if fused el...  80.7 us
    pallas_call x1, Pallas kernels, ffn_forward(): pl.pallas_call(functools.partial(ffn_forward_body, length // FFN_ROWS), g...  64.6 us
    pallas_call x1, Pallas kernels, mixer_forward(): pl.pallas_call(functools.partial(*([fwd_gather_body, length] if fused els...  51.7 us
  transfers between devices with their start and end apart: 7, of which 0 were waited for; matrix products, arithmetic and copies ran while one was open for 4% of the time, Pallas kernels for 74%

profile of v5, /device:TPU:14, one launch (start us, length us, event | category | flops | bytes accessed | tf_op | source)
XLA Modules:
  0.0 966.0 jit_solution(15038358874424621495)
XLA Ops:
  7.3 1.4 fusion.18
  11.4 1.3 multiply_convert_fusion.2
  13.7 0.6 pad_bitcast_fusion.small_ref
  14.3 1.3 pad_maximum_fusion.w_ref
  15.6 129.6 %ring_gather_0.1 = (bf16[2048,3072]{1,0:T(8,128)(2,1)}, bf16[8,32,128]{2,1,0:T(8,128)(2,1)}) custom-call(bf16[256,3072]{1,0:T(8,128)(2,1)} %pad_maximum_fusion.w_ref, bf16[32,128]{1,0:T(8,128)(2,1)} %pad_bitcast_fusion.small_ref), custom_call_target="tpu_custom_call" | custom-call | bytes 117964800 | tf_op jit(solution)/shard_map/ring_gather_0/pallas_call | solution.py:679
  145.2 0.9 copy.59
  147.4 0.7 pad.31.refs_7_.refs_10_
  148.0 0.6 pad.29.refs_5_.refs_8_
  148.6 0.6 pad.30.refs_6_.refs_9_
  149.3 0.7 select_maximum_fusion.refs_8_.refs_11_
  150.0 20.3 %fusion.47.refs_0_.refs_1_.refs_2_.refs_3_.refs_5_.refs_6_.refs_7_ = f32[1024,3072]{1,0:T(8,128)} fusion(bf16[1024,2048]{1,0:T(8,128)(2,1)} %all-gather.5.cloned.1.call-done.left_ref, bf16[2048,3072]{1,0:T(8,128)(2,1)} %get-tuple-element.63.full_ref), kind=kOutput, calls=%fused_computation.150 | convolution fusion | flops 12884901888 | bytes 29360128 | tf_op jit(solution)/shard_map/dot_general | solution.py:1207
  170.3 2.0 fusion.11.refs_4_
  172.3 51.7 %mixer_forward.1 = (bf16[1024,1024]{1,0:T(8,128)(2,1)}, f32[1024,1024]{1,0:T(8,128)}, bf16[1024,1024]{1,0:T(8,128)(2,1)}, bf16[1024,512]{1,0:T(8,128)(2,1)}, bf1...) custom-call(f32[1024,3072]{1,0:T(8,128)} %fusion.47.refs_0_.refs_1_.refs_2_.refs_3_.refs_5_.refs_6_.refs_7_, ...), custom_call_target="tpu_custom_call" | custom-call | flops 20000000000 | bytes 40000000 | tf_op jit(solution)/shard_map/mixer_forward/pallas_call | solution.py:390
  224.0 9.3 convolution_convert_fusion
  233.5 64.7 %ring_gather_2.1.gate_ref.gate_hbm = bf16[2048,1408]{1,0:T(8,128)(2,1)} custom-call(bf16[256,1408]{1,0:T(8,128)(2,1)} %w_ref.1), custom_call_target="tpu_custom_call" | custom-call | bytes 54067200 | tf_op jit(solution)/shard_map/ring_gather_2/pallas_call | solution.py:675
  298.3 1.7 multiply_reduce_fusion
  301.1 1.5 multiply_convert_fusion.1
  304.6 0.6 copy-done.9
  305.2 0.8 copy-done.11
  306.0 1.2 fusion.5
  307.2 58.4 %ring_gather_3.1.up_ref.up_hbm = bf16[2048,1408]{1,0:T(8,128)(2,1)} custom-call(bf16[256,1408]{1,0:T(8,128)(2,1)} %w_ref.2), custom_call_target="tpu_custom_call" | custom-call | bytes 54067200 | tf_op jit(solution)/shard_map/ring_gather_3/pallas_call | solution.py:675
  365.7 64.6 %ffn_forward.1 = (bf16[1024,1408]{1,0:T(8,128)(2,1)}, bf16[1024,1408]{1,0:T(8,128)(2,1)}, bf16[1024,1408]{1,0:T(8,128)(2,1)}, bf16[2048,1408]{1,0:T(8,128)(2,1)}) custom-call(bf16[1024,2048]{1,0:T(8,128)(2,1)} %all-gather.9.cloned.1.call-done.x_ref.left_ref, bf16[2048,1408]{1,0:T(8,128)(2,1)} %ring_gather_2.1.gate_ref.gate_hbm, ...), custom_call_target="tpu_custom_call" | custom-call | flops 70000001024 | bytes 30000000 | tf_op jit(solution)/shard_map/ffn_forward/pallas_call | solution.py:1120
  430.3 82.7 %ffn_backward.1 = (bf16[1024,1408]{1,0:T(8,128)(2,1)}, bf16[1024,1408]{1,0:T(8,128)(2,1)}, bf16[1024,2048]{1,0:T(8,128)(2,1)}, bf16[1024,2048]{1,0:T(8,128)(2,1)}, f32[256,1408]{1,0:T(8,128)}) custom-call(bf16[1024,2048]{1,0:T(8,128)(2,1)} %all-gather.7.cloned.1.call-done.left_ref, bf16[1024,1408]{1,0:T(8,128)(2,1)} %get-tuple-element.71.hid_ref, ...), custom_call_target="tpu_custom_call" | custom-call | flops 89999998976 | bytes 50000000 | tf_op jit(solution)/shard_map/ffn_backward/pallas_call | solution.py:1187
  513.1 73.5 %ring_scatter_6.1 = f32[256,1408]{1,0:T(8,128)} custom-call(bf16[1024,2048]{1,0:T(8,128)(2,1)} %all-gather.9.cloned.1.call-done.x_ref.left_ref, bf16[1024,1408]{1,0:T(8,128)(2,1)} %get-tuple-element.78.right_ref), custom_call_target="tpu_custom_call" | custom-call | bytes 432537600 | tf_op jit(solution)/shard_map/ring_scatter_6/pallas_call | solution.py:1069
  586.8 2.3 fusion.3
  589.2 2.6 fusion.14
  591.8 1.9 pad.28.fab_ref
  593.8 1.6 fusion.13.z_ref
  595.4 71.5 %ring_scatter_7.1 = f32[256,1408]{1,0:T(8,128)} custom-call(bf16[1024,2048]{1,0:T(8,128)(2,1)} %all-gather.9.cloned.1.call-done.x_ref.left_ref, bf16[1024,1408]{1,0:T(8,128)(2,1)} %get-tuple-element.81.right_ref), custom_call_target="tpu_custom_call" | custom-call | bytes 432537600 | tf_op jit(solution)/shard_map/ring_scatter_7/pallas_call | solution.py:1069
  667.1 10.0 %fusion.48.refs_13_ = f32[1024,1024]{1,0:T(8,128)} fusion(bf16[1024,2048]{1,0:T(8,128)(2,1)} %all-gather.11.cloned.1.call-done.refs_18_, bf16[2048,1024]{1,0:T(8,128)(2,1)} %get-tuple-element.66), kind=kOutput, calls=%fused_computation.151 | convolution fusion | flops 4294967296 | bytes 12582912 | tf_op jit(solution)/shard_map/dot_general | solution.py:1207
  677.0 80.7 %mixer_backward.1 = (bf16[1024,3072]{1,0:T(8,128)(2,1)}, bf16[1024,128]{1,0:T(8,128)(2,1)}, f32[8,512]{1,0:T(8,128)}, f32[8,512]{1,0:T(8,128)}, f32[8,1024]{1,0:...) custom-call(f32[1024,3072]{1,0:T(8,128)} %fusion.47.refs_0_.refs_1_.refs_2_.refs_3_.refs_5_.refs_6_.refs_7_, ...), custom_call_target="tpu_custom_call" | custom-call | flops 40000000000 | bytes 60000000 | tf_op jit(solution)/shard_map/mixer_backward/pallas_call | solution.py:441
  757.7 0.8 bitcast_dynamic-update-slice_fusion
  758.5 0.8 bitcast_dynamic-update-slice_fusion.1
  759.4 0.7 concatenate.395
  760.1 0.8 slice.554
  761.1 0.7 slice.552
  762.1 0.7 slice.553
  763.1 0.6 copy.60
  763.7 3.0 fusion.6
  766.7 0.6 reshape.1392.few_ref
  767.3 0.6 pad.33
  767.9 167.4 %ring_scatter_9.1 = (f32[256,512]{1,0:T(8,128)}, f32[256,512]{1,0:T(8,128)}, f32[256,1024]{1,0:T(8,128)}, f32[256,1024]{1,0:T(8,128)}, f32[16,128]{1,0:T(8,128)}...) custom-call(bf16[1024,2048]{1,0:T(8,128)(2,1)} %all-gather.5.cloned.1.call-done.left_ref, ...), custom_call_target="tpu_custom_call" | custom-call | bytes 943718400 | tf_op jit(solution)/shard_map/ring_scatter_9/pallas_call | solution.py:1029
  935.3 0.7 fusion.30
  936.0 0.6 slice.578
  937.2 0.7 slice.583
  937.9 0.8 fusion.39
  938.6 0.7 reshape.1402
  939.3 0.7 reshape.1403
  940.0 0.7 reshape.1404
  940.7 1.2 slice_bitcast_fusion.2
  941.9 1.3 fusion.28
  943.2 1.3 slice_bitcast_fusion
  944.6 2.3 multiply_convert_fusion
  948.0 1.0 copy-done.15
  949.0 1.3 copy.96
  950.4 0.8 copy.97
  951.2 0.8 copy.98
  952.0 1.0 copy.99
  952.9 1.0 copy.100
  953.9 1.0 copy.101
  954.9 1.1 copy.102
  956.0 1.1 copy.103
  957.1 0.8 copy-done.16
  957.9 1.1 copy.104
  (236 shorter events, 9.9 us)
Async XLA Ops:
  7.2 142.8 %all-gather.5.cloned.1.call-start = ((), (), s32[]{:S(2)}) async-start(), calls=%async_computation.3 | async-start | bytes 5242880 | tf_op jit(solution)/shard_map/all_gather | solution.py:1344
  8.7 0.7 copy-start.37
  8.7 0.7 copy-start.38
  10.1 290.5 %copy-start.1 = (bf16[256,1024]{1,0:T(8,128)(2,1)}, bf16[256,1024]{1,0:T(8,128)(2,1)S(1)}, u32[]{:S(2)}) copy-start(bf16[256,1024]{1,0:T(8,128)(2,1)S(1)} %maximum_select_fusion.1) | copy-start | bytes 1572868
  10.3 290.3 %copy-start.3 = (bf16[256,1024]{1,0:T(8,128)(2,1)}, bf16[256,1024]{1,0:T(8,128)(2,1)S(1)}, u32[]{:S(2)}) copy-start(bf16[256,1024]{1,0:T(8,128)(2,1)S(1)} %maximum_select_fusion.3) | copy-start | bytes 1572868
  10.3 2.5 copy-start.42
  10.3 2.5 copy-start.43
  10.3 2.5 copy-start.40
  10.3 2.6 copy-start.41
  10.3 2.7 copy-start.39
  10.3 4.0 copy-start.23
  10.4 4.0 copy-start.24
  10.4 3.9 copy-start.25
  10.4 3.9 copy-start.26
  10.8 0.6 copy-start.29
  12.7 285.5 %reduce-scatter.4.cloned.1.call-start = ((), (), s32[]{:S(2)}) async-start(), calls=%async_computation.4 | async-start | bytes 5242880 | tf_op jit(solution)/shard_map/reduce_scatter | solution.py:1348
  15.6 133.6 %copy-start.44 = (f32[16]{0:T(128)S(1)}, f32[16]{0:T(128)}, u32[]{:S(2)}) copy-start(f32[16]{0:T(128)} %param.35) | copy-start | bytes 196
  15.6 133.6 %copy-start.45 = (f32[16]{0:T(128)S(1)}, f32[16]{0:T(128)}, u32[]{:S(2)}) copy-start(f32[16]{0:T(128)} %param.34) | copy-start | bytes 196
  147.3 22.9 %copy-start.13 = (bf16[8,8,256]{0,2,1:T(8,128)(2,1)}, bf16[8,8,256]{0,2,1:T(8,128)(2,1)S(1)}, u32[]{:S(2)}) copy-start(bf16[8,8,256]{0,2,1:T(8,128)(2,1)S(1)} %copy.44) | copy-start | bytes 98308
  150.0 20.3 %copy-start = (bf16[1024,2048]{1,0:T(8,128)(2,1)S(1)}, bf16[1024,2048]{1,0:T(8,128)(2,1)}, u32[]{:S(2)}) copy-start(bf16[1024,2048]{1,0:T(8,128)(2,1)} %all-gather.5.cloned.1.call-done.left_ref) | copy-start | bytes 12582916
  233.4 132.3 %all-gather.9.cloned.1.call-start = ((), (), s32[]{:S(2)}) async-start(), calls=%async_computation.6 | async-start | bytes 5242880 | tf_op jit(solution)/shard_map/all_gather | solution.py:1344
  233.5 67.0 %copy-start.27 = (f32[1,2048]{1,0:T(1,128)}, f32[1,2048]{1,0:T(1,128)S(1)}, u32[]{:S(2)}) copy-start(f32[1,2048]{1,0:T(1,128)S(1)} %pad_maximum_fusion.8) | copy-start | bytes 24580
  298.3 2.9 copy-start.5
  300.0 0.6 copy-start.35
  300.6 0.6 copy-start.32
  301.1 1.5 copy-start.17
  302.6 127.7 %all-gather.7.cloned.1.call-start = ((), (), s32[]{:S(2)}) async-start(), calls=%async_computation.5 | async-start | bytes 5242880 | tf_op jit(solution)/shard_map/all_gather | solution.py:1344
  303.8 0.7 copy-start.30
  304.4 0.8 copy-start.9
  305.2 0.8 copy-start.11
  307.2 279.6 %reduce-scatter.6.cloned.1.call-start = ((), (), s32[]{:S(2)}) async-start(), calls=%async_computation.7 | async-start | bytes 5242880 | tf_op jit(solution)/shard_map/reduce_scatter | solution.py:1348
  513.0 153.9 %all-gather.11.cloned.1.call-start = ((), (), s32[]{:S(2)}) async-start(), calls=%async_computation.8 | async-start | bytes 5242880 | tf_op jit(solution)/shard_map/all_gather | solution.py:1344
  513.1 73.7 %copy-start.2 = (bf16[256,1024]{1,0:T(8,128)(2,1)S(1)}, bf16[256,1024]{1,0:T(8,128)(2,1)}, u32[]{:S(2)}) copy-start(bf16[256,1024]{1,0:T(8,128)(2,1)} %copy-done.1) | copy-start | bytes 1572868
  513.1 73.7 %copy-start.4 = (bf16[256,1024]{1,0:T(8,128)(2,1)S(1)}, bf16[256,1024]{1,0:T(8,128)(2,1)}, u32[]{:S(2)}) copy-start(bf16[256,1024]{1,0:T(8,128)(2,1)} %copy-done.3) | copy-start | bytes 1572868
  513.1 73.7 %copy-start.6 = (bf16[256,2048]{1,0:T(8,128)(2,1)S(1)}, bf16[256,2048]{1,0:T(8,128)(2,1)}, u32[]{:S(2)}) copy-start(bf16[256,2048]{1,0:T(8,128)(2,1)} %reduce-scatter.4.cloned.1.call-done) | copy-start | bytes 3145732
  513.1 73.7 %copy-start.28 = (f32[1,2048]{1,0:T(1,128)S(1)}, f32[1,2048]{1,0:T(1,128)}, u32[]{:S(2)}) copy-start(f32[1,2048]{1,0:T(1,128)} %copy-done.27) | copy-start | bytes 24580
  513.1 73.7 %copy-start.33 = (f32[256]{0:T(256)S(1)}, f32[256]{0:T(256)}, u32[]{:S(2)}) copy-start(f32[256]{0:T(256)} %copy-done.32) | copy-start | bytes 3076
  586.7 2.5 copy-start.36
  586.7 2.5 copy-start.10
  586.7 2.5 copy-start.31
  586.8 2.4 copy-start.12
  586.8 2.4 copy-start.14
  591.8 352.8 %reduce-scatter.8.cloned.1.call-start = ((), (), s32[]{:S(2)}) async-start(), calls=%async_computation.9 | async-start | bytes 5242880 | tf_op jit(solution)/shard_map/reduce_scatter | solution.py:1348
  947.4 1.6 copy-start.15
  948.0 2.3 copy-start.34
  949.0 1.4 copy-start.22
  949.0 2.2 copy-start.21
  949.0 3.0 copy-start.20
  950.4 2.6 copy-start.19
  952.0 1.9 copy-start.18
  952.9 1.9 copy-start.7
  953.9 2.1 copy-start.8
  956.0 1.9 copy-start.16
Sparse Core Ops, SparseCore 0:
  12.8 34.6 all-gather.4
  233.5 49.3 reduce-scatter.3
  302.7 33.6 all-gather.8
  338.5 34.4 all-gather.6
  513.2 46.0 reduce-scatter.5
  591.9 35.1 all-gather.10
  667.1 45.1 reduce-scatter.7

commit v6 on v5

--- a/solution.py
+++ b/solution.py
@@ -512,7 +512,7 @@
 
 GATHER_CHUNKS = 8
 CROSS_FIRST = 1
-GATHER_LAG = 2
+GATHER_LAG = 3
 
 
 def gather_sems():
@@ -1138,7 +1138,7 @@
     glow_ref, ulow_ref, back_ref, ffn_ref, out_ref, down_ref, gate_ref, up_ref, load_sem, *scratch,
 ):
     step, steps = pl.program_id(0), pl.num_programs(0)
-    scatter = Scatter(2, CHUNKS, left_ref, hid_ref, out_ref, *scratch)
+    scatter = Scatter(3, CHUNKS, left_ref, hid_ref, out_ref, *scratch)
     loads = [
         pltpu.make_async_copy(src, dst, load_sem.at[i])
         for i, (src, dst) in enumerate(((down_hbm, down_ref), (gate_hbm, gate_ref), (up_hbm, up_ref)))

time: 978 us -> 971 us (level)
  transfers between devices with their start and end apart: 7 -> 7, of which waited for: 0 -> 0; matrix products, arithmetic and copies ran while one was open for 4% -> 4% of each run, Pallas kernels for 74% -> 73%
where the time goes in v6:
time: 971 us; the launch traced here: 959 us
  Pallas kernels  838 us (86%)
  matrix products  44.6 us (5%)
  local copies, waits for them, and re-layouts  40.6 us (4%)
  other arithmetic  19.2 us (2%)
  between operations  16.4 us (2%)
    pallas_call x1, Pallas kernels, ring_scatter_last(): pl.pallas_call(functools.partial(scatter_last_body, t_size), in_specs=[vm...  168 us
    pallas_call x2, Pallas kernels, ring_scatter(): pl.pallas_call(scatter_body, in_specs=[vmem] * 2, out_specs=vmem, out_sha...  144 us
    pallas_call x1, Pallas kernels, ring_gather(): pl.pallas_call(gather_small_body, in_specs=[any_ref] * 2, out_specs=[any_...  130 us
    pallas_call x2, Pallas kernels, ring_gather(): pl.pallas_call(gather_body, in_specs=[any_ref], out_specs=any_ref, out_sh...  120 us
    pallas_call x1, Pallas kernels, mixer_backward(): pl.pallas_call(functools.partial(*([bwd_scatter_body, length] if fused el...  80.7 us
    pallas_call x1, Pallas kernels, ffn_backward(): pl.pallas_call(ffn_backward_body, grid=(length // FFN_ROWS,), in_specs=[o...  79.4 us
    pallas_call x1, Pallas kernels, ffn_forward(): pl.pallas_call(functools.partial(ffn_forward_body, length // FFN_ROWS), g...  62.5 us
    pallas_call x1, Pallas kernels, mixer_forward(): pl.pallas_call(functools.partial(*([fwd_gather_body, length] if fused els...  53.6 us
  transfers between devices with their start and end apart: 7, of which 0 were waited for; matrix products, arithmetic and copies ran while one was open for 4% of the time, Pallas kernels for 73%

profile of v6, /device:TPU:14, one launch (start us, length us, event | category | flops | bytes accessed | tf_op | source)
XLA Modules:
  0.0 959.0 jit_solution(194133056299241718)
XLA Ops:
  7.3 1.4 fusion.18
  11.4 1.3 multiply_convert_fusion.2
  13.7 0.6 pad_bitcast_fusion.small_ref
  14.3 1.3 pad_maximum_fusion.w_ref
  15.6 129.6 %ring_gather_0.1 = (bf16[2048,3072]{1,0:T(8,128)(2,1)}, bf16[8,32,128]{2,1,0:T(8,128)(2,1)}) custom-call(bf16[256,3072]{1,0:T(8,128)(2,1)} %pad_maximum_fusion.w_ref, bf16[32,128]{1,0:T(8,128)(2,1)} %pad_bitcast_fusion.small_ref), custom_call_target="tpu_custom_call" | custom-call | bytes 117964800 | tf_op jit(solution)/shard_map/ring_gather_0/pallas_call | solution.py:679
  145.2 0.9 copy.59
  147.4 0.7 pad.31.refs_7_.refs_10_
  148.0 0.6 pad.29.refs_5_.refs_8_
  148.6 0.6 pad.30.refs_6_.refs_9_
  149.3 0.7 select_maximum_fusion.refs_8_.refs_11_
  150.0 20.3 %fusion.47.refs_0_.refs_1_.refs_2_.refs_3_.refs_5_.refs_6_.refs_7_ = f32[1024,3072]{1,0:T(8,128)} fusion(bf16[1024,2048]{1,0:T(8,128)(2,1)} %all-gather.5.cloned.1.call-done.left_ref, bf16[2048,3072]{1,0:T(8,128)(2,1)} %get-tuple-element.63.full_ref), kind=kOutput, calls=%fused_computation.150 | convolution fusion | flops 12884901888 | bytes 29360128 | tf_op jit(solution)/shard_map/dot_general | solution.py:1207
  170.3 2.0 fusion.11.refs_4_
  172.3 53.6 %mixer_forward.1 = (bf16[1024,1024]{1,0:T(8,128)(2,1)}, f32[1024,1024]{1,0:T(8,128)}, bf16[1024,1024]{1,0:T(8,128)(2,1)}, bf16[1024,512]{1,0:T(8,128)(2,1)}, bf1...) custom-call(f32[1024,3072]{1,0:T(8,128)} %fusion.47.refs_0_.refs_1_.refs_2_.refs_3_.refs_5_.refs_6_.refs_7_, ...), custom_call_target="tpu_custom_call" | custom-call | flops 20000000000 | bytes 40000000 | tf_op jit(solution)/shard_map/mixer_forward/pallas_call | solution.py:390
  225.9 9.3 convolution_convert_fusion
  235.4 62.8 %ring_gather_2.1.gate_ref.gate_hbm = bf16[2048,1408]{1,0:T(8,128)(2,1)} custom-call(bf16[256,1408]{1,0:T(8,128)(2,1)} %w_ref.1), custom_call_target="tpu_custom_call" | custom-call | bytes 54067200 | tf_op jit(solution)/shard_map/ring_gather_2/pallas_call | solution.py:675
  298.3 1.7 multiply_reduce_fusion
  301.1 1.5 multiply_convert_fusion.1
  304.6 0.6 copy-done.9
  305.2 0.8 copy-done.11
  306.0 1.2 fusion.5
  307.2 57.1 %ring_gather_3.1.up_ref.up_hbm = bf16[2048,1408]{1,0:T(8,128)(2,1)} custom-call(bf16[256,1408]{1,0:T(8,128)(2,1)} %w_ref.2), custom_call_target="tpu_custom_call" | custom-call | bytes 54067200 | tf_op jit(solution)/shard_map/ring_gather_3/pallas_call | solution.py:675
  364.4 62.5 %ffn_forward.1 = (bf16[1024,1408]{1,0:T(8,128)(2,1)}, bf16[1024,1408]{1,0:T(8,128)(2,1)}, bf16[1024,1408]{1,0:T(8,128)(2,1)}, bf16[2048,1408]{1,0:T(8,128)(2,1)}) custom-call(bf16[1024,2048]{1,0:T(8,128)(2,1)} %all-gather.9.cloned.1.call-done.x_ref.left_ref, bf16[2048,1408]{1,0:T(8,128)(2,1)} %ring_gather_2.1.gate_ref.gate_hbm, ...), custom_call_target="tpu_custom_call" | custom-call | flops 70000001024 | bytes 30000000 | tf_op jit(solution)/shard_map/ffn_forward/pallas_call | solution.py:1120
  426.8 79.4 %ffn_backward.1 = (bf16[1024,1408]{1,0:T(8,128)(2,1)}, bf16[1024,1408]{1,0:T(8,128)(2,1)}, bf16[1024,2048]{1,0:T(8,128)(2,1)}, bf16[1024,2048]{1,0:T(8,128)(2,1)}, f32[256,1408]{1,0:T(8,128)}) custom-call(bf16[1024,2048]{1,0:T(8,128)(2,1)} %all-gather.7.cloned.1.call-done.left_ref, bf16[1024,1408]{1,0:T(8,128)(2,1)} %get-tuple-element.71.hid_ref, ...), custom_call_target="tpu_custom_call" | custom-call | flops 89999998976 | bytes 50000000 | tf_op jit(solution)/shard_map/ffn_backward/pallas_call | solution.py:1187
  506.3 72.6 %ring_scatter_6.1 = f32[256,1408]{1,0:T(8,128)} custom-call(bf16[1024,2048]{1,0:T(8,128)(2,1)} %all-gather.9.cloned.1.call-done.x_ref.left_ref, bf16[1024,1408]{1,0:T(8,128)(2,1)} %get-tuple-element.78.right_ref), custom_call_target="tpu_custom_call" | custom-call | bytes 432537600 | tf_op jit(solution)/shard_map/ring_scatter_6/pallas_call | solution.py:1069
  579.1 2.3 fusion.3
  581.4 2.6 fusion.14
  584.1 1.9 pad.28.fab_ref
  586.0 1.6 fusion.13.z_ref
  587.6 71.2 %ring_scatter_7.1 = f32[256,1408]{1,0:T(8,128)} custom-call(bf16[1024,2048]{1,0:T(8,128)(2,1)} %all-gather.9.cloned.1.call-done.x_ref.left_ref, bf16[1024,1408]{1,0:T(8,128)(2,1)} %get-tuple-element.81.right_ref), custom_call_target="tpu_custom_call" | custom-call | bytes 432537600 | tf_op jit(solution)/shard_map/ring_scatter_7/pallas_call | solution.py:1069
  659.0 10.0 %fusion.48.refs_13_ = f32[1024,1024]{1,0:T(8,128)} fusion(bf16[1024,2048]{1,0:T(8,128)(2,1)} %all-gather.11.cloned.1.call-done.refs_18_, bf16[2048,1024]{1,0:T(8,128)(2,1)} %get-tuple-element.66), kind=kOutput, calls=%fused_computation.151 | convolution fusion | flops 4294967296 | bytes 12582912 | tf_op jit(solution)/shard_map/dot_general | solution.py:1207
  669.0 80.7 %mixer_backward.1 = (bf16[1024,3072]{1,0:T(8,128)(2,1)}, bf16[1024,128]{1,0:T(8,128)(2,1)}, f32[8,512]{1,0:T(8,128)}, f32[8,512]{1,0:T(8,128)}, f32[8,1024]{1,0:...) custom-call(f32[1024,3072]{1,0:T(8,128)} %fusion.47.refs_0_.refs_1_.refs_2_.refs_3_.refs_5_.refs_6_.refs_7_, ...), custom_call_target="tpu_custom_call" | custom-call | flops 40000000000 | bytes 60000000 | tf_op jit(solution)/shard_map/mixer_backward/pallas_call | solution.py:441
  749.7 0.8 bitcast_dynamic-update-slice_fusion
  750.5 0.8 bitcast_dynamic-update-slice_fusion.1
  751.4 0.7 concatenate.395
  752.1 0.8 slice.554
  753.1 0.7 slice.552
  754.1 0.7 slice.553
  755.1 0.6 copy.60
  755.7 3.0 fusion.6
  758.7 0.6 reshape.1392.few_ref
  759.3 0.6 pad.33
  759.9 168.3 %ring_scatter_9.1 = (f32[256,512]{1,0:T(8,128)}, f32[256,512]{1,0:T(8,128)}, f32[256,1024]{1,0:T(8,128)}, f32[256,1024]{1,0:T(8,128)}, f32[16,128]{1,0:T(8,128)}...) custom-call(bf16[1024,2048]{1,0:T(8,128)(2,1)} %all-gather.5.cloned.1.call-done.left_ref, ...), custom_call_target="tpu_custom_call" | custom-call | bytes 943718400 | tf_op jit(solution)/shard_map/ring_scatter_9/pallas_call | solution.py:1029
  928.2 0.7 fusion.30
  928.9 0.6 slice.578
  930.1 0.7 slice.583
  930.8 0.8 fusion.39
  931.5 0.7 reshape.1402
  932.2 0.7 reshape.1403
  932.9 0.7 reshape.1404
  933.6 1.2 slice_bitcast_fusion.2
  934.8 1.3 fusion.28
  936.2 1.3 slice_bitcast_fusion
  937.5 2.3 multiply_convert_fusion
  940.9 1.0 copy-done.15
  941.9 1.3 copy.96
  943.3 0.8 copy.97
  944.1 0.8 copy.98
  944.9 1.0 copy.99
  945.9 1.0 copy.100
  946.8 1.0 copy.101
  947.8 1.1 copy.102
  948.9 1.1 copy.103
  950.0 0.8 copy-done.16
  950.8 1.1 copy.104
  (236 shorter events, 9.9 us)
Async XLA Ops:
  7.2 142.8 %all-gather.5.cloned.1.call-start = ((), (), s32[]{:S(2)}) async-start(), calls=%async_computation.3 | async-start | bytes 5242880 | tf_op jit(solution)/shard_map/all_gather | solution.py:1344
  8.7 0.7 copy-start.37
  8.7 0.7 copy-start.38
  10.1 290.5 %copy-start.1 = (bf16[256,1024]{1,0:T(8,128)(2,1)}, bf16[256,1024]{1,0:T(8,128)(2,1)S(1)}, u32[]{:S(2)}) copy-start(bf16[256,1024]{1,0:T(8,128)(2,1)S(1)} %maximum_select_fusion.1) | copy-start | bytes 1572868
  10.3 290.3 %copy-start.3 = (bf16[256,1024]{1,0:T(8,128)(2,1)}, bf16[256,1024]{1,0:T(8,128)(2,1)S(1)}, u32[]{:S(2)}) copy-start(bf16[256,1024]{1,0:T(8,128)(2,1)S(1)} %maximum_select_fusion.3) | copy-start | bytes 1572868
  10.3 2.5 copy-start.42
  10.3 2.5 copy-start.43
  10.3 2.5 copy-start.40
  10.3 2.6 copy-start.41
  10.3 2.7 copy-start.39
  10.3 4.0 copy-start.23
  10.4 4.0 copy-start.24
  10.4 3.9 copy-start.25
  10.4 3.9 copy-start.26
  10.8 0.6 copy-start.29
  12.7 285.5 %reduce-scatter.4.cloned.1.call-start = ((), (), s32[]{:S(2)}) async-start(), calls=%async_computation.4 | async-start | bytes 5242880 | tf_op jit(solution)/shard_map/reduce_scatter | solution.py:1348
  15.6 133.6 %copy-start.44 = (f32[16]{0:T(128)S(1)}, f32[16]{0:T(128)}, u32[]{:S(2)}) copy-start(f32[16]{0:T(128)} %param.35) | copy-start | bytes 196
  15.6 133.6 %copy-start.45 = (f32[16]{0:T(128)S(1)}, f32[16]{0:T(128)}, u32[]{:S(2)}) copy-start(f32[16]{0:T(128)} %param.34) | copy-start | bytes 196
  147.3 22.9 %copy-start.13 = (bf16[8,8,256]{0,2,1:T(8,128)(2,1)}, bf16[8,8,256]{0,2,1:T(8,128)(2,1)S(1)}, u32[]{:S(2)}) copy-start(bf16[8,8,256]{0,2,1:T(8,128)(2,1)S(1)} %copy.44) | copy-start | bytes 98308
  150.0 20.3 %copy-start = (bf16[1024,2048]{1,0:T(8,128)(2,1)S(1)}, bf16[1024,2048]{1,0:T(8,128)(2,1)}, u32[]{:S(2)}) copy-start(bf16[1024,2048]{1,0:T(8,128)(2,1)} %all-gather.5.cloned.1.call-done.left_ref) | copy-start | bytes 12582916
  235.3 129.1 %all-gather.9.cloned.1.call-start = ((), (), s32[]{:S(2)}) async-start(), calls=%async_computation.6 | async-start | bytes 5242880 | tf_op jit(solution)/shard_map/all_gather | solution.py:1344
  235.4 65.2 %copy-start.27 = (f32[1,2048]{1,0:T(1,128)}, f32[1,2048]{1,0:T(1,128)S(1)}, u32[]{:S(2)}) copy-start(f32[1,2048]{1,0:T(1,128)S(1)} %pad_maximum_fusion.8) | copy-start | bytes 24580
  298.3 2.9 copy-start.5
  300.0 0.6 copy-start.35
  300.6 0.6 copy-start.32
  301.1 1.5 copy-start.17
  302.6 124.2 %all-gather.7.cloned.1.call-start = ((), (), s32[]{:S(2)}) async-start(), calls=%async_computation.5 | async-start | bytes 5242880 | tf_op jit(solution)/shard_map/all_gather | solution.py:1344
  303.8 0.7 copy-start.30
  304.4 0.8 copy-start.9
  305.2 0.8 copy-start.11
  307.2 271.8 %reduce-scatter.6.cloned.1.call-start = ((), (), s32[]{:S(2)}) async-start(), calls=%async_computation.7 | async-start | bytes 5242880 | tf_op jit(solution)/shard_map/reduce_scatter | solution.py:1348
  506.2 152.7 %all-gather.11.cloned.1.call-start = ((), (), s32[]{:S(2)}) async-start(), calls=%async_computation.8 | async-start | bytes 5242880 | tf_op jit(solution)/shard_map/all_gather | solution.py:1344
  506.3 72.7 %copy-start.2 = (bf16[256,1024]{1,0:T(8,128)(2,1)S(1)}, bf16[256,1024]{1,0:T(8,128)(2,1)}, u32[]{:S(2)}) copy-start(bf16[256,1024]{1,0:T(8,128)(2,1)} %copy-done.1) | copy-start | bytes 1572868
  506.3 72.7 %copy-start.4 = (bf16[256,1024]{1,0:T(8,128)(2,1)S(1)}, bf16[256,1024]{1,0:T(8,128)(2,1)}, u32[]{:S(2)}) copy-start(bf16[256,1024]{1,0:T(8,128)(2,1)} %copy-done.3) | copy-start | bytes 1572868
  506.3 72.7 %copy-start.6 = (bf16[256,2048]{1,0:T(8,128)(2,1)S(1)}, bf16[256,2048]{1,0:T(8,128)(2,1)}, u32[]{:S(2)}) copy-start(bf16[256,2048]{1,0:T(8,128)(2,1)} %reduce-scatter.4.cloned.1.call-done) | copy-start | bytes 3145732
  506.3 72.7 %copy-start.28 = (f32[1,2048]{1,0:T(1,128)S(1)}, f32[1,2048]{1,0:T(1,128)}, u32[]{:S(2)}) copy-start(f32[1,2048]{1,0:T(1,128)} %copy-done.27) | copy-start | bytes 24580
  506.3 72.7 %copy-start.33 = (f32[256]{0:T(256)S(1)}, f32[256]{0:T(256)}, u32[]{:S(2)}) copy-start(f32[256]{0:T(256)} %copy-done.32) | copy-start | bytes 3076
  578.9 2.5 copy-start.36
  578.9 2.5 copy-start.10
  579.0 2.5 copy-start.31
  579.0 2.4 copy-start.12
  579.1 2.4 copy-start.14
  584.0 353.5 %reduce-scatter.8.cloned.1.call-start = ((), (), s32[]{:S(2)}) async-start(), calls=%async_computation.9 | async-start | bytes 5242880 | tf_op jit(solution)/shard_map/reduce_scatter | solution.py:1348
  940.3 1.6 copy-start.15
  940.9 2.3 copy-start.34
  941.9 1.4 copy-start.22
  941.9 2.2 copy-start.21
  941.9 3.0 copy-start.20
  943.3 2.6 copy-start.19
  944.9 1.9 copy-start.18
  945.9 1.9 copy-start.7
  946.8 2.1 copy-start.8
  948.9 1.9 copy-start.16
Sparse Core Ops, SparseCore 0:
  12.8 34.6 all-gather.4
  235.4 48.6 reduce-scatter.3
  302.7 33.5 all-gather.8
  338.4 34.4 all-gather.6
  506.4 44.6 reduce-scatter.5
  584.1 35.1 all-gather.10
  659.1 45.1 reduce-scatter.7
